TPU v7x, 128 devices: a whole 4x4x4 slice. The times are simulated.
128 devices in a mesh: seq: 32 (over z, y, core), head: 4 (over x).
Axes of the slice: x: 4, y: 4, z: 4, core: 2. Of those that a mesh axis runs over, the one named last changes fastest.
Arguments:
- tokens: bfloat16 [16384, 2560], P('seq'), may hold values from -6 to 6
- proj_inner: bfloat16 [2560, 5120], P(None, 'head'), may hold values from -0.125 to 0.125
- proj_gate: bfloat16 [2560, 5120], P(None, 'head'), may hold values from -0.125 to 0.125
- proj_bc: bfloat16 [2560, 256], replicated, may hold values from -0.03125 to 0.03125
- proj_step: bfloat16 [2560, 80], P(None, 'head'), may hold values from -0.125 to 0.125
- conv_inner: float32 [4, 5120], P(None, 'head'), may hold values from -3 to 3
- conv_bc: float32 [4, 256], replicated, may hold values from -3 to 3
- offset_inner: float32 [5120], P('head'), may hold values from -3 to 3
- offset_bc: float32 [256], replicated, may hold values from -1.2 to 1.2
- step_bias: float32 [80], P('head'), as said below
- decay_log: float32 [80], P('head'), as said below
- skip_gain: float32 [80], P('head'), may hold values from 0.5 to 2
- norm_weight: float32 [5120], P('head'), may hold values from 0.25 to 1.75
- out_weight: bfloat16 [5120, 2560], P('head'), may hold values from -0.078125 to 0.078125
Outputs:
- layer_out: bfloat16 [16384, 2560], P(('seq', 'head'))
Inputs may be any that keep to these rules, and one draw needn't show every extreme that they name: step_bias holds one value for each head, the same for every token. decay_log holds one value for each head, the same for every token.
All inputs are finite; a program needn't handle non-finite values.
Results may differ from a plain program's by a relative error of at most 0.013.
Values may be sent and summed in bfloat16 or wider, within the bound.
No kernel may reach another device: no remote copies, remote signals or barrier semaphores. Data moves between devices by JAX's collectives and lax.ppermute only.
A program may use at most 128 MiB of HBM per device.

v0:
```python
import jax
import jax.numpy as jnp
from jax import lax
from jax.sharding import Mesh
from jax.sharding import PartitionSpec as P

HEADS = 80
HEADDIM = 64
STATE = 128
KERNEL = 4
SPAN = 128
SEQ = ("seq_0", "seq_1", "seq_2")
SEQ_HEAD = ("seq_0", "seq_1", "seq_2", "head")


def passed_along(block, axis, distance):
    devices = range(lax.axis_size(axis))
    route = [(i - distance, i) for i in devices if i - distance in devices]
    return lax.ppermute(block, axis, route)


def neutral_like(x, identity):
    return jax.tree.map(
        lambda a, e: jnp.broadcast_to(jnp.asarray(e, a.dtype), a.shape), x, identity
    )


def carried_in(x, axes, combine, identity):
    before = start = neutral_like(x, identity)
    running = x
    for axis in reversed(axes):
        size, index = (lax.axis_size(axis), lax.axis_index(axis))
        pieces = jax.tree.map(lambda part: lax.all_gather(part, axis), running)
        inside, running = (start, start)
        for k in range(size):
            passed = k < index
            running = combine(running, jax.tree.map(lambda part: part[k], pieces))
            inside = jax.tree.map(lambda new, old: jnp.where(passed, new, old), running, inside)
        before = combine(inside, before)
    return before


def sent_to_all(x, axis):
    copies = jnp.broadcast_to(x, (lax.axis_size(axis), *x.shape))
    return lax.all_to_all(copies, axis, split_axis=0, concat_axis=0, tiled=True)


def taken_together(x, axis):
    return sent_to_all(x, axis).sum(axis=0)


def in_blocks(x, dim, size):
    before, after = (x.shape[:dim], x.shape[dim + 1 :])
    return jnp.moveaxis(x.reshape(*before, size, -1, *after), dim, 0)


def summed_on_arrival(x, axis, dim):
    pieces = in_blocks(x, dim, lax.axis_size(axis))
    arrived = lax.all_to_all(pieces, axis, split_axis=0, concat_axis=0, tiled=True)
    return arrived.astype(jnp.float32).sum(axis=0)


def causal(padded, weight, offset, length):
    summed = jnp.zeros((length, weight.shape[1]), jnp.float32) + offset[None, :]
    for tap_index in range(weight.shape[0]):
        summed = summed + weight[tap_index][None, :] * padded[
            tap_index : tap_index + length
        ].astype(jnp.float32)
    return jax.nn.silu(summed).astype(jnp.bfloat16)


def combine_states(first_part, second_part):
    return (
        first_part[0] * second_part[0],
        second_part[0][:, None, None] * first_part[1] + second_part[1],
    )


def per_device(
    tokens,
    proj_inner,
    proj_gate,
    proj_bc,
    proj_step,
    conv_inner,
    conv_bc,
    offset_inner,
    offset_bc,
    step_bias,
    decay_log,
    skip_gain,
    norm_weight,
    out_weight,
):
    tok_rows = tokens.shape[0]
    head_count = step_bias.shape[0]
    inner_raw = jnp.dot(tokens, proj_inner, preferred_element_type=jnp.float32).astype(jnp.bfloat16)
    gate_raw = jnp.dot(tokens, proj_gate, preferred_element_type=jnp.float32).astype(jnp.bfloat16)
    bc_raw = jnp.dot(tokens, proj_bc, preferred_element_type=jnp.float32).astype(jnp.bfloat16)
    step_raw = jnp.dot(tokens, proj_step, preferred_element_type=jnp.float32)
    edge_inner, edge_bc = passed_along(
        (inner_raw[tok_rows - (KERNEL - 1) :], bc_raw[tok_rows - (KERNEL - 1) :]), SEQ, 1
    )
    inner_conv = causal(
        jnp.concatenate([edge_inner, inner_raw], 0), conv_inner, offset_inner, tok_rows
    )
    bc_conv = causal(jnp.concatenate([edge_bc, bc_raw], 0), conv_bc, offset_bc, tok_rows)
    step_sizes = jax.nn.softplus(step_raw + step_bias[None, :])
    log_decay = -jnp.exp(decay_log)[None, :] * step_sizes
    span_total = tok_rows // SPAN
    inner_blocks = inner_conv.reshape(span_total, SPAN, head_count, HEADDIM)
    write_blocks = bc_conv[:, :STATE].reshape(span_total, SPAN, STATE)
    read_blocks = bc_conv[:, STATE:].reshape(span_total, SPAN, STATE)
    step_blocks = step_sizes.reshape(span_total, SPAN, head_count)
    cumulative = jnp.cumsum(log_decay.reshape(span_total, SPAN, head_count), axis=1)
    scores = jnp.einsum(
        "cin,cjn->cij", read_blocks, write_blocks, preferred_element_type=jnp.float32
    )
    cum_t = jnp.swapaxes(cumulative, 1, 2)
    step_t = jnp.swapaxes(step_blocks, 1, 2)
    log_gaps = cum_t[:, :, :, None] - cum_t[:, :, None, :]
    causal_mask = jnp.tril(jnp.ones((SPAN, SPAN), bool))[None, None]
    decays = jnp.where(causal_mask, jnp.exp(jnp.where(causal_mask, log_gaps, 0.0)), 0.0)
    weights = (scores[:, None] * decays * step_t[:, :, None, :]).astype(jnp.bfloat16)
    intra_out = jnp.einsum(
        "chij,cjhp->cihp", weights, inner_blocks, preferred_element_type=jnp.float32
    )
    end_weights = jnp.exp(cumulative[:, -1:, :] - cumulative) * step_blocks
    local_states = jnp.einsum(
        "cjn,cjh,cjhp->chnp",
        write_blocks.astype(jnp.float32),
        end_weights,
        inner_blocks.astype(jnp.float32),
        precision=lax.Precision.HIGHEST,
    )
    span_decay = jnp.exp(cumulative[:, -1, :])
    read_wide = read_blocks.astype(jnp.float32)
    read_scale = jnp.exp(cumulative)[..., None]
    running = jnp.zeros((head_count, STATE, HEADDIM), jnp.float32)
    prior_states = []
    for number in range(span_total):
        prior_states.append(running)
        running = span_decay[number][:, None, None] * running + local_states[number]
    device_decay = jnp.prod(span_decay, axis=0)
    prefix_decay, incoming = carried_in(
        (device_decay, running),
        SEQ,
        combine_states,
        (jnp.ones_like(device_decay), jnp.zeros_like(running)),
    )
    inter_out = read_scale * jnp.einsum(
        "cin,chnp->cihp", read_wide, jnp.stack(prior_states), precision=lax.Precision.HIGHEST
    )
    leading_list = []
    product = jnp.ones((head_count,), jnp.float32)
    for number in range(span_total):
        leading_list.append(product)
        product = product * span_decay[number]
    leading = jnp.stack(leading_list)
    inter_out = inter_out + read_scale * leading[:, None, :, None] * jnp.einsum(
        "cin,hnp->cihp", read_wide, incoming, precision=lax.Precision.HIGHEST
    )
    mixed_out = (intra_out + inter_out).reshape(tok_rows, head_count, HEADDIM) + skip_gain[
        None, :, None
    ] * inner_conv.reshape(tok_rows, head_count, HEADDIM).astype(jnp.float32)
    gated_pre = mixed_out.reshape(tok_rows, head_count * HEADDIM) * jax.nn.silu(
        gate_raw.astype(jnp.float32)
    )
    squares = taken_together(jnp.sum(gated_pre * gated_pre, axis=1), "head")
    scale = 1.0 / jnp.sqrt(squares / (HEADS * HEADDIM) + 0.25)
    gated_out = (gated_pre * scale[:, None] * norm_weight[None, :]).astype(jnp.bfloat16)
    out_share = summed_on_arrival(
        jnp.dot(gated_out, out_weight, preferred_element_type=jnp.float32).astype(jnp.bfloat16),
        "head",
        0,
    )
    return out_share.astype(jnp.bfloat16)


def solution(mesh):
    torus = Mesh(
        mesh.devices.reshape(4, 4, 2, mesh.shape["head"]), ("seq_0", "seq_1", "seq_2", "head")
    )
    return jax.shard_map(
        per_device,
        mesh=torus,
        in_specs=(
            P(SEQ, None),
            P(None, "head"),
            P(None, "head"),
            P(),
            P(None, "head"),
            P(None, "head"),
            P(),
            P("head"),
            P(),
            P("head"),
            P("head"),
            P("head"),
            P("head"),
            P("head", None),
        ),
        out_specs=P(SEQ_HEAD, None),
        check_vma=False,
    )
```

profile of v0, /device:TPU:0, one launch (start us, length us, event | category | flops | bytes accessed | tf_op | source)
XLA Modules:
  0.0 222.9 jit_solution(7218201387096128753)
XLA Ops:
  6.5 1.7 copy-done
  8.3 2.2 convolution_convert_fusion.3
  10.4 0.6 slice.207
  11.2 1.4 collective-permute-start.1
  12.6 6.4 %convolution_convert_fusion.2 = bf16[512,1280]{1,0:T(8,128)(2,1)S(1)} fusion(bf16[512,2560]{1,0:T(8,128)(2,1)S(1)} %copy-done, bf16[2560,1280]{1,0:T(8,128)(2,1)} %param.15), kind=kOutput, calls=%fused_computation.5 | convolution fusion | flops 3356098560 | bytes 10485760 | tf_op jit(solution)/shard_map/dot_general | solution.py:97
  19.0 1.1 copy-done.4
  20.1 4.3 %collective-permute-start = (bf16[3,1280]{1,0:T(4,128)(2,1)S(1)}, bf16[3,1280]{1,0:T(4,128)(2,1)S(1)}, u32[]{:S(2)}, u32[]{:S(2)}) collective-permute-start(bf16[3,1280]{1,0:T(4,128)(2,1)S(1)} %slice.202), channel_id=1, source_target_pairs={{0,4},{4,8},{8,12},{12,16},{16,20},{20,24},{24,28},{28,32},{32,36}... | collective-permute-start | bytes 23048 | tf_op jit(solution)/shard_map/ppermute | solution.py:19
  24.5 0.8 broadcast_multiply_fusion.1
  26.6 0.9 fusion.67
  27.7 1.8 multiply_convert_fusion.5
  29.5 0.7 fusion.68
  30.2 5.2 %multiply_convert_fusion.3 = bf16[512,1280]{1,0:T(8,128)(2,1)} fusion(bf16[512,1280]{1,0:T(8,128)(2,1)} %copy-done.4, bf16[3,1280]{1,0:T(4,128)(2,1)S(1)} %collective-permute-done, f32[1280]{0:T(1024)S(1)} %get-tuple-element.7, f32[1280]{0:T(1024)S(1)} %get-tuple-element.8, f32[1280]{0:T(1024)S(1)} %get-tuple-element.6, f32[1280]{0:T(1024)S(1)} %get-tuple-element.5, ...), kind=kLoop, calls=%fused_computation.24 | loop fusion | flops 17039360 | bytes 2654720 | tf_op jit(solution)/shard_map/convert_element_type | solution.py:69
  35.4 2.4 %copy.65 = bf16[512,1280]{0,1:T(8,128)(2,1)} copy(bf16[512,1280]{1,0:T(8,128)(2,1)} %multiply_convert_fusion.3) | data formatting | bytes 2621440 | tf_op jit(solution)/shard_map/convert_element_type | solution.py:69
  37.8 3.6 %reshape.130 = bf16[4,128,20,64]{1,0,3,2:T(4,128)(2,1)} reshape(bf16[512,1280]{0,1:T(8,128)(2,1)} %copy.65) | data formatting | bytes 2621440 | tf_op jit(solution)/shard_map/reshape | solution.py:111
  41.4 1.9 convert_multiply_fusion.1
  43.3 1.4 fusion.13
  44.7 1.5 slice_add_fusion.10
  46.3 1.2 dynamic-slice.1
  47.5 1.3 dynamic-slice
  50.0 0.8 dynamic-update-slice
  50.8 2.4 %all-reduce = f32[40]{0:T(128)S(1)} all-reduce(f32[40]{0:T(128)S(1)} %dynamic-update-slice), channel_id=2, replica_groups=mesh['seq_0'=4,'seq_1'=4,'seq_2'=2,'head'=4] {'seq_2'}, use_global_device_ids=true, to_apply=%add | all-reduce | flops 40 | bytes 320
  53.3 0.7 fusion.66
  53.9 10.7 %all-reduce.1 = f32[80]{0:T(128)S(1)} all-reduce(f32[80]{0:T(128)S(1)} %get-tuple-element.45), channel_id=3, replica_groups=mesh['seq_0'=4,'seq_1'=4,'seq_2'=2,'head'=4] {'seq_1'}, use_global_device_ids=true, to_apply=%add.1 | all-reduce | flops 80 | bytes 640
  64.6 0.6 multiply_bitcast_fusion.1
  65.3 2.3 %slice_add_fusion.8 = f32[1,20,128,64]{2,3,1,0:T(8,128)} fusion(f32[2,20,128,64]{2,3,1,0:T(8,128)} %all-gather.7.cloned.1.call-done, f32[20]{0:T(128)S(1)} %get-tuple-element.42, f32[20]{0:T(128)} %get-tuple-element.46), kind=kLoop, calls=%fused_computation.49 | loop fusion | flops 491520 | bytes 1966240 | tf_op jit(solution)/shard_map/add | solution.py:75
  67.6 0.6 fusion.70
  68.3 34.2 %all-gather.9.cloned.1.call-done = f32[4,20,128,64]{2,3,1,0:T(8,128)} async-done(((f32[1,20,128,64]{2,3,1,0:T(8,128)}), f32[4,20,128,64]{2,3,1,0:T(8,128)}) %all-gather.9.cloned.1.call-update) | async-done | bytes 2621456 | tf_op jit(solution)/shard_map/all_gather | solution.py:33
  102.5 2.8 %slice_add_fusion.4 = f32[1,20,128,64]{2,3,1,0:T(8,128)} fusion(f32[4,20,128,64]{2,3,1,0:T(8,128)} %all-gather.9.cloned.1.call-done, f32[20]{0:T(128)} %get-tuple-element.44, f32[20]{0:T(128)} %get-tuple-element.43, f32[20]{0:T(128)S(1)} %get-tuple-element.38, f32[20]{0:T(128)S(1)} %copy-done.13), kind=kLoop, calls=%fused_computation.45 | loop fusion | flops 1146880 | bytes 3277120 | tf_op jit(solution)/shard_map/add | solution.py:75
  105.3 1.4 copy.69
  106.7 0.7 copy.67
  107.4 1.1 copy.75
  108.5 1.1 copy.71
  109.6 0.7 mul.500
  110.4 10.3 %all-gather.2 = f32[4,1,20]{2,1,0:T(1,128)S(1)} all-gather(f32[1,1,20]{2,1,0:T(1,128)} %get-tuple-element.37), channel_id=1, replica_groups=mesh['seq_0'=4,'seq_1'=4,'seq_2'=2,'head'=4] {'seq_0'}, dimensions={0}, use_global_device_ids=true | all-gather | bytes 400 | tf_op jit(solution)/shard_map/all_gather | solution.py:33
  120.7 1.2 fusion.71
  122.0 1.6 pad_maximum_fusion
  123.6 2.8 %fusion.72 = f32[4,128,1280]{1,2,0} fusion(bf16[4,128,128]{2,1,0:T(8,128)(2,1)S(1)} %bitcast.85, f32[4,128,1280]{1,2,0:T(8,128)S(1)} %bitcast.78), kind=kOutput, calls=%fused_computation.139 | convolution fusion | flops 1006632960 | bytes 5373952
  126.5 3.6 %fusion = f32[4,20,64,128]{3,2,1,0:T(8,128)} fusion(f32[4,20,128]{2,1,0:T(8,128)S(1)} %copy-done.10, f32[4,20,128]{2,1,0:T(8,128)S(1)} %copy-done.9, f32[4,128,128]{2,1,0:T(8,128)S(1)} %fusion.71, pred[128,128]{1,0:T(8,128)(4,1)S(1)} %iota_compare_fusion, bf16[4,128,20,64]{1,0,3,2:T(4,128)(2,1)S(1)} %copy-done.2), kind=kOutput, calls=%fused_computation.6 | convolution fusion | flops 175636480 | bytes 4292608 | tf_op jit(solution)/shard_map/chij,cjhp->cihp/dot_general | solution.py:125
  130.1 10.8 %all-gather.11.cloned.1.call-done = f32[4,20,128,64]{2,3,1,0:T(8,128)} async-done(((f32[1,20,128,64]{2,3,1,0:T(8,128)}), f32[4,20,128,64]{2,3,1,0:T(8,128)}) %all-gather.11.cloned.1.call-update) | async-done | bytes 2621456 | tf_op jit(solution)/shard_map/all_gather | solution.py:33
  140.9 6.0 %bitcast_add_fusion = f32[4,128,20,64]{1,3,2,0:T(8,128)S(1)} fusion(f32[4,20,64,128]{3,2,1,0:T(8,128)} %fusion, f32[4,128,20,64]{1,3,2,0:T(8,128)} %bitcast.81, bf16[4,128,128,1]{2,1,3,0:T(8,128)(2,1)S(1)} %bitcast.86, f32[4,128,20]{1,2,0:T(8,128)S(1)} %copy.75, f32[4,128,20]{1,2,0:T(8,128)S(1)} %copy.71, ...), kind=kOutput, calls=%fused_computation.13 | convolution fusion | flops 1013678080 | bytes 14631722 | tf_op jit(solution)/shard_map/cin,hnp->cihp/dot_general | solution.py:160
  146.9 1.9 copy.76
  148.9 1.8 copy.91
  150.7 3.2 %copy.77 = f32[512,1280]{1,0:T(8,128)} copy(f32[512,1280]{0,1:T(8,128)} %bitcast.80) | data formatting | bytes 5242880 | tf_op jit(solution)/shard_map/reshape | solution.py:163
  153.9 8.7 %multiply_reduce_fusion = (f32[512]{0:T(512)S(1)}, f32[512,1280]{1,0:T(8,128)}) fusion(bf16[512,2560]{1,0:T(8,128)(2,1)S(1)} %copy-done, bf16[2560,1280]{1,0:T(8,128)(2,1)} %param.16, f32[512,1280]{1,0:T(8,128)} %copy.77, bf16[512,1280]{1,0:T(8,128)(2,1)} %multiply_convert_fusion.3, f32[1280]{0:T(1024)S(1)} %mul.501), kind=kOutput, calls=%fused_computation.17 | convolution fusion | flops 3363307008 | bytes 15735808 | tf_op jit(solution)/shard_map/dot_general | solution.py:98
  162.6 9.4 %all_to_all.11 = f32[4,1,512]{2,1,0:T(1,128)S(1)} all-to-all(f32[4,1,512]{2,1,0:T(1,128)S(1)} %broadcast_in_dim.24), channel_id=1, replica_groups=mesh['seq_0'=4,'seq_1'=4,'seq_2'=2,'head'=4] {'head'}, dimensions={0} | all-to-all | bytes 16384 | tf_op jit(solution)/shard_map/all_to_all | solution.py:45
  172.0 7.3 %convolution_convert_fusion = bf16[512,2560]{1,0:T(8,128)(2,1)S(1)} fusion(bf16[1280,2560]{1,0:T(8,128)(2,1)} %param.27, f32[512,1280]{1,0:T(8,128)} %get-tuple-element.50, f32[1280]{0:T(1024)S(1)} %copy-done.19, f32[512]{0:T(512)S(1)} %add_rsqrt_fusion), kind=kOutput, calls=%fused_computation.1 | convolution fusion | flops 3358720000 | bytes 11803648 | tf_op jit(solution)/shard_map/dot_general | solution.py:173
  179.3 33.9 %all_to_all.12 = bf16[4,128,2560]{2,1,0:T(8,128)(2,1)} all-to-all(bf16[4,128,2560]{2,1,0:T(8,128)(2,1)S(1)} %bitcast.82), channel_id=1, replica_groups=mesh['seq_0'=4,'seq_1'=4,'seq_2'=2,'head'=4] {'head'}, dimensions={0} | all-to-all | bytes 5242880 | tf_op jit(solution)/shard_map/all_to_all | solution.py:59
  213.2 3.1 %reduce_sum.32 = bf16[128,2560]{1,0:T(8,128)(2,1)} reduce(bf16[4,128,2560]{2,1,0:T(8,128)(2,1)} %all_to_all.12, bf16[]{:T(256)} %constant.50.clone.1), dimensions={0}, to_apply=%region_4.5 | reduce | flops 983040 | bytes 3276802 | tf_op jit(solution)/shard_map/reduce_sum | solution.py:60
  (72 shorter events, 1.9 us)
Async XLA Ops:
  6.5 1.7 copy-start
  6.5 58.7 %all-gather.7.cloned.1.call-start = ((), (), s32[]{:S(2)}) async-start(), calls=%async_computation.2 | async-start | bytes 1966080 | tf_op jit(solution)/shard_map/all_gather | solution.py:33
  10.4 0.7 copy-start.7
  11.1 13.3 %copy-start.20 = (f32[20]{0:T(128)S(1)}, f32[20]{0:T(128)}, u32[]{:S(2)}) copy-start(f32[20]{0:T(128)} %param.24) | copy-start | bytes 244
  11.1 13.3 %copy-start.8 = (bf16[2560,20]{0,1:T(8,128)(2,1)S(1)}, bf16[2560,20]{0,1:T(8,128)(2,1)}, u32[]{:S(2)}) copy-start(bf16[2560,20]{0,1:T(8,128)(2,1)} %param.18) | copy-start | bytes 307204
  11.1 13.3 %copy-start.18 = (f32[20]{0:T(128)S(1)}, f32[20]{0:T(128)}, u32[]{:S(2)}) copy-start(f32[20]{0:T(128)} %param.23) | copy-start | bytes 244
  11.2 16.5 %collective-permute-start.1 = (bf16[3,256]{1,0:T(4,128)(2,1)}, bf16[3,256]{1,0:T(4,128)(2,1)S(1)}, u32[]{:S(2)}, u32[]{:S(2)}) collective-permute-start(bf16[3,256]{1,0:T(4,128)(2,1)} %slice.207), channel_id=1, source_target_pairs={{0,4},{4,8},{8,12},{12,16},{16,20},{20,24},{24,28},{28,32},{32,36}... | collective-permute-start | bytes 4616 | tf_op jit(solution)/shard_map/ppermute | solution.py:19
  19.0 1.1 copy-start.4
  20.1 5.4 %copy-start.15 = (f32[4,256]{1,0:T(4,128)S(1)}, f32[4,256]{1,0:T(4,128)}, u32[]{:S(2)}) copy-start(f32[4,256]{1,0:T(4,128)} %param.20) | copy-start | bytes 12292
  20.1 10.1 %collective-permute-start = (bf16[3,1280]{1,0:T(4,128)(2,1)S(1)}, bf16[3,1280]{1,0:T(4,128)(2,1)S(1)}, u32[]{:S(2)}, u32[]{:S(2)}) collective-permute-start(bf16[3,1280]{1,0:T(4,128)(2,1)S(1)} %slice.202), channel_id=1, source_target_pairs={{0,4},{4,8},{8,12},{12,16},{16,20},{20,24},{24,28},{28,32},{32,36}... | collective-permute-start | bytes 23048 | tf_op jit(solution)/shard_map/ppermute | solution.py:19
  24.5 3.1 %copy-start.11 = (f32[4,1280]{1,0:T(4,128)S(1)}, f32[4,1280]{1,0:T(4,128)}, u32[]{:S(2)}) copy-start(f32[4,1280]{1,0:T(4,128)} %param.19) | copy-start | bytes 61444
  25.3 4.9 %copy-start.12 = (f32[1280]{0:T(1024)S(1)}, f32[1280]{0:T(1024)}, u32[]{:S(2)}) copy-start(f32[1280]{0:T(1024)} %param.21) | copy-start | bytes 15364
  25.3 1.2 copy-start.6
  30.2 13.1 %copy-start.5 = (bf16[512,128]{1,0:T(8,128)(2,1)}, bf16[512,128]{1,0:T(8,128)(2,1)S(1)}, u32[]{:S(2)}) copy-start(bf16[512,128]{1,0:T(8,128)(2,1)S(1)} %get-tuple-element.20) | copy-start | bytes 393220
  46.2 56.3 %all-gather.9.cloned.1.call-start = ((), (), s32[]{:S(2)}) async-start(), calls=%async_computation.3 | async-start | bytes 3276800 | tf_op jit(solution)/shard_map/all_gather | solution.py:33
  65.3 37.2 %copy-start.13 = (f32[20]{0:T(128)S(1)}, f32[20]{0:T(128)}, u32[]{:S(2)}) copy-start(f32[20]{0:T(128)} %get-tuple-element.39) | copy-start | bytes 244
  67.6 73.3 %all-gather.11.cloned.1.call-start = ((), (), s32[]{:S(2)}) async-start(), calls=%async_computation.4 | async-start | bytes 3276800 | tf_op jit(solution)/shard_map/all_gather | solution.py:33
  122.0 1.6 copy-start.3
  123.6 2.8 %copy-start.2 = (bf16[4,128,20,64]{1,0,3,2:T(4,128)(2,1)S(1)}, bf16[4,128,20,64]{1,0,3,2:T(4,128)(2,1)}, u32[]{:S(2)}) copy-start(bf16[4,128,20,64]{1,0,3,2:T(4,128)(2,1)} %reshape.130) | copy-start | bytes 3932164
  123.6 2.8 %copy-start.9 = (f32[4,20,128]{2,1,0:T(8,128)S(1)}, f32[4,20,128]{2,1,0:T(8,128)}, u32[]{:S(2)}) copy-start(f32[4,20,128]{2,1,0:T(8,128)} %copy.67) | copy-start | bytes 122884
  123.6 2.8 %copy-start.10 = (f32[4,20,128]{2,1,0:T(8,128)S(1)}, f32[4,20,128]{2,1,0:T(8,128)}, u32[]{:S(2)}) copy-start(f32[4,20,128]{2,1,0:T(8,128)} %copy.69) | copy-start | bytes 122884
  126.4 14.5 %copy-start.1 = (f32[1,20,128,64]{2,3,1,0:T(8,128)S(1)}, f32[1,20,128,64]{2,3,1,0:T(8,128)}, u32[]{:S(2)}) copy-start(f32[1,20,128,64]{2,3,1,0:T(8,128)} %slice_add_fusion.8) | copy-start | bytes 1966084
  126.4 14.5 %copy-start.14 = (f32[20]{0:T(128)S(1)}, f32[20]{0:T(128)}, u32[]{:S(2)}) copy-start(f32[20]{0:T(128)} %get-tuple-element.44) | copy-start | bytes 244
  126.4 14.5 %copy-start.16 = (f32[20]{0:T(128)S(1)}, f32[20]{0:T(128)}, u32[]{:S(2)}) copy-start(f32[20]{0:T(128)} %get-tuple-element.40) | copy-start | bytes 244
  126.4 14.5 %copy-start.17 = (f32[20]{0:T(128)S(1)}, f32[20]{0:T(128)}, u32[]{:S(2)}) copy-start(f32[20]{0:T(128)} %get-tuple-element.41) | copy-start | bytes 244
  153.9 18.1 %copy-start.19 = (f32[1280]{0:T(1024)S(1)}, f32[1280]{0:T(1024)}, u32[]{:S(2)}) copy-start(f32[1280]{0:T(1024)} %param.26) | copy-start | bytes 15364
Sparse Core Ops, SparseCore 0:
  46.3 14.1 all-gather.6
  67.7 34.7 all-gather.8
  105.4 35.4 all-gather.10
where the time goes:
time: 224 us; the launch traced here: 223 us
  blocking collectives  66.8 us (30%)
  waiting for transfers between devices  45.1 us (20%)
  matrix products  40.4 us (18%)
  local copies, waits for them, and re-layouts  26.8 us (12%)
  other arithmetic  23.3 us (10%)
  between operations  14.7 us (7%)
  starting transfers between devices  5.82 us (3%)
    all_gather x3, waiting for transfers between devices, carried_in(): pieces = jax.tree.map(lambda part: lax.all_gather(part, axis), running)  45 us
    all_to_all x1, blocking collectives, summed_on_arrival(): lax.all_to_all(pieces, axis, split_axis=0, concat_axis=0, tiled=True)  33.9 us
    unnamed x2, blocking collectives  13.2 us
    all_gather x1, blocking collectives, carried_in(): pieces = jax.tree.map(lambda part: lax.all_gather(part, axis), running)  10.3 us
    all_to_all x1, blocking collectives, sent_to_all(): return lax.all_to_all(copies, axis, split_axis=0, concat_axis=0, tiled=True)  9.36 us
    dot_general x1, matrix products, per_device(): jnp.dot(tokens, proj_gate, preferred_element_type=jnp.float32)  8.71 us
    unnamed x48, local copies, waits for them, and re-layouts  8.04 us
    dot_general x1, matrix products, per_device(): jnp.dot(gated_out, out_weight, preferred_element_type=jnp.float32)  7.28 us
  transfers between devices with their start and end apart: 5, of which 2 were waited for; matrix products, arithmetic and copies ran while one was open for 14% of the time, Pallas kernels for 0%

commit v1 on v0

v1 whole, which is shorter than its diff:
```python
import functools

import jax
import jax.numpy as jnp
from jax import lax
from jax.experimental import pallas as pl
from jax.experimental.pallas import tpu as pltpu
from jax.sharding import Mesh
from jax.sharding import PartitionSpec as P

HEADS = 80
HEADDIM = 64
STATE = 128
KERNEL = 4
SPAN = 128
LANES = 128
EDGE = 8
BLOCK = 256
SEQ = ("seq_0", "seq_1", "seq_2")
SEQ_HEAD = ("seq_0", "seq_1", "seq_2", "head")

F32 = jnp.float32
BF16 = jnp.bfloat16


def dot(a, b):
    return jnp.dot(a, b, preferred_element_type=F32)


def silu(v):
    return v * (0.5 + 0.5 * jnp.tanh(0.5 * v))


def lane_pair(first, second):
    lane = lax.broadcasted_iota(jnp.int32, (first.shape[0], LANES), 1)
    return jnp.where(lane < HEADDIM, first, second)


def front_kernel(
    tok, edge, w_bc, w_step, w_in, taps, offset, taps_bc, offset_bc, step_bias, decay_log,
    x_out, bc_out, cum_out, dt_out, lead_out, local_out, prior_out, decay_out,
    padded, end_w, span_d, write_t,
):
    step = pl.program_id(0)
    rows = tok.shape[0]
    spans = rows // SPAN
    heads = step_bias.shape[1]
    per = BLOCK // HEADDIM
    groups = heads // per

    def conv(weight, tap, off):
        padded[EDGE:, :] = dot(tok[...], weight).astype(BF16).astype(F32)
        padded[:EDGE, :] = dot(edge[...], weight).astype(BF16).astype(F32)
        total = off + tap[0:1, :] * padded[EDGE - 3 : EDGE - 3 + rows, :]
        for k in range(1, KERNEL):
            total = total + tap[k : k + 1, :] * padded[EDGE - 3 + k : EDGE - 3 + k + rows, :]
        return silu(total).astype(BF16)

    @pl.when(step == 0)
    def _():
        bc = conv(w_bc[...], taps_bc, offset_bc[...])
        bc_out[...] = bc
        for s in range(spans):
            block = bc[s * SPAN : (s + 1) * SPAN, :STATE].astype(F32)
            write_t[s] = jnp.transpose(block).astype(BF16)
        v = dot(tok[...], w_step[...]) + step_bias[...]
        dt = jnp.maximum(v, 0.0) + jnp.log1p(jnp.exp(-jnp.abs(v)))
        log_decay = -jnp.exp(decay_log[...]) * dt
        cum_out[...] = jnp.zeros_like(cum_out)
        dt_out[...] = jnp.zeros_like(dt_out)
        lead_out[...] = jnp.zeros_like(lead_out)
        dt_out[:, :heads] = dt
        row = lax.broadcasted_iota(jnp.int32, (SPAN, SPAN), 0)
        col = lax.broadcasted_iota(jnp.int32, (SPAN, SPAN), 1)
        lower = (row >= col).astype(F32)
        lead = jnp.zeros((1, heads), F32)
        for s in range(spans):
            at = slice(s * SPAN, (s + 1) * SPAN)
            cum = jnp.dot(
                lower, log_decay[at], preferred_element_type=F32, precision=lax.Precision.HIGHEST
            )
            cum_out[at, :heads] = cum
            lead_out[at, :heads] = jnp.exp(cum + lead)
            last = cum[SPAN - 1 :, :]
            lead = lead + last
            ends = jnp.exp(last - cum) * dt[at]
            gone = jnp.exp(last)
            for g in range(groups):
                end_w[g, at, :per] = ends[:, g * per : (g + 1) * per]
                span_d[g, s : s + 1, :per] = gone[:, g * per : (g + 1) * per]
        total = jnp.exp(lead)
        for g in range(groups):
            span_d[g, spans : spans + 1, :per] = total[:, g * per : (g + 1) * per]

    @pl.when(step > 0)
    def _():
        g = step - 1
        x = conv(w_in[...], taps, offset[...])
        x_out[...] = x
        ends = end_w[g]
        gone = span_d[g]
        wide = jnp.concatenate(
            [lane_pair(ends[:, t : t + 1], ends[:, t + 1 : t + 2]) for t in range(0, per, 2)], axis=1
        )
        gone_wide = jnp.concatenate(
            [lane_pair(gone[:, t : t + 1], gone[:, t + 1 : t + 2]) for t in range(0, per, 2)], axis=1
        )
        weighted = (x.astype(F32) * wide).astype(BF16)
        running = jnp.zeros((STATE, BLOCK), F32)
        tiles = BLOCK // LANES
        for s in range(spans):
            if s > 0:
                for t in range(tiles):
                    prior_out[s - 1, t] = running[:, t * LANES : (t + 1) * LANES].astype(BF16)
            local = dot(write_t[s], weighted[s * SPAN : (s + 1) * SPAN])
            running = gone_wide[s : s + 1] * running + local
        for t in range(tiles):
            local_out[t] = running[:, t * LANES : (t + 1) * LANES].astype(BF16)
            decay_out[t] = jnp.broadcast_to(
                gone_wide[spans : spans + 1, t * LANES : (t + 1) * LANES], (8, LANES)
            )


def front(tokens, edge, w_bc, w_step, w_in, taps, offset, taps_bc, offset_bc, step_bias, decay_log):
    rows, width = tokens.shape
    channels = w_in.shape[1]
    heads = step_bias.shape[1]
    groups = channels // BLOCK
    spans = rows // SPAN
    tiles = channels // LANES
    per_block = BLOCK // LANES

    def whole(a):
        return pl.BlockSpec(a.shape, lambda i: (0,) * a.ndim)

    def late(shape, dim):
        return pl.BlockSpec(
            shape,
            lambda i: tuple(jnp.maximum(i - 1, 0) if d == dim else 0 for d in range(len(shape))),
        )

    head_shape = jax.ShapeDtypeStruct((rows, LANES), F32)
    head_spec = pl.BlockSpec((rows, LANES), lambda i: (0, 0))
    return pl.pallas_call(
        front_kernel,
        grid=(groups + 1,),
        in_specs=[
            whole(tokens), whole(edge), whole(w_bc), whole(w_step),
            late((width, BLOCK), 1), late((KERNEL, BLOCK), 1), late((1, BLOCK), 1),
            whole(taps_bc), whole(offset_bc), whole(step_bias), whole(decay_log),
        ],
        out_specs=[
            late((rows, BLOCK), 1),
            pl.BlockSpec((rows, 2 * STATE), lambda i: (0, 0)),
            head_spec, head_spec, head_spec,
            late((per_block, STATE, LANES), 0),
            late((spans - 1, per_block, STATE, LANES), 1),
            late((per_block, 8, LANES), 0),
        ],
        out_shape=[
            jax.ShapeDtypeStruct((rows, channels), BF16),
            jax.ShapeDtypeStruct((rows, 2 * STATE), BF16),
            head_shape, head_shape, head_shape,
            jax.ShapeDtypeStruct((tiles, STATE, LANES), BF16),
            jax.ShapeDtypeStruct((spans - 1, tiles, STATE, LANES), BF16),
            jax.ShapeDtypeStruct((tiles, 8, LANES), F32),
        ],
        scratch_shapes=[
            pltpu.VMEM((rows + EDGE, BLOCK), F32),
            pltpu.VMEM((groups, rows, LANES), F32),
            pltpu.VMEM((groups, 8, LANES), F32),
            pltpu.VMEM((spans, STATE, SPAN), BF16),
        ],
        compiler_params=pltpu.CompilerParams(vmem_limit_bytes=28 * 2**20),
        cost_estimate=pl.CostEstimate(
            flops=2 * rows * width * (channels + 2 * STATE + LANES),
            bytes_accessed=2 * width * (rows + channels + 2 * STATE),
            transcendentals=rows * channels,
        ),
        name="front",
    )(tokens, edge, w_bc, w_step, w_in, taps, offset, taps_bc, offset_bc, step_bias, decay_log)


def inside_kernel(first, x_ref, bc_ref, cum_ref, dt_ref, prior_ref, skip_ref, out_ref):
    tiles = x_ref.shape[1] // LANES
    write = bc_ref[:, :STATE]
    read = bc_ref[:, STATE:]
    scores = lax.dot_general(read, write, (((1,), (1,)), ((), ())), preferred_element_type=F32)
    row = lax.broadcasted_iota(jnp.int32, (SPAN, SPAN), 0)
    col = lax.broadcasted_iota(jnp.int32, (SPAN, SPAN), 1)
    scores = jnp.where(row >= col, scores, 0.0)
    cum = cum_ref[...]
    cum_t = jnp.transpose(cum)
    dt_t = jnp.transpose(dt_ref[...])
    grown = jnp.exp(cum)
    lane = lax.broadcasted_iota(jnp.int32, (SPAN, LANES), 1)
    for t in range(tiles):
        at = slice(t * LANES, (t + 1) * LANES)
        x = x_ref[:, at]
        both = []
        for h in (2 * t, 2 * t + 1):
            gap = jnp.minimum(cum[:, h : h + 1] - cum_t[h : h + 1, :], 0.0)
            both.append((scores * jnp.exp(gap) * dt_t[h : h + 1, :]).astype(BF16))
        zero = jnp.zeros_like(x)
        stacked = jnp.concatenate(
            [jnp.where(lane < HEADDIM, x, zero), jnp.where(lane < HEADDIM, zero, x)], axis=0
        )
        total = dot(jnp.concatenate(both, axis=1), stacked)
        total = total + skip_ref[:, at] * x.astype(F32)
        if not first:
            scale = jnp.where(
                lane < HEADDIM, grown[:, 2 * t : 2 * t + 1], grown[:, 2 * t + 1 : 2 * t + 2]
            )
            total = total + scale * dot(read, prior_ref[0, t])
        out_ref[:, at] = total


def inside(span, x, bc, cum, dt, prior, skip):
    channels = x.shape[1]
    tiles = channels // LANES
    at = lambda i: (span, 0)
    return pl.pallas_call(
        functools.partial(inside_kernel, span == 0),
        grid=(1,),
        in_specs=[
            pl.BlockSpec((SPAN, channels), at),
            pl.BlockSpec((SPAN, 2 * STATE), at),
            pl.BlockSpec((SPAN, LANES), at),
            pl.BlockSpec((SPAN, LANES), at),
            pl.BlockSpec((1, tiles, STATE, LANES), lambda i: (max(span - 1, 0), 0, 0, 0)),
            pl.BlockSpec((1, channels), lambda i: (0, 0)),
        ],
        out_specs=pl.BlockSpec((SPAN, channels), lambda i: (0, 0)),
        out_shape=jax.ShapeDtypeStruct((SPAN, channels), F32),
        compiler_params=pltpu.CompilerParams(vmem_limit_bytes=12 * 2**20),
        cost_estimate=pl.CostEstimate(
            flops=1_500_000_000, bytes_accessed=2 * SPAN * channels, transcendentals=0
        ),
        name="inside",
    )(x, bc, cum, dt, prior, skip)


def tail_kernel(
    which, bc_ref, lead_ref, local_ref, gate_ref, state_ref, norm_ref, w_ref,
    left_ref, right_ref, squares_ref, gated,
):
    del which
    n = pl.program_id(1)
    tiles = local_ref.shape[2] // LANES

    @pl.when(n == 0)
    def _():
        read = bc_ref[:, STATE:]
        lead = lead_ref[...]
        squares = jnp.zeros((SPAN, LANES), F32)
        for t in range(tiles):
            at = slice(t * LANES, (t + 1) * LANES)
            scale = lane_pair(lead[:, 2 * t : 2 * t + 1], lead[:, 2 * t + 1 : 2 * t + 2])
            mixed = local_ref[0, :, at] + scale * dot(read, state_ref[t])
            pre = mixed * silu(gate_ref[:, at].astype(F32))
            squares = squares + pre * pre
            gated[:, at] = (pre * norm_ref[:, at]).astype(BF16)
        total = jnp.sum(squares, axis=1, keepdims=True)
        squares_ref[0] = jnp.transpose(jnp.broadcast_to(total, (SPAN, LANES)))[:8]

    part = dot(gated[...], w_ref[...]).astype(BF16)
    half = pl.num_programs(1) // 2

    @pl.when(n < half)
    def _():
        left_ref[0] = part

    @pl.when(n >= half)
    def _():
        right_ref[0] = part


def tail(which, bc, lead, local, gate, state, norm, weight):
    count = which.shape[0]
    channels = local.shape[2]
    width = weight.shape[1]
    tiles = channels // LANES
    parts = 4
    block = width // parts
    half = parts // 2
    at = lambda i, n, w: (w[i], 0)
    fixed = lambda i, n, w: (0, 0)
    side = jax.ShapeDtypeStruct((count, SPAN, width // 2), BF16)
    return pl.pallas_call(
        tail_kernel,
        grid_spec=pltpu.PrefetchScalarGridSpec(
            num_scalar_prefetch=1,
            grid=(count, parts),
            in_specs=[
                pl.BlockSpec((SPAN, 2 * STATE), at),
                pl.BlockSpec((SPAN, LANES), at),
                pl.BlockSpec((1, SPAN, channels), lambda i, n, w: (w[i], 0, 0)),
                pl.BlockSpec((SPAN, channels), at),
                pl.BlockSpec((tiles, STATE, LANES), lambda i, n, w: (0, 0, 0)),
                pl.BlockSpec((1, channels), fixed),
                pl.BlockSpec((channels, block), lambda i, n, w: (0, n)),
            ],
            out_specs=[
                pl.BlockSpec(
                    (1, SPAN, block), lambda i, n, w: (i, 0, jnp.minimum(n, half - 1))
                ),
                pl.BlockSpec(
                    (1, SPAN, block), lambda i, n, w: (i, 0, jnp.maximum(n - half, 0))
                ),
                pl.BlockSpec((1, 8, LANES), lambda i, n, w: (i, 0, 0)),
            ],
            scratch_shapes=[pltpu.VMEM((SPAN, channels), BF16)],
        ),
        out_shape=[side, side, jax.ShapeDtypeStruct((count, 8, LANES), F32)],
        compiler_params=pltpu.CompilerParams(vmem_limit_bytes=20 * 2**20),
        cost_estimate=pl.CostEstimate(
            flops=2 * count * SPAN * channels * width,
            bytes_accessed=2 * channels * width,
            transcendentals=0,
        ),
        name="tail",
    )(which, bc, lead, local, gate, state, norm, weight)


def ring(value, axis, distance):
    size = lax.axis_size(axis)
    return lax.ppermute(value, axis, [(i, (i + distance) % size) for i in range(size)])


def onward(value, axis, distance):
    size = lax.axis_size(axis)
    return lax.ppermute(
        value, axis, [(i, i + distance) for i in range(size) if i + distance < size]
    )


def pick(values, index):
    out = values[0]
    for k in range(1, len(values)):
        out = jnp.where(index == k, values[k], out)
    return out


def packed(state, decay):
    tiles = state.shape[0]
    high = decay.astype(BF16)
    low = (decay - high.astype(F32)).astype(BF16)
    spare = jnp.zeros((16 - 2 * tiles, LANES), BF16)
    return jnp.concatenate([state.astype(BF16).reshape(-1, LANES), high, low, spare], 0)


def unpacked(message, tiles):
    rows = message.shape[0] - 16
    state = message[:rows].reshape(tiles, rows // tiles, LANES).astype(F32)
    high = message[rows : rows + tiles].astype(F32)
    low = message[rows + tiles : rows + 2 * tiles].astype(F32)
    return state, (high + low)[:, None, :]


def incoming_state(local, decay):
    z_axis, y_axis, c_axis = SEQ
    z, y, c = (lax.axis_index(a) for a in SEQ)
    ys, zs = lax.axis_size(y_axis), lax.axis_size(z_axis)
    tiles = local.shape[0] // 2
    first = c == 0
    here = jnp.where(first, local[:tiles], local[tiles:])
    there = jnp.where(first, local[tiles:], local[:tiles])
    here_d = jnp.where(first, decay[:tiles], decay[tiles:])
    there_d = jnp.where(first, decay[tiles:], decay[:tiles])

    got = ring(packed(there, there_d), c_axis, 1)
    other, other_d = unpacked(got, tiles)
    here, here_d = here.astype(F32), here_d[:, None, :]
    s0, d0 = jnp.where(first, here, other), jnp.where(first, here_d, other_d)
    s1, d1 = jnp.where(first, other, here), jnp.where(first, other_d, here_d)
    chip, chip_d = d1 * s0 + s1, d0 * d1

    part = STATE // ys
    quarters = [chip[:, q * part : (q + 1) * part] for q in range(ys)]
    sent = [pick(quarters, (y + k) % ys) for k in range(ys)]
    got = [
        unpacked(ring(packed(sent[k], chip_d[:, 0]), y_axis, k), tiles) for k in range(1, ys)
    ]
    by_shift = [(sent[0], chip_d)] + got
    states = [pick([g[0] for g in by_shift], (y - q) % ys) for q in range(ys)]
    decays = [pick([g[1] for g in by_shift], (y - q) % ys) for q in range(ys)]
    plane, plane_d = states[0], decays[0]
    for q in range(1, ys):
        plane, plane_d = decays[q] * plane + states[q], decays[q] * plane_d

    message = packed(plane, plane_d[:, 0])
    got = [unpacked(onward(message, z_axis, k), tiles) for k in range(1, zs)]
    before = jnp.zeros_like(plane)
    for q in range(zs - 1):
        s = pick([g[0] for g in got], z - q - 1)
        d = pick([g[1] for g in got], z - q - 1)
        before = jnp.where(q < z, d * before + s, before)

    prefix = [before]
    for q in range(ys - 1):
        prefix.append(decays[q] * prefix[-1] + states[q])
    sent = [pick(prefix, (y + k) % ys).astype(BF16) for k in range(ys)]
    got = [sent[0]] + [ring(sent[k], y_axis, k) for k in range(1, ys)]
    chip_in = jnp.concatenate([pick(got, (y - q) % ys) for q in range(ys)], axis=1)
    second_in = (d0 * chip_in.astype(F32) + s0).astype(BF16)
    mine = jnp.where(first, chip_in, second_in)
    got = ring(jnp.where(first, second_in, chip_in), c_axis, 1)
    return jnp.concatenate([jnp.where(first, mine, got), jnp.where(first, got, mine)], axis=0)


def per_device(
    tokens,
    proj_inner,
    proj_gate,
    proj_bc,
    proj_step,
    conv_inner,
    conv_bc,
    offset_inner,
    offset_bc,
    step_bias,
    decay_log,
    skip_gain,
    norm_weight,
    out_weight,
):
    rows = tokens.shape[0]
    spans = rows // SPAN
    devices = lax.axis_size(SEQ)
    edge = lax.ppermute(tokens[rows - EDGE :], SEQ, [(i, i + 1) for i in range(devices - 1)])
    gate_raw = dot(tokens, proj_gate).astype(BF16)
    edge, gate_raw = lax.optimization_barrier((edge, gate_raw))
    x, bc, cum, dt, lead, local, prior, decay = front(
        tokens, edge, proj_bc, proj_step, proj_inner, conv_inner, offset_inner[None],
        conv_bc, offset_bc[None], step_bias[None], decay_log[None],
    )
    state = incoming_state(local, decay[:, 0])
    skip = jnp.repeat(skip_gain, HEADDIM)[None]
    inner = jnp.stack([inside(s, x, bc, cum, dt, prior, skip) for s in range(spans)])

    head = lax.axis_index("head")
    size = lax.axis_size("head")
    run = lambda which: tail(
        jnp.stack([(head + k) % size for k in which]).astype(jnp.int32),
        bc, lead, inner, gate_raw, state, norm_weight[None], out_weight,
    )
    far_left, far_right, far_sq = run((2,))
    relay_up = ring(far_left[0], "head", 1)
    relay_down = ring(far_right[0], "head", -1)
    near_left, near_right, near_sq = run((1, 3))
    direct_up = ring(near_right[0], "head", 1)
    direct_down = ring(near_left[1], "head", -1)
    up = ring((near_left[0].astype(F32) + relay_up.astype(F32)).astype(BF16), "head", 1)
    down = ring((near_right[1].astype(F32) + relay_down.astype(F32)).astype(BF16), "head", -1)
    own_left, own_right, own_sq = run((0,))
    squares = (
        own_sq[0, 0]
        + ring(near_sq[0], "head", 1)[0]
        + ring(near_sq[1], "head", -1)[0]
        + ring(far_sq[0], "head", 2)[0]
    )
    scale = lax.rsqrt(squares / (HEADS * HEADDIM) + 0.25)[:, None]
    left = own_left[0].astype(F32) + up.astype(F32) + direct_down.astype(F32)
    right = own_right[0].astype(F32) + direct_up.astype(F32) + down.astype(F32)
    return jnp.concatenate([(left * scale).astype(BF16), (right * scale).astype(BF16)], axis=1)


def solution(mesh):
    torus = Mesh(
        mesh.devices.reshape(4, 4, 2, mesh.shape["head"]), ("seq_0", "seq_1", "seq_2", "head")
    )
    return jax.shard_map(
        per_device,
        mesh=torus,
        in_specs=(
            P(SEQ, None),
            P(None, "head"),
            P(None, "head"),
            P(),
            P(None, "head"),
            P(None, "head"),
            P(),
            P("head"),
            P(),
            P("head"),
            P("head"),
            P("head"),
            P("head"),
            P("head", None),
        ),
        out_specs=P(SEQ_HEAD, None),
        check_vma=False,
    )
```

time: 224 us -> 115 us (0.51)
  blocking collectives: 66.8 us -> 0 us
  matrix products: 40.4 us -> 8.33 us
  Pallas kernels: 0 us -> 29.2 us
  starting transfers between devices: 5.82 us -> 32.4 us
  waiting for transfers between devices: 45.1 us -> 22.9 us
  other arithmetic: 23.3 us -> 5.26 us
  between operations: 14.7 us -> 0.72 us
  local copies, waits for them, and re-layouts: 26.8 us -> 15.5 us
    all_gather x3 -> x0, waiting for transfers between devices: 45 us -> none  [carried_in(): pieces = jax.tree.map(lambda part: lax.all_gather(part, axis), running)]
    all_to_all x2 -> x0, blocking collectives: 43.3 us -> none  [the longest x1 33.9 us: summed_on_arrival(): lax.all_to_all(pieces, axis, split_axis=0, concat_axis=0, tiled=True)]
    dot_general x9 -> x1, matrix products: 37.6 us -> 8.33 us  [dot(): return jnp.dot(a, b, preferred_element_type=F32)]
    pallas_call x0 -> x8, Pallas kernels: none -> 29.2 us  [the longest x3 13.3 us: tail(): pl.pallas_call(tail_kernel, grid_spec=pltpu.PrefetchScalarGridSpec(num_sc...]
    ppermute x2 -> x21, starting transfers between devices: 5.74 us -> 32.4 us  [the longest x17 21.4 us: ring(): lax.ppermute(value, axis, [(i, (i + distance) % size) for i in range(size)])]
    ppermute x2 -> x21, waiting for transfers between devices: 0.01 us -> 22.9 us  [the longest x17 22.2 us: ring(): lax.ppermute(value, axis, [(i, (i + distance) % size) for i in range(size)])]
    unnamed x2 -> x0, blocking collectives: 13.2 us -> none
    all_gather x1 -> x0, blocking collectives: 10.3 us -> none  [carried_in(): pieces = jax.tree.map(lambda part: lax.all_gather(part, axis), running)]
  transfers between devices with their start and end apart: 5 -> 21, of which waited for: 2 -> 10; matrix products, arithmetic and copies ran while one was open for 14% -> 11% of each run, Pallas kernels for 0% -> 12%
where the time goes in v1:
time: 115 us; the launch traced here: 114 us
  starting transfers between devices  32.4 us (28%)
  Pallas kernels  29.2 us (25%)
  waiting for transfers between devices  22.9 us (20%)
  local copies, waits for them, and re-layouts  15.5 us (13%)
  matrix products  8.33 us (7%)
  other arithmetic  5.26 us (5%)
    ppermute x17, waiting for transfers between devices, ring(): lax.ppermute(value, axis, [(i, (i + distance) % size) for i in range(size)])  22.2 us
    ppermute x17, starting transfers between devices, ring(): lax.ppermute(value, axis, [(i, (i + distance) % size) for i in range(size)])  21.4 us
    pallas_call x3, Pallas kernels, tail(): pl.pallas_call(tail_kernel, grid_spec=pltpu.PrefetchScalarGridSpec(num_sc...  13.3 us
    unnamed x45, local copies, waits for them, and re-layouts  13 us
    pallas_call x1, Pallas kernels, front(): pl.pallas_call(front_kernel, grid=(groups + 1,), in_specs=[whole(tokens),...  12.2 us
    ppermute x3, starting transfers between devices, onward(): lax.ppermute(value, axis, [(i, i + distance) for i in range(size) if i +...  9.52 us
    dot_general x1, matrix products, dot(): return jnp.dot(a, b, preferred_element_type=F32)  8.33 us
    pallas_call x4, Pallas kernels, inside(): pl.pallas_call(functools.partial(inside_kernel, span == 0), grid=(1,), in...  3.67 us
  transfers between devices with their start and end apart: 21, of which 10 were waited for; matrix products, arithmetic and copies ran while one was open for 11% of the time, Pallas kernels for 12%

profile of v1, /device:TPU:0, one launch (start us, length us, event | category | flops | bytes accessed | tf_op | source)
XLA Modules:
  0.0 114.2 jit_solution(17286107573327946694)
XLA Ops:
  0.0 0.8 slice.129
  0.9 1.4 %collective-permute-start = (bf16[8,2560]{1,0:T(8,128)(2,1)S(1)}, bf16[8,2560]{1,0:T(8,128)(2,1)S(1)}, u32[]{:S(2)}, u32[]{:S(2)}) collective-permute-start(bf16[8,2560]{1,0:T(8,128)(2,1)S(1)} %slice.129), channel_id=1, source_target_pairs={{0,4},{4,8},{8,12},{12,16},{16,20},{20,24},{24,28},{28,32},{32,36}... | collective-permute-start | bytes 122888 | tf_op jit(solution)/shard_map/ppermute | solution.py:430
  2.3 8.3 %convolution_convert_fusion.gate_ref = bf16[512,1280]{1,0:T(8,128)(2,1)} fusion(bf16[512,2560]{1,0:T(8,128)(2,1)} %tok.1, bf16[2560,1280]{1,0:T(8,128)(2,1)} %param.16), kind=kOutput, calls=%fused_computation | convolution fusion | flops 3356098560 | bytes 10485760 | tf_op jit(solution)/shard_map/dot_general | solution.py:27
  11.1 1.7 %copy-done.3 = bf16[512,2560]{1,0:T(8,128)(2,1)S(1)} copy-done((bf16[512,2560]{1,0:T(8,128)(2,1)S(1)}, bf16[512,2560]{1,0:T(8,128)(2,1)}, u32[]{:S(2)}) %copy-start.3) | copy-done | bytes 2621464
  12.8 2.9 %copy-done.4 = bf16[2560,1280]{1,0:T(8,128)(2,1)S(1)} copy-done((bf16[2560,1280]{1,0:T(8,128)(2,1)S(1)}, bf16[2560,1280]{1,0:T(8,128)(2,1)}, u32[]{:S(2)}) %copy-start.4) | copy-done | bytes 6553624
  15.7 12.2 %front.1 = (bf16[512,1280]{1,0:T(8,128)(2,1)S(1)}, bf16[512,256]{1,0:T(8,128)(2,1)S(1)}, f32[512,128]{1,0:T(8,128)S(1)}, f32[512,128]{1,0:T(8,128)S(1)}, f32[512...) custom-call(bf16[512,2560]{1,0:T(8,128)(2,1)S(1)} %copy-done.3, ...), custom_call_target="tpu_custom_call" | custom-call | flops 4362076160 | bytes 10485760 | tf_op jit(solution)/shard_map/front/pallas_call | solution.py:144
  27.9 1.1 copy-done.11
  29.1 2.5 %collective-permute-start.1 = (bf16[656,128]{1,0:T(8,128)(2,1)S(1)}, bf16[656,128]{1,0:T(8,128)(2,1)S(1)}, u32[]{:S(2)}, u32[]{:S(2)}) collective-permute-start(bf16[656,128]{1,0:T(8,128)(2,1)S(1)} %pad_maximum_fusion.3), channel_id=1, source_target_pairs={{0,4},{4,0},{1,5},{5,1},{2,6},{6,2},{3,7},{7,3},{8,12},{12,8},{9,1... | collective-permute-start | bytes 503816 | tf_op jit(solution)/shard_map/ppermute | solution.py:327
  32.0 1.3 %copy-done.12 = bf16[512,1280]{1,0:T(8,128)(2,1)S(1)} copy-done((bf16[512,1280]{1,0:T(8,128)(2,1)S(1)}, bf16[512,1280]{1,0:T(8,128)(2,1)}, u32[]{:S(2)}) %copy-start.12) | copy-done | bytes 1310744
  33.3 1.2 %copy-done.15 = bf16[3,10,128,128]{3,2,1,0:T(8,128)(2,1)S(1)} copy-done((bf16[3,10,128,128]{3,2,1,0:T(8,128)(2,1)S(1)}, bf16[3,10,128,128]{3,2,1,0:T(8,128)(2,1)}, u32[]{:S(2)}) %copy-start.15) | copy-done | bytes 983064
  34.5 0.7 inside.4
  35.4 3.1 %collective-permute-start.2 = (bf16[176,128]{1,0:T(8,128)(2,1)S(1)}, bf16[176,128]{1,0:T(8,128)(2,1)S(1)}, u32[]{:S(2)}, u32[]{:S(2)}) collective-permute-start(bf16[176,128]{1,0:T(8,128)(2,1)S(1)} %get-tuple-element.83), channel_id=1, source_target_pairs={{0,24},{8,0},{16,8},{24,16},{1,25},{9,1},{17,9},{25,17},{2,26},{10... | collective-permute-start | bytes 135176 | tf_op jit(solution)/shard_map/ppermute | solution.py:327
  38.5 0.6 collective-permute-start.3
  39.1 0.7 collective-permute-start.4
  39.8 1.0 inside.5
  41.2 3.2 %collective-permute-done.3 = bf16[176,128]{1,0:T(8,128)(2,1)S(1)} collective-permute-done((bf16[176,128]{1,0:T(8,128)(2,1)S(1)}, bf16[176,128]{1,0:T(8,128)(2,1)S(1)}, u32[]{:S(2)}, u32[]{:S(2)}) %collective-permute-start.3) | collective-permute-done | bytes 45088 | tf_op jit(solution)/shard_map/ppermute | solution.py:327
  44.3 0.5 collective-permute-done.4
  45.0 5.5 %collective-permute-start.5 = (bf16[176,128]{1,0:T(8,128)(2,1)S(1)}, bf16[176,128]{1,0:T(8,128)(2,1)S(1)}, u32[]{:S(2)}, u32[]{:S(2)}) collective-permute-start(bf16[176,128]{1,0:T(8,128)(2,1)S(1)} %pad_maximum_fusion.5), channel_id=1, source_target_pairs={{0,96},{1,97},{2,98},{3,99},{4,100},{5,101},{6,102},{7,103},{8,104... | collective-permute-start | bytes 135176 | tf_op jit(solution)/shard_map/ppermute | solution.py:332
  50.5 1.3 %collective-permute-start.6 = (bf16[176,128]{1,0:T(8,128)(2,1)S(1)}, bf16[176,128]{1,0:T(8,128)(2,1)S(1)}, u32[]{:S(2)}, u32[]{:S(2)}) collective-permute-start(bf16[176,128]{1,0:T(8,128)(2,1)S(1)} %pad_maximum_fusion.5), channel_id=1, source_target_pairs={{0,64},{32,96},{1,65},{33,97},{2,66},{34,98},{3,67},{35,99},{4,68}... | collective-permute-start | bytes 135176 | tf_op jit(solution)/shard_map/ppermute | solution.py:332
  51.8 2.8 %collective-permute-start.7 = (bf16[176,128]{1,0:T(8,128)(2,1)S(1)}, bf16[176,128]{1,0:T(8,128)(2,1)S(1)}, u32[]{:S(2)}, u32[]{:S(2)}) collective-permute-start(bf16[176,128]{1,0:T(8,128)(2,1)S(1)} %pad_maximum_fusion.5), channel_id=1, source_target_pairs={{0,32},{32,64},{64,96},{1,33},{33,65},{65,97},{2,34},{34,66},{66,9... | collective-permute-start | bytes 135176 | tf_op jit(solution)/shard_map/ppermute | solution.py:332
  54.5 1.0 inside.6
  55.6 0.7 collective-permute-done.7
  56.6 1.6 %collective-permute-start.9 = (bf16[5,32,128]{2,1,0:T(8,128)(2,1)S(1)}, bf16[5,32,128]{2,1,0:T(8,128)(2,1)S(1)}, u32[]{:S(2)}, u32[]{:S(2)}) collective-permute-start(bf16[5,32,128]{2,1,0:T(8,128)(2,1)S(1)} %get-tuple-element.65), channel_id=1, source_target_pairs={{0,16},{8,24},{16,0},{24,8},{1,17},{9,25},{17,1},{25,9},{2,18},{10... | collective-permute-start | bytes 122888 | tf_op jit(solution)/shard_map/ppermute | solution.py:327
  58.2 0.7 collective-permute-start.10
  58.9 1.0 inside.7
  59.9 0.6 collective-permute-done.8
  60.5 1.8 %collective-permute-done.9 = bf16[5,32,128]{2,1,0:T(8,128)(2,1)S(1)} collective-permute-done((bf16[5,32,128]{2,1,0:T(8,128)(2,1)S(1)}, bf16[5,32,128]{2,1,0:T(8,128)(2,1)S(1)}, u32[]{:S(2)}, u32[]{:S(2)}) %collective-permute-start.9) | collective-permute-done | bytes 40992 | tf_op jit(solution)/shard_map/ppermute | solution.py:327
  62.3 1.1 collective-permute-done.10
  64.0 1.2 %collective-permute-done.11 = bf16[5,128,128]{2,1,0:T(8,128)(2,1)S(1)} collective-permute-done((bf16[5,128,128]{2,1,0:T(8,128)(2,1)S(1)}, bf16[5,128,128]{2,1,0:T(8,128)(2,1)S(1)}, u32[]{:S(2)}, u32[]{:S(2)}) %collective-permute-start.11) | collective-permute-done | bytes 163872 | tf_op jit(solution)/shard_map/ppermute | solution.py:327
  65.6 3.2 %tail.5 = (bf16[1,128,1280]{2,1,0:T(8,128)(2,1)S(1)}, bf16[1,128,1280]{2,1,0:T(8,128)(2,1)S(1)}, f32[1,8,128]{2,1,0:T(8,128)S(1)}) custom-call(s32[1]{0:T(128)} %bitcast.29.which, bf16[512,256]{1,0:T(8,128)(2,1)S(1)} %get-tuple-element.25.bc_ref, f32[512,128]{1,0:T(8,128)S(1)} %get-tuple-element.26.lead_ref, f32[4,128,1280]{2,1,0:T(8,128)S(1)} %pad_maximum_fusion.local_ref, ...), custom_call_target="tpu_custom_call" | custom-call | flops 838860800 | bytes 6553600 | tf_op jit(solution)/shard_map/tail/pallas_call | solution.py:289
  68.8 2.8 %collective-permute-start.19 = (bf16[128,1280]{1,0:T(8,128)(2,1)S(1)}, bf16[128,1280]{1,0:T(8,128)(2,1)S(1)}, u32[]{:S(2)}, u32[]{:S(2)}) collective-permute-start(bf16[128,1280]{1,0:T(8,128)(2,1)S(1)} %bitcast.95), channel_id=1, source_target_pairs={{0,3},{1,0},{2,1},{3,2},{4,7},{5,4},{6,5},{7,6},{8,11},{9,8},{10,9... | collective-permute-start | bytes 983048 | tf_op jit(solution)/shard_map/ppermute | solution.py:327
  71.6 7.0 %tail.4 = (bf16[2,128,1280]{2,1,0:T(8,128)(2,1)S(1)}, bf16[2,128,1280]{2,1,0:T(8,128)(2,1)S(1)}, f32[2,8,128]{2,1,0:T(8,128)S(1)}) custom-call(s32[2]{0:T(128)S(1)} %pad_add_fusion.which, bf16[512,256]{1,0:T(8,128)(2,1)S(1)} %get-tuple-element.25.bc_ref, f32[512,128]{1,0:T(8,128)S(1)} %get-tuple-element.26.lead_ref, ...), custom_call_target="tpu_custom_call" | custom-call | flops 1677721600 | bytes 6553600 | tf_op jit(solution)/shard_map/tail/pallas_call | solution.py:289
  78.6 0.9 collective-permute-start.17
  79.5 0.9 collective-permute-start.12
  80.4 0.7 slice_bitcast_fusion.1
  81.1 2.4 %collective-permute-start.14 = (bf16[128,1280]{1,0:T(8,128)(2,1)}, bf16[128,1280]{1,0:T(8,128)(2,1)}, u32[]{:S(2)}, u32[]{:S(2)}) collective-permute-start(bf16[128,1280]{1,0:T(8,128)(2,1)} %slice_bitcast_fusion.1), channel_id=1, source_target_pairs={{0,3},{1,0},{2,1},{3,2},{4,7},{5,4},{6,5},{7,6},{8,11},{9,8},{10,9... | collective-permute-start | bytes 983048 | tf_op jit(solution)/shard_map/ppermute | solution.py:327
  83.5 0.7 slice_bitcast_fusion
  84.2 0.8 fusion
  85.0 3.2 %collective-permute-start.20 = (bf16[128,1280]{1,0:T(8,128)(2,1)}, bf16[128,1280]{1,0:T(8,128)(2,1)}, u32[]{:S(2)}, u32[]{:S(2)}) collective-permute-start(bf16[128,1280]{1,0:T(8,128)(2,1)} %fusion), channel_id=1, source_target_pairs={{0,3},{1,0},{2,1},{3,2},{4,7},{5,4},{6,5},{7,6},{8,11},{9,8},{10,9... | collective-permute-start | bytes 983048 | tf_op jit(solution)/shard_map/ppermute | solution.py:327
  88.2 3.0 %collective-permute-done.12 = bf16[128,1280]{1,0:T(8,128)(2,1)S(1)} collective-permute-done((bf16[128,1280]{1,0:T(8,128)(2,1)S(1)}, bf16[128,1280]{1,0:T(8,128)(2,1)S(1)}, u32[]{:S(2)}, u32[]{:S(2)}) %collective-permute-start.12) | collective-permute-done | bytes 327712 | tf_op jit(solution)/shard_map/ppermute | solution.py:327
  91.3 0.8 fusion.4
  92.1 1.5 %collective-permute-start.15 = (f32[8,128]{1,0:T(8,128)S(1)}, f32[8,128]{1,0:T(8,128)S(1)}, u32[]{:S(2)}, u32[]{:S(2)}) collective-permute-start(f32[8,128]{1,0:T(8,128)S(1)} %get-tuple-element.79), channel_id=1, source_target_pairs={{0,1},{1,2},{2,3},{3,0},{4,5},{5,6},{6,7},{7,4},{8,9},{9,10},{10,1... | collective-permute-start | bytes 12296 | tf_op jit(solution)/shard_map/ppermute | solution.py:327
  93.5 10.4 %collective-permute-done.15 = f32[8,128]{1,0:T(8,128)S(1)} collective-permute-done((f32[8,128]{1,0:T(8,128)S(1)}, f32[8,128]{1,0:T(8,128)S(1)}, u32[]{:S(2)}, u32[]{:S(2)}) %collective-permute-start.15) | collective-permute-done | bytes 4128 | tf_op jit(solution)/shard_map/ppermute | solution.py:327
  104.3 2.9 %copy-done = bf16[1280,2560]{1,0:T(8,128)(2,1)S(1)} copy-done((bf16[1280,2560]{1,0:T(8,128)(2,1)S(1)}, bf16[1280,2560]{1,0:T(8,128)(2,1)}, u32[]{:S(2)}) %copy-start) | copy-done | bytes 6553624
  107.2 1.3 %copy-done.2 = bf16[512,1280]{1,0:T(8,128)(2,1)S(1)} copy-done((bf16[512,1280]{1,0:T(8,128)(2,1)S(1)}, bf16[512,1280]{1,0:T(8,128)(2,1)}, u32[]{:S(2)}) %copy-start.2) | copy-done | bytes 1310744
  108.5 3.2 %tail.3 = (bf16[1,128,1280]{2,1,0:T(8,128)(2,1)S(1)}, bf16[1,128,1280]{2,1,0:T(8,128)(2,1)S(1)}, f32[1,8,128]{2,1,0:T(8,128)S(1)}) custom-call(s32[1]{0:T(128)} %bitcast.which, bf16[512,256]{1,0:T(8,128)(2,1)S(1)} %get-tuple-element.25.bc_ref, f32[512,128]{1,0:T(8,128)S(1)} %get-tuple-element.26.lead_ref, f32[4,128,1280]{2,1,0:T(8,128)S(1)} %pad_maximum_fusion.local_ref, ...), custom_call_target="tpu_custom_call" | custom-call | flops 838860800 | bytes 6553600 | tf_op jit(solution)/shard_map/tail/pallas_call | solution.py:289
  111.7 1.6 %fusion.7 = (bf16[128,1280]{1,0:T(8,128)(2,1)S(1)}, bf16[128,1280]{1,0:T(8,128)(2,1)S(1)}) fusion(bf16[128,1280]{1,0:T(8,128)(2,1)} %collective-permute-done.14, bf16[128,1280]{1,0:T(8,128)(2,1)} %collective-permute-done.13, bf16[1,128,1280]{2,1,0:T(8,128)(2,1)S(1)} %get-tuple-element.34, f32[128]{0:T(128)S(1)} %fusion.14, ...), kind=kLoop, calls=%fused_computation.14 | loop fusion | flops 2293760 | bytes 2621952 | tf_op jit(solution)/shard_map/convert_element_type | solution.py:465
  113.3 0.9 pad_maximum_fusion.1
  (96 shorter events, 3.2 us)
Async XLA Ops:
  0.8 9.8 %copy-start.16 = (bf16[2560,20]{0,1:T(8,128)(2,1)S(1)}, bf16[2560,20]{0,1:T(8,128)(2,1)}, u32[]{:S(2)}) copy-start(bf16[2560,20]{0,1:T(8,128)(2,1)} %param.18) | copy-start | bytes 307204
  0.8 10.2 %copy-start.17 = (f32[1280]{0:T(1024)S(1)}, f32[1280]{0:T(1024)}, u32[]{:S(2)}) copy-start(f32[1280]{0:T(1024)} %param.21) | copy-start | bytes 15364
  0.8 10.2 %copy-start.5 = (bf16[2560,256]{1,0:T(8,128)(2,1)S(1)}, bf16[2560,256]{1,0:T(8,128)(2,1)}, u32[]{:S(2)}) copy-start(bf16[2560,256]{1,0:T(8,128)(2,1)} %w_bc.1) | copy-start | bytes 3932164
  0.8 10.2 %copy-start.6 = (f32[4,1280]{1,0:T(4,128)S(1)}, f32[4,1280]{1,0:T(4,128)}, u32[]{:S(2)}) copy-start(f32[4,1280]{1,0:T(4,128)} %taps.1) | copy-start | bytes 61444
  0.8 10.2 %copy-start.7 = (f32[4,256]{1,0:T(4,128)S(1)}, f32[4,256]{1,0:T(4,128)}, u32[]{:S(2)}) copy-start(f32[4,256]{1,0:T(4,128)} %taps_bc.1) | copy-start | bytes 12292
  0.8 10.2 %copy-start.8 = (f32[256]{0:T(256)S(1)}, f32[256]{0:T(256)}, u32[]{:S(2)}) copy-start(f32[256]{0:T(256)} %param.22) | copy-start | bytes 3076
  0.8 10.2 %copy-start.9 = (f32[20]{0:T(128)S(1)}, f32[20]{0:T(128)}, u32[]{:S(2)}) copy-start(f32[20]{0:T(128)} %param.23) | copy-start | bytes 244
  0.8 10.2 %copy-start.10 = (f32[20]{0:T(128)S(1)}, f32[20]{0:T(128)}, u32[]{:S(2)}) copy-start(f32[20]{0:T(128)} %param.24) | copy-start | bytes 244
  0.9 10.2 %collective-permute-start = (bf16[8,2560]{1,0:T(8,128)(2,1)S(1)}, bf16[8,2560]{1,0:T(8,128)(2,1)S(1)}, u32[]{:S(2)}, u32[]{:S(2)}) collective-permute-start(bf16[8,2560]{1,0:T(8,128)(2,1)S(1)} %slice.129), channel_id=1, source_target_pairs={{0,4},{4,8},{8,12},{12,16},{16,20},{20,24},{24,28},{28,32},{32,36}... | collective-permute-start | bytes 122888 | tf_op jit(solution)/shard_map/ppermute | solution.py:430
  11.1 1.7 %copy-start.3 = (bf16[512,2560]{1,0:T(8,128)(2,1)S(1)}, bf16[512,2560]{1,0:T(8,128)(2,1)}, u32[]{:S(2)}) copy-start(bf16[512,2560]{1,0:T(8,128)(2,1)} %tok.1) | copy-start | bytes 7864324
  12.8 2.9 %copy-start.4 = (bf16[2560,1280]{1,0:T(8,128)(2,1)S(1)}, bf16[2560,1280]{1,0:T(8,128)(2,1)}, u32[]{:S(2)}) copy-start(bf16[2560,1280]{1,0:T(8,128)(2,1)} %w_in.1) | copy-start | bytes 19660804
  15.7 16.1 %copy-start.19 = (f32[20]{0:T(128)S(1)}, f32[20]{0:T(128)}, u32[]{:S(2)}) copy-start(f32[20]{0:T(128)} %param.25) | copy-start | bytes 244
  15.7 16.2 %copy-start.18 = (f32[1280]{0:T(1024)S(1)}, f32[1280]{0:T(1024)}, u32[]{:S(2)}) copy-start(f32[1280]{0:T(1024)} %param.26) | copy-start | bytes 15364
  27.9 1.1 copy-start.11
  29.0 2.6 %copy-start.14 = (bf16[3,10,128,128]{3,2,1,0:T(8,128)(2,1)}, bf16[3,10,128,128]{3,2,1,0:T(8,128)(2,1)S(1)}, u32[]{:S(2)}) copy-start(bf16[3,10,128,128]{3,2,1,0:T(8,128)(2,1)S(1)} %get-tuple-element.30.prior_ref) | copy-start | bytes 2949124
  29.1 6.1 %collective-permute-start.1 = (bf16[656,128]{1,0:T(8,128)(2,1)S(1)}, bf16[656,128]{1,0:T(8,128)(2,1)S(1)}, u32[]{:S(2)}, u32[]{:S(2)}) collective-permute-start(bf16[656,128]{1,0:T(8,128)(2,1)S(1)} %pad_maximum_fusion.3), channel_id=1, source_target_pairs={{0,4},{4,0},{1,5},{5,1},{2,6},{6,2},{3,7},{7,3},{8,12},{12,8},{9,1... | collective-permute-start | bytes 503816 | tf_op jit(solution)/shard_map/ppermute | solution.py:327
  31.9 1.3 %copy-start.12 = (bf16[512,1280]{1,0:T(8,128)(2,1)S(1)}, bf16[512,1280]{1,0:T(8,128)(2,1)}, u32[]{:S(2)}) copy-start(bf16[512,1280]{1,0:T(8,128)(2,1)} %copy-done.11) | copy-start | bytes 3932164
  33.3 1.2 %copy-start.15 = (bf16[3,10,128,128]{3,2,1,0:T(8,128)(2,1)S(1)}, bf16[3,10,128,128]{3,2,1,0:T(8,128)(2,1)}, u32[]{:S(2)}) copy-start(bf16[3,10,128,128]{3,2,1,0:T(8,128)(2,1)} %copy-done.14) | copy-start | bytes 2949124
  34.5 5.3 %copy-start.13 = (bf16[512,1280]{1,0:T(8,128)(2,1)S(1)}, bf16[512,1280]{1,0:T(8,128)(2,1)}, u32[]{:S(2)}) copy-start(bf16[512,1280]{1,0:T(8,128)(2,1)} %copy-done.11) | copy-start | bytes 3932164
  35.4 5.8 %collective-permute-start.2 = (bf16[176,128]{1,0:T(8,128)(2,1)S(1)}, bf16[176,128]{1,0:T(8,128)(2,1)S(1)}, u32[]{:S(2)}, u32[]{:S(2)}) collective-permute-start(bf16[176,128]{1,0:T(8,128)(2,1)S(1)} %get-tuple-element.83), channel_id=1, source_target_pairs={{0,24},{8,0},{16,8},{24,16},{1,25},{9,1},{17,9},{25,17},{2,26},{10... | collective-permute-start | bytes 135176 | tf_op jit(solution)/shard_map/ppermute | solution.py:327
  38.5 5.9 %collective-permute-start.3 = (bf16[176,128]{1,0:T(8,128)(2,1)S(1)}, bf16[176,128]{1,0:T(8,128)(2,1)S(1)}, u32[]{:S(2)}, u32[]{:S(2)}) collective-permute-start(bf16[176,128]{1,0:T(8,128)(2,1)S(1)} %get-tuple-element.82), channel_id=1, source_target_pairs={{0,16},{8,24},{16,0},{24,8},{1,17},{9,25},{17,1},{25,9},{2,18},{10... | collective-permute-start | bytes 135176 | tf_op jit(solution)/shard_map/ppermute | solution.py:327
  39.1 5.7 %collective-permute-start.4 = (bf16[176,128]{1,0:T(8,128)(2,1)S(1)}, bf16[176,128]{1,0:T(8,128)(2,1)S(1)}, u32[]{:S(2)}, u32[]{:S(2)}) collective-permute-start(bf16[176,128]{1,0:T(8,128)(2,1)S(1)} %get-tuple-element.81), channel_id=1, source_target_pairs={{0,8},{8,16},{16,24},{24,0},{1,9},{9,17},{17,25},{25,1},{2,10},{10... | collective-permute-start | bytes 135176 | tf_op jit(solution)/shard_map/ppermute | solution.py:327
  45.0 10.5 %collective-permute-start.5 = (bf16[176,128]{1,0:T(8,128)(2,1)S(1)}, bf16[176,128]{1,0:T(8,128)(2,1)S(1)}, u32[]{:S(2)}, u32[]{:S(2)}) collective-permute-start(bf16[176,128]{1,0:T(8,128)(2,1)S(1)} %pad_maximum_fusion.5), channel_id=1, source_target_pairs={{0,96},{1,97},{2,98},{3,99},{4,100},{5,101},{6,102},{7,103},{8,104... | collective-permute-start | bytes 135176 | tf_op jit(solution)/shard_map/ppermute | solution.py:332
  50.5 5.1 %collective-permute-start.6 = (bf16[176,128]{1,0:T(8,128)(2,1)S(1)}, bf16[176,128]{1,0:T(8,128)(2,1)S(1)}, u32[]{:S(2)}, u32[]{:S(2)}) collective-permute-start(bf16[176,128]{1,0:T(8,128)(2,1)S(1)} %pad_maximum_fusion.5), channel_id=1, source_target_pairs={{0,64},{32,96},{1,65},{33,97},{2,66},{34,98},{3,67},{35,99},{4,68}... | collective-permute-start | bytes 135176 | tf_op jit(solution)/shard_map/ppermute | solution.py:332
  51.8 4.5 %collective-permute-start.7 = (bf16[176,128]{1,0:T(8,128)(2,1)S(1)}, bf16[176,128]{1,0:T(8,128)(2,1)S(1)}, u32[]{:S(2)}, u32[]{:S(2)}) collective-permute-start(bf16[176,128]{1,0:T(8,128)(2,1)S(1)} %pad_maximum_fusion.5), channel_id=1, source_target_pairs={{0,32},{32,64},{64,96},{1,33},{33,65},{65,97},{2,34},{34,66},{66,9... | collective-permute-start | bytes 135176 | tf_op jit(solution)/shard_map/ppermute | solution.py:332
  56.3 9.0 %slice-start = ((s8[6553600]{0:T(1024)(128)(4,1)}), s8[4194304]{0:T(1024)(128)(4,1)S(1)}, s32[]{:S(2)}) async-start(s8[6553600]{0:T(1024)(128)(4,1)} %bitcast.88), calls=%async_computation | async-start | bytes 8388608
  56.5 4.1 %collective-permute-start.8 = (bf16[5,32,128]{2,1,0:T(8,128)(2,1)S(1)}, bf16[5,32,128]{2,1,0:T(8,128)(2,1)S(1)}, u32[]{:S(2)}, u32[]{:S(2)}) collective-permute-start(bf16[5,32,128]{2,1,0:T(8,128)(2,1)S(1)} %get-tuple-element.66), channel_id=1, source_target_pairs={{0,24},{8,0},{16,8},{24,16},{1,25},{9,1},{17,9},{25,17},{2,26},{10... | collective-permute-start | bytes 122888 | tf_op jit(solution)/shard_map/ppermute | solution.py:327
  56.6 5.7 %collective-permute-start.9 = (bf16[5,32,128]{2,1,0:T(8,128)(2,1)S(1)}, bf16[5,32,128]{2,1,0:T(8,128)(2,1)S(1)}, u32[]{:S(2)}, u32[]{:S(2)}) collective-permute-start(bf16[5,32,128]{2,1,0:T(8,128)(2,1)S(1)} %get-tuple-element.65), channel_id=1, source_target_pairs={{0,16},{8,24},{16,0},{24,8},{1,17},{9,25},{17,1},{25,9},{2,18},{10... | collective-permute-start | bytes 122888 | tf_op jit(solution)/shard_map/ppermute | solution.py:327
  58.2 5.2 %collective-permute-start.10 = (bf16[5,32,128]{2,1,0:T(8,128)(2,1)S(1)}, bf16[5,32,128]{2,1,0:T(8,128)(2,1)S(1)}, u32[]{:S(2)}, u32[]{:S(2)}) collective-permute-start(bf16[5,32,128]{2,1,0:T(8,128)(2,1)S(1)} %get-tuple-element.47), channel_id=1, source_target_pairs={{0,8},{8,16},{16,24},{24,0},{1,9},{9,17},{17,25},{25,1},{2,10},{10... | collective-permute-start | bytes 122888 | tf_op jit(solution)/shard_map/ppermute | solution.py:327
  63.5 1.8 %slice-start.1 = ((s8[6553600]{0:T(1024)(128)(4,1)}), s8[2359296]{0:T(1024)(128)(4,1)S(1)}, s32[]{:S(2)}) async-start(s8[6553600]{0:T(1024)(128)(4,1)} %bitcast.88), calls=%async_computation.1 | async-start | bytes 4718592
  63.6 1.5 %collective-permute-start.11 = (bf16[5,128,128]{2,1,0:T(8,128)(2,1)S(1)}, bf16[5,128,128]{2,1,0:T(8,128)(2,1)S(1)}, u32[]{:S(2)}, u32[]{:S(2)}) collective-permute-start(bf16[5,128,128]{2,1,0:T(8,128)(2,1)S(1)} %broadcast_select_fusion.2), channel_id=1, source_target_pairs={{0,4},{4,0},{1,5},{5,1},{2,6},{6,2},{3,7},{7,3},{8,12},{12,8},{9,1... | collective-permute-start | bytes 491528 | tf_op jit(solution)/shard_map/ppermute | solution.py:327
  63.7 1.9 %copy-start.1 = (bf16[512,1280]{1,0:T(8,128)(2,1)S(1)}, bf16[512,1280]{1,0:T(8,128)(2,1)}, u32[]{:S(2)}) copy-start(bf16[512,1280]{1,0:T(8,128)(2,1)} %convolution_convert_fusion.gate_ref) | copy-start | bytes 3932164
  68.8 15.4 %collective-permute-start.19 = (bf16[128,1280]{1,0:T(8,128)(2,1)S(1)}, bf16[128,1280]{1,0:T(8,128)(2,1)S(1)}, u32[]{:S(2)}, u32[]{:S(2)}) collective-permute-start(bf16[128,1280]{1,0:T(8,128)(2,1)S(1)} %bitcast.95), channel_id=1, source_target_pairs={{0,3},{1,0},{2,1},{3,2},{4,7},{5,4},{6,5},{7,6},{8,11},{9,8},{10,9... | collective-permute-start | bytes 983048 | tf_op jit(solution)/shard_map/ppermute | solution.py:327
  78.6 13.5 %collective-permute-start.17 = (f32[8,128]{1,0:T(8,128)S(1)}, f32[8,128]{1,0:T(8,128)S(1)}, u32[]{:S(2)}, u32[]{:S(2)}) collective-permute-start(f32[8,128]{1,0:T(8,128)S(1)} %bitcast.96), channel_id=1, source_target_pairs={{0,2},{1,3},{2,0},{3,1},{4,6},{5,7},{6,4},{7,5},{8,10},{9,11},{10,... | collective-permute-start | bytes 12296 | tf_op jit(solution)/shard_map/ppermute | solution.py:327
  79.5 11.8 %collective-permute-start.12 = (bf16[128,1280]{1,0:T(8,128)(2,1)S(1)}, bf16[128,1280]{1,0:T(8,128)(2,1)S(1)}, u32[]{:S(2)}, u32[]{:S(2)}) collective-permute-start(bf16[128,1280]{1,0:T(8,128)(2,1)S(1)} %bitcast.94), channel_id=1, source_target_pairs={{0,1},{1,2},{2,3},{3,0},{4,5},{5,6},{6,7},{7,4},{8,9},{9,10},{10,1... | collective-permute-start | bytes 983048 | tf_op jit(solution)/shard_map/ppermute | solution.py:327
  81.1 30.6 %collective-permute-start.14 = (bf16[128,1280]{1,0:T(8,128)(2,1)}, bf16[128,1280]{1,0:T(8,128)(2,1)}, u32[]{:S(2)}, u32[]{:S(2)}) collective-permute-start(bf16[128,1280]{1,0:T(8,128)(2,1)} %slice_bitcast_fusion.1), channel_id=1, source_target_pairs={{0,3},{1,0},{2,1},{3,2},{4,7},{5,4},{6,5},{7,6},{8,11},{9,8},{10,9... | collective-permute-start | bytes 983048 | tf_op jit(solution)/shard_map/ppermute | solution.py:327
  84.2 27.5 %collective-permute-start.18 = (bf16[128,1280]{1,0:T(8,128)(2,1)}, bf16[128,1280]{1,0:T(8,128)(2,1)}, u32[]{:S(2)}, u32[]{:S(2)}) collective-permute-start(bf16[128,1280]{1,0:T(8,128)(2,1)} %slice_bitcast_fusion), channel_id=1, source_target_pairs={{0,1},{1,2},{2,3},{3,0},{4,5},{5,6},{6,7},{7,4},{8,9},{9,10},{10,1... | collective-permute-start | bytes 983048 | tf_op jit(solution)/shard_map/ppermute | solution.py:327
  85.0 26.7 %collective-permute-start.20 = (bf16[128,1280]{1,0:T(8,128)(2,1)}, bf16[128,1280]{1,0:T(8,128)(2,1)}, u32[]{:S(2)}, u32[]{:S(2)}) collective-permute-start(bf16[128,1280]{1,0:T(8,128)(2,1)} %fusion), channel_id=1, source_target_pairs={{0,3},{1,0},{2,1},{3,2},{4,7},{5,4},{6,5},{7,6},{8,11},{9,8},{10,9... | collective-permute-start | bytes 983048 | tf_op jit(solution)/shard_map/ppermute | solution.py:327
  92.1 19.7 %collective-permute-start.13 = (bf16[128,1280]{1,0:T(8,128)(2,1)}, bf16[128,1280]{1,0:T(8,128)(2,1)}, u32[]{:S(2)}, u32[]{:S(2)}) collective-permute-start(bf16[128,1280]{1,0:T(8,128)(2,1)} %fusion.4), channel_id=1, source_target_pairs={{0,1},{1,2},{2,3},{3,0},{4,5},{5,6},{6,7},{7,4},{8,9},{9,10},{10,1... | collective-permute-start | bytes 983048 | tf_op jit(solution)/shard_map/ppermute | solution.py:327
  92.1 11.8 %collective-permute-start.15 = (f32[8,128]{1,0:T(8,128)S(1)}, f32[8,128]{1,0:T(8,128)S(1)}, u32[]{:S(2)}, u32[]{:S(2)}) collective-permute-start(f32[8,128]{1,0:T(8,128)S(1)} %get-tuple-element.79), channel_id=1, source_target_pairs={{0,1},{1,2},{2,3},{3,0},{4,5},{5,6},{6,7},{7,4},{8,9},{9,10},{10,1... | collective-permute-start | bytes 12296 | tf_op jit(solution)/shard_map/ppermute | solution.py:327
  103.9 7.7 %collective-permute-start.16 = (f32[8,128]{1,0:T(8,128)S(1)}, f32[8,128]{1,0:T(8,128)S(1)}, u32[]{:S(2)}, u32[]{:S(2)}) collective-permute-start(f32[8,128]{1,0:T(8,128)S(1)} %get-tuple-element.80), channel_id=1, source_target_pairs={{0,3},{1,0},{2,1},{3,2},{4,7},{5,4},{6,5},{7,6},{8,11},{9,8},{10,9... | collective-permute-start | bytes 12296 | tf_op jit(solution)/shard_map/ppermute | solution.py:327
  104.3 2.9 %copy-start = (bf16[1280,2560]{1,0:T(8,128)(2,1)S(1)}, bf16[1280,2560]{1,0:T(8,128)(2,1)}, u32[]{:S(2)}) copy-start(bf16[1280,2560]{1,0:T(8,128)(2,1)} %w_ref.5) | copy-start | bytes 19660804
  107.2 1.3 %copy-start.2 = (bf16[512,1280]{1,0:T(8,128)(2,1)S(1)}, bf16[512,1280]{1,0:T(8,128)(2,1)}, u32[]{:S(2)}) copy-start(bf16[512,1280]{1,0:T(8,128)(2,1)} %convolution_convert_fusion.gate_ref) | copy-start | bytes 3932164

commit v2 on v1

--- a/solution.py
+++ b/solution.py
@@ -7,6 +7,7 @@
 from jax.experimental.pallas import tpu as pltpu
 from jax.sharding import Mesh
 from jax.sharding import PartitionSpec as P
+
 
 HEADS = 80
 HEADDIM = 64
@@ -19,6 +20,15 @@
 SEQ = ("seq_0", "seq_1", "seq_2")
 SEQ_HEAD = ("seq_0", "seq_1", "seq_2", "head")
 
+MIB = 2**20
+RAW_LIMIT = 60 * MIB
+GATE_LIMIT = 40 * MIB
+FRONT_LIMIT = 24 * MIB
+INSIDE_LIMIT = 8 * MIB
+TAIL_LIMIT = 24 * MIB
+SMALL_LIMIT = 8 * MIB
+
+
 F32 = jnp.float32
 BF16 = jnp.bfloat16
 
@@ -36,21 +46,105 @@
     return jnp.where(lane < HEADDIM, first, second)
 
 
+def raw_kernel(tok, w_bc, w_step, w_in, in_out, bc_out, step_out, edge_out):
+    step = pl.program_id(0)
+    rows = tok.shape[0]
+
+    @pl.when(step == 0)
+    def _():
+        bc = dot(tok[...], w_bc[...]).astype(BF16)
+        bc_out[...] = bc
+        edge_out[...] = bc[rows - EDGE :]
+        heads = w_step.shape[0]
+        step_out[:, :heads] = lax.dot_general(
+            tok[...], w_step[...], (((1,), (1,)), ((), ())), preferred_element_type=F32
+        )
+
+    @pl.when(step > 0)
+    def _():
+        raw = dot(tok[...], w_in[...]).astype(BF16)
+        in_out[...] = raw
+        edge_out[...] = raw[rows - EDGE :]
+
+
+def raw_projections(tokens, w_bc, w_step, w_in):
+    rows, width = tokens.shape
+    channels = w_in.shape[1]
+    groups = channels // BLOCK
+    before = lambda i: (0, jnp.maximum(i - 1, 0))
+    fixed = lambda i: (0, 0)
+    return pl.pallas_call(
+        raw_kernel,
+        grid=(groups + 1,),
+        in_specs=[
+            pl.BlockSpec(tokens.shape, fixed),
+            pl.BlockSpec(w_bc.shape, fixed),
+            pl.BlockSpec(w_step.shape, fixed),
+            pl.BlockSpec((width, BLOCK), before),
+        ],
+        out_specs=[
+            pl.BlockSpec((rows, BLOCK), before),
+            pl.BlockSpec((rows, BLOCK), fixed),
+            pl.BlockSpec((rows, LANES), fixed),
+            pl.BlockSpec((EDGE, BLOCK), lambda i: (0, i)),
+        ],
+        out_shape=[
+            jax.ShapeDtypeStruct((rows, channels), BF16),
+            jax.ShapeDtypeStruct((rows, BLOCK), BF16),
+            jax.ShapeDtypeStruct((rows, LANES), F32),
+            jax.ShapeDtypeStruct((EDGE, channels + BLOCK), BF16),
+        ],
+        compiler_params=pltpu.CompilerParams(vmem_limit_bytes=RAW_LIMIT),
+        cost_estimate=pl.CostEstimate(
+            flops=2 * rows * width * (channels + BLOCK + LANES),
+            bytes_accessed=2 * width * (rows + channels + BLOCK),
+            transcendentals=0,
+        ),
+        name="raw",
+    )(tokens, w_bc, w_step, w_in)
+
+
+def gate_kernel(tok, w, out):
+    out[...] = dot(tok[...], w[...]).astype(BF16)
+
+
+def gate_projection(tokens, weight, start, count):
+    rows, width = tokens.shape
+    block = LANES
+    return pl.pallas_call(
+        gate_kernel,
+        grid=(count // block,),
+        in_specs=[
+            pl.BlockSpec(tokens.shape, lambda i: (0, 0)),
+            pl.BlockSpec((width, block), lambda i: (0, i + start // block)),
+        ],
+        out_specs=pl.BlockSpec((rows, block), lambda i: (0, i)),
+        out_shape=jax.ShapeDtypeStruct((rows, count), BF16),
+        compiler_params=pltpu.CompilerParams(vmem_limit_bytes=GATE_LIMIT),
+        cost_estimate=pl.CostEstimate(
+            flops=2 * rows * width * count,
+            bytes_accessed=2 * width * (rows + count),
+            transcendentals=0,
+        ),
+        name="gate",
+    )(tokens, weight)
+
+
 def front_kernel(
-    tok, edge, w_bc, w_step, w_in, taps, offset, taps_bc, offset_bc, step_bias, decay_log,
+    raw_in, raw_bc, raw_step, edge, taps, offset, taps_bc, offset_bc, step_bias, decay_log,
     x_out, bc_out, cum_out, dt_out, lead_out, local_out, prior_out, decay_out,
     padded, end_w, span_d, write_t,
 ):
     step = pl.program_id(0)
-    rows = tok.shape[0]
+    rows = raw_in.shape[0]
     spans = rows // SPAN
     heads = step_bias.shape[1]
     per = BLOCK // HEADDIM
     groups = heads // per
 
-    def conv(weight, tap, off):
-        padded[EDGE:, :] = dot(tok[...], weight).astype(BF16).astype(F32)
-        padded[:EDGE, :] = dot(edge[...], weight).astype(BF16).astype(F32)
+    def conv(raw, tap, off):
+        padded[EDGE:, :] = raw[...].astype(F32)
+        padded[:EDGE, :] = edge[...].astype(F32)
         total = off + tap[0:1, :] * padded[EDGE - 3 : EDGE - 3 + rows, :]
         for k in range(1, KERNEL):
             total = total + tap[k : k + 1, :] * padded[EDGE - 3 + k : EDGE - 3 + k + rows, :]
@@ -58,12 +152,12 @@
 
     @pl.when(step == 0)
     def _():
-        bc = conv(w_bc[...], taps_bc, offset_bc[...])
+        bc = conv(raw_bc, taps_bc, offset_bc[...])
         bc_out[...] = bc
         for s in range(spans):
             block = bc[s * SPAN : (s + 1) * SPAN, :STATE].astype(F32)
             write_t[s] = jnp.transpose(block).astype(BF16)
-        v = dot(tok[...], w_step[...]) + step_bias[...]
+        v = raw_step[:, :heads] + step_bias[...]
         dt = jnp.maximum(v, 0.0) + jnp.log1p(jnp.exp(-jnp.abs(v)))
         log_decay = -jnp.exp(decay_log[...]) * dt
         cum_out[...] = jnp.zeros_like(cum_out)
@@ -95,7 +189,7 @@
     @pl.when(step > 0)
     def _():
         g = step - 1
-        x = conv(w_in[...], taps, offset[...])
+        x = conv(raw_in, taps, offset[...])
         x_out[...] = x
         ends = end_w[g]
         gone = span_d[g]
@@ -121,10 +215,8 @@
             )
 
 
-def front(tokens, edge, w_bc, w_step, w_in, taps, offset, taps_bc, offset_bc, step_bias, decay_log):
-    rows, width = tokens.shape
-    channels = w_in.shape[1]
-    heads = step_bias.shape[1]
+def front(raw_in, raw_bc, raw_step, edge, taps, offset, taps_bc, offset_bc, step_bias, decay_log):
+    rows, channels = raw_in.shape
     groups = channels // BLOCK
     spans = rows // SPAN
     tiles = channels // LANES
@@ -145,8 +237,9 @@
         front_kernel,
         grid=(groups + 1,),
         in_specs=[
-            whole(tokens), whole(edge), whole(w_bc), whole(w_step),
-            late((width, BLOCK), 1), late((KERNEL, BLOCK), 1), late((1, BLOCK), 1),
+            late((rows, BLOCK), 1), whole(raw_bc), whole(raw_step),
+            pl.BlockSpec((EDGE, BLOCK), lambda i: (0, i)),
+            late((KERNEL, BLOCK), 1), late((1, BLOCK), 1),
             whole(taps_bc), whole(offset_bc), whole(step_bias), whole(decay_log),
         ],
         out_specs=[
@@ -171,14 +264,14 @@
             pltpu.VMEM((groups, 8, LANES), F32),
             pltpu.VMEM((spans, STATE, SPAN), BF16),
         ],
-        compiler_params=pltpu.CompilerParams(vmem_limit_bytes=28 * 2**20),
+        compiler_params=pltpu.CompilerParams(vmem_limit_bytes=FRONT_LIMIT),
         cost_estimate=pl.CostEstimate(
-            flops=2 * rows * width * (channels + 2 * STATE + LANES),
-            bytes_accessed=2 * width * (rows + channels + 2 * STATE),
+            flops=2 * rows * 2560 * channels,
+            bytes_accessed=4 * rows * channels,
             transcendentals=rows * channels,
         ),
         name="front",
-    )(tokens, edge, w_bc, w_step, w_in, taps, offset, taps_bc, offset_bc, step_bias, decay_log)
+    )(raw_in, raw_bc, raw_step, edge, taps, offset, taps_bc, offset_bc, step_bias, decay_log)
 
 
 def inside_kernel(first, x_ref, bc_ref, cum_ref, dt_ref, prior_ref, skip_ref, out_ref):
@@ -232,7 +325,7 @@
         ],
         out_specs=pl.BlockSpec((SPAN, channels), lambda i: (0, 0)),
         out_shape=jax.ShapeDtypeStruct((SPAN, channels), F32),
-        compiler_params=pltpu.CompilerParams(vmem_limit_bytes=12 * 2**20),
+        compiler_params=pltpu.CompilerParams(vmem_limit_bytes=INSIDE_LIMIT),
         cost_estimate=pl.CostEstimate(
             flops=1_500_000_000, bytes_accessed=2 * SPAN * channels, transcendentals=0
         ),
@@ -240,86 +333,158 @@
     )(x, bc, cum, dt, prior, skip)
 
 
+def split3(v):
+    high = v.astype(BF16)
+    rest = v - high.astype(F32)
+    mid = rest.astype(BF16)
+    return high, mid, (rest - mid.astype(F32)).astype(BF16)
+
+
+def joined(message, rows):
+    return (
+        message[rows : rows + 1].astype(F32)
+        + message[rows + 1 : rows + 2].astype(F32)
+        + message[rows + 2 : rows + 3].astype(F32)
+    )
+
+
+def squares_rows(total):
+    index = lax.broadcasted_iota(jnp.int32, (16, LANES), 0)
+    high, mid, low = (p.astype(F32) for p in split3(total))
+    out = jnp.where(index == 0, high, jnp.where(index == 1, mid, jnp.where(index == 2, low, 0.0)))
+    return out.astype(BF16)
+
+
 def tail_kernel(
-    which, bc_ref, lead_ref, local_ref, gate_ref, state_ref, norm_ref, w_ref,
-    left_ref, right_ref, squares_ref, gated,
+    inner_total, which, bc_ref, lead_ref, l0, l1, l2, l3, gate_a, gate_b, state_ref, norm_ref,
+    w_ref, *refs,
 ):
-    del which
-    n = pl.program_id(1)
-    tiles = local_ref.shape[2] // LANES
-
-    @pl.when(n == 0)
-    def _():
-        read = bc_ref[:, STATE:]
-        lead = lead_ref[...]
+    *outs, gated = refs
+    count = which.shape[0]
+    local_refs = (l0, l1, l2, l3)
+    channels = l0.shape[1]
+    tiles = channels // LANES
+    half = tiles // 2
+    sums = []
+    for i in range(count):
+        span = which[i]
+        at_rows = pl.ds(pl.multiple_of(span * SPAN, SPAN), SPAN)
+        read = bc_ref[at_rows, STATE:]
+        lead = lead_ref[at_rows, :]
         squares = jnp.zeros((SPAN, LANES), F32)
         for t in range(tiles):
             at = slice(t * LANES, (t + 1) * LANES)
             scale = lane_pair(lead[:, 2 * t : 2 * t + 1], lead[:, 2 * t + 1 : 2 * t + 2])
-            mixed = local_ref[0, :, at] + scale * dot(read, state_ref[t])
-            pre = mixed * silu(gate_ref[:, at].astype(F32))
+            local = local_refs[0][:, at]
+            for k in range(1, len(local_refs)):
+                local = jnp.where(span == k, local_refs[k][:, at], local)
+            mixed = local + scale * dot(read, state_ref[t])
+            gate_ref = gate_a if t < half else gate_b
+            gate = gate_ref[at_rows, (t % half) * LANES : (t % half + 1) * LANES].astype(F32)
+            pre = mixed * silu(gate)
             squares = squares + pre * pre
-            gated[:, at] = (pre * norm_ref[:, at]).astype(BF16)
-        total = jnp.sum(squares, axis=1, keepdims=True)
-        squares_ref[0] = jnp.transpose(jnp.broadcast_to(total, (SPAN, LANES)))[:8]
-
-    part = dot(gated[...], w_ref[...]).astype(BF16)
-    half = pl.num_programs(1) // 2
-
-    @pl.when(n < half)
-    def _():
-        left_ref[0] = part
-
-    @pl.when(n >= half)
-    def _():
-        right_ref[0] = part
-
-
-def tail(which, bc, lead, local, gate, state, norm, weight):
+            gated[i * SPAN : (i + 1) * SPAN, at] = (pre * norm_ref[:, at]).astype(BF16)
+        total = jnp.sum(squares, axis=1, keepdims=True) * (1.0 / inner_total)
+        sums.append(jnp.transpose(jnp.broadcast_to(total, (SPAN, LANES)))[:1])
+    width = w_ref.shape[1]
+    side_rows = width // 2 // LANES * SPAN
+    for j in range(width // BLOCK):
+        part = dot(gated[...], w_ref[:, j * BLOCK : (j + 1) * BLOCK]).astype(outs[0].dtype)
+        for u in range(BLOCK // LANES):
+            tile = j * (BLOCK // LANES) + u
+            side, tile = divmod(tile, width // 2 // LANES)
+            for i in range(count):
+                outs[2 * i + side][tile * SPAN : (tile + 1) * SPAN, :] = part[
+                    i * SPAN : (i + 1) * SPAN, u * LANES : (u + 1) * LANES
+                ]
+    for i in range(count):
+        for side in range(2):
+            out = outs[2 * i + side]
+            if out.shape[0] == side_rows + 16:
+                out[side_rows:, :] = squares_rows(sums[i])
+    if len(outs) > 2 * count:
+        outs[2 * count][...] = jnp.broadcast_to(sums[0], (8, LANES))
+
+
+def tail(which, bc, lead, inner, gate, state, norm, weight, squares_in):
     count = which.shape[0]
-    channels = local.shape[2]
+    channels = inner[0].shape[1]
     width = weight.shape[1]
-    tiles = channels // LANES
-    parts = 4
-    block = width // parts
-    half = parts // 2
-    at = lambda i, n, w: (w[i], 0)
-    fixed = lambda i, n, w: (0, 0)
-    side = jax.ShapeDtypeStruct((count, SPAN, width // 2), BF16)
+    side_rows = width // 2 // LANES * SPAN
+    vmem = pl.BlockSpec(memory_space=pltpu.VMEM)
+    shapes = []
+    for i in range(count):
+        for side in range(2):
+            extra = 16 if (i, side) in squares_in else 0
+            shapes.append(jax.ShapeDtypeStruct((side_rows + extra, LANES), BF16))
+    if not squares_in:
+        shapes.append(jax.ShapeDtypeStruct((8, LANES), F32))
     return pl.pallas_call(
-        tail_kernel,
-        grid_spec=pltpu.PrefetchScalarGridSpec(
-            num_scalar_prefetch=1,
-            grid=(count, parts),
-            in_specs=[
-                pl.BlockSpec((SPAN, 2 * STATE), at),
-                pl.BlockSpec((SPAN, LANES), at),
-                pl.BlockSpec((1, SPAN, channels), lambda i, n, w: (w[i], 0, 0)),
-                pl.BlockSpec((SPAN, channels), at),
-                pl.BlockSpec((tiles, STATE, LANES), lambda i, n, w: (0, 0, 0)),
-                pl.BlockSpec((1, channels), fixed),
-                pl.BlockSpec((channels, block), lambda i, n, w: (0, n)),
-            ],
-            out_specs=[
-                pl.BlockSpec(
-                    (1, SPAN, block), lambda i, n, w: (i, 0, jnp.minimum(n, half - 1))
-                ),
-                pl.BlockSpec(
-                    (1, SPAN, block), lambda i, n, w: (i, 0, jnp.maximum(n - half, 0))
-                ),
-                pl.BlockSpec((1, 8, LANES), lambda i, n, w: (i, 0, 0)),
-            ],
-            scratch_shapes=[pltpu.VMEM((SPAN, channels), BF16)],
-        ),
-        out_shape=[side, side, jax.ShapeDtypeStruct((count, 8, LANES), F32)],
-        compiler_params=pltpu.CompilerParams(vmem_limit_bytes=20 * 2**20),
+        functools.partial(tail_kernel, HEADS * HEADDIM),
+        in_specs=[pl.BlockSpec(memory_space=pltpu.SMEM)] + [vmem] * 11,
+        out_specs=[vmem] * len(shapes),
+        out_shape=shapes,
+        scratch_shapes=[pltpu.VMEM((count * SPAN, channels), BF16)],
+        compiler_params=pltpu.CompilerParams(vmem_limit_bytes=TAIL_LIMIT),
         cost_estimate=pl.CostEstimate(
             flops=2 * count * SPAN * channels * width,
             bytes_accessed=2 * channels * width,
             transcendentals=0,
         ),
-        name="tail",
-    )(which, bc, lead, local, gate, state, norm, weight)
+    )(which, bc, lead, *inner, *gate, state, norm, weight)
+
+
+def merge_kernel(a_ref, b_ref, b_squares, out_ref):
+    rows = a_ref.shape[0] - 16
+    out_ref[:rows, :] = (a_ref[:rows, :].astype(F32) + b_ref[:rows, :].astype(F32)).astype(BF16)
+    total = joined(a_ref, rows)
+    if b_squares:
+        total = total + joined(b_ref, rows)
+    out_ref[rows:, :] = squares_rows(total)
+
+
+def merge(near, relayed, with_squares):
+    vmem = pl.BlockSpec(memory_space=pltpu.VMEM)
+
+    def body(a_ref, b_ref, out_ref):
+        merge_kernel(a_ref, b_ref, with_squares, out_ref)
+
+    return pl.pallas_call(
+        body,
+        in_specs=[vmem] * 2,
+        out_specs=vmem,
+        out_shape=jax.ShapeDtypeStruct(near.shape, BF16),
+        compiler_params=pltpu.CompilerParams(vmem_limit_bytes=SMALL_LIMIT),
+        cost_estimate=pl.CostEstimate(flops=1000000, bytes_accessed=10**6, transcendentals=0),
+    )(near, relayed)
+
+
+def final_kernel(own_l, own_r, own_sq, up, down, direct_l, direct_r, out_ref):
+    rows = own_l.shape[0]
+    tiles = rows // SPAN
+    total = own_sq[0:1, :] + joined(up, rows) + joined(down, rows)
+    scale = lax.rsqrt(total + 0.25)
+    column = jnp.transpose(jnp.broadcast_to(scale, (LANES, SPAN)))
+    for side, parts in enumerate(((own_l, up, direct_l), (own_r, direct_r, down))):
+        for t in range(tiles):
+            at = slice(t * SPAN, (t + 1) * SPAN)
+            added = sum(p[at, :].astype(F32) for p in parts)
+            to = slice((side * tiles + t) * LANES, (side * tiles + t + 1) * LANES)
+            out_ref[:, to] = (added * column).astype(BF16)
+
+
+def final(*parts):
+    vmem = pl.BlockSpec(memory_space=pltpu.VMEM)
+    tiles = parts[0].shape[0] // SPAN
+    return pl.pallas_call(
+        final_kernel,
+        in_specs=[vmem] * len(parts),
+        out_specs=vmem,
+        out_shape=jax.ShapeDtypeStruct((SPAN, 2 * tiles * LANES), BF16),
+        compiler_params=pltpu.CompilerParams(vmem_limit_bytes=SMALL_LIMIT),
+        cost_estimate=pl.CostEstimate(flops=1000000, bytes_accessed=10**6, transcendentals=0),
+        name="final",
+    )(*parts)
 
 
 def ring(value, axis, distance):
@@ -426,43 +591,47 @@
 ):
     rows = tokens.shape[0]
     spans = rows // SPAN
+    channels = proj_inner.shape[1]
     devices = lax.axis_size(SEQ)
-    edge = lax.ppermute(tokens[rows - EDGE :], SEQ, [(i, i + 1) for i in range(devices - 1)])
-    gate_raw = dot(tokens, proj_gate).astype(BF16)
-    edge, gate_raw = lax.optimization_barrier((edge, gate_raw))
+    raw_in, raw_bc, raw_step, edge = raw_projections(tokens, proj_bc, proj_step.T, proj_inner)
+    edge = lax.ppermute(edge, SEQ, [(i, i + 1) for i in range(devices - 1)])
+    gate_a = gate_projection(tokens, proj_gate, 0, channels // 2)
     x, bc, cum, dt, lead, local, prior, decay = front(
-        tokens, edge, proj_bc, proj_step, proj_inner, conv_inner, offset_inner[None],
+        raw_in, raw_bc, raw_step, edge, conv_inner, offset_inner[None],
         conv_bc, offset_bc[None], step_bias[None], decay_log[None],
     )
+    gate_b = gate_projection(tokens, proj_gate, channels // 2, channels // 2)
     state = incoming_state(local, decay[:, 0])
     skip = jnp.repeat(skip_gain, HEADDIM)[None]
-    inner = jnp.stack([inside(s, x, bc, cum, dt, prior, skip) for s in range(spans)])
+    inner = []
+    for s in range(spans):
+        inner.append(inside(s, x, bc, cum, dt, prior, skip))
 
     head = lax.axis_index("head")
     size = lax.axis_size("head")
-    run = lambda which: tail(
-        jnp.stack([(head + k) % size for k in which]).astype(jnp.int32),
-        bc, lead, inner, gate_raw, state, norm_weight[None], out_weight,
-    )
-    far_left, far_right, far_sq = run((2,))
-    relay_up = ring(far_left[0], "head", 1)
-    relay_down = ring(far_right[0], "head", -1)
-    near_left, near_right, near_sq = run((1, 3))
-    direct_up = ring(near_right[0], "head", 1)
-    direct_down = ring(near_left[1], "head", -1)
-    up = ring((near_left[0].astype(F32) + relay_up.astype(F32)).astype(BF16), "head", 1)
-    down = ring((near_right[1].astype(F32) + relay_down.astype(F32)).astype(BF16), "head", -1)
-    own_left, own_right, own_sq = run((0,))
-    squares = (
-        own_sq[0, 0]
-        + ring(near_sq[0], "head", 1)[0]
-        + ring(near_sq[1], "head", -1)[0]
-        + ring(far_sq[0], "head", 2)[0]
-    )
-    scale = lax.rsqrt(squares / (HEADS * HEADDIM) + 0.25)[:, None]
-    left = own_left[0].astype(F32) + up.astype(F32) + direct_down.astype(F32)
-    right = own_right[0].astype(F32) + direct_up.astype(F32) + down.astype(F32)
-    return jnp.concatenate([(left * scale).astype(BF16), (right * scale).astype(BF16)], axis=1)
+
+    def run(which, squares_in):
+        order = jnp.stack([(head + k) & (size - 1) for k in which]).astype(jnp.int32)
+        return tail(
+            order, bc, lead, inner, (gate_a, gate_b), state, norm_weight[None], out_weight,
+            squares_in,
+        )
+
+    def moved(value, distance):
+        return ring(value, "head", distance)
+
+    far_left, far_right = run((2,), {(0, 0), (0, 1)})
+    relay_up = moved(far_left, 1)
+    relay_down = moved(far_right, -1)
+    next_left, next_right, last_left, last_right = run((1, 3), {(0, 0), (1, 1)})
+    direct_up = moved(next_right, 1)
+    direct_down = moved(last_left, -1)
+    own_left, own_right, own_squares = run((0,), set())
+    up = merge(next_left, relay_up, True)
+    up = moved(up, 1)
+    down = merge(last_right, relay_down, False)
+    down = moved(down, -1)
+    return final(own_left, own_right, own_squares, up, down, direct_down, direct_up)
 
 
 def solution(mesh):

time: 115 us -> 121 us (1.052)
  Pallas kernels: 29.2 us -> 44 us
  local copies, waits for them, and re-layouts: 15.5 us -> 27.2 us
  waiting for transfers between devices: 22.9 us -> 11.3 us
  matrix products: 8.33 us -> 0 us
  other arithmetic: 5.26 us -> 3.02 us
  starting transfers between devices: 32.4 us -> 33.8 us
    pallas_call x4 -> x10, Pallas kernels: 25.5 us -> 40.4 us  [the longest x1 10.7 us: raw_projections(): pl.pallas_call(raw_kernel, grid=(groups + 1,), in_specs=[pl.BlockSpec(tok...]
    unnamed x45 -> x96, local copies, waits for them, and re-layouts: 13 us -> 26.1 us
    ppermute x17 -> x14, waiting for transfers between devices: 22.2 us -> 10.3 us  [ring(): lax.ppermute(value, axis, [(i, (i + distance) % size) for i in range(size)])]
    dot_general x1 -> x0, matrix products: 8.33 us -> none  [dot(): return jnp.dot(a, b, preferred_element_type=F32)]
    convert_element_type x3 -> x0, other arithmetic: 3.16 us -> none  [the longest x1 1.57 us: per_device(): (left * scale).astype(BF16)]
    squeeze x3 -> x0, local copies, waits for them, and re-layouts: 1.48 us -> none  [the longest x1 0.75 us: per_device(): direct_down = ring(near_left[1], 'head', -1)]
    convert_element_type x3, other arithmetic: 0.02 us -> 1.37 us  [packed(): low = (decay - high.astype(F32)).astype(BF16)]
    ppermute x17 -> x14, starting transfers between devices: 21.4 us -> 22.5 us  [ring(): lax.ppermute(value, axis, [(i, (i + distance) % size) for i in range(size)])]
  transfers between devices with their start and end apart: 21 -> 18, of which waited for: 10 -> 5; matrix products, arithmetic and copies ran while one was open for 11% -> 0% of each run, Pallas kernels for 12% -> 19%
where the time goes in v2:
time: 121 us; the launch traced here: 120 us
  Pallas kernels  44 us (36%)
  starting transfers between devices  33.8 us (28%)
  local copies, waits for them, and re-layouts  27.2 us (22%)
  waiting for transfers between devices  11.3 us (9%)
  other arithmetic  3.02 us (2%)
    unnamed x96, local copies, waits for them, and re-layouts  26.1 us
    ppermute x14, starting transfers between devices, ring(): lax.ppermute(value, axis, [(i, (i + distance) % size) for i in range(size)])  22.5 us
    pallas_call x1, Pallas kernels, raw_projections(): pl.pallas_call(raw_kernel, grid=(groups + 1,), in_specs=[pl.BlockSpec(tok...  10.7 us
    ppermute x14, waiting for transfers between devices, ring(): lax.ppermute(value, axis, [(i, (i + distance) % size) for i in range(size)])  10.3 us
    ppermute x3, starting transfers between devices, onward(): lax.ppermute(value, axis, [(i, i + distance) for i in range(size) if i +...  9.99 us
    pallas_call x2, Pallas kernels, gate_projection(): pl.pallas_call(gate_kernel, grid=(count // block,), in_specs=[pl.BlockSpe...  9.79 us
    pallas_call x3, Pallas kernels, tail(): pl.pallas_call(functools.partial(tail_kernel, HEADS * HEADDIM), in_specs=...  8.01 us
    pallas_call x1, Pallas kernels, front(): pl.pallas_call(front_kernel, grid=(groups + 1,), in_specs=[late((rows, BL...  5.87 us
  transfers between devices with their start and end apart: 18, of which 5 were waited for; matrix products, arithmetic and copies ran while one was open for 0% of the time, Pallas kernels for 19%

profile of v2, /device:TPU:0, one launch (start us, length us, event | category | flops | bytes accessed | tf_op | source)
XLA Modules:
  0.0 120.1 jit_solution(17534493505853490192)
XLA Ops:
  0.0 10.7 %raw.1 = (bf16[512,1280]{1,0:T(8,128)(2,1)}, bf16[512,256]{1,0:T(8,128)(2,1)}, f32[512,128]{1,0:T(8,128)}, bf16[8,1536]{1,0:T(8,128)(2,1)}) custom-call(bf16[512,2560]{1,0:T(8,128)(2,1)} %tok.5, bf16[2560,256]{1,0:T(8,128)(2,1)} %w_bc.1, bf16[20,2560]{1,0:T(8,128)(2,1)} %bitcast.55, bf16[2560,1280]{1,0:T(8,128)(2,1)} %w_in.1), custom_call_target="tpu_custom_call" | custom-call | flops 4362076160 | bytes 10485760 | tf_op jit(solution)/shard_map/raw/pallas_call | solution.py:76
  10.7 1.3 %collective-permute-start = (bf16[8,1536]{1,0:T(8,128)(2,1)}, bf16[8,1536]{1,0:T(8,128)(2,1)S(1)}, u32[]{:S(2)}, u32[]{:S(2)}) collective-permute-start(bf16[8,1536]{1,0:T(8,128)(2,1)} %get-tuple-element.29), channel_id=1, source_target_pairs={{0,4},{4,8},{8,12},{12,16},{16,20},{20,24},{24,28},{28,32},{32,36}... | collective-permute-start | bytes 73736 | tf_op jit(solution)/shard_map/ppermute | solution.py:597
  12.0 1.0 collective-permute-done.edge
  13.1 1.3 %copy-done.35 = bf16[512,1280]{1,0:T(8,128)(2,1)S(1)} copy-done((bf16[512,1280]{1,0:T(8,128)(2,1)S(1)}, bf16[512,1280]{1,0:T(8,128)(2,1)}, u32[]{:S(2)}) %copy-start.35) | copy-done | bytes 1310744
  14.4 0.9 copy-done.36
  15.3 0.9 copy-done.37
  16.3 5.9 %front.1 = (bf16[512,1280]{1,0:T(8,128)(2,1)S(1)}, bf16[512,256]{1,0:T(8,128)(2,1)S(1)}, f32[512,128]{1,0:T(8,128)S(1)}, f32[512,128]{1,0:T(8,128)S(1)}, f32[512...) custom-call(bf16[512,1280]{1,0:T(8,128)(2,1)S(1)} %copy-done.35, ...), custom_call_target="tpu_custom_call" | custom-call | flops 3355443200 | bytes 2621440 | tf_op jit(solution)/shard_map/front/pallas_call | solution.py:236
  22.2 1.1 copy-done.23
  23.2 1.0 copy-done.26
  26.5 2.5 %collective-permute-start.1 = (bf16[656,128]{1,0:T(8,128)(2,1)}, bf16[656,128]{1,0:T(8,128)(2,1)}, u32[]{:S(2)}, u32[]{:S(2)}) collective-permute-start(bf16[656,128]{1,0:T(8,128)(2,1)} %pad_maximum_fusion.1), channel_id=1, source_target_pairs={{0,4},{4,0},{1,5},{5,1},{2,6},{6,2},{3,7},{7,3},{8,12},{12,8},{9,1... | collective-permute-start | bytes 503816 | tf_op jit(solution)/shard_map/ppermute | solution.py:492
  29.0 2.9 %copy-done.2 = bf16[2560,1280]{1,0:T(8,128)(2,1)S(1)} copy-done((bf16[2560,1280]{1,0:T(8,128)(2,1)S(1)}, bf16[2560,1280]{1,0:T(8,128)(2,1)}, u32[]{:S(2)}) %copy-start.2) | copy-done | bytes 6553624
  31.9 4.9 %gate.2.gate_a = bf16[512,640]{1,0:T(8,128)(2,1)S(1)} custom-call(bf16[512,2560]{1,0:T(8,128)(2,1)S(1)} %copy-done.3, bf16[2560,1280]{1,0:T(8,128)(2,1)S(1)} %copy-done.2), custom_call_target="tpu_custom_call" | custom-call | flops 1677721600 | bytes 5898240 | tf_op jit(solution)/shard_map/gate/pallas_call | solution.py:114
  37.7 1.4 %subtract_convert_fusion.1 = (bf16[5,128]{1,0:T(8,128)(2,1)S(1)}, bf16[5,128]{1,0:T(8,128)(2,1)S(1)}, f32[5,128]{1,0:T(8,128)S(1)}, f32[5,128]{1,0:T(8,128)S(1)}, f32[5,128]{1,0:T(8,128)}) fusion(f32[5,1,128]{2,1,0:T(1,128)S(1)} %get-tuple-element.81, bf16[656,128]{1,0:T(8,128)(2,1)} %collective-permute-done.1, pred[]{:T(512)S(6)} %eq.150), kind=kLoop, calls=%fused_computation.79 | loop fusion | flops 6400 | bytes 15361 | tf_op jit(solution)/shard_map/convert_element_type | solution.py:512
  39.3 3.7 %collective-permute-start.2 = (bf16[176,128]{1,0:T(8,128)(2,1)S(1)}, bf16[176,128]{1,0:T(8,128)(2,1)S(1)}, u32[]{:S(2)}, u32[]{:S(2)}) collective-permute-start(bf16[176,128]{1,0:T(8,128)(2,1)S(1)} %get-tuple-element.85), channel_id=1, source_target_pairs={{0,24},{8,0},{16,8},{24,16},{1,25},{9,1},{17,9},{25,17},{2,26},{10... | collective-permute-start | bytes 135176 | tf_op jit(solution)/shard_map/ppermute | solution.py:492
  43.6 1.0 collective-permute-start.4
  44.7 4.9 %gate.3.gate_b = bf16[512,640]{1,0:T(8,128)(2,1)S(1)} custom-call(bf16[512,2560]{1,0:T(8,128)(2,1)S(1)} %copy-done.4, bf16[2560,1280]{1,0:T(8,128)(2,1)S(1)} %copy-done.2), custom_call_target="tpu_custom_call" | custom-call | flops 1677721600 | bytes 5898240 | tf_op jit(solution)/shard_map/gate/pallas_call | solution.py:114
  50.1 5.9 %collective-permute-start.5 = (bf16[176,128]{1,0:T(8,128)(2,1)S(1)}, bf16[176,128]{1,0:T(8,128)(2,1)S(1)}, u32[]{:S(2)}, u32[]{:S(2)}) collective-permute-start(bf16[176,128]{1,0:T(8,128)(2,1)S(1)} %pad_maximum_fusion.3), channel_id=1, source_target_pairs={{0,96},{1,97},{2,98},{3,99},{4,100},{5,101},{6,102},{7,103},{8,104... | collective-permute-start | bytes 135176 | tf_op jit(solution)/shard_map/ppermute | solution.py:497
  56.0 1.3 %collective-permute-start.6 = (bf16[176,128]{1,0:T(8,128)(2,1)S(1)}, bf16[176,128]{1,0:T(8,128)(2,1)S(1)}, u32[]{:S(2)}, u32[]{:S(2)}) collective-permute-start(bf16[176,128]{1,0:T(8,128)(2,1)S(1)} %pad_maximum_fusion.3), channel_id=1, source_target_pairs={{0,64},{32,96},{1,65},{33,97},{2,66},{34,98},{3,67},{35,99},{4,68}... | collective-permute-start | bytes 135176 | tf_op jit(solution)/shard_map/ppermute | solution.py:497
  57.3 2.8 %collective-permute-start.7 = (bf16[176,128]{1,0:T(8,128)(2,1)S(1)}, bf16[176,128]{1,0:T(8,128)(2,1)S(1)}, u32[]{:S(2)}, u32[]{:S(2)}) collective-permute-start(bf16[176,128]{1,0:T(8,128)(2,1)S(1)} %pad_maximum_fusion.3), channel_id=1, source_target_pairs={{0,32},{32,64},{64,96},{1,33},{33,65},{65,97},{2,34},{34,66},{66,9... | collective-permute-start | bytes 135176 | tf_op jit(solution)/shard_map/ppermute | solution.py:497
  60.1 1.2 copy-done.27
  61.3 0.9 copy-done.30
  62.3 0.9 copy-done.33
  63.2 1.0 inside.7.l3
  64.5 2.3 %collective-permute-start.8 = (bf16[5,32,128]{2,1,0:T(8,128)(2,1)S(1)}, bf16[5,32,128]{2,1,0:T(8,128)(2,1)S(1)}, u32[]{:S(2)}, u32[]{:S(2)}) collective-permute-start(bf16[5,32,128]{2,1,0:T(8,128)(2,1)S(1)} %get-tuple-element.70), channel_id=1, source_target_pairs={{0,24},{8,0},{16,8},{24,16},{1,25},{9,1},{17,9},{25,17},{2,26},{10... | collective-permute-start | bytes 122888 | tf_op jit(solution)/shard_map/ppermute | solution.py:492
  66.8 1.7 %collective-permute-start.9 = (bf16[5,32,128]{2,1,0:T(8,128)(2,1)S(1)}, bf16[5,32,128]{2,1,0:T(8,128)(2,1)S(1)}, u32[]{:S(2)}, u32[]{:S(2)}) collective-permute-start(bf16[5,32,128]{2,1,0:T(8,128)(2,1)S(1)} %get-tuple-element.69), channel_id=1, source_target_pairs={{0,16},{8,24},{16,0},{24,8},{1,17},{9,25},{17,1},{25,9},{2,18},{10... | collective-permute-start | bytes 122888 | tf_op jit(solution)/shard_map/ppermute | solution.py:492
  68.5 1.1 collective-permute-start.10
  69.6 1.0 inside.6.l2
  70.6 1.7 %collective-permute-done.9 = bf16[5,32,128]{2,1,0:T(8,128)(2,1)S(1)} collective-permute-done((bf16[5,32,128]{2,1,0:T(8,128)(2,1)S(1)}, bf16[5,32,128]{2,1,0:T(8,128)(2,1)S(1)}, u32[]{:S(2)}, u32[]{:S(2)}) %collective-permute-start.9) | collective-permute-done | bytes 40992 | tf_op jit(solution)/shard_map/ppermute | solution.py:492
  72.3 1.4 %collective-permute-done.10 = bf16[5,32,128]{2,1,0:T(8,128)(2,1)S(1)} collective-permute-done((bf16[5,32,128]{2,1,0:T(8,128)(2,1)S(1)}, bf16[5,32,128]{2,1,0:T(8,128)(2,1)S(1)}, u32[]{:S(2)}, u32[]{:S(2)}) %collective-permute-start.10) | collective-permute-done | bytes 40992 | tf_op jit(solution)/shard_map/ppermute | solution.py:492
  74.3 1.0 inside.5.l1
  76.4 1.3 %slice-done.1 = s8[2359296]{0:T(1024)(128)(4,1)S(1)} async-done(((s8[6553600]{0:T(1024)(128)(4,1)}), s8[2359296]{0:T(1024)(128)(4,1)S(1)}, s32[]{:S(2)}) %slice-start.1) | async-done | bytes 2359320
  77.8 2.3 %shard_map.138 = (bf16[1296,128]{1,0:T(8,128)(2,1)}, bf16[1296,128]{1,0:T(8,128)(2,1)}) custom-call(s32[1]{0:T(128)} %bitcast.24.which, bf16[512,256]{1,0:T(8,128)(2,1)S(1)} %get-tuple-element.30.bc_ref, f32[512,128]{1,0:T(8,128)S(1)} %copy-done.15, f32[128,1280]{1,0:T(8,128)S(1)} %inside.4.l0, f32[128,1280]{1,0:T(8,128)S(1)} %inside.5.l1, ...), custom_call_target="tpu_custom_call" | custom-call | flops 838860800 | bytes 6553600 | tf_op jit(solution)/shard_map/pallas_call | solution.py:422
  80.1 2.8 %collective-permute-start.14 = (bf16[1296,128]{1,0:T(8,128)(2,1)}, bf16[1296,128]{1,0:T(8,128)(2,1)}, u32[]{:S(2)}, u32[]{:S(2)}) collective-permute-start(bf16[1296,128]{1,0:T(8,128)(2,1)} %get-tuple-element.44), channel_id=1, source_target_pairs={{0,3},{1,0},{2,1},{3,2},{4,7},{5,4},{6,5},{7,6},{8,11},{9,8},{10,9... | collective-permute-start | bytes 995336 | tf_op jit(solution)/shard_map/ppermute | solution.py:492
  82.9 2.9 %copy-done = bf16[1280,2560]{1,0:T(8,128)(2,1)S(1)} copy-done((bf16[1280,2560]{1,0:T(8,128)(2,1)S(1)}, bf16[1280,2560]{1,0:T(8,128)(2,1)}, u32[]{:S(2)}) %copy-start) | copy-done | bytes 6553624
  85.8 1.1 copy-done.6
  86.9 1.0 copy-done.9
  88.8 4.1 %shard_map.137 = (bf16[1296,128]{1,0:T(8,128)(2,1)S(1)}, bf16[1280,128]{1,0:T(8,128)(2,1)}, bf16[1280,128]{1,0:T(8,128)(2,1)}, bf16[1296,128]{1,0:T(8,128)(2,1)S(1)}) custom-call(s32[2]{0:T(128)S(1)} %pad_add_fusion.which, bf16[512,256]{1,0:T(8,128)(2,1)S(1)} %get-tuple-element.30.bc_ref, f32[512,128]{1,0:T(8,128)S(1)} %copy-done.16, ...), custom_call_target="tpu_custom_call" | custom-call | flops 1677721600 | bytes 6553600 | tf_op jit(solution)/shard_map/pallas_call | solution.py:422
  92.9 1.8 %shard_map.140 = bf16[1296,128]{1,0:T(8,128)(2,1)} custom-call(bf16[1296,128]{1,0:T(8,128)(2,1)S(1)} %get-tuple-element.43.a_ref, bf16[1296,128]{1,0:T(8,128)(2,1)} %collective-permute-done.14.b_ref), custom_call_target="tpu_custom_call" | custom-call | flops 1000000 | bytes 1000000 | tf_op jit(solution)/shard_map/pallas_call | solution.py:452
  94.7 3.2 %collective-permute-start.15 = (bf16[1296,128]{1,0:T(8,128)(2,1)}, bf16[1296,128]{1,0:T(8,128)(2,1)}, u32[]{:S(2)}, u32[]{:S(2)}) collective-permute-start(bf16[1296,128]{1,0:T(8,128)(2,1)} %shard_map.140), channel_id=1, source_target_pairs={{0,3},{1,0},{2,1},{3,2},{4,7},{5,4},{6,5},{7,6},{8,11},{9,8},{10,9... | collective-permute-start | bytes 995336 | tf_op jit(solution)/shard_map/ppermute | solution.py:492
  97.9 1.8 %shard_map.139 = bf16[1296,128]{1,0:T(8,128)(2,1)} custom-call(bf16[1296,128]{1,0:T(8,128)(2,1)S(1)} %get-tuple-element.41.a_ref, bf16[1296,128]{1,0:T(8,128)(2,1)} %collective-permute-done.12.b_ref), custom_call_target="tpu_custom_call" | custom-call | flops 1000000 | bytes 1000000 | tf_op jit(solution)/shard_map/pallas_call | solution.py:452
  99.8 3.2 %collective-permute-start.16 = (bf16[1280,128]{1,0:T(8,128)(2,1)}, bf16[1280,128]{1,0:T(8,128)(2,1)}, u32[]{:S(2)}, u32[]{:S(2)}) collective-permute-start(bf16[1280,128]{1,0:T(8,128)(2,1)} %get-tuple-element.45), channel_id=1, source_target_pairs={{0,3},{1,0},{2,1},{3,2},{4,7},{5,4},{6,5},{7,6},{8,11},{9,8},{10,9... | collective-permute-start | bytes 983048 | tf_op jit(solution)/shard_map/ppermute | solution.py:492
  103.0 2.9 %copy-done.1 = bf16[1280,2560]{1,0:T(8,128)(2,1)S(1)} copy-done((bf16[1280,2560]{1,0:T(8,128)(2,1)S(1)}, bf16[1280,2560]{1,0:T(8,128)(2,1)}, u32[]{:S(2)}) %copy-start.1) | copy-done | bytes 6553624
  105.9 1.1 copy-done.7
  106.9 1.0 copy-done.10
  108.9 1.6 %shard_map.136 = (bf16[1280,128]{1,0:T(8,128)(2,1)S(1)}, bf16[1280,128]{1,0:T(8,128)(2,1)S(1)}, f32[8,128]{1,0:T(8,128)S(1)}) custom-call(s32[1]{0:T(128)} %bitcast.which, bf16[512,256]{1,0:T(8,128)(2,1)S(1)} %get-tuple-element.30.bc_ref, f32[512,128]{1,0:T(8,128)S(1)} %copy-done.17, f32[128,1280]{1,0:T(8,128)S(1)} %copy-done.7, f32[128,1280]{1,0:T(8,128)S(1)} %inside.5.l1, ...), custom_call_target="tpu_custom_call" | custom-call | flops 838860800 | bytes 6553600 | tf_op jit(solution)/shard_map/pallas_call | solution.py:422
  110.5 1.9 %collective-permute-done.16.direct_l = bf16[1280,128]{1,0:T(8,128)(2,1)} collective-permute-done((bf16[1280,128]{1,0:T(8,128)(2,1)}, bf16[1280,128]{1,0:T(8,128)(2,1)}, u32[]{:S(2)}, u32[]{:S(2)}) %collective-permute-start.16) | collective-permute-done | bytes 327712 | tf_op jit(solution)/shard_map/ppermute | solution.py:492
  112.4 5.3 %collective-permute-done.17.direct_r = bf16[1280,128]{1,0:T(8,128)(2,1)} collective-permute-done((bf16[1280,128]{1,0:T(8,128)(2,1)}, bf16[1280,128]{1,0:T(8,128)(2,1)}, u32[]{:S(2)}, u32[]{:S(2)}) %collective-permute-start.17) | collective-permute-done | bytes 327712 | tf_op jit(solution)/shard_map/ppermute | solution.py:492
  117.7 2.4 %final.1 = bf16[128,2560]{1,0:T(8,128)(2,1)} custom-call(bf16[1280,128]{1,0:T(8,128)(2,1)S(1)} %get-tuple-element.38.own_l, bf16[1280,128]{1,0:T(8,128)(2,1)S(1)} %get-tuple-element.39.own_r, f32[8,128]{1,0:T(8,128)S(1)} %get-tuple-element.40.own_sq, bf16[1296,128]{1,0:T(8,128)(2,1)} %collective-permute-done.13.up, ...), custom_call_target="tpu_custom_call" | custom-call | flops 1000000 | bytes 1000000 | tf_op jit(solution)/shard_map/final/pallas_call | solution.py:479
  (136 shorter events, 8.2 us)
Async XLA Ops:
  0.0 12.0 %copy-start.43 = (f32[1280]{0:T(1024)S(1)}, f32[1280]{0:T(1024)}, u32[]{:S(2)}) copy-start(f32[1280]{0:T(1024)} %param.21) | copy-start | bytes 15364
  0.0 13.0 %copy-start.18 = (f32[4,1280]{1,0:T(4,128)S(1)}, f32[4,1280]{1,0:T(4,128)}, u32[]{:S(2)}) copy-start(f32[4,1280]{1,0:T(4,128)} %taps.1) | copy-start | bytes 61444
  0.0 13.0 %copy-start.19 = (f32[4,256]{1,0:T(4,128)S(1)}, f32[4,256]{1,0:T(4,128)}, u32[]{:S(2)}) copy-start(f32[4,256]{1,0:T(4,128)} %taps_bc.1) | copy-start | bytes 12292
  0.0 13.0 %copy-start.20 = (f32[256]{0:T(256)S(1)}, f32[256]{0:T(256)}, u32[]{:S(2)}) copy-start(f32[256]{0:T(256)} %param.22) | copy-start | bytes 3076
  0.0 13.0 %copy-start.21 = (f32[20]{0:T(128)S(1)}, f32[20]{0:T(128)}, u32[]{:S(2)}) copy-start(f32[20]{0:T(128)} %param.23) | copy-start | bytes 244
  0.0 13.0 %copy-start.22 = (f32[20]{0:T(128)S(1)}, f32[20]{0:T(128)}, u32[]{:S(2)}) copy-start(f32[20]{0:T(128)} %param.24) | copy-start | bytes 244
  10.7 2.3 %collective-permute-start = (bf16[8,1536]{1,0:T(8,128)(2,1)}, bf16[8,1536]{1,0:T(8,128)(2,1)S(1)}, u32[]{:S(2)}, u32[]{:S(2)}) collective-permute-start(bf16[8,1536]{1,0:T(8,128)(2,1)} %get-tuple-element.29), channel_id=1, source_target_pairs={{0,4},{4,8},{8,12},{12,16},{16,20},{20,24},{24,28},{28,32},{32,36}... | collective-permute-start | bytes 73736 | tf_op jit(solution)/shard_map/ppermute | solution.py:597
  13.0 1.3 %copy-start.35 = (bf16[512,1280]{1,0:T(8,128)(2,1)S(1)}, bf16[512,1280]{1,0:T(8,128)(2,1)}, u32[]{:S(2)}) copy-start(bf16[512,1280]{1,0:T(8,128)(2,1)} %get-tuple-element.26.raw_in) | copy-start | bytes 3932164
  16.3 12.7 %copy-start.3 = (bf16[512,2560]{1,0:T(8,128)(2,1)S(1)}, bf16[512,2560]{1,0:T(8,128)(2,1)}, u32[]{:S(2)}) copy-start(bf16[512,2560]{1,0:T(8,128)(2,1)} %tok.5) | copy-start | bytes 7864324
  25.8 13.4 %copy-start.41 = (bf16[6,128]{1,0:T(8,128)(2,1)}, bf16[6,128]{1,0:T(8,128)(2,1)S(1)}, u32[]{:S(2)}) copy-start(bf16[6,128]{1,0:T(8,128)(2,1)S(1)} %broadcast.55) | copy-start | bytes 4612
  26.5 10.3 %collective-permute-start.1 = (bf16[656,128]{1,0:T(8,128)(2,1)}, bf16[656,128]{1,0:T(8,128)(2,1)}, u32[]{:S(2)}, u32[]{:S(2)}) collective-permute-start(bf16[656,128]{1,0:T(8,128)(2,1)} %pad_maximum_fusion.1), channel_id=1, source_target_pairs={{0,4},{4,0},{1,5},{5,1},{2,6},{6,2},{3,7},{7,3},{8,12},{12,8},{9,1... | collective-permute-start | bytes 503816 | tf_op jit(solution)/shard_map/ppermute | solution.py:492
  29.0 2.9 %copy-start.2 = (bf16[2560,1280]{1,0:T(8,128)(2,1)S(1)}, bf16[2560,1280]{1,0:T(8,128)(2,1)}, u32[]{:S(2)}) copy-start(bf16[2560,1280]{1,0:T(8,128)(2,1)} %w.3) | copy-start | bytes 19660804
  31.9 7.2 %copy-start.12 = (bf16[10,128,128]{2,1,0:T(8,128)(2,1)S(1)}, bf16[10,128,128]{2,1,0:T(8,128)(2,1)}, u32[]{:S(2)}) copy-start(bf16[10,128,128]{2,1,0:T(8,128)(2,1)} %copy-done.11) | copy-start | bytes 983044
  31.9 12.8 %copy-start.4 = (bf16[512,2560]{1,0:T(8,128)(2,1)S(1)}, bf16[512,2560]{1,0:T(8,128)(2,1)}, u32[]{:S(2)}) copy-start(bf16[512,2560]{1,0:T(8,128)(2,1)} %tok.5) | copy-start | bytes 7864324
  37.7 5.9 %copy-start.38 = (bf16[640,128]{1,0:T(8,128)(2,1)}, bf16[640,128]{1,0:T(8,128)(2,1)S(1)}, u32[]{:S(2)}) copy-start(bf16[640,128]{1,0:T(8,128)(2,1)S(1)} %slice.128) | copy-start | bytes 491524
  39.3 10.6 %collective-permute-start.2 = (bf16[176,128]{1,0:T(8,128)(2,1)S(1)}, bf16[176,128]{1,0:T(8,128)(2,1)S(1)}, u32[]{:S(2)}, u32[]{:S(2)}) collective-permute-start(bf16[176,128]{1,0:T(8,128)(2,1)S(1)} %get-tuple-element.85), channel_id=1, source_target_pairs={{0,24},{8,0},{16,8},{24,16},{1,25},{9,1},{17,9},{25,17},{2,26},{10... | collective-permute-start | bytes 135176 | tf_op jit(solution)/shard_map/ppermute | solution.py:492
  43.0 6.9 %collective-permute-start.3 = (bf16[176,128]{1,0:T(8,128)(2,1)S(1)}, bf16[176,128]{1,0:T(8,128)(2,1)S(1)}, u32[]{:S(2)}, u32[]{:S(2)}) collective-permute-start(bf16[176,128]{1,0:T(8,128)(2,1)S(1)} %get-tuple-element.84), channel_id=1, source_target_pairs={{0,16},{8,24},{16,0},{24,8},{1,17},{9,25},{17,1},{25,9},{2,18},{10... | collective-permute-start | bytes 135176 | tf_op jit(solution)/shard_map/ppermute | solution.py:492
  43.6 6.1 %copy-start.45 = (f32[20]{0:T(128)S(1)}, f32[20]{0:T(128)}, u32[]{:S(2)}) copy-start(f32[20]{0:T(128)} %param.25) | copy-start | bytes 244
  43.6 6.2 %copy-start.44 = (f32[1280]{0:T(1024)S(1)}, f32[1280]{0:T(1024)}, u32[]{:S(2)}) copy-start(f32[1280]{0:T(1024)} %param.26) | copy-start | bytes 15364
  43.6 6.5 %copy-start.42 = (bf16[6,128]{1,0:T(8,128)(2,1)S(1)}, bf16[6,128]{1,0:T(8,128)(2,1)}, u32[]{:S(2)}) copy-start(bf16[6,128]{1,0:T(8,128)(2,1)} %copy-done.41) | copy-start | bytes 4612
  43.6 16.5 %copy-start.24 = (bf16[512,1280]{1,0:T(8,128)(2,1)S(1)}, bf16[512,1280]{1,0:T(8,128)(2,1)}, u32[]{:S(2)}) copy-start(bf16[512,1280]{1,0:T(8,128)(2,1)} %copy-done.23) | copy-start | bytes 3932164
  43.6 6.3 %collective-permute-start.4 = (bf16[176,128]{1,0:T(8,128)(2,1)S(1)}, bf16[176,128]{1,0:T(8,128)(2,1)S(1)}, u32[]{:S(2)}, u32[]{:S(2)}) collective-permute-start(bf16[176,128]{1,0:T(8,128)(2,1)S(1)} %get-tuple-element.83), channel_id=1, source_target_pairs={{0,8},{8,16},{16,24},{24,0},{1,9},{9,17},{17,25},{25,1},{2,10},{10... | collective-permute-start | bytes 135176 | tf_op jit(solution)/shard_map/ppermute | solution.py:492
  50.1 14.1 %collective-permute-start.5 = (bf16[176,128]{1,0:T(8,128)(2,1)S(1)}, bf16[176,128]{1,0:T(8,128)(2,1)S(1)}, u32[]{:S(2)}, u32[]{:S(2)}) collective-permute-start(bf16[176,128]{1,0:T(8,128)(2,1)S(1)} %pad_maximum_fusion.3), channel_id=1, source_target_pairs={{0,96},{1,97},{2,98},{3,99},{4,100},{5,101},{6,102},{7,103},{8,104... | collective-permute-start | bytes 135176 | tf_op jit(solution)/shard_map/ppermute | solution.py:497
  56.0 8.2 %collective-permute-start.6 = (bf16[176,128]{1,0:T(8,128)(2,1)S(1)}, bf16[176,128]{1,0:T(8,128)(2,1)S(1)}, u32[]{:S(2)}, u32[]{:S(2)}) collective-permute-start(bf16[176,128]{1,0:T(8,128)(2,1)S(1)} %pad_maximum_fusion.3), channel_id=1, source_target_pairs={{0,64},{32,96},{1,65},{33,97},{2,66},{34,98},{3,67},{35,99},{4,68}... | collective-permute-start | bytes 135176 | tf_op jit(solution)/shard_map/ppermute | solution.py:497
  57.3 6.9 %collective-permute-start.7 = (bf16[176,128]{1,0:T(8,128)(2,1)S(1)}, bf16[176,128]{1,0:T(8,128)(2,1)S(1)}, u32[]{:S(2)}, u32[]{:S(2)}) collective-permute-start(bf16[176,128]{1,0:T(8,128)(2,1)S(1)} %pad_maximum_fusion.3), channel_id=1, source_target_pairs={{0,32},{32,64},{64,96},{1,33},{33,65},{65,97},{2,34},{34,66},{66,9... | collective-permute-start | bytes 135176 | tf_op jit(solution)/shard_map/ppermute | solution.py:497
  63.2 6.4 %copy-start.25 = (bf16[512,1280]{1,0:T(8,128)(2,1)S(1)}, bf16[512,1280]{1,0:T(8,128)(2,1)}, u32[]{:S(2)}) copy-start(bf16[512,1280]{1,0:T(8,128)(2,1)} %copy-done.23) | copy-start | bytes 3932164
  63.2 6.4 %copy-start.28 = (bf16[3,10,128,128]{3,2,1,0:T(8,128)(2,1)S(1)}, bf16[3,10,128,128]{3,2,1,0:T(8,128)(2,1)}, u32[]{:S(2)}) copy-start(bf16[3,10,128,128]{3,2,1,0:T(8,128)(2,1)} %copy-done.26) | copy-start | bytes 2949124
  63.2 6.4 %copy-start.31 = (f32[512,128]{1,0:T(8,128)S(1)}, f32[512,128]{1,0:T(8,128)}, u32[]{:S(2)}) copy-start(f32[512,128]{1,0:T(8,128)} %copy-done.29) | copy-start | bytes 786436
  64.5 6.1 %collective-permute-start.8 = (bf16[5,32,128]{2,1,0:T(8,128)(2,1)S(1)}, bf16[5,32,128]{2,1,0:T(8,128)(2,1)S(1)}, u32[]{:S(2)}, u32[]{:S(2)}) collective-permute-start(bf16[5,32,128]{2,1,0:T(8,128)(2,1)S(1)} %get-tuple-element.70), channel_id=1, source_target_pairs={{0,24},{8,0},{16,8},{24,16},{1,25},{9,1},{17,9},{25,17},{2,26},{10... | collective-permute-start | bytes 122888 | tf_op jit(solution)/shard_map/ppermute | solution.py:492
  66.8 5.5 %collective-permute-start.9 = (bf16[5,32,128]{2,1,0:T(8,128)(2,1)S(1)}, bf16[5,32,128]{2,1,0:T(8,128)(2,1)S(1)}, u32[]{:S(2)}, u32[]{:S(2)}) collective-permute-start(bf16[5,32,128]{2,1,0:T(8,128)(2,1)S(1)} %get-tuple-element.69), channel_id=1, source_target_pairs={{0,16},{8,24},{16,0},{24,8},{1,17},{9,25},{17,1},{25,9},{2,18},{10... | collective-permute-start | bytes 122888 | tf_op jit(solution)/shard_map/ppermute | solution.py:492
  68.5 5.3 %copy-start.13 = (bf16[10,128,128]{2,1,0:T(8,128)(2,1)S(1)}, bf16[10,128,128]{2,1,0:T(8,128)(2,1)}, u32[]{:S(2)}) copy-start(bf16[10,128,128]{2,1,0:T(8,128)(2,1)} %copy-done.11) | copy-start | bytes 983044
  68.5 5.3 %copy-start.39 = (bf16[640,128]{1,0:T(8,128)(2,1)S(1)}, bf16[640,128]{1,0:T(8,128)(2,1)}, u32[]{:S(2)}) copy-start(bf16[640,128]{1,0:T(8,128)(2,1)} %copy-done.38) | copy-start | bytes 491524
  68.5 5.3 %copy-start.40 = (f32[5,128]{1,0:T(8,128)S(1)}, f32[5,128]{1,0:T(8,128)}, u32[]{:S(2)}) copy-start(f32[5,128]{1,0:T(8,128)} %get-tuple-element.68) | copy-start | bytes 7684
  68.5 5.2 %collective-permute-start.10 = (bf16[5,32,128]{2,1,0:T(8,128)(2,1)S(1)}, bf16[5,32,128]{2,1,0:T(8,128)(2,1)S(1)}, u32[]{:S(2)}, u32[]{:S(2)}) collective-permute-start(bf16[5,32,128]{2,1,0:T(8,128)(2,1)S(1)} %get-tuple-element.51), channel_id=1, source_target_pairs={{0,8},{8,16},{16,24},{24,0},{1,9},{9,17},{17,25},{25,1},{2,10},{10... | collective-permute-start | bytes 122888 | tf_op jit(solution)/shard_map/ppermute | solution.py:492
  74.0 2.0 %collective-permute-start.11 = (bf16[5,128,128]{2,1,0:T(8,128)(2,1)S(1)}, bf16[5,128,128]{2,1,0:T(8,128)(2,1)S(1)}, u32[]{:S(2)}, u32[]{:S(2)}) collective-permute-start(bf16[5,128,128]{2,1,0:T(8,128)(2,1)S(1)} %broadcast_select_fusion.2), channel_id=1, source_target_pairs={{0,4},{4,0},{1,5},{5,1},{2,6},{6,2},{3,7},{7,3},{8,12},{12,8},{9,1... | collective-permute-start | bytes 491528 | tf_op jit(solution)/shard_map/ppermute | solution.py:492
  74.2 2.2 %slice-start = ((s8[6553600]{0:T(1024)(128)(4,1)}), s8[4194304]{0:T(1024)(128)(4,1)S(1)}, s32[]{:S(2)}) async-start(s8[6553600]{0:T(1024)(128)(4,1)} %bitcast.36), calls=%async_computation | async-start | bytes 8388608
  75.2 2.5 %slice-start.1 = ((s8[6553600]{0:T(1024)(128)(4,1)}), s8[2359296]{0:T(1024)(128)(4,1)S(1)}, s32[]{:S(2)}) async-start(s8[6553600]{0:T(1024)(128)(4,1)} %bitcast.36), calls=%async_computation.1 | async-start | bytes 4718592
  75.3 2.5 %copy-start.15 = (f32[512,128]{1,0:T(8,128)S(1)}, f32[512,128]{1,0:T(8,128)}, u32[]{:S(2)}) copy-start(f32[512,128]{1,0:T(8,128)} %copy-done.14) | copy-start | bytes 786436
  75.9 4.1 %copy-start.5 = (f32[128,1280]{1,0:T(8,128)}, f32[128,1280]{1,0:T(8,128)S(1)}, u32[]{:S(2)}) copy-start(f32[128,1280]{1,0:T(8,128)S(1)} %inside.4.l0) | copy-start | bytes 1966084
  76.2 3.9 %copy-start.8 = (bf16[10,128,128]{2,1,0:T(8,128)(2,1)}, bf16[10,128,128]{2,1,0:T(8,128)(2,1)S(1)}, u32[]{:S(2)}) copy-start(bf16[10,128,128]{2,1,0:T(8,128)(2,1)S(1)} %pad_maximum_fusion.state_ref) | copy-start | bytes 983044
  80.1 12.8 %collective-permute-start.14 = (bf16[1296,128]{1,0:T(8,128)(2,1)}, bf16[1296,128]{1,0:T(8,128)(2,1)}, u32[]{:S(2)}, u32[]{:S(2)}) collective-permute-start(bf16[1296,128]{1,0:T(8,128)(2,1)} %get-tuple-element.44), channel_id=1, source_target_pairs={{0,3},{1,0},{2,1},{3,2},{4,7},{5,4},{6,5},{7,6},{8,11},{9,8},{10,9... | collective-permute-start | bytes 995336 | tf_op jit(solution)/shard_map/ppermute | solution.py:492
  82.8 15.1 %collective-permute-start.12 = (bf16[1296,128]{1,0:T(8,128)(2,1)}, bf16[1296,128]{1,0:T(8,128)(2,1)}, u32[]{:S(2)}, u32[]{:S(2)}) collective-permute-start(bf16[1296,128]{1,0:T(8,128)(2,1)} %get-tuple-element.42), channel_id=1, source_target_pairs={{0,1},{1,2},{2,3},{3,0},{4,5},{5,6},{6,7},{7,4},{8,9},{9,10},{10,1... | collective-permute-start | bytes 995336 | tf_op jit(solution)/shard_map/ppermute | solution.py:492
  82.9 2.9 %copy-start = (bf16[1280,2560]{1,0:T(8,128)(2,1)S(1)}, bf16[1280,2560]{1,0:T(8,128)(2,1)}, u32[]{:S(2)}) copy-start(bf16[1280,2560]{1,0:T(8,128)(2,1)} %w_ref.5) | copy-start | bytes 19660804
  94.7 23.0 %collective-permute-start.15 = (bf16[1296,128]{1,0:T(8,128)(2,1)}, bf16[1296,128]{1,0:T(8,128)(2,1)}, u32[]{:S(2)}, u32[]{:S(2)}) collective-permute-start(bf16[1296,128]{1,0:T(8,128)(2,1)} %shard_map.140), channel_id=1, source_target_pairs={{0,3},{1,0},{2,1},{3,2},{4,7},{5,4},{6,5},{7,6},{8,11},{9,8},{10,9... | collective-permute-start | bytes 995336 | tf_op jit(solution)/shard_map/ppermute | solution.py:492
  99.7 17.9 %collective-permute-start.13 = (bf16[1296,128]{1,0:T(8,128)(2,1)}, bf16[1296,128]{1,0:T(8,128)(2,1)}, u32[]{:S(2)}, u32[]{:S(2)}) collective-permute-start(bf16[1296,128]{1,0:T(8,128)(2,1)} %shard_map.139), channel_id=1, source_target_pairs={{0,1},{1,2},{2,3},{3,0},{4,5},{5,6},{6,7},{7,4},{8,9},{9,10},{10,1... | collective-permute-start | bytes 995336 | tf_op jit(solution)/shard_map/ppermute | solution.py:492
  99.8 12.6 %collective-permute-start.16 = (bf16[1280,128]{1,0:T(8,128)(2,1)}, bf16[1280,128]{1,0:T(8,128)(2,1)}, u32[]{:S(2)}, u32[]{:S(2)}) collective-permute-start(bf16[1280,128]{1,0:T(8,128)(2,1)} %get-tuple-element.45), channel_id=1, source_target_pairs={{0,3},{1,0},{2,1},{3,2},{4,7},{5,4},{6,5},{7,6},{8,11},{9,8},{10,9... | collective-permute-start | bytes 983048 | tf_op jit(solution)/shard_map/ppermute | solution.py:492
  103.0 14.7 %collective-permute-start.17 = (bf16[1280,128]{1,0:T(8,128)(2,1)}, bf16[1280,128]{1,0:T(8,128)(2,1)}, u32[]{:S(2)}, u32[]{:S(2)}) collective-permute-start(bf16[1280,128]{1,0:T(8,128)(2,1)} %get-tuple-element.46), channel_id=1, source_target_pairs={{0,1},{1,2},{2,3},{3,0},{4,5},{5,6},{6,7},{7,4},{8,9},{9,10},{10,1... | collective-permute-start | bytes 983048 | tf_op jit(solution)/shard_map/ppermute | solution.py:492
  103.0 2.9 %copy-start.1 = (bf16[1280,2560]{1,0:T(8,128)(2,1)S(1)}, bf16[1280,2560]{1,0:T(8,128)(2,1)}, u32[]{:S(2)}) copy-start(bf16[1280,2560]{1,0:T(8,128)(2,1)} %w_ref.5) | copy-start | bytes 19660804
  (18 other events, 17.5 us)

commit v3 on v2

--- a/solution.py
+++ b/solution.py
@@ -21,8 +21,7 @@
 SEQ_HEAD = ("seq_0", "seq_1", "seq_2", "head")
 
 MIB = 2**20
-RAW_LIMIT = 60 * MIB
-GATE_LIMIT = 40 * MIB
+RAW_LIMIT = 24 * MIB
 FRONT_LIMIT = 24 * MIB
 INSIDE_LIMIT = 8 * MIB
 TAIL_LIMIT = 24 * MIB
@@ -30,7 +29,12 @@
 
 
 F32 = jnp.float32
+X_SPACE = pltpu.HBM
 BF16 = jnp.bfloat16
+
+
+def in_hbm(*arrays):
+    return [pltpu.with_memory_space_constraint(a, pltpu.HBM) for a in arrays]
 
 
 def dot(a, b):
@@ -46,101 +50,128 @@
     return jnp.where(lane < HEADDIM, first, second)
 
 
-def raw_kernel(tok, w_bc, w_step, w_in, in_out, bc_out, step_out, edge_out):
-    step = pl.program_id(0)
+def raw_kernel(
+    tok_hbm, bc_hbm, step_hbm, in_hbm, gate_hbm,
+    in_out, bc_out, step_out, edge_out, gate_out,
+    tok, w_bc, w_step, w_wide, sems,
+):
     rows = tok.shape[0]
-
-    @pl.when(step == 0)
-    def _():
-        bc = dot(tok[...], w_bc[...]).astype(BF16)
-        bc_out[...] = bc
-        edge_out[...] = bc[rows - EDGE :]
-        heads = w_step.shape[0]
-        step_out[:, :heads] = lax.dot_general(
-            tok[...], w_step[...], (((1,), (1,)), ((), ())), preferred_element_type=F32
-        )
-
-    @pl.when(step > 0)
-    def _():
-        raw = dot(tok[...], w_in[...]).astype(BF16)
-        in_out[...] = raw
-        edge_out[...] = raw[rows - EDGE :]
-
-
-def raw_projections(tokens, w_bc, w_step, w_in):
+    heads = w_step.shape[0]
+    width = in_hbm.shape[1] // 2
+
+    def part(k):
+        source = in_hbm if k < 2 else gate_hbm
+        at = slice(k % 2 * width, (k % 2 + 1) * width)
+        return pltpu.make_async_copy(source.at[:, at], w_wide.at[k], sems.at[3 + k])
+
+    first = [
+        pltpu.make_async_copy(tok_hbm, tok, sems.at[0]),
+        pltpu.make_async_copy(bc_hbm, w_bc, sems.at[1]),
+        pltpu.make_async_copy(step_hbm, w_step, sems.at[2]),
+    ]
+    for copy in first:
+        copy.start()
+    for copy in first:
+        copy.wait()
+    part(0).start()
+    bc = dot(tok[...], w_bc[...]).astype(BF16)
+    bc_out[...] = bc
+    edge_out[:, :BLOCK] = bc[rows - EDGE :]
+    step_out[:, :heads] = lax.dot_general(
+        tok[...], w_step[...], (((1,), (1,)), ((), ())), preferred_element_type=F32
+    )
+    for k in range(4):
+        part(k).wait()
+        if k < 3:
+            part(k + 1).start()
+        at = slice(k % 2 * width, (k % 2 + 1) * width)
+        raw = dot(tok[...], w_wide[k]).astype(BF16)
+        if k < 2:
+            in_out[:, at] = raw
+            edge_out[:, BLOCK + k * width : BLOCK + (k + 1) * width] = raw[rows - EDGE :]
+        else:
+            gate_out[:, at] = raw
+
+
+def raw_projections(tokens, w_bc, w_step, w_in, w_gate):
     rows, width = tokens.shape
     channels = w_in.shape[1]
-    groups = channels // BLOCK
-    before = lambda i: (0, jnp.maximum(i - 1, 0))
-    fixed = lambda i: (0, 0)
+    vmem = pl.BlockSpec(memory_space=pltpu.VMEM)
     return pl.pallas_call(
         raw_kernel,
-        grid=(groups + 1,),
-        in_specs=[
-            pl.BlockSpec(tokens.shape, fixed),
-            pl.BlockSpec(w_bc.shape, fixed),
-            pl.BlockSpec(w_step.shape, fixed),
-            pl.BlockSpec((width, BLOCK), before),
-        ],
-        out_specs=[
-            pl.BlockSpec((rows, BLOCK), before),
-            pl.BlockSpec((rows, BLOCK), fixed),
-            pl.BlockSpec((rows, LANES), fixed),
-            pl.BlockSpec((EDGE, BLOCK), lambda i: (0, i)),
-        ],
+        in_specs=[pl.BlockSpec(memory_space=pltpu.HBM)] * 5,
+        out_specs=[vmem] * 5,
         out_shape=[
             jax.ShapeDtypeStruct((rows, channels), BF16),
             jax.ShapeDtypeStruct((rows, BLOCK), BF16),
             jax.ShapeDtypeStruct((rows, LANES), F32),
             jax.ShapeDtypeStruct((EDGE, channels + BLOCK), BF16),
+            jax.ShapeDtypeStruct((rows, channels), BF16),
+        ],
+        scratch_shapes=[
+            pltpu.VMEM(tokens.shape, BF16),
+            pltpu.VMEM(w_bc.shape, BF16),
+            pltpu.VMEM(w_step.shape, BF16),
+            pltpu.VMEM((4, width, channels // 2), BF16),
+            pltpu.SemaphoreType.DMA((7,)),
         ],
         compiler_params=pltpu.CompilerParams(vmem_limit_bytes=RAW_LIMIT),
         cost_estimate=pl.CostEstimate(
-            flops=2 * rows * width * (channels + BLOCK + LANES),
-            bytes_accessed=2 * width * (rows + channels + BLOCK),
+            flops=2 * rows * width * (2 * channels + BLOCK + LANES),
+            bytes_accessed=2 * width * (rows + 2 * channels + BLOCK),
             transcendentals=0,
         ),
         name="raw",
-    )(tokens, w_bc, w_step, w_in)
-
-
-def gate_kernel(tok, w, out):
-    out[...] = dot(tok[...], w[...]).astype(BF16)
-
-
-def gate_projection(tokens, weight, start, count):
-    rows, width = tokens.shape
-    block = LANES
+    )(*in_hbm(tokens, w_bc, w_step, w_in, w_gate))
+
+
+def steps_kernel(raw_step, step_bias, decay_log, cum_out, dt_out, lead_out):
+    rows = raw_step.shape[0]
+    heads = step_bias.shape[1]
+    v = raw_step[:, :heads] + step_bias[...]
+    dt = jnp.maximum(v, 0.0) + jnp.log1p(jnp.exp(-jnp.abs(v)))
+    log_decay = -jnp.exp(decay_log[...]) * dt
+    cum_out[...] = jnp.zeros_like(cum_out)
+    dt_out[...] = jnp.zeros_like(dt_out)
+    lead_out[...] = jnp.zeros_like(lead_out)
+    dt_out[:, :heads] = dt
+    row = lax.broadcasted_iota(jnp.int32, (SPAN, SPAN), 0)
+    col = lax.broadcasted_iota(jnp.int32, (SPAN, SPAN), 1)
+    lower = (row >= col).astype(F32)
+    lead = jnp.zeros((1, heads), F32)
+    for s in range(rows // SPAN):
+        at = slice(s * SPAN, (s + 1) * SPAN)
+        cum = jnp.dot(
+            lower, log_decay[at], preferred_element_type=F32, precision=lax.Precision.HIGHEST
+        )
+        cum_out[at, :heads] = cum
+        lead_out[at, :heads] = jnp.exp(cum + lead)
+        lead = lead + cum[SPAN - 1 :, :]
+
+
+def steps(raw_step, step_bias, decay_log):
+    vmem = pl.BlockSpec(memory_space=pltpu.VMEM)
     return pl.pallas_call(
-        gate_kernel,
-        grid=(count // block,),
-        in_specs=[
-            pl.BlockSpec(tokens.shape, lambda i: (0, 0)),
-            pl.BlockSpec((width, block), lambda i: (0, i + start // block)),
-        ],
-        out_specs=pl.BlockSpec((rows, block), lambda i: (0, i)),
-        out_shape=jax.ShapeDtypeStruct((rows, count), BF16),
-        compiler_params=pltpu.CompilerParams(vmem_limit_bytes=GATE_LIMIT),
-        cost_estimate=pl.CostEstimate(
-            flops=2 * rows * width * count,
-            bytes_accessed=2 * width * (rows + count),
-            transcendentals=0,
-        ),
-        name="gate",
-    )(tokens, weight)
+        steps_kernel,
+        in_specs=[vmem] * 3,
+        out_specs=[vmem] * 3,
+        out_shape=[jax.ShapeDtypeStruct(raw_step.shape, F32)] * 3,
+        compiler_params=pltpu.CompilerParams(vmem_limit_bytes=SMALL_LIMIT),
+        cost_estimate=pl.CostEstimate(flops=10**9, bytes_accessed=10**6, transcendentals=0),
+        name="steps",
+    )(raw_step, step_bias, decay_log)
 
 
 def front_kernel(
-    raw_in, raw_bc, raw_step, edge, taps, offset, taps_bc, offset_bc, step_bias, decay_log,
-    x_out, bc_out, cum_out, dt_out, lead_out, local_out, prior_out, decay_out,
+    raw_in, raw_bc, edge, cum_ref, dt_ref, lead_ref, taps, offset, taps_bc, offset_bc,
+    x_out, bc_out, local_out, prior_out, decay_out,
     padded, end_w, span_d, write_t,
 ):
     step = pl.program_id(0)
     rows = raw_in.shape[0]
     spans = rows // SPAN
-    heads = step_bias.shape[1]
     per = BLOCK // HEADDIM
-    groups = heads // per
+    groups = end_w.shape[0]
 
     def conv(raw, tap, off):
         padded[EDGE:, :] = raw[...].astype(F32)
@@ -157,34 +188,17 @@
         for s in range(spans):
             block = bc[s * SPAN : (s + 1) * SPAN, :STATE].astype(F32)
             write_t[s] = jnp.transpose(block).astype(BF16)
-        v = raw_step[:, :heads] + step_bias[...]
-        dt = jnp.maximum(v, 0.0) + jnp.log1p(jnp.exp(-jnp.abs(v)))
-        log_decay = -jnp.exp(decay_log[...]) * dt
-        cum_out[...] = jnp.zeros_like(cum_out)
-        dt_out[...] = jnp.zeros_like(dt_out)
-        lead_out[...] = jnp.zeros_like(lead_out)
-        dt_out[:, :heads] = dt
-        row = lax.broadcasted_iota(jnp.int32, (SPAN, SPAN), 0)
-        col = lax.broadcasted_iota(jnp.int32, (SPAN, SPAN), 1)
-        lower = (row >= col).astype(F32)
-        lead = jnp.zeros((1, heads), F32)
         for s in range(spans):
             at = slice(s * SPAN, (s + 1) * SPAN)
-            cum = jnp.dot(
-                lower, log_decay[at], preferred_element_type=F32, precision=lax.Precision.HIGHEST
-            )
-            cum_out[at, :heads] = cum
-            lead_out[at, :heads] = jnp.exp(cum + lead)
+            cum = cum_ref[at, :]
             last = cum[SPAN - 1 :, :]
-            lead = lead + last
-            ends = jnp.exp(last - cum) * dt[at]
+            ends = jnp.exp(last - cum) * dt_ref[at, :]
             gone = jnp.exp(last)
             for g in range(groups):
                 end_w[g, at, :per] = ends[:, g * per : (g + 1) * per]
                 span_d[g, s : s + 1, :per] = gone[:, g * per : (g + 1) * per]
-        total = jnp.exp(lead)
         for g in range(groups):
-            span_d[g, spans : spans + 1, :per] = total[:, g * per : (g + 1) * per]
+            span_d[g, spans : spans + 1, :per] = lead_ref[rows - 1 :, g * per : (g + 1) * per]
 
     @pl.when(step > 0)
     def _():
@@ -215,7 +229,7 @@
             )
 
 
-def front(raw_in, raw_bc, raw_step, edge, taps, offset, taps_bc, offset_bc, step_bias, decay_log):
+def front(raw_in, raw_bc, edge, cum, dt, lead, taps, offset, taps_bc, offset_bc):
     rows, channels = raw_in.shape
     groups = channels // BLOCK
     spans = rows // SPAN
@@ -231,31 +245,28 @@
             lambda i: tuple(jnp.maximum(i - 1, 0) if d == dim else 0 for d in range(len(shape))),
         )
 
-    head_shape = jax.ShapeDtypeStruct((rows, LANES), F32)
-    head_spec = pl.BlockSpec((rows, LANES), lambda i: (0, 0))
     return pl.pallas_call(
         front_kernel,
         grid=(groups + 1,),
         in_specs=[
-            late((rows, BLOCK), 1), whole(raw_bc), whole(raw_step),
+            late((rows, BLOCK), 1), whole(raw_bc),
             pl.BlockSpec((EDGE, BLOCK), lambda i: (0, i)),
+            whole(cum), whole(dt), whole(lead),
             late((KERNEL, BLOCK), 1), late((1, BLOCK), 1),
-            whole(taps_bc), whole(offset_bc), whole(step_bias), whole(decay_log),
+            whole(taps_bc), whole(offset_bc),
         ],
         out_specs=[
             late((rows, BLOCK), 1),
             pl.BlockSpec((rows, 2 * STATE), lambda i: (0, 0)),
-            head_spec, head_spec, head_spec,
             late((per_block, STATE, LANES), 0),
             late((spans - 1, per_block, STATE, LANES), 1),
             late((per_block, 8, LANES), 0),
         ],
         out_shape=[
-            jax.ShapeDtypeStruct((rows, channels), BF16),
+            X_SPACE((rows, channels), BF16),
             jax.ShapeDtypeStruct((rows, 2 * STATE), BF16),
-            head_shape, head_shape, head_shape,
             jax.ShapeDtypeStruct((tiles, STATE, LANES), BF16),
-            jax.ShapeDtypeStruct((spans - 1, tiles, STATE, LANES), BF16),
+            X_SPACE((spans - 1, tiles, STATE, LANES), BF16),
             jax.ShapeDtypeStruct((tiles, 8, LANES), F32),
         ],
         scratch_shapes=[
@@ -271,7 +282,7 @@
             transcendentals=rows * channels,
         ),
         name="front",
-    )(raw_in, raw_bc, raw_step, edge, taps, offset, taps_bc, offset_bc, step_bias, decay_log)
+    )(raw_in, raw_bc, edge, cum, dt, lead, taps, offset, taps_bc, offset_bc)
 
 
 def inside_kernel(first, x_ref, bc_ref, cum_ref, dt_ref, prior_ref, skip_ref, out_ref):
@@ -330,7 +341,7 @@
             flops=1_500_000_000, bytes_accessed=2 * SPAN * channels, transcendentals=0
         ),
         name="inside",
-    )(x, bc, cum, dt, prior, skip)
+    )(*in_hbm(x), bc, cum, dt, *in_hbm(prior), skip)
 
 
 def split3(v):
@@ -356,7 +367,7 @@
 
 
 def tail_kernel(
-    inner_total, which, bc_ref, lead_ref, l0, l1, l2, l3, gate_a, gate_b, state_ref, norm_ref,
+    inner_total, which, bc_ref, lead_ref, l0, l1, l2, l3, gate_ref, state_ref, norm_ref,
     w_ref, *refs,
 ):
     *outs, gated = refs
@@ -364,7 +375,6 @@
     local_refs = (l0, l1, l2, l3)
     channels = l0.shape[1]
     tiles = channels // LANES
-    half = tiles // 2
     sums = []
     for i in range(count):
         span = which[i]
@@ -379,8 +389,7 @@
             for k in range(1, len(local_refs)):
                 local = jnp.where(span == k, local_refs[k][:, at], local)
             mixed = local + scale * dot(read, state_ref[t])
-            gate_ref = gate_a if t < half else gate_b
-            gate = gate_ref[at_rows, (t % half) * LANES : (t % half + 1) * LANES].astype(F32)
+            gate = gate_ref[at_rows, at].astype(F32)
             pre = mixed * silu(gate)
             squares = squares + pre * pre
             gated[i * SPAN : (i + 1) * SPAN, at] = (pre * norm_ref[:, at]).astype(BF16)
@@ -421,7 +430,7 @@
         shapes.append(jax.ShapeDtypeStruct((8, LANES), F32))
     return pl.pallas_call(
         functools.partial(tail_kernel, HEADS * HEADDIM),
-        in_specs=[pl.BlockSpec(memory_space=pltpu.SMEM)] + [vmem] * 11,
+        in_specs=[pl.BlockSpec(memory_space=pltpu.SMEM)] + [vmem] * 10,
         out_specs=[vmem] * len(shapes),
         out_shape=shapes,
         scratch_shapes=[pltpu.VMEM((count * SPAN, channels), BF16)],
@@ -431,7 +440,7 @@
             bytes_accessed=2 * channels * width,
             transcendentals=0,
         ),
-    )(which, bc, lead, *inner, *gate, state, norm, weight)
+    )(which, bc, lead, *inner, gate, state, norm, weight)
 
 
 def merge_kernel(a_ref, b_ref, b_squares, out_ref):
@@ -543,9 +552,9 @@
     part = STATE // ys
     quarters = [chip[:, q * part : (q + 1) * part] for q in range(ys)]
     sent = [pick(quarters, (y + k) % ys) for k in range(ys)]
-    got = [
-        unpacked(ring(packed(sent[k], chip_d[:, 0]), y_axis, k), tiles) for k in range(1, ys)
-    ]
+    messages = [packed(sent[k], chip_d[:, 0]) for k in range(1, ys)]
+    got = [ring(message, y_axis, k + 1) for k, message in enumerate(messages)]
+    got = [unpacked(message, tiles) for message in got]
     by_shift = [(sent[0], chip_d)] + got
     states = [pick([g[0] for g in by_shift], (y - q) % ys) for q in range(ys)]
     decays = [pick([g[1] for g in by_shift], (y - q) % ys) for q in range(ys)]
@@ -554,7 +563,8 @@
         plane, plane_d = decays[q] * plane + states[q], decays[q] * plane_d
 
     message = packed(plane, plane_d[:, 0])
-    got = [unpacked(onward(message, z_axis, k), tiles) for k in range(1, zs)]
+    got = [onward(message, z_axis, k) for k in range(1, zs)]
+    got = [unpacked(message, tiles) for message in got]
     before = jnp.zeros_like(plane)
     for q in range(zs - 1):
         s = pick([g[0] for g in got], z - q - 1)
@@ -569,7 +579,8 @@
     chip_in = jnp.concatenate([pick(got, (y - q) % ys) for q in range(ys)], axis=1)
     second_in = (d0 * chip_in.astype(F32) + s0).astype(BF16)
     mine = jnp.where(first, chip_in, second_in)
-    got = ring(jnp.where(first, second_in, chip_in), c_axis, 1)
+    message = jnp.where(first, second_in, chip_in)
+    got = ring(message, c_axis, 1)
     return jnp.concatenate([jnp.where(first, mine, got), jnp.where(first, got, mine)], axis=0)
 
 
@@ -591,16 +602,16 @@
 ):
     rows = tokens.shape[0]
     spans = rows // SPAN
-    channels = proj_inner.shape[1]
     devices = lax.axis_size(SEQ)
-    raw_in, raw_bc, raw_step, edge = raw_projections(tokens, proj_bc, proj_step.T, proj_inner)
+    raw_in, raw_bc, raw_step, edge, gate = raw_projections(
+        tokens, proj_bc, proj_step.T, proj_inner, proj_gate
+    )
     edge = lax.ppermute(edge, SEQ, [(i, i + 1) for i in range(devices - 1)])
-    gate_a = gate_projection(tokens, proj_gate, 0, channels // 2)
-    x, bc, cum, dt, lead, local, prior, decay = front(
-        raw_in, raw_bc, raw_step, edge, conv_inner, offset_inner[None],
-        conv_bc, offset_bc[None], step_bias[None], decay_log[None],
+    cum, dt, lead = steps(raw_step, step_bias[None], decay_log[None])
+    x, bc, local, prior, decay = front(
+        raw_in, raw_bc, edge, cum, dt, lead, conv_inner, offset_inner[None],
+        conv_bc, offset_bc[None],
     )
-    gate_b = gate_projection(tokens, proj_gate, channels // 2, channels // 2)
     state = incoming_state(local, decay[:, 0])
     skip = jnp.repeat(skip_gain, HEADDIM)[None]
     inner = []
@@ -613,7 +624,7 @@
     def run(which, squares_in):
         order = jnp.stack([(head + k) & (size - 1) for k in which]).astype(jnp.int32)
         return tail(
-            order, bc, lead, inner, (gate_a, gate_b), state, norm_weight[None], out_weight,
+            order, bc, lead, inner, gate, state, norm_weight[None], out_weight,
             squares_in,
         )
 

time: 121 us -> 110 us (0.909)
  local copies, waits for them, and re-layouts: 27.2 us -> 16.2 us
  waiting for transfers between devices: 11.3 us -> 13.6 us
  starting transfers between devices: 33.8 us -> 32.2 us
  other arithmetic: 3.02 us -> 1.63 us
    unnamed x96 -> x74, local copies, waits for them, and re-layouts: 26.1 us -> 16 us
    pallas_call x4, Pallas kernels: 3.59 us -> 8.24 us  [inside(): pl.pallas_call(functools.partial(inside_kernel, span == 0), grid=(1,), in...]
    pallas_call x3 -> x2, Pallas kernels: 20.4 us -> 16 us  [the longest x1 15.6 us: raw_projections(): pl.pallas_call(raw_kernel, in_specs=[pl.BlockSpec(memory_space=pltpu.HBM)...]
    ppermute x14, waiting for transfers between devices: 10.3 us -> 13.4 us  [ring(): lax.ppermute(value, axis, [(i, (i + distance) % size) for i in range(size)])]
    ppermute x14, starting transfers between devices: 22.5 us -> 20.6 us  [ring(): lax.ppermute(value, axis, [(i, (i + distance) % size) for i in range(size)])]
    convert_element_type x3, other arithmetic: 1.37 us -> 0.02 us  [packed(): low = (decay - high.astype(F32)).astype(BF16)]
  transfers between devices with their start and end apart: 18 -> 18, of which waited for: 5 -> 9; matrix products, arithmetic and copies ran while one was open for 0% -> 0% of each run, Pallas kernels for 19% -> 17%
where the time goes in v3:
time: 110 us; the launch traced here: 109 us
  Pallas kernels  44.5 us (40%)
  starting transfers between devices  32.2 us (29%)
  local copies, waits for them, and re-layouts  16.2 us (15%)
  waiting for transfers between devices  13.6 us (12%)
  other arithmetic  1.63 us (1%)
    ppermute x14, starting transfers between devices, ring(): lax.ppermute(value, axis, [(i, (i + distance) % size) for i in range(size)])  20.6 us
    unnamed x74, local copies, waits for them, and re-layouts  16 us
    pallas_call x1, Pallas kernels, raw_projections(): pl.pallas_call(raw_kernel, in_specs=[pl.BlockSpec(memory_space=pltpu.HBM)...  15.6 us
    ppermute x14, waiting for transfers between devices, ring(): lax.ppermute(value, axis, [(i, (i + distance) % size) for i in range(size)])  13.4 us
    ppermute x3, starting transfers between devices, onward(): lax.ppermute(value, axis, [(i, i + distance) for i in range(size) if i +...  10.2 us
    pallas_call x4, Pallas kernels, inside(): pl.pallas_call(functools.partial(inside_kernel, span == 0), grid=(1,), in...  8.24 us
    pallas_call x3, Pallas kernels, tail(): pl.pallas_call(functools.partial(tail_kernel, HEADS * HEADDIM), in_specs=...  8 us
    pallas_call x1, Pallas kernels, front(): pl.pallas_call(front_kernel, grid=(groups + 1,), in_specs=[late((rows, BL...  6.22 us
  transfers between devices with their start and end apart: 18, of which 9 were waited for; matrix products, arithmetic and copies ran while one was open for 0% of the time, Pallas kernels for 17%

profile of v3, /device:TPU:0, one launch (start us, length us, event | category | flops | bytes accessed | tf_op | source)
XLA Modules:
  0.0 108.8 jit_solution(4807784805859218120)
XLA Ops:
  0.0 15.6 %raw.1 = (bf16[512,1280]{1,0:T(8,128)(2,1)S(1)}, bf16[512,256]{1,0:T(8,128)(2,1)S(1)}, f32[512,128]{1,0:T(8,128)S(1)}, bf16[8,1536]{1,0:T(8,128)(2,1)S(1)}, bf16[512,1280]{1,0:T(8,128)(2,1)S(1)}) custom-call(bf16[512,2560]{1,0:T(8,128)(2,1)} %tok_hbm.1, bf16[2560,256]{1,0:T(8,128)(2,1)} %bc_hbm.1, bf16[20,2560]{1,0:T(8,128)(2,1)} %bitcast.55, ...), custom_call_target="tpu_custom_call" | custom-call | flops 7717519360 | bytes 17039360 | tf_op jit(solution)/shard_map/raw/pallas_call | solution.py:100
  15.6 1.4 %collective-permute-start = (bf16[8,1536]{1,0:T(8,128)(2,1)S(1)}, bf16[8,1536]{1,0:T(8,128)(2,1)S(1)}, u32[]{:S(2)}, u32[]{:S(2)}) collective-permute-start(bf16[8,1536]{1,0:T(8,128)(2,1)S(1)} %get-tuple-element.29), channel_id=1, source_target_pairs={{0,4},{4,8},{8,12},{12,16},{16,20},{20,24},{24,28},{28,32},{32,36}... | collective-permute-start | bytes 73736 | tf_op jit(solution)/shard_map/ppermute | solution.py:609
  17.1 0.5 steps.1
  17.6 0.3 collective-permute-done.edge
  17.9 1.3 %copy-done.27 = bf16[512,1280]{1,0:T(8,128)(2,1)S(1)} copy-done((bf16[512,1280]{1,0:T(8,128)(2,1)S(1)}, bf16[512,1280]{1,0:T(8,128)(2,1)}, u32[]{:S(2)}) %copy-start.27) | copy-done | bytes 1310744
  19.2 6.2 %front.1 = (bf16[512,1280]{1,0:T(8,128)(2,1)}, bf16[512,256]{1,0:T(8,128)(2,1)S(1)}, bf16[10,128,128]{2,1,0:T(8,128)(2,1)S(1)}, bf16[3,10,128,128]{3,2,1,0:T(8,128)(2,1)}, f32[10,8,128]{2,1,0:T(8,128)S(1)}) custom-call(bf16[512,1280]{1,0:T(8,128)(2,1)S(1)} %copy-done.27, bf16[512,256]{1,0:T(8,128)(2,1)S(1)} %get-tuple-element.28.raw_bc, ...), custom_call_target="tpu_custom_call" | custom-call | flops 3355443200 | bytes 2621440 | tf_op jit(solution)/shard_map/front/pallas_call | solution.py:248
  25.6 2.6 %collective-permute-start.1 = (bf16[656,128]{1,0:T(8,128)(2,1)S(1)}, bf16[656,128]{1,0:T(8,128)(2,1)S(1)}, u32[]{:S(2)}, u32[]{:S(2)}) collective-permute-start(bf16[656,128]{1,0:T(8,128)(2,1)S(1)} %pad_maximum_fusion.1), channel_id=1, source_target_pairs={{0,4},{4,0},{1,5},{5,1},{2,6},{6,2},{3,7},{7,3},{8,12},{12,8},{9,1... | collective-permute-start | bytes 503816 | tf_op jit(solution)/shard_map/ppermute | solution.py:501
  28.2 1.0 collective-permute-done.1
  29.4 0.6 pad_maximum_fusion.4
  30.0 4.0 %collective-permute-start.2 = (bf16[176,128]{1,0:T(8,128)(2,1)}, bf16[176,128]{1,0:T(8,128)(2,1)S(1)}, u32[]{:S(2)}, u32[]{:S(2)}) collective-permute-start(bf16[176,128]{1,0:T(8,128)(2,1)} %get-tuple-element.87), channel_id=1, source_target_pairs={{0,24},{8,0},{16,8},{24,16},{1,25},{9,1},{17,9},{25,17},{2,26},{10... | collective-permute-start | bytes 135176 | tf_op jit(solution)/shard_map/ppermute | solution.py:501
  34.0 0.6 collective-permute-start.3
  34.7 1.0 collective-permute-start.4
  35.8 0.3 collective-permute-done.2
  36.2 3.4 %collective-permute-done.3 = bf16[176,128]{1,0:T(8,128)(2,1)S(1)} collective-permute-done((bf16[176,128]{1,0:T(8,128)(2,1)S(1)}, bf16[176,128]{1,0:T(8,128)(2,1)S(1)}, u32[]{:S(2)}, u32[]{:S(2)}) %collective-permute-start.3) | collective-permute-done | bytes 45088 | tf_op jit(solution)/shard_map/ppermute | solution.py:501
  39.6 0.5 collective-permute-done.4
  40.3 5.9 %collective-permute-start.5 = (bf16[176,128]{1,0:T(8,128)(2,1)S(1)}, bf16[176,128]{1,0:T(8,128)(2,1)S(1)}, u32[]{:S(2)}, u32[]{:S(2)}) collective-permute-start(bf16[176,128]{1,0:T(8,128)(2,1)S(1)} %pad_maximum_fusion.3), channel_id=1, source_target_pairs={{0,96},{1,97},{2,98},{3,99},{4,100},{5,101},{6,102},{7,103},{8,104... | collective-permute-start | bytes 135176 | tf_op jit(solution)/shard_map/ppermute | solution.py:506
  46.2 1.3 %collective-permute-start.6 = (bf16[176,128]{1,0:T(8,128)(2,1)S(1)}, bf16[176,128]{1,0:T(8,128)(2,1)S(1)}, u32[]{:S(2)}, u32[]{:S(2)}) collective-permute-start(bf16[176,128]{1,0:T(8,128)(2,1)S(1)} %pad_maximum_fusion.3), channel_id=1, source_target_pairs={{0,64},{32,96},{1,65},{33,97},{2,66},{34,98},{3,67},{35,99},{4,68}... | collective-permute-start | bytes 135176 | tf_op jit(solution)/shard_map/ppermute | solution.py:506
  47.5 2.9 %collective-permute-start.7 = (bf16[176,128]{1,0:T(8,128)(2,1)S(1)}, bf16[176,128]{1,0:T(8,128)(2,1)S(1)}, u32[]{:S(2)}, u32[]{:S(2)}) collective-permute-start(bf16[176,128]{1,0:T(8,128)(2,1)S(1)} %pad_maximum_fusion.3), channel_id=1, source_target_pairs={{0,32},{32,64},{64,96},{1,33},{33,65},{65,97},{2,34},{34,66},{66,9... | collective-permute-start | bytes 135176 | tf_op jit(solution)/shard_map/ppermute | solution.py:506
  50.5 2.0 %inside.7.l3 = f32[128,1280]{1,0:T(8,128)S(1)} custom-call(bf16[512,1280]{1,0:T(8,128)(2,1)} %get-tuple-element.35.x_ref, bf16[512,256]{1,0:T(8,128)(2,1)S(1)} %get-tuple-element.34.bc_ref, f32[512,128]{1,0:T(8,128)S(1)} %get-tuple-element.31.cum_ref, f32[512,128]{1,0:T(8,128)S(1)} %get-tuple-element.32.dt_ref, ...), custom_call_target="tpu_custom_call" | custom-call | flops 1500000000 | bytes 327680 | tf_op jit(solution)/shard_map/inside/pallas_call | solution.py:326
  52.8 1.9 %collective-permute-start.8 = (bf16[5,32,128]{2,1,0:T(8,128)(2,1)S(1)}, bf16[5,32,128]{2,1,0:T(8,128)(2,1)S(1)}, u32[]{:S(2)}, u32[]{:S(2)}) collective-permute-start(bf16[5,32,128]{2,1,0:T(8,128)(2,1)S(1)} %get-tuple-element.72), channel_id=1, source_target_pairs={{0,24},{8,0},{16,8},{24,16},{1,25},{9,1},{17,9},{25,17},{2,26},{10... | collective-permute-start | bytes 122888 | tf_op jit(solution)/shard_map/ppermute | solution.py:501
  54.7 0.9 collective-permute-start.9
  55.8 0.9 copy-done.21
  56.8 0.9 copy-done.24
  57.7 2.1 %inside.6.l2 = f32[128,1280]{1,0:T(8,128)S(1)} custom-call(bf16[512,1280]{1,0:T(8,128)(2,1)} %get-tuple-element.35.x_ref, bf16[512,256]{1,0:T(8,128)(2,1)S(1)} %get-tuple-element.34.bc_ref, f32[512,128]{1,0:T(8,128)S(1)} %copy-done.21, f32[512,128]{1,0:T(8,128)S(1)} %copy-done.24, bf16[3,10,128,128]{3,2,1,0:T(8,128)(2,1)} %get-tuple-element.36.prior_ref, ...), custom_call_target="tpu_custom_call" | custom-call | flops 1500000000 | bytes 327680 | tf_op jit(solution)/shard_map/inside/pallas_call | solution.py:326
  59.9 0.3 collective-permute-done.9
  60.2 0.6 collective-permute-done.10
  61.2 0.9 copy-done.11
  62.1 2.2 %inside.5.l1 = f32[128,1280]{1,0:T(8,128)S(1)} custom-call(bf16[512,1280]{1,0:T(8,128)(2,1)} %get-tuple-element.35.x_ref, bf16[512,256]{1,0:T(8,128)(2,1)S(1)} %copy-done.11, f32[512,128]{1,0:T(8,128)S(1)} %copy-done.22, f32[512,128]{1,0:T(8,128)S(1)} %copy-done.25, bf16[3,10,128,128]{3,2,1,0:T(8,128)(2,1)} %get-tuple-element.36.prior_ref, ...), custom_call_target="tpu_custom_call" | custom-call | flops 1500000000 | bytes 327680 | tf_op jit(solution)/shard_map/inside/pallas_call | solution.py:326
  64.3 1.9 %inside.4.l0 = f32[128,1280]{1,0:T(8,128)S(1)} custom-call(bf16[512,1280]{1,0:T(8,128)(2,1)} %get-tuple-element.35.x_ref, bf16[512,256]{1,0:T(8,128)(2,1)S(1)} %copy-done.11, f32[512,128]{1,0:T(8,128)S(1)} %copy-done.22, f32[512,128]{1,0:T(8,128)S(1)} %copy-done.25, bf16[3,10,128,128]{3,2,1,0:T(8,128)(2,1)} %get-tuple-element.36.prior_ref, ...), custom_call_target="tpu_custom_call" | custom-call | flops 1500000000 | bytes 327680 | tf_op jit(solution)/shard_map/inside/pallas_call | solution.py:326
  66.6 2.3 %shard_map.138 = (bf16[1296,128]{1,0:T(8,128)(2,1)}, bf16[1296,128]{1,0:T(8,128)(2,1)}) custom-call(s32[1]{0:T(128)} %bitcast.24.which, bf16[512,256]{1,0:T(8,128)(2,1)S(1)} %copy-done.12, f32[512,128]{1,0:T(8,128)S(1)} %get-tuple-element.33.lead_ref, f32[128,1280]{1,0:T(8,128)S(1)} %inside.4.l0, f32[128,1280]{1,0:T(8,128)S(1)} %inside.5.l1, ...), custom_call_target="tpu_custom_call" | custom-call | flops 838860800 | bytes 6553600 | tf_op jit(solution)/shard_map/pallas_call | solution.py:431
  68.9 2.8 %collective-permute-start.14 = (bf16[1296,128]{1,0:T(8,128)(2,1)}, bf16[1296,128]{1,0:T(8,128)(2,1)}, u32[]{:S(2)}, u32[]{:S(2)}) collective-permute-start(bf16[1296,128]{1,0:T(8,128)(2,1)} %get-tuple-element.46), channel_id=1, source_target_pairs={{0,3},{1,0},{2,1},{3,2},{4,7},{5,4},{6,5},{7,6},{8,11},{9,8},{10,9... | collective-permute-start | bytes 995336 | tf_op jit(solution)/shard_map/ppermute | solution.py:501
  71.7 2.9 %copy-done = bf16[1280,2560]{1,0:T(8,128)(2,1)S(1)} copy-done((bf16[1280,2560]{1,0:T(8,128)(2,1)S(1)}, bf16[1280,2560]{1,0:T(8,128)(2,1)}, u32[]{:S(2)}) %copy-start) | copy-done | bytes 6553624
  74.6 1.1 copy-done.3
  75.7 1.0 copy-done.6
  76.6 0.9 copy-done.13
  77.6 4.1 %shard_map.137 = (bf16[1296,128]{1,0:T(8,128)(2,1)S(1)}, bf16[1280,128]{1,0:T(8,128)(2,1)}, bf16[1280,128]{1,0:T(8,128)(2,1)}, bf16[1296,128]{1,0:T(8,128)(2,1)S(1)}) custom-call(s32[2]{0:T(128)S(1)} %pad_add_fusion.which, bf16[512,256]{1,0:T(8,128)(2,1)S(1)} %copy-done.13, f32[512,128]{1,0:T(8,128)S(1)} %get-tuple-element.33.lead_ref, ...), custom_call_target="tpu_custom_call" | custom-call | flops 1677721600 | bytes 6553600 | tf_op jit(solution)/shard_map/pallas_call | solution.py:431
  81.7 1.8 %shard_map.140 = bf16[1296,128]{1,0:T(8,128)(2,1)} custom-call(bf16[1296,128]{1,0:T(8,128)(2,1)S(1)} %get-tuple-element.45.a_ref, bf16[1296,128]{1,0:T(8,128)(2,1)} %collective-permute-done.14.b_ref), custom_call_target="tpu_custom_call" | custom-call | flops 1000000 | bytes 1000000 | tf_op jit(solution)/shard_map/pallas_call | solution.py:461
  83.4 3.2 %collective-permute-start.15 = (bf16[1296,128]{1,0:T(8,128)(2,1)}, bf16[1296,128]{1,0:T(8,128)(2,1)}, u32[]{:S(2)}, u32[]{:S(2)}) collective-permute-start(bf16[1296,128]{1,0:T(8,128)(2,1)} %shard_map.140), channel_id=1, source_target_pairs={{0,3},{1,0},{2,1},{3,2},{4,7},{5,4},{6,5},{7,6},{8,11},{9,8},{10,9... | collective-permute-start | bytes 995336 | tf_op jit(solution)/shard_map/ppermute | solution.py:501
  86.7 1.8 %shard_map.139 = bf16[1296,128]{1,0:T(8,128)(2,1)} custom-call(bf16[1296,128]{1,0:T(8,128)(2,1)S(1)} %get-tuple-element.43.a_ref, bf16[1296,128]{1,0:T(8,128)(2,1)} %collective-permute-done.12.b_ref), custom_call_target="tpu_custom_call" | custom-call | flops 1000000 | bytes 1000000 | tf_op jit(solution)/shard_map/pallas_call | solution.py:461
  88.5 3.2 %collective-permute-start.16 = (bf16[1280,128]{1,0:T(8,128)(2,1)}, bf16[1280,128]{1,0:T(8,128)(2,1)}, u32[]{:S(2)}, u32[]{:S(2)}) collective-permute-start(bf16[1280,128]{1,0:T(8,128)(2,1)} %get-tuple-element.47), channel_id=1, source_target_pairs={{0,3},{1,0},{2,1},{3,2},{4,7},{5,4},{6,5},{7,6},{8,11},{9,8},{10,9... | collective-permute-start | bytes 983048 | tf_op jit(solution)/shard_map/ppermute | solution.py:501
  91.7 2.9 %copy-done.1 = bf16[1280,2560]{1,0:T(8,128)(2,1)S(1)} copy-done((bf16[1280,2560]{1,0:T(8,128)(2,1)S(1)}, bf16[1280,2560]{1,0:T(8,128)(2,1)}, u32[]{:S(2)}) %copy-start.1) | copy-done | bytes 6553624
  94.6 1.1 copy-done.4
  95.7 1.0 copy-done.7
  96.7 0.9 copy-done.14
  97.6 1.6 %shard_map.136 = (bf16[1280,128]{1,0:T(8,128)(2,1)S(1)}, bf16[1280,128]{1,0:T(8,128)(2,1)S(1)}, f32[8,128]{1,0:T(8,128)S(1)}) custom-call(s32[1]{0:T(128)} %bitcast.which, bf16[512,256]{1,0:T(8,128)(2,1)S(1)} %copy-done.14, f32[512,128]{1,0:T(8,128)S(1)} %get-tuple-element.33.lead_ref, f32[128,1280]{1,0:T(8,128)S(1)} %copy-done.4, ...), custom_call_target="tpu_custom_call" | custom-call | flops 838860800 | bytes 6553600 | tf_op jit(solution)/shard_map/pallas_call | solution.py:431
  99.2 1.9 %collective-permute-done.16.direct_l = bf16[1280,128]{1,0:T(8,128)(2,1)} collective-permute-done((bf16[1280,128]{1,0:T(8,128)(2,1)}, bf16[1280,128]{1,0:T(8,128)(2,1)}, u32[]{:S(2)}, u32[]{:S(2)}) %collective-permute-start.16) | collective-permute-done | bytes 327712 | tf_op jit(solution)/shard_map/ppermute | solution.py:501
  101.2 5.2 %collective-permute-done.17.direct_r = bf16[1280,128]{1,0:T(8,128)(2,1)} collective-permute-done((bf16[1280,128]{1,0:T(8,128)(2,1)}, bf16[1280,128]{1,0:T(8,128)(2,1)}, u32[]{:S(2)}, u32[]{:S(2)}) %collective-permute-start.17) | collective-permute-done | bytes 327712 | tf_op jit(solution)/shard_map/ppermute | solution.py:501
  106.4 2.4 %final.1 = bf16[128,2560]{1,0:T(8,128)(2,1)} custom-call(bf16[1280,128]{1,0:T(8,128)(2,1)S(1)} %get-tuple-element.40.own_l, bf16[1280,128]{1,0:T(8,128)(2,1)S(1)} %get-tuple-element.41.own_r, f32[8,128]{1,0:T(8,128)S(1)} %get-tuple-element.42.own_sq, bf16[1296,128]{1,0:T(8,128)(2,1)} %collective-permute-done.13.up, ...), custom_call_target="tpu_custom_call" | custom-call | flops 1000000 | bytes 1000000 | tf_op jit(solution)/shard_map/final/pallas_call | solution.py:488
  (113 shorter events, 1.7 us)
Async XLA Ops:
  0.0 17.1 %copy-start.18 = (f32[20]{0:T(128)S(1)}, f32[20]{0:T(128)}, u32[]{:S(2)}) copy-start(f32[20]{0:T(128)} %param.23) | copy-start | bytes 244
  0.0 17.1 %copy-start.19 = (f32[20]{0:T(128)S(1)}, f32[20]{0:T(128)}, u32[]{:S(2)}) copy-start(f32[20]{0:T(128)} %param.24) | copy-start | bytes 244
  15.6 2.0 %copy-start.26 = (bf16[512,1280]{1,0:T(8,128)(2,1)}, bf16[512,1280]{1,0:T(8,128)(2,1)S(1)}, u32[]{:S(2)}) copy-start(bf16[512,1280]{1,0:T(8,128)(2,1)S(1)} %get-tuple-element.27.raw_in) | copy-start | bytes 3932164
  15.6 2.0 %copy-start.32 = (f32[1280]{0:T(1024)S(1)}, f32[1280]{0:T(1024)}, u32[]{:S(2)}) copy-start(f32[1280]{0:T(1024)} %param.21) | copy-start | bytes 15364
  15.6 2.3 %copy-start.15 = (f32[4,1280]{1,0:T(4,128)S(1)}, f32[4,1280]{1,0:T(4,128)}, u32[]{:S(2)}) copy-start(f32[4,1280]{1,0:T(4,128)} %taps.1) | copy-start | bytes 61444
  15.6 2.3 %copy-start.16 = (f32[4,256]{1,0:T(4,128)S(1)}, f32[4,256]{1,0:T(4,128)}, u32[]{:S(2)}) copy-start(f32[4,256]{1,0:T(4,128)} %taps_bc.1) | copy-start | bytes 12292
  15.6 2.3 %copy-start.17 = (f32[256]{0:T(256)S(1)}, f32[256]{0:T(256)}, u32[]{:S(2)}) copy-start(f32[256]{0:T(256)} %param.22) | copy-start | bytes 3076
  15.6 2.3 %collective-permute-start = (bf16[8,1536]{1,0:T(8,128)(2,1)S(1)}, bf16[8,1536]{1,0:T(8,128)(2,1)S(1)}, u32[]{:S(2)}, u32[]{:S(2)}) collective-permute-start(bf16[8,1536]{1,0:T(8,128)(2,1)S(1)} %get-tuple-element.29), channel_id=1, source_target_pairs={{0,4},{4,8},{8,12},{12,16},{16,20},{20,24},{24,28},{28,32},{32,36}... | collective-permute-start | bytes 73736 | tf_op jit(solution)/shard_map/ppermute | solution.py:609
  17.6 32.9 %copy-start.20 = (f32[512,128]{1,0:T(8,128)}, f32[512,128]{1,0:T(8,128)S(1)}, u32[]{:S(2)}) copy-start(f32[512,128]{1,0:T(8,128)S(1)} %get-tuple-element.31.cum_ref) | copy-start | bytes 786436
  17.6 32.9 %copy-start.23 = (f32[512,128]{1,0:T(8,128)}, f32[512,128]{1,0:T(8,128)S(1)}, u32[]{:S(2)}) copy-start(f32[512,128]{1,0:T(8,128)S(1)} %get-tuple-element.32.dt_ref) | copy-start | bytes 786436
  17.9 1.3 %copy-start.27 = (bf16[512,1280]{1,0:T(8,128)(2,1)S(1)}, bf16[512,1280]{1,0:T(8,128)(2,1)}, u32[]{:S(2)}) copy-start(bf16[512,1280]{1,0:T(8,128)(2,1)} %copy-done.26) | copy-start | bytes 3932164
  25.4 30.4 %copy-start.10 = (bf16[512,256]{1,0:T(8,128)(2,1)}, bf16[512,256]{1,0:T(8,128)(2,1)S(1)}, u32[]{:S(2)}) copy-start(bf16[512,256]{1,0:T(8,128)(2,1)S(1)} %get-tuple-element.34.bc_ref) | copy-start | bytes 786436
  25.4 35.5 %copy-start.8 = (bf16[10,128,128]{2,1,0:T(8,128)(2,1)}, bf16[10,128,128]{2,1,0:T(8,128)(2,1)S(1)}, u32[]{:S(2)}) copy-start(bf16[10,128,128]{2,1,0:T(8,128)(2,1)S(1)} %get-tuple-element.38) | copy-start | bytes 983044
  25.4 10.2 %copy-start.34 = (f32[20]{0:T(128)S(1)}, f32[20]{0:T(128)}, u32[]{:S(2)}) copy-start(f32[20]{0:T(128)} %param.25) | copy-start | bytes 244
  25.4 10.4 %copy-start.33 = (f32[1280]{0:T(1024)S(1)}, f32[1280]{0:T(1024)}, u32[]{:S(2)}) copy-start(f32[1280]{0:T(1024)} %param.26) | copy-start | bytes 15364
  25.6 3.6 %collective-permute-start.1 = (bf16[656,128]{1,0:T(8,128)(2,1)S(1)}, bf16[656,128]{1,0:T(8,128)(2,1)S(1)}, u32[]{:S(2)}, u32[]{:S(2)}) collective-permute-start(bf16[656,128]{1,0:T(8,128)(2,1)S(1)} %pad_maximum_fusion.1), channel_id=1, source_target_pairs={{0,4},{4,0},{1,5},{5,1},{2,6},{6,2},{3,7},{7,3},{8,12},{12,8},{9,1... | collective-permute-start | bytes 503816 | tf_op jit(solution)/shard_map/ppermute | solution.py:501
  29.2 21.2 %copy-start.28 = (bf16[640,128]{1,0:T(8,128)(2,1)}, bf16[640,128]{1,0:T(8,128)(2,1)S(1)}, u32[]{:S(2)}) copy-start(bf16[640,128]{1,0:T(8,128)(2,1)S(1)} %slice.128) | copy-start | bytes 491524
  29.2 31.7 %copy-start.30 = (f32[5,128]{1,0:T(8,128)}, f32[5,128]{1,0:T(8,128)S(1)}, u32[]{:S(2)}) copy-start(f32[5,128]{1,0:T(8,128)S(1)} %get-tuple-element.70) | copy-start | bytes 7684
  30.0 6.1 %collective-permute-start.2 = (bf16[176,128]{1,0:T(8,128)(2,1)}, bf16[176,128]{1,0:T(8,128)(2,1)S(1)}, u32[]{:S(2)}, u32[]{:S(2)}) collective-permute-start(bf16[176,128]{1,0:T(8,128)(2,1)} %get-tuple-element.87), channel_id=1, source_target_pairs={{0,24},{8,0},{16,8},{24,16},{1,25},{9,1},{17,9},{25,17},{2,26},{10... | collective-permute-start | bytes 135176 | tf_op jit(solution)/shard_map/ppermute | solution.py:501
  34.0 5.6 %collective-permute-start.3 = (bf16[176,128]{1,0:T(8,128)(2,1)S(1)}, bf16[176,128]{1,0:T(8,128)(2,1)S(1)}, u32[]{:S(2)}, u32[]{:S(2)}) collective-permute-start(bf16[176,128]{1,0:T(8,128)(2,1)S(1)} %get-tuple-element.86), channel_id=1, source_target_pairs={{0,16},{8,24},{16,0},{24,8},{1,17},{9,25},{17,1},{25,9},{2,18},{10... | collective-permute-start | bytes 135176 | tf_op jit(solution)/shard_map/ppermute | solution.py:501
  34.7 5.4 %collective-permute-start.4 = (bf16[176,128]{1,0:T(8,128)(2,1)S(1)}, bf16[176,128]{1,0:T(8,128)(2,1)S(1)}, u32[]{:S(2)}, u32[]{:S(2)}) collective-permute-start(bf16[176,128]{1,0:T(8,128)(2,1)S(1)} %get-tuple-element.85), channel_id=1, source_target_pairs={{0,8},{8,16},{16,24},{24,0},{1,9},{9,17},{17,25},{25,1},{2,10},{10... | collective-permute-start | bytes 135176 | tf_op jit(solution)/shard_map/ppermute | solution.py:501
  40.3 12.3 %collective-permute-start.5 = (bf16[176,128]{1,0:T(8,128)(2,1)S(1)}, bf16[176,128]{1,0:T(8,128)(2,1)S(1)}, u32[]{:S(2)}, u32[]{:S(2)}) collective-permute-start(bf16[176,128]{1,0:T(8,128)(2,1)S(1)} %pad_maximum_fusion.3), channel_id=1, source_target_pairs={{0,96},{1,97},{2,98},{3,99},{4,100},{5,101},{6,102},{7,103},{8,104... | collective-permute-start | bytes 135176 | tf_op jit(solution)/shard_map/ppermute | solution.py:506
  46.2 6.3 %collective-permute-start.6 = (bf16[176,128]{1,0:T(8,128)(2,1)S(1)}, bf16[176,128]{1,0:T(8,128)(2,1)S(1)}, u32[]{:S(2)}, u32[]{:S(2)}) collective-permute-start(bf16[176,128]{1,0:T(8,128)(2,1)S(1)} %pad_maximum_fusion.3), channel_id=1, source_target_pairs={{0,64},{32,96},{1,65},{33,97},{2,66},{34,98},{3,67},{35,99},{4,68}... | collective-permute-start | bytes 135176 | tf_op jit(solution)/shard_map/ppermute | solution.py:506
  47.5 5.1 %collective-permute-start.7 = (bf16[176,128]{1,0:T(8,128)(2,1)S(1)}, bf16[176,128]{1,0:T(8,128)(2,1)S(1)}, u32[]{:S(2)}, u32[]{:S(2)}) collective-permute-start(bf16[176,128]{1,0:T(8,128)(2,1)S(1)} %pad_maximum_fusion.3), channel_id=1, source_target_pairs={{0,32},{32,64},{64,96},{1,33},{33,65},{65,97},{2,34},{34,66},{66,9... | collective-permute-start | bytes 135176 | tf_op jit(solution)/shard_map/ppermute | solution.py:506
  52.8 7.1 %collective-permute-start.8 = (bf16[5,32,128]{2,1,0:T(8,128)(2,1)S(1)}, bf16[5,32,128]{2,1,0:T(8,128)(2,1)S(1)}, u32[]{:S(2)}, u32[]{:S(2)}) collective-permute-start(bf16[5,32,128]{2,1,0:T(8,128)(2,1)S(1)} %get-tuple-element.72), channel_id=1, source_target_pairs={{0,24},{8,0},{16,8},{24,16},{1,25},{9,1},{17,9},{25,17},{2,26},{10... | collective-permute-start | bytes 122888 | tf_op jit(solution)/shard_map/ppermute | solution.py:501
  54.7 5.5 %collective-permute-start.9 = (bf16[5,32,128]{2,1,0:T(8,128)(2,1)S(1)}, bf16[5,32,128]{2,1,0:T(8,128)(2,1)S(1)}, u32[]{:S(2)}, u32[]{:S(2)}) collective-permute-start(bf16[5,32,128]{2,1,0:T(8,128)(2,1)S(1)} %get-tuple-element.71), channel_id=1, source_target_pairs={{0,16},{8,24},{16,0},{24,8},{1,17},{9,25},{17,1},{25,9},{2,18},{10... | collective-permute-start | bytes 122888 | tf_op jit(solution)/shard_map/ppermute | solution.py:501
  55.6 5.2 %collective-permute-start.10 = (bf16[5,32,128]{2,1,0:T(8,128)(2,1)S(1)}, bf16[5,32,128]{2,1,0:T(8,128)(2,1)S(1)}, u32[]{:S(2)}, u32[]{:S(2)}) collective-permute-start(bf16[5,32,128]{2,1,0:T(8,128)(2,1)S(1)} %get-tuple-element.53), channel_id=1, source_target_pairs={{0,8},{8,16},{16,24},{24,0},{1,9},{9,17},{17,25},{25,1},{2,10},{10... | collective-permute-start | bytes 122888 | tf_op jit(solution)/shard_map/ppermute | solution.py:501
  57.7 3.2 %copy-start.29 = (bf16[640,128]{1,0:T(8,128)(2,1)S(1)}, bf16[640,128]{1,0:T(8,128)(2,1)}, u32[]{:S(2)}) copy-start(bf16[640,128]{1,0:T(8,128)(2,1)} %copy-done.28) | copy-start | bytes 491524
  57.7 3.4 %copy-start.22 = (f32[512,128]{1,0:T(8,128)S(1)}, f32[512,128]{1,0:T(8,128)}, u32[]{:S(2)}) copy-start(f32[512,128]{1,0:T(8,128)} %copy-done.20) | copy-start | bytes 786436
  57.7 3.4 %copy-start.25 = (f32[512,128]{1,0:T(8,128)S(1)}, f32[512,128]{1,0:T(8,128)}, u32[]{:S(2)}) copy-start(f32[512,128]{1,0:T(8,128)} %copy-done.23) | copy-start | bytes 786436
  61.0 5.2 %collective-permute-start.11 = (bf16[5,128,128]{2,1,0:T(8,128)(2,1)S(1)}, bf16[5,128,128]{2,1,0:T(8,128)(2,1)S(1)}, u32[]{:S(2)}, u32[]{:S(2)}) collective-permute-start(bf16[5,128,128]{2,1,0:T(8,128)(2,1)S(1)} %broadcast_select_fusion.2), channel_id=1, source_target_pairs={{0,4},{4,0},{1,5},{5,1},{2,6},{6,2},{3,7},{7,3},{8,12},{12,8},{9,1... | collective-permute-start | bytes 491528 | tf_op jit(solution)/shard_map/ppermute | solution.py:501
  62.1 4.4 %slice-start = ((s8[6553600]{0:T(1024)(128)(4,1)}), s8[4194304]{0:T(1024)(128)(4,1)S(1)}, s32[]{:S(2)}) async-start(s8[6553600]{0:T(1024)(128)(4,1)} %bitcast.36), calls=%async_computation | async-start | bytes 8388608
  64.3 2.0 %copy-start.9 = (bf16[10,128,128]{2,1,0:T(8,128)(2,1)S(1)}, bf16[10,128,128]{2,1,0:T(8,128)(2,1)}, u32[]{:S(2)}) copy-start(bf16[10,128,128]{2,1,0:T(8,128)(2,1)} %copy-done.8) | copy-start | bytes 983044
  64.3 2.0 %copy-start.31 = (f32[5,128]{1,0:T(8,128)S(1)}, f32[5,128]{1,0:T(8,128)}, u32[]{:S(2)}) copy-start(f32[5,128]{1,0:T(8,128)} %copy-done.30) | copy-start | bytes 7684
  64.3 2.2 %slice-start.1 = ((s8[6553600]{0:T(1024)(128)(4,1)}), s8[2359296]{0:T(1024)(128)(4,1)S(1)}, s32[]{:S(2)}) async-start(s8[6553600]{0:T(1024)(128)(4,1)} %bitcast.36), calls=%async_computation.1 | async-start | bytes 4718592
  64.3 2.2 %copy-start.12 = (bf16[512,256]{1,0:T(8,128)(2,1)S(1)}, bf16[512,256]{1,0:T(8,128)(2,1)}, u32[]{:S(2)}) copy-start(bf16[512,256]{1,0:T(8,128)(2,1)} %copy-done.10) | copy-start | bytes 786436
  66.2 2.6 %copy-start.2 = (f32[128,1280]{1,0:T(8,128)}, f32[128,1280]{1,0:T(8,128)S(1)}, u32[]{:S(2)}) copy-start(f32[128,1280]{1,0:T(8,128)S(1)} %inside.4.l0) | copy-start | bytes 1966084
  66.5 2.3 %copy-start.5 = (bf16[10,128,128]{2,1,0:T(8,128)(2,1)}, bf16[10,128,128]{2,1,0:T(8,128)(2,1)S(1)}, u32[]{:S(2)}) copy-start(bf16[10,128,128]{2,1,0:T(8,128)(2,1)S(1)} %pad_maximum_fusion.state_ref) | copy-start | bytes 983044
  68.9 12.8 %collective-permute-start.14 = (bf16[1296,128]{1,0:T(8,128)(2,1)}, bf16[1296,128]{1,0:T(8,128)(2,1)}, u32[]{:S(2)}, u32[]{:S(2)}) collective-permute-start(bf16[1296,128]{1,0:T(8,128)(2,1)} %get-tuple-element.46), channel_id=1, source_target_pairs={{0,3},{1,0},{2,1},{3,2},{4,7},{5,4},{6,5},{7,6},{8,11},{9,8},{10,9... | collective-permute-start | bytes 995336 | tf_op jit(solution)/shard_map/ppermute | solution.py:501
  71.6 15.1 %collective-permute-start.12 = (bf16[1296,128]{1,0:T(8,128)(2,1)}, bf16[1296,128]{1,0:T(8,128)(2,1)}, u32[]{:S(2)}, u32[]{:S(2)}) collective-permute-start(bf16[1296,128]{1,0:T(8,128)(2,1)} %get-tuple-element.44), channel_id=1, source_target_pairs={{0,1},{1,2},{2,3},{3,0},{4,5},{5,6},{6,7},{7,4},{8,9},{9,10},{10,1... | collective-permute-start | bytes 995336 | tf_op jit(solution)/shard_map/ppermute | solution.py:501
  71.7 2.9 %copy-start = (bf16[1280,2560]{1,0:T(8,128)(2,1)S(1)}, bf16[1280,2560]{1,0:T(8,128)(2,1)}, u32[]{:S(2)}) copy-start(bf16[1280,2560]{1,0:T(8,128)(2,1)} %w_ref.5) | copy-start | bytes 19660804
  74.6 1.1 copy-start.3
  83.4 22.9 %collective-permute-start.15 = (bf16[1296,128]{1,0:T(8,128)(2,1)}, bf16[1296,128]{1,0:T(8,128)(2,1)}, u32[]{:S(2)}, u32[]{:S(2)}) collective-permute-start(bf16[1296,128]{1,0:T(8,128)(2,1)} %shard_map.140), channel_id=1, source_target_pairs={{0,3},{1,0},{2,1},{3,2},{4,7},{5,4},{6,5},{7,6},{8,11},{9,8},{10,9... | collective-permute-start | bytes 995336 | tf_op jit(solution)/shard_map/ppermute | solution.py:501
  88.5 17.9 %collective-permute-start.13 = (bf16[1296,128]{1,0:T(8,128)(2,1)}, bf16[1296,128]{1,0:T(8,128)(2,1)}, u32[]{:S(2)}, u32[]{:S(2)}) collective-permute-start(bf16[1296,128]{1,0:T(8,128)(2,1)} %shard_map.139), channel_id=1, source_target_pairs={{0,1},{1,2},{2,3},{3,0},{4,5},{5,6},{6,7},{7,4},{8,9},{9,10},{10,1... | collective-permute-start | bytes 995336 | tf_op jit(solution)/shard_map/ppermute | solution.py:501
  88.5 12.7 %collective-permute-start.16 = (bf16[1280,128]{1,0:T(8,128)(2,1)}, bf16[1280,128]{1,0:T(8,128)(2,1)}, u32[]{:S(2)}, u32[]{:S(2)}) collective-permute-start(bf16[1280,128]{1,0:T(8,128)(2,1)} %get-tuple-element.47), channel_id=1, source_target_pairs={{0,3},{1,0},{2,1},{3,2},{4,7},{5,4},{6,5},{7,6},{8,11},{9,8},{10,9... | collective-permute-start | bytes 983048 | tf_op jit(solution)/shard_map/ppermute | solution.py:501
  91.7 14.6 %collective-permute-start.17 = (bf16[1280,128]{1,0:T(8,128)(2,1)}, bf16[1280,128]{1,0:T(8,128)(2,1)}, u32[]{:S(2)}, u32[]{:S(2)}) collective-permute-start(bf16[1280,128]{1,0:T(8,128)(2,1)} %get-tuple-element.48), channel_id=1, source_target_pairs={{0,1},{1,2},{2,3},{3,0},{4,5},{5,6},{6,7},{7,4},{8,9},{9,10},{10,1... | collective-permute-start | bytes 983048 | tf_op jit(solution)/shard_map/ppermute | solution.py:501
  91.7 2.9 %copy-start.1 = (bf16[1280,2560]{1,0:T(8,128)(2,1)S(1)}, bf16[1280,2560]{1,0:T(8,128)(2,1)}, u32[]{:S(2)}) copy-start(bf16[1280,2560]{1,0:T(8,128)(2,1)} %w_ref.5) | copy-start | bytes 19660804
  94.6 1.1 copy-start.4
  (7 other events, 6.7 us)

commit v4 on v3

--- a/solution.py
+++ b/solution.py
@@ -23,13 +23,12 @@
 MIB = 2**20
 RAW_LIMIT = 24 * MIB
 FRONT_LIMIT = 24 * MIB
-INSIDE_LIMIT = 8 * MIB
+INSIDE_LIMIT = 12 * MIB
 TAIL_LIMIT = 24 * MIB
 SMALL_LIMIT = 8 * MIB
 
 
 F32 = jnp.float32
-X_SPACE = pltpu.HBM
 BF16 = jnp.bfloat16
 
 
@@ -53,67 +52,71 @@
 def raw_kernel(
     tok_hbm, bc_hbm, step_hbm, in_hbm, gate_hbm,
     in_out, bc_out, step_out, edge_out, gate_out,
-    tok, w_bc, w_step, w_wide, sems,
+    tok, w_bc, w_step, w_in, w_gate, inner, gate, sems,
 ):
     rows = tok.shape[0]
     heads = w_step.shape[0]
-    width = in_hbm.shape[1] // 2
-
-    def part(k):
-        source = in_hbm if k < 2 else gate_hbm
-        at = slice(k % 2 * width, (k % 2 + 1) * width)
-        return pltpu.make_async_copy(source.at[:, at], w_wide.at[k], sems.at[3 + k])
-
     first = [
         pltpu.make_async_copy(tok_hbm, tok, sems.at[0]),
         pltpu.make_async_copy(bc_hbm, w_bc, sems.at[1]),
         pltpu.make_async_copy(step_hbm, w_step, sems.at[2]),
     ]
+    inner_copy = pltpu.make_async_copy(in_hbm, w_in, sems.at[3])
+    gate_copy = pltpu.make_async_copy(gate_hbm, w_gate, sems.at[4])
     for copy in first:
         copy.start()
     for copy in first:
         copy.wait()
-    part(0).start()
+    inner_copy.start()
     bc = dot(tok[...], w_bc[...]).astype(BF16)
     bc_out[...] = bc
     edge_out[:, :BLOCK] = bc[rows - EDGE :]
     step_out[:, :heads] = lax.dot_general(
         tok[...], w_step[...], (((1,), (1,)), ((), ())), preferred_element_type=F32
     )
-    for k in range(4):
-        part(k).wait()
-        if k < 3:
-            part(k + 1).start()
-        at = slice(k % 2 * width, (k % 2 + 1) * width)
-        raw = dot(tok[...], w_wide[k]).astype(BF16)
-        if k < 2:
-            in_out[:, at] = raw
-            edge_out[:, BLOCK + k * width : BLOCK + (k + 1) * width] = raw[rows - EDGE :]
-        else:
-            gate_out[:, at] = raw
+    inner_copy.wait()
+    gate_copy.start()
+    raw = dot(tok[...], w_in[...]).astype(BF16)
+    inner[...] = raw
+    edge_out[:, BLOCK:] = raw[rows - EDGE :]
+    stored = [pltpu.make_async_copy(inner, in_out, sems.at[7])]
+    stored[0].start()
+    gate_copy.wait()
+    half = rows // 2
+    for k in range(2):
+        at = slice(k * half, (k + 1) * half)
+        gate[at, :] = dot(tok[at, :], w_gate[...]).astype(BF16)
+        stored.append(pltpu.make_async_copy(gate.at[at, :], gate_out.at[at, :], sems.at[5 + k]))
+        stored[-1].start()
+    for copy in stored:
+        copy.wait()
 
 
 def raw_projections(tokens, w_bc, w_step, w_in, w_gate):
     rows, width = tokens.shape
     channels = w_in.shape[1]
     vmem = pl.BlockSpec(memory_space=pltpu.VMEM)
+    hbm = pl.BlockSpec(memory_space=pltpu.HBM)
     return pl.pallas_call(
         raw_kernel,
-        in_specs=[pl.BlockSpec(memory_space=pltpu.HBM)] * 5,
-        out_specs=[vmem] * 5,
+        in_specs=[hbm] * 5,
+        out_specs=[hbm] + [vmem] * 3 + [hbm],
         out_shape=[
-            jax.ShapeDtypeStruct((rows, channels), BF16),
+            pltpu.HBM((rows, channels), BF16),
             jax.ShapeDtypeStruct((rows, BLOCK), BF16),
             jax.ShapeDtypeStruct((rows, LANES), F32),
             jax.ShapeDtypeStruct((EDGE, channels + BLOCK), BF16),
-            jax.ShapeDtypeStruct((rows, channels), BF16),
+            pltpu.HBM((rows, channels), BF16),
         ],
         scratch_shapes=[
             pltpu.VMEM(tokens.shape, BF16),
             pltpu.VMEM(w_bc.shape, BF16),
             pltpu.VMEM(w_step.shape, BF16),
-            pltpu.VMEM((4, width, channels // 2), BF16),
-            pltpu.SemaphoreType.DMA((7,)),
+            pltpu.VMEM((width, channels), BF16),
+            pltpu.VMEM((width, channels), BF16),
+            pltpu.VMEM((rows, channels), BF16),
+            pltpu.VMEM((rows, channels), BF16),
+            pltpu.SemaphoreType.DMA((8,)),
         ],
         compiler_params=pltpu.CompilerParams(vmem_limit_bytes=RAW_LIMIT),
         cost_estimate=pl.CostEstimate(
@@ -125,7 +128,7 @@
     )(*in_hbm(tokens, w_bc, w_step, w_in, w_gate))
 
 
-def steps_kernel(raw_step, step_bias, decay_log, cum_out, dt_out, lead_out):
+def steps_kernel(raw_step, step_bias, decay_log, cum_out, dt_out, lead_out, *later):
     rows = raw_step.shape[0]
     heads = step_bias.shape[1]
     v = raw_step[:, :heads] + step_bias[...]
@@ -147,6 +150,8 @@
         cum_out[at, :heads] = cum
         lead_out[at, :heads] = jnp.exp(cum + lead)
         lead = lead + cum[SPAN - 1 :, :]
+    for out, value in zip(later, (cum_out, dt_out, lead_out)):
+        out[...] = value[...]
 
 
 def steps(raw_step, step_bias, decay_log):
@@ -154,8 +159,9 @@
     return pl.pallas_call(
         steps_kernel,
         in_specs=[vmem] * 3,
-        out_specs=[vmem] * 3,
-        out_shape=[jax.ShapeDtypeStruct(raw_step.shape, F32)] * 3,
+        out_specs=[vmem] * 6,
+        out_shape=[jax.ShapeDtypeStruct(raw_step.shape, F32)] * 3
+        + [pltpu.HBM(raw_step.shape, F32)] * 3,
         compiler_params=pltpu.CompilerParams(vmem_limit_bytes=SMALL_LIMIT),
         cost_estimate=pl.CostEstimate(flops=10**9, bytes_accessed=10**6, transcendentals=0),
         name="steps",
@@ -164,7 +170,7 @@
 
 def front_kernel(
     raw_in, raw_bc, edge, cum_ref, dt_ref, lead_ref, taps, offset, taps_bc, offset_bc,
-    x_out, bc_out, local_out, prior_out, decay_out,
+    x_out, bc_out, read_out, local_out, prior_out, decay_out,
     padded, end_w, span_d, write_t,
 ):
     step = pl.program_id(0)
@@ -185,6 +191,7 @@
     def _():
         bc = conv(raw_bc, taps_bc, offset_bc[...])
         bc_out[...] = bc
+        read_out[...] = bc[:, STATE:]
         for s in range(spans):
             block = bc[s * SPAN : (s + 1) * SPAN, :STATE].astype(F32)
             write_t[s] = jnp.transpose(block).astype(BF16)
@@ -258,15 +265,17 @@
         out_specs=[
             late((rows, BLOCK), 1),
             pl.BlockSpec((rows, 2 * STATE), lambda i: (0, 0)),
+            pl.BlockSpec((rows, STATE), lambda i: (0, 0)),
             late((per_block, STATE, LANES), 0),
             late((spans - 1, per_block, STATE, LANES), 1),
             late((per_block, 8, LANES), 0),
         ],
         out_shape=[
-            X_SPACE((rows, channels), BF16),
-            jax.ShapeDtypeStruct((rows, 2 * STATE), BF16),
+            pltpu.HBM((rows, channels), BF16),
+            pltpu.HBM((rows, 2 * STATE), BF16),
+            pltpu.HBM((rows, STATE), BF16),
             jax.ShapeDtypeStruct((tiles, STATE, LANES), BF16),
-            X_SPACE((spans - 1, tiles, STATE, LANES), BF16),
+            pltpu.HBM((spans - 1, tiles, STATE, LANES), BF16),
             jax.ShapeDtypeStruct((tiles, 8, LANES), F32),
         ],
         scratch_shapes=[
@@ -282,22 +291,22 @@
             transcendentals=rows * channels,
         ),
         name="front",
-    )(raw_in, raw_bc, edge, cum, dt, lead, taps, offset, taps_bc, offset_bc)
-
-
-def inside_kernel(first, x_ref, bc_ref, cum_ref, dt_ref, prior_ref, skip_ref, out_ref):
+    )(*in_hbm(raw_in), raw_bc, edge, cum, dt, lead, taps, offset, taps_bc, offset_bc)
+
+
+def inside_kernel(x_ref, bc_ref, cum_ref, dt_ref, prior_ref, skip_ref, out_ref):
     tiles = x_ref.shape[1] // LANES
+    row = lax.broadcasted_iota(jnp.int32, (SPAN, SPAN), 0)
+    col = lax.broadcasted_iota(jnp.int32, (SPAN, SPAN), 1)
+    lane = lax.broadcasted_iota(jnp.int32, (SPAN, LANES), 1)
     write = bc_ref[:, :STATE]
     read = bc_ref[:, STATE:]
     scores = lax.dot_general(read, write, (((1,), (1,)), ((), ())), preferred_element_type=F32)
-    row = lax.broadcasted_iota(jnp.int32, (SPAN, SPAN), 0)
-    col = lax.broadcasted_iota(jnp.int32, (SPAN, SPAN), 1)
     scores = jnp.where(row >= col, scores, 0.0)
     cum = cum_ref[...]
     cum_t = jnp.transpose(cum)
     dt_t = jnp.transpose(dt_ref[...])
-    grown = jnp.exp(cum)
-    lane = lax.broadcasted_iota(jnp.int32, (SPAN, LANES), 1)
+    grown = jnp.where(pl.program_id(0) > 0, jnp.exp(cum), 0.0)
     for t in range(tiles):
         at = slice(t * LANES, (t + 1) * LANES)
         x = x_ref[:, at]
@@ -311,37 +320,35 @@
         )
         total = dot(jnp.concatenate(both, axis=1), stacked)
         total = total + skip_ref[:, at] * x.astype(F32)
-        if not first:
-            scale = jnp.where(
-                lane < HEADDIM, grown[:, 2 * t : 2 * t + 1], grown[:, 2 * t + 1 : 2 * t + 2]
-            )
-            total = total + scale * dot(read, prior_ref[0, t])
-        out_ref[:, at] = total
-
-
-def inside(span, x, bc, cum, dt, prior, skip):
-    channels = x.shape[1]
+        scale = jnp.where(
+            lane < HEADDIM, grown[:, 2 * t : 2 * t + 1], grown[:, 2 * t + 1 : 2 * t + 2]
+        )
+        out_ref[:, at] = total + scale * dot(read, prior_ref[0, t])
+
+
+def inside(x, bc, cum, dt, prior, skip):
+    rows, channels = x.shape
     tiles = channels // LANES
-    at = lambda i: (span, 0)
+    at = lambda s: (s, 0)
     return pl.pallas_call(
-        functools.partial(inside_kernel, span == 0),
-        grid=(1,),
+        inside_kernel,
+        grid=(rows // SPAN,),
         in_specs=[
             pl.BlockSpec((SPAN, channels), at),
             pl.BlockSpec((SPAN, 2 * STATE), at),
             pl.BlockSpec((SPAN, LANES), at),
             pl.BlockSpec((SPAN, LANES), at),
-            pl.BlockSpec((1, tiles, STATE, LANES), lambda i: (max(span - 1, 0), 0, 0, 0)),
-            pl.BlockSpec((1, channels), lambda i: (0, 0)),
+            pl.BlockSpec((1, tiles, STATE, LANES), lambda s: (jnp.maximum(s - 1, 0), 0, 0, 0)),
+            pl.BlockSpec((1, channels), lambda s: (0, 0)),
         ],
-        out_specs=pl.BlockSpec((SPAN, channels), lambda i: (0, 0)),
-        out_shape=jax.ShapeDtypeStruct((SPAN, channels), F32),
+        out_specs=pl.BlockSpec((SPAN, channels), at),
+        out_shape=pltpu.HBM(x.shape, F32),
         compiler_params=pltpu.CompilerParams(vmem_limit_bytes=INSIDE_LIMIT),
         cost_estimate=pl.CostEstimate(
-            flops=1_500_000_000, bytes_accessed=2 * SPAN * channels, transcendentals=0
+            flops=1_000_000, bytes_accessed=1_000_000, transcendentals=0
         ),
         name="inside",
-    )(*in_hbm(x), bc, cum, dt, *in_hbm(prior), skip)
+    )(*in_hbm(x, bc, cum, dt, prior), skip)
 
 
 def split3(v):
@@ -367,45 +374,66 @@
 
 
 def tail_kernel(
-    inner_total, which, bc_ref, lead_ref, l0, l1, l2, l3, gate_ref, state_ref, norm_ref,
-    w_ref, *refs,
+    inner_total, which, read_hbm, lead_hbm, local_hbm, gate_hbm, state_ref, norm_ref, w_hbm, *refs,
 ):
-    *outs, gated = refs
+    *outs, read_ref, lead_ref, local_ref, gate_ref, gated, w_ref, sems, w_sems = refs
     count = which.shape[0]
-    local_refs = (l0, l1, l2, l3)
-    channels = l0.shape[1]
+    channels = local_ref.shape[1]
     tiles = channels // LANES
+    side_width = w_ref.shape[2]
+    side_rows = side_width // LANES * SPAN
+
+    def rows_of(i):
+        span = pl.ds(pl.multiple_of(which[i] * SPAN, SPAN), SPAN)
+        pairs = (
+            (read_hbm, read_ref), (lead_hbm, lead_ref), (local_hbm, local_ref), (gate_hbm, gate_ref)
+        )
+        return [
+            pltpu.make_async_copy(
+                source.at[span, :], target.at[pl.ds(i * SPAN, SPAN), :], sems.at[4 * i + k]
+            )
+            for k, (source, target) in enumerate(pairs)
+        ]
+
+    def weights(side):
+        at = slice(side * side_width, (side + 1) * side_width)
+        return pltpu.make_async_copy(w_hbm.at[:, at], w_ref.at[side], w_sems.at[side])
+
+    copies = [rows_of(i) for i in range(count)]
+    for group in copies:
+        for copy in group:
+            copy.start()
+    weights(0).start()
     sums = []
     for i in range(count):
-        span = which[i]
-        at_rows = pl.ds(pl.multiple_of(span * SPAN, SPAN), SPAN)
-        read = bc_ref[at_rows, STATE:]
-        lead = lead_ref[at_rows, :]
+        for copy in copies[i]:
+            copy.wait()
+        if i == count - 1:
+            weights(1).start()
+        rows = slice(i * SPAN, (i + 1) * SPAN)
+        read = read_ref[rows, :]
+        lead = lead_ref[rows, :]
         squares = jnp.zeros((SPAN, LANES), F32)
         for t in range(tiles):
             at = slice(t * LANES, (t + 1) * LANES)
             scale = lane_pair(lead[:, 2 * t : 2 * t + 1], lead[:, 2 * t + 1 : 2 * t + 2])
-            local = local_refs[0][:, at]
-            for k in range(1, len(local_refs)):
-                local = jnp.where(span == k, local_refs[k][:, at], local)
-            mixed = local + scale * dot(read, state_ref[t])
-            gate = gate_ref[at_rows, at].astype(F32)
-            pre = mixed * silu(gate)
+            mixed = local_ref[rows, at] + scale * dot(read, state_ref[t])
+            pre = mixed * silu(gate_ref[rows, at].astype(F32))
             squares = squares + pre * pre
-            gated[i * SPAN : (i + 1) * SPAN, at] = (pre * norm_ref[:, at]).astype(BF16)
+            gated[rows, at] = (pre * norm_ref[:, at]).astype(BF16)
         total = jnp.sum(squares, axis=1, keepdims=True) * (1.0 / inner_total)
         sums.append(jnp.transpose(jnp.broadcast_to(total, (SPAN, LANES)))[:1])
-    width = w_ref.shape[1]
-    side_rows = width // 2 // LANES * SPAN
-    for j in range(width // BLOCK):
-        part = dot(gated[...], w_ref[:, j * BLOCK : (j + 1) * BLOCK]).astype(outs[0].dtype)
-        for u in range(BLOCK // LANES):
-            tile = j * (BLOCK // LANES) + u
-            side, tile = divmod(tile, width // 2 // LANES)
-            for i in range(count):
-                outs[2 * i + side][tile * SPAN : (tile + 1) * SPAN, :] = part[
-                    i * SPAN : (i + 1) * SPAN, u * LANES : (u + 1) * LANES
-                ]
+    for side in range(2):
+        weights(side).wait()
+        for j in range(side_width // BLOCK):
+            part = dot(gated[...], w_ref[side, :, j * BLOCK : (j + 1) * BLOCK])
+            part = part.astype(outs[0].dtype)
+            for u in range(BLOCK // LANES):
+                tile = j * (BLOCK // LANES) + u
+                for i in range(count):
+                    outs[2 * i + side][tile * SPAN : (tile + 1) * SPAN, :] = part[
+                        i * SPAN : (i + 1) * SPAN, u * LANES : (u + 1) * LANES
+                    ]
     for i in range(count):
         for side in range(2):
             out = outs[2 * i + side]
@@ -415,12 +443,13 @@
         outs[2 * count][...] = jnp.broadcast_to(sums[0], (8, LANES))
 
 
-def tail(which, bc, lead, inner, gate, state, norm, weight, squares_in):
+def tail(which, read, lead, inner, gate, state, norm, weight, squares_in):
     count = which.shape[0]
-    channels = inner[0].shape[1]
+    channels = inner.shape[1]
     width = weight.shape[1]
     side_rows = width // 2 // LANES * SPAN
     vmem = pl.BlockSpec(memory_space=pltpu.VMEM)
+    hbm = pl.BlockSpec(memory_space=pltpu.HBM)
     shapes = []
     for i in range(count):
         for side in range(2):
@@ -428,19 +457,29 @@
             shapes.append(jax.ShapeDtypeStruct((side_rows + extra, LANES), BF16))
     if not squares_in:
         shapes.append(jax.ShapeDtypeStruct((8, LANES), F32))
+    rows = count * SPAN
     return pl.pallas_call(
         functools.partial(tail_kernel, HEADS * HEADDIM),
-        in_specs=[pl.BlockSpec(memory_space=pltpu.SMEM)] + [vmem] * 10,
+        in_specs=[pl.BlockSpec(memory_space=pltpu.SMEM)] + [hbm] * 4 + [vmem] * 2 + [hbm],
         out_specs=[vmem] * len(shapes),
         out_shape=shapes,
-        scratch_shapes=[pltpu.VMEM((count * SPAN, channels), BF16)],
+        scratch_shapes=[
+            pltpu.VMEM((rows, STATE), BF16),
+            pltpu.VMEM((rows, LANES), F32),
+            pltpu.VMEM((rows, channels), F32),
+            pltpu.VMEM((rows, channels), BF16),
+            pltpu.VMEM((rows, channels), BF16),
+            pltpu.VMEM((2, channels, width // 2), BF16),
+            pltpu.SemaphoreType.DMA((4 * count,)),
+            pltpu.SemaphoreType.DMA((2,)),
+        ],
         compiler_params=pltpu.CompilerParams(vmem_limit_bytes=TAIL_LIMIT),
         cost_estimate=pl.CostEstimate(
             flops=2 * count * SPAN * channels * width,
             bytes_accessed=2 * channels * width,
             transcendentals=0,
         ),
-    )(which, bc, lead, *inner, gate, state, norm, weight)
+    )(which, *in_hbm(read, lead, inner, gate), state, norm, *in_hbm(weight))
 
 
 def merge_kernel(a_ref, b_ref, b_squares, out_ref):
@@ -501,13 +540,6 @@
     return lax.ppermute(value, axis, [(i, (i + distance) % size) for i in range(size)])
 
 
-def onward(value, axis, distance):
-    size = lax.axis_size(axis)
-    return lax.ppermute(
-        value, axis, [(i, i + distance) for i in range(size) if i + distance < size]
-    )
-
-
 def pick(values, index):
     out = values[0]
     for k in range(1, len(values)):
@@ -563,7 +595,7 @@
         plane, plane_d = decays[q] * plane + states[q], decays[q] * plane_d
 
     message = packed(plane, plane_d[:, 0])
-    got = [onward(message, z_axis, k) for k in range(1, zs)]
+    got = [ring(message, z_axis, k) for k in range(1, zs)]
     got = [unpacked(message, tiles) for message in got]
     before = jnp.zeros_like(plane)
     for q in range(zs - 1):
@@ -600,23 +632,19 @@
     norm_weight,
     out_weight,
 ):
-    rows = tokens.shape[0]
-    spans = rows // SPAN
     devices = lax.axis_size(SEQ)
     raw_in, raw_bc, raw_step, edge, gate = raw_projections(
         tokens, proj_bc, proj_step.T, proj_inner, proj_gate
     )
     edge = lax.ppermute(edge, SEQ, [(i, i + 1) for i in range(devices - 1)])
-    cum, dt, lead = steps(raw_step, step_bias[None], decay_log[None])
-    x, bc, local, prior, decay = front(
+    cum, dt, lead, *later = steps(raw_step, step_bias[None], decay_log[None])
+    x, bc, read, local, prior, decay = front(
         raw_in, raw_bc, edge, cum, dt, lead, conv_inner, offset_inner[None],
         conv_bc, offset_bc[None],
     )
     state = incoming_state(local, decay[:, 0])
     skip = jnp.repeat(skip_gain, HEADDIM)[None]
-    inner = []
-    for s in range(spans):
-        inner.append(inside(s, x, bc, cum, dt, prior, skip))
+    inner = inside(x, bc, *later[:2], prior, skip)
 
     head = lax.axis_index("head")
     size = lax.axis_size("head")
@@ -624,7 +652,7 @@
     def run(which, squares_in):
         order = jnp.stack([(head + k) & (size - 1) for k in which]).astype(jnp.int32)
         return tail(
-            order, bc, lead, inner, gate, state, norm_weight[None], out_weight,
+            order, read, later[2], inner, gate, state, norm_weight[None], out_weight,
             squares_in,
         )
 

time: 110 us -> 102 us (0.927)
  local copies, waits for them, and re-layouts: 16.2 us -> 0.25 us
  waiting for transfers between devices: 13.6 us -> 26.6 us
  starting transfers between devices: 32.2 us -> 27.6 us
    unnamed x74 -> x16, local copies, waits for them, and re-layouts: 16 us -> 0.05 us
    ppermute x14 -> x17, waiting for transfers between devices: 13.4 us -> 26.6 us  [ring(): lax.ppermute(value, axis, [(i, (i + distance) % size) for i in range(size)])]
    ppermute x3 -> x0, starting transfers between devices: 10.2 us -> none  [onward(): lax.ppermute(value, axis, [(i, i + distance) for i in range(size) if i +...]
    pallas_call x3, Pallas kernels: 8 us -> 14.2 us  [tail(): pl.pallas_call(functools.partial(tail_kernel, HEADS * HEADDIM), in_specs=...]
    ppermute x14 -> x17, starting transfers between devices: 20.6 us -> 26.2 us  [ring(): lax.ppermute(value, axis, [(i, (i + distance) % size) for i in range(size)])]
    pallas_call x2, Pallas kernels: 3.58 us -> 0.18 us  [merge(): pl.pallas_call(body, in_specs=[vmem] * 2, out_specs=vmem, out_shape=jax.S...]
    pallas_call x6 -> x3, Pallas kernels: 24.3 us -> 22.1 us  [the longest x1 14.3 us: raw_projections(): pl.pallas_call(raw_kernel, in_specs=[hbm] * 5, out_specs=[hbm] + [vmem] *...]
    pallas_call x1, Pallas kernels: 6.22 us -> 7.75 us  [front(): pl.pallas_call(front_kernel, grid=(groups + 1,), in_specs=[late((rows, BL...]
  transfers between devices with their start and end apart: 18 -> 18, of which waited for: 9 -> 13; matrix products, arithmetic and copies ran while one was open for 0% -> 0% of each run, Pallas kernels for 17% -> 18%
where the time goes in v4:
time: 102 us; the launch traced here: 101 us
  Pallas kernels  45.4 us (45%)
  starting transfers between devices  27.6 us (27%)
  waiting for transfers between devices  26.6 us (26%)
    ppermute x17, waiting for transfers between devices, ring(): lax.ppermute(value, axis, [(i, (i + distance) % size) for i in range(size)])  26.6 us
    ppermute x17, starting transfers between devices, ring(): lax.ppermute(value, axis, [(i, (i + distance) % size) for i in range(size)])  26.2 us
    pallas_call x1, Pallas kernels, raw_projections(): pl.pallas_call(raw_kernel, in_specs=[hbm] * 5, out_specs=[hbm] + [vmem] *...  14.3 us
    pallas_call x3, Pallas kernels, tail(): pl.pallas_call(functools.partial(tail_kernel, HEADS * HEADDIM), in_specs=...  14.2 us
    pallas_call x1, Pallas kernels, front(): pl.pallas_call(front_kernel, grid=(groups + 1,), in_specs=[late((rows, BL...  7.75 us
    pallas_call x1, Pallas kernels, inside(): pl.pallas_call(inside_kernel, grid=(rows // SPAN,), in_specs=[pl.BlockSpe...  6.42 us
  transfers between devices with their start and end apart: 18, of which 13 were waited for; matrix products, arithmetic and copies ran while one was open for 0% of the time, Pallas kernels for 18%

profile of v4, /device:TPU:0, one launch (start us, length us, event | category | flops | bytes accessed | tf_op | source)
XLA Modules:
  0.0 101.2 jit_solution(18426412754592544247)
XLA Ops:
  0.0 14.3 %raw.1 = (bf16[512,1280]{1,0:T(8,128)(2,1)}, bf16[512,256]{1,0:T(8,128)(2,1)S(1)}, f32[512,128]{1,0:T(8,128)S(1)}, bf16[8,1536]{1,0:T(8,128)(2,1)S(1)}, bf16[512,1280]{1,0:T(8,128)(2,1)}) custom-call(bf16[512,2560]{1,0:T(8,128)(2,1)} %tok_hbm.1, bf16[2560,256]{1,0:T(8,128)(2,1)} %bc_hbm.1, bf16[20,2560]{1,0:T(8,128)(2,1)} %bitcast.53, ...), custom_call_target="tpu_custom_call" | custom-call | flops 7717519360 | bytes 17039360 | tf_op jit(solution)/shard_map/raw/pallas_call | solution.py:100
  14.4 1.4 %collective-permute-start = (bf16[8,1536]{1,0:T(8,128)(2,1)S(1)}, bf16[8,1536]{1,0:T(8,128)(2,1)S(1)}, u32[]{:S(2)}, u32[]{:S(2)}) collective-permute-start(bf16[8,1536]{1,0:T(8,128)(2,1)S(1)} %get-tuple-element.33), channel_id=1, source_target_pairs={{0,4},{4,8},{8,12},{12,16},{16,20},{20,24},{24,28},{28,32},{32,36}... | collective-permute-start | bytes 73736 | tf_op jit(solution)/shard_map/ppermute | solution.py:639
  15.8 1.4 %steps.1 = (f32[512,128]{1,0:T(8,128)S(1)}, f32[512,128]{1,0:T(8,128)S(1)}, f32[512,128]{1,0:T(8,128)S(1)}, f32[512,128]{1,0:T(8,128)}, f32[512,128]{1,0:T(8,128)}, /*index=5*/f32[512,128]{1,0:T(8,128)}) custom-call(f32[512,128]{1,0:T(8,128)S(1)} %get-tuple-element.34.raw_step, f32[1,20]{1,0:T(1,128)S(1)} %bitcast.37, f32[1,20]{1,0:T(1,128)S(1)} %bitcast.38), custom_call_target="tpu_custom_call" | custom-call | flops 1000000000 | bytes 1000000 | tf_op jit(solution)/shard_map/steps/pallas_call | solution.py:159
  17.2 7.7 %front.1 = (bf16[512,1280]{1,0:T(8,128)(2,1)}, bf16[512,256]{1,0:T(8,128)(2,1)}, bf16[512,128]{1,0:T(8,128)(2,1)}, bf16[10,128,128]{2,1,0:T(8,128)(2,1)S(1)}, bf...) custom-call(bf16[512,1280]{1,0:T(8,128)(2,1)} %get-tuple-element.31.raw_in, ...), custom_call_target="tpu_custom_call" | custom-call | flops 3355443200 | bytes 2621440 | tf_op jit(solution)/shard_map/front/pallas_call | solution.py:255
  25.1 2.5 %collective-permute-start.1 = (bf16[656,128]{1,0:T(8,128)(2,1)S(1)}, bf16[656,128]{1,0:T(8,128)(2,1)S(1)}, u32[]{:S(2)}, u32[]{:S(2)}) collective-permute-start(bf16[656,128]{1,0:T(8,128)(2,1)S(1)} %pad_maximum_fusion.1), channel_id=1, source_target_pairs={{0,4},{4,0},{1,5},{5,1},{2,6},{6,2},{3,7},{7,3},{8,12},{12,8},{9,1... | collective-permute-start | bytes 503816 | tf_op jit(solution)/shard_map/ppermute | solution.py:540
  27.6 1.0 %collective-permute-done.1 = bf16[656,128]{1,0:T(8,128)(2,1)S(1)} collective-permute-done((bf16[656,128]{1,0:T(8,128)(2,1)S(1)}, bf16[656,128]{1,0:T(8,128)(2,1)S(1)}, u32[]{:S(2)}, u32[]{:S(2)}) %collective-permute-start.1) | collective-permute-done | bytes 167968 | tf_op jit(solution)/shard_map/ppermute | solution.py:540
  28.7 0.1 fusion
  28.9 3.5 %collective-permute-start.2 = (bf16[176,128]{1,0:T(8,128)(2,1)S(1)}, bf16[176,128]{1,0:T(8,128)(2,1)S(1)}, u32[]{:S(2)}, u32[]{:S(2)}) collective-permute-start(bf16[176,128]{1,0:T(8,128)(2,1)S(1)} %get-tuple-element.95), channel_id=1, source_target_pairs={{0,24},{8,0},{16,8},{24,16},{1,25},{9,1},{17,9},{25,17},{2,26},{10... | collective-permute-start | bytes 135176 | tf_op jit(solution)/shard_map/ppermute | solution.py:540
  32.4 0.6 collective-permute-start.3
  33.1 1.0 collective-permute-start.4
  34.1 0.4 collective-permute-done.2
  34.5 3.5 %collective-permute-done.3 = bf16[176,128]{1,0:T(8,128)(2,1)S(1)} collective-permute-done((bf16[176,128]{1,0:T(8,128)(2,1)S(1)}, bf16[176,128]{1,0:T(8,128)(2,1)S(1)}, u32[]{:S(2)}, u32[]{:S(2)}) %collective-permute-start.3) | collective-permute-done | bytes 45088 | tf_op jit(solution)/shard_map/ppermute | solution.py:540
  38.0 0.5 collective-permute-done.4
  38.5 0.1 fusion.2
  38.7 4.1 %collective-permute-start.5 = (bf16[176,128]{1,0:T(8,128)(2,1)S(1)}, bf16[176,128]{1,0:T(8,128)(2,1)S(1)}, u32[]{:S(2)}, u32[]{:S(2)}) collective-permute-start(bf16[176,128]{1,0:T(8,128)(2,1)S(1)} %pad_maximum_fusion.3), channel_id=1, source_target_pairs={{0,96},{32,0},{64,32},{96,64},{1,97},{33,1},{65,33},{97,65},{2,98}... | collective-permute-start | bytes 135176 | tf_op jit(solution)/shard_map/ppermute | solution.py:540
  42.8 1.3 %collective-permute-start.7 = (bf16[176,128]{1,0:T(8,128)(2,1)S(1)}, bf16[176,128]{1,0:T(8,128)(2,1)S(1)}, u32[]{:S(2)}, u32[]{:S(2)}) collective-permute-start(bf16[176,128]{1,0:T(8,128)(2,1)S(1)} %pad_maximum_fusion.3), channel_id=1, source_target_pairs={{0,32},{32,64},{64,96},{96,0},{1,33},{33,65},{65,97},{97,1},{2,34}... | collective-permute-start | bytes 135176 | tf_op jit(solution)/shard_map/ppermute | solution.py:540
  44.0 0.5 collective-permute-done.5
  44.5 3.9 %collective-permute-done.6 = bf16[176,128]{1,0:T(8,128)(2,1)S(1)} collective-permute-done((bf16[176,128]{1,0:T(8,128)(2,1)S(1)}, bf16[176,128]{1,0:T(8,128)(2,1)S(1)}, u32[]{:S(2)}, u32[]{:S(2)}) %collective-permute-start.6) | collective-permute-done | bytes 45088 | tf_op jit(solution)/shard_map/ppermute | solution.py:540
  48.4 0.1 collective-permute-done.7
  48.6 0.1 select_convert_fusion.1
  48.7 0.1 select_convert_fusion.2
  48.7 2.1 %collective-permute-start.8 = (bf16[5,32,128]{2,1,0:T(8,128)(2,1)S(1)}, bf16[5,32,128]{2,1,0:T(8,128)(2,1)S(1)}, u32[]{:S(2)}, u32[]{:S(2)}) collective-permute-start(bf16[5,32,128]{2,1,0:T(8,128)(2,1)S(1)} %get-tuple-element.80), channel_id=1, source_target_pairs={{0,24},{8,0},{16,8},{24,16},{1,25},{9,1},{17,9},{25,17},{2,26},{10... | collective-permute-start | bytes 122888 | tf_op jit(solution)/shard_map/ppermute | solution.py:540
  50.8 0.9 collective-permute-start.9
  51.7 0.3 collective-permute-start.10
  51.9 1.0 %collective-permute-done.8 = bf16[5,32,128]{2,1,0:T(8,128)(2,1)S(1)} collective-permute-done((bf16[5,32,128]{2,1,0:T(8,128)(2,1)S(1)}, bf16[5,32,128]{2,1,0:T(8,128)(2,1)S(1)}, u32[]{:S(2)}, u32[]{:S(2)}) %collective-permute-start.8) | collective-permute-done | bytes 40992 | tf_op jit(solution)/shard_map/ppermute | solution.py:540
  53.0 3.3 %collective-permute-done.9 = bf16[5,32,128]{2,1,0:T(8,128)(2,1)S(1)} collective-permute-done((bf16[5,32,128]{2,1,0:T(8,128)(2,1)S(1)}, bf16[5,32,128]{2,1,0:T(8,128)(2,1)S(1)}, u32[]{:S(2)}, u32[]{:S(2)}) %collective-permute-start.9) | collective-permute-done | bytes 40992 | tf_op jit(solution)/shard_map/ppermute | solution.py:540
  56.3 0.6 collective-permute-done.10
  56.9 0.1 select_select_fusion.4
  57.0 0.1 broadcast_select_fusion.2
  57.1 0.1 collective-permute-start.11
  57.2 0.1 broadcast_in_dim.37
  57.3 0.1 broadcast_in_dim_reshape.3.skip_ref
  57.4 6.4 %inside.1.local_hbm = f32[512,1280]{1,0:T(8,128)} custom-call(bf16[512,1280]{1,0:T(8,128)(2,1)} %get-tuple-element.40.x_ref, bf16[512,256]{1,0:T(8,128)(2,1)} %get-tuple-element.41.bc_ref, f32[512,128]{1,0:T(8,128)} %get-tuple-element.42.cum_ref, f32[512,128]{1,0:T(8,128)} %get-tuple-element.43.dt_ref, ...), custom_call_target="tpu_custom_call" | custom-call | flops 1000000 | bytes 1000000 | tf_op jit(solution)/shard_map/inside/pallas_call | solution.py:333
  63.8 0.1 broadcast_select_fusion.1
  64.0 4.2 %shard_map.138 = (bf16[1296,128]{1,0:T(8,128)(2,1)S(1)}, bf16[1296,128]{1,0:T(8,128)(2,1)S(1)}) custom-call(s32[1]{0:T(128)} %bitcast.24.which, bf16[512,128]{1,0:T(8,128)(2,1)} %get-tuple-element.38.read_hbm, f32[512,128]{1,0:T(8,128)} %get-tuple-element.39.lead_hbm, f32[512,1280]{1,0:T(8,128)} %inside.1.local_hbm, ...), custom_call_target="tpu_custom_call" | custom-call | flops 838860800 | bytes 6553600 | tf_op jit(solution)/shard_map/pallas_call | solution.py:461
  68.3 2.8 %collective-permute-start.14 = (bf16[1296,128]{1,0:T(8,128)(2,1)S(1)}, bf16[1296,128]{1,0:T(8,128)(2,1)S(1)}, u32[]{:S(2)}, u32[]{:S(2)}) collective-permute-start(bf16[1296,128]{1,0:T(8,128)(2,1)S(1)} %get-tuple-element.54), channel_id=1, source_target_pairs={{0,3},{1,0},{2,1},{3,2},{4,7},{5,4},{6,5},{7,6},{8,11},{9,8},{10,9... | collective-permute-start | bytes 995336 | tf_op jit(solution)/shard_map/ppermute | solution.py:540
  71.1 0.1 pad_add_fusion.which
  71.2 5.8 %shard_map.137 = (bf16[1296,128]{1,0:T(8,128)(2,1)S(1)}, bf16[1280,128]{1,0:T(8,128)(2,1)S(1)}, bf16[1280,128]{1,0:T(8,128)(2,1)S(1)}, bf16[1296,128]{1,0:T(8,128)(2,1)S(1)}) custom-call(s32[2]{0:T(128)S(1)} %pad_add_fusion.which, bf16[512,128]{1,0:T(8,128)(2,1)} %get-tuple-element.38.read_hbm, f32[512,128]{1,0:T(8,128)} %get-tuple-element.39.lead_hbm, ...), custom_call_target="tpu_custom_call" | custom-call | flops 1677721600 | bytes 6553600 | tf_op jit(solution)/shard_map/pallas_call | solution.py:461
  76.9 1.9 %collective-permute-done.14.b_ref = bf16[1296,128]{1,0:T(8,128)(2,1)S(1)} collective-permute-done((bf16[1296,128]{1,0:T(8,128)(2,1)S(1)}, bf16[1296,128]{1,0:T(8,128)(2,1)S(1)}, u32[]{:S(2)}, u32[]{:S(2)}) %collective-permute-start.14) | collective-permute-done | bytes 331808 | tf_op jit(solution)/shard_map/ppermute | solution.py:540
  78.8 0.1 shard_map.140
  78.9 3.8 %collective-permute-start.15 = (bf16[1296,128]{1,0:T(8,128)(2,1)S(1)}, bf16[1296,128]{1,0:T(8,128)(2,1)S(1)}, u32[]{:S(2)}, u32[]{:S(2)}) collective-permute-start(bf16[1296,128]{1,0:T(8,128)(2,1)S(1)} %shard_map.140), channel_id=1, source_target_pairs={{0,3},{1,0},{2,1},{3,2},{4,7},{5,4},{6,5},{7,6},{8,11},{9,8},{10,9... | collective-permute-start | bytes 995336 | tf_op jit(solution)/shard_map/ppermute | solution.py:540
  82.6 0.1 shard_map.139
  82.7 0.1 collective-permute-start.13
  82.8 3.2 %collective-permute-start.16 = (bf16[1280,128]{1,0:T(8,128)(2,1)S(1)}, bf16[1280,128]{1,0:T(8,128)(2,1)S(1)}, u32[]{:S(2)}, u32[]{:S(2)}) collective-permute-start(bf16[1280,128]{1,0:T(8,128)(2,1)S(1)} %get-tuple-element.55), channel_id=1, source_target_pairs={{0,3},{1,0},{2,1},{3,2},{4,7},{5,4},{6,5},{7,6},{8,11},{9,8},{10,9... | collective-permute-start | bytes 983048 | tf_op jit(solution)/shard_map/ppermute | solution.py:540
  86.0 4.2 %shard_map.136 = (bf16[1280,128]{1,0:T(8,128)(2,1)S(1)}, bf16[1280,128]{1,0:T(8,128)(2,1)S(1)}, f32[8,128]{1,0:T(8,128)S(1)}) custom-call(s32[1]{0:T(128)} %bitcast.which, bf16[512,128]{1,0:T(8,128)(2,1)} %get-tuple-element.38.read_hbm, f32[512,128]{1,0:T(8,128)} %get-tuple-element.39.lead_hbm, f32[512,1280]{1,0:T(8,128)} %inside.1.local_hbm, ...), custom_call_target="tpu_custom_call" | custom-call | flops 838860800 | bytes 6553600 | tf_op jit(solution)/shard_map/pallas_call | solution.py:461
  90.3 6.2 %collective-permute-done.16.direct_l = bf16[1280,128]{1,0:T(8,128)(2,1)S(1)} collective-permute-done((bf16[1280,128]{1,0:T(8,128)(2,1)S(1)}, bf16[1280,128]{1,0:T(8,128)(2,1)S(1)}, u32[]{:S(2)}, u32[]{:S(2)}) %collective-permute-start.16) | collective-permute-done | bytes 327712 | tf_op jit(solution)/shard_map/ppermute | solution.py:540
  96.5 3.6 %collective-permute-done.17.direct_r = bf16[1280,128]{1,0:T(8,128)(2,1)S(1)} collective-permute-done((bf16[1280,128]{1,0:T(8,128)(2,1)S(1)}, bf16[1280,128]{1,0:T(8,128)(2,1)S(1)}, u32[]{:S(2)}, u32[]{:S(2)}) %collective-permute-start.17) | collective-permute-done | bytes 327712 | tf_op jit(solution)/shard_map/ppermute | solution.py:540
  100.1 1.2 %final.1 = bf16[128,2560]{1,0:T(8,128)(2,1)} custom-call(bf16[1280,128]{1,0:T(8,128)(2,1)S(1)} %get-tuple-element.48.own_l, bf16[1280,128]{1,0:T(8,128)(2,1)S(1)} %get-tuple-element.49.own_r, f32[8,128]{1,0:T(8,128)S(1)} %get-tuple-element.50.own_sq, bf16[1296,128]{1,0:T(8,128)(2,1)S(1)} %collective-permute-done.13.up, ...), custom_call_target="tpu_custom_call" | custom-call | flops 1000000 | bytes 1000000 | tf_op jit(solution)/shard_map/final/pallas_call | solution.py:527
  (51 shorter events, 0.4 us)
Async XLA Ops:
  0.0 15.8 %copy-start.3 = (f32[20]{0:T(128)S(1)}, f32[20]{0:T(128)}, u32[]{:S(2)}) copy-start(f32[20]{0:T(128)} %param.23) | copy-start | bytes 244
  0.0 15.8 %copy-start.4 = (f32[20]{0:T(128)S(1)}, f32[20]{0:T(128)}, u32[]{:S(2)}) copy-start(f32[20]{0:T(128)} %param.24) | copy-start | bytes 244
  14.3 2.9 %copy-start.5 = (f32[1280]{0:T(1024)S(1)}, f32[1280]{0:T(1024)}, u32[]{:S(2)}) copy-start(f32[1280]{0:T(1024)} %param.21) | copy-start | bytes 15364
  14.3 2.9 %copy-start = (f32[4,1280]{1,0:T(4,128)S(1)}, f32[4,1280]{1,0:T(4,128)}, u32[]{:S(2)}) copy-start(f32[4,1280]{1,0:T(4,128)} %taps.1) | copy-start | bytes 61444
  14.3 2.9 %copy-start.1 = (f32[4,256]{1,0:T(4,128)S(1)}, f32[4,256]{1,0:T(4,128)}, u32[]{:S(2)}) copy-start(f32[4,256]{1,0:T(4,128)} %taps_bc.1) | copy-start | bytes 12292
  14.4 2.9 %copy-start.2 = (f32[256]{0:T(256)S(1)}, f32[256]{0:T(256)}, u32[]{:S(2)}) copy-start(f32[256]{0:T(256)} %param.22) | copy-start | bytes 3076
  14.4 2.8 %collective-permute-start = (bf16[8,1536]{1,0:T(8,128)(2,1)S(1)}, bf16[8,1536]{1,0:T(8,128)(2,1)S(1)}, u32[]{:S(2)}, u32[]{:S(2)}) collective-permute-start(bf16[8,1536]{1,0:T(8,128)(2,1)S(1)} %get-tuple-element.33), channel_id=1, source_target_pairs={{0,4},{4,8},{8,12},{12,16},{16,20},{20,24},{24,28},{28,32},{32,36}... | collective-permute-start | bytes 73736 | tf_op jit(solution)/shard_map/ppermute | solution.py:639
  25.1 3.5 %collective-permute-start.1 = (bf16[656,128]{1,0:T(8,128)(2,1)S(1)}, bf16[656,128]{1,0:T(8,128)(2,1)S(1)}, u32[]{:S(2)}, u32[]{:S(2)}) collective-permute-start(bf16[656,128]{1,0:T(8,128)(2,1)S(1)} %pad_maximum_fusion.1), channel_id=1, source_target_pairs={{0,4},{4,0},{1,5},{5,1},{2,6},{6,2},{3,7},{7,3},{8,12},{12,8},{9,1... | collective-permute-start | bytes 503816 | tf_op jit(solution)/shard_map/ppermute | solution.py:540
  28.8 28.4 %copy-start.7 = (f32[20]{0:T(128)S(1)}, f32[20]{0:T(128)}, u32[]{:S(2)}) copy-start(f32[20]{0:T(128)} %param.25) | copy-start | bytes 244
  28.8 28.6 %copy-start.6 = (f32[1280]{0:T(1024)S(1)}, f32[1280]{0:T(1024)}, u32[]{:S(2)}) copy-start(f32[1280]{0:T(1024)} %param.26) | copy-start | bytes 15364
  28.9 5.6 %collective-permute-start.2 = (bf16[176,128]{1,0:T(8,128)(2,1)S(1)}, bf16[176,128]{1,0:T(8,128)(2,1)S(1)}, u32[]{:S(2)}, u32[]{:S(2)}) collective-permute-start(bf16[176,128]{1,0:T(8,128)(2,1)S(1)} %get-tuple-element.95), channel_id=1, source_target_pairs={{0,24},{8,0},{16,8},{24,16},{1,25},{9,1},{17,9},{25,17},{2,26},{10... | collective-permute-start | bytes 135176 | tf_op jit(solution)/shard_map/ppermute | solution.py:540
  32.4 5.6 %collective-permute-start.3 = (bf16[176,128]{1,0:T(8,128)(2,1)S(1)}, bf16[176,128]{1,0:T(8,128)(2,1)S(1)}, u32[]{:S(2)}, u32[]{:S(2)}) collective-permute-start(bf16[176,128]{1,0:T(8,128)(2,1)S(1)} %get-tuple-element.94), channel_id=1, source_target_pairs={{0,16},{8,24},{16,0},{24,8},{1,17},{9,25},{17,1},{25,9},{2,18},{10... | collective-permute-start | bytes 135176 | tf_op jit(solution)/shard_map/ppermute | solution.py:540
  33.1 5.4 %collective-permute-start.4 = (bf16[176,128]{1,0:T(8,128)(2,1)S(1)}, bf16[176,128]{1,0:T(8,128)(2,1)S(1)}, u32[]{:S(2)}, u32[]{:S(2)}) collective-permute-start(bf16[176,128]{1,0:T(8,128)(2,1)S(1)} %get-tuple-element.93), channel_id=1, source_target_pairs={{0,8},{8,16},{16,24},{24,0},{1,9},{9,17},{17,25},{25,1},{2,10},{10... | collective-permute-start | bytes 135176 | tf_op jit(solution)/shard_map/ppermute | solution.py:540
  38.7 5.8 %collective-permute-start.5 = (bf16[176,128]{1,0:T(8,128)(2,1)S(1)}, bf16[176,128]{1,0:T(8,128)(2,1)S(1)}, u32[]{:S(2)}, u32[]{:S(2)}) collective-permute-start(bf16[176,128]{1,0:T(8,128)(2,1)S(1)} %pad_maximum_fusion.3), channel_id=1, source_target_pairs={{0,96},{32,0},{64,32},{96,64},{1,97},{33,1},{65,33},{97,65},{2,98}... | collective-permute-start | bytes 135176 | tf_op jit(solution)/shard_map/ppermute | solution.py:540
  42.8 5.6 %collective-permute-start.6 = (bf16[176,128]{1,0:T(8,128)(2,1)S(1)}, bf16[176,128]{1,0:T(8,128)(2,1)S(1)}, u32[]{:S(2)}, u32[]{:S(2)}) collective-permute-start(bf16[176,128]{1,0:T(8,128)(2,1)S(1)} %pad_maximum_fusion.3), channel_id=1, source_target_pairs={{0,64},{32,96},{64,0},{96,32},{1,65},{33,97},{65,1},{97,33},{2,66}... | collective-permute-start | bytes 135176 | tf_op jit(solution)/shard_map/ppermute | solution.py:540
  42.8 5.7 %collective-permute-start.7 = (bf16[176,128]{1,0:T(8,128)(2,1)S(1)}, bf16[176,128]{1,0:T(8,128)(2,1)S(1)}, u32[]{:S(2)}, u32[]{:S(2)}) collective-permute-start(bf16[176,128]{1,0:T(8,128)(2,1)S(1)} %pad_maximum_fusion.3), channel_id=1, source_target_pairs={{0,32},{32,64},{64,96},{96,0},{1,33},{33,65},{65,97},{97,1},{2,34}... | collective-permute-start | bytes 135176 | tf_op jit(solution)/shard_map/ppermute | solution.py:540
  48.7 4.3 %collective-permute-start.8 = (bf16[5,32,128]{2,1,0:T(8,128)(2,1)S(1)}, bf16[5,32,128]{2,1,0:T(8,128)(2,1)S(1)}, u32[]{:S(2)}, u32[]{:S(2)}) collective-permute-start(bf16[5,32,128]{2,1,0:T(8,128)(2,1)S(1)} %get-tuple-element.80), channel_id=1, source_target_pairs={{0,24},{8,0},{16,8},{24,16},{1,25},{9,1},{17,9},{25,17},{2,26},{10... | collective-permute-start | bytes 122888 | tf_op jit(solution)/shard_map/ppermute | solution.py:540
  50.8 5.5 %collective-permute-start.9 = (bf16[5,32,128]{2,1,0:T(8,128)(2,1)S(1)}, bf16[5,32,128]{2,1,0:T(8,128)(2,1)S(1)}, u32[]{:S(2)}, u32[]{:S(2)}) collective-permute-start(bf16[5,32,128]{2,1,0:T(8,128)(2,1)S(1)} %get-tuple-element.79), channel_id=1, source_target_pairs={{0,16},{8,24},{16,0},{24,8},{1,17},{9,25},{17,1},{25,9},{2,18},{10... | collective-permute-start | bytes 122888 | tf_op jit(solution)/shard_map/ppermute | solution.py:540
  51.7 5.2 %collective-permute-start.10 = (bf16[5,32,128]{2,1,0:T(8,128)(2,1)S(1)}, bf16[5,32,128]{2,1,0:T(8,128)(2,1)S(1)}, u32[]{:S(2)}, u32[]{:S(2)}) collective-permute-start(bf16[5,32,128]{2,1,0:T(8,128)(2,1)S(1)} %get-tuple-element.61), channel_id=1, source_target_pairs={{0,8},{8,16},{16,24},{24,0},{1,9},{9,17},{17,25},{25,1},{2,10},{10... | collective-permute-start | bytes 122888 | tf_op jit(solution)/shard_map/ppermute | solution.py:540
  57.1 6.7 %collective-permute-start.11 = (bf16[5,128,128]{2,1,0:T(8,128)(2,1)S(1)}, bf16[5,128,128]{2,1,0:T(8,128)(2,1)S(1)}, u32[]{:S(2)}, u32[]{:S(2)}) collective-permute-start(bf16[5,128,128]{2,1,0:T(8,128)(2,1)S(1)} %broadcast_select_fusion.2), channel_id=1, source_target_pairs={{0,4},{4,0},{1,5},{5,1},{2,6},{6,2},{3,7},{7,3},{8,12},{12,8},{9,1... | collective-permute-start | bytes 491528 | tf_op jit(solution)/shard_map/ppermute | solution.py:540
  68.3 10.5 %collective-permute-start.14 = (bf16[1296,128]{1,0:T(8,128)(2,1)S(1)}, bf16[1296,128]{1,0:T(8,128)(2,1)S(1)}, u32[]{:S(2)}, u32[]{:S(2)}) collective-permute-start(bf16[1296,128]{1,0:T(8,128)(2,1)S(1)} %get-tuple-element.54), channel_id=1, source_target_pairs={{0,3},{1,0},{2,1},{3,2},{4,7},{5,4},{6,5},{7,6},{8,11},{9,8},{10,9... | collective-permute-start | bytes 995336 | tf_op jit(solution)/shard_map/ppermute | solution.py:540
  71.1 11.6 %collective-permute-start.12 = (bf16[1296,128]{1,0:T(8,128)(2,1)S(1)}, bf16[1296,128]{1,0:T(8,128)(2,1)S(1)}, u32[]{:S(2)}, u32[]{:S(2)}) collective-permute-start(bf16[1296,128]{1,0:T(8,128)(2,1)S(1)} %get-tuple-element.52), channel_id=1, source_target_pairs={{0,1},{1,2},{2,3},{3,0},{4,5},{5,6},{6,7},{7,4},{8,9},{9,10},{10,1... | collective-permute-start | bytes 995336 | tf_op jit(solution)/shard_map/ppermute | solution.py:540
  78.9 21.2 %collective-permute-start.15 = (bf16[1296,128]{1,0:T(8,128)(2,1)S(1)}, bf16[1296,128]{1,0:T(8,128)(2,1)S(1)}, u32[]{:S(2)}, u32[]{:S(2)}) collective-permute-start(bf16[1296,128]{1,0:T(8,128)(2,1)S(1)} %shard_map.140), channel_id=1, source_target_pairs={{0,3},{1,0},{2,1},{3,2},{4,7},{5,4},{6,5},{7,6},{8,11},{9,8},{10,9... | collective-permute-start | bytes 995336 | tf_op jit(solution)/shard_map/ppermute | solution.py:540
  82.7 17.4 %collective-permute-start.13 = (bf16[1296,128]{1,0:T(8,128)(2,1)S(1)}, bf16[1296,128]{1,0:T(8,128)(2,1)S(1)}, u32[]{:S(2)}, u32[]{:S(2)}) collective-permute-start(bf16[1296,128]{1,0:T(8,128)(2,1)S(1)} %shard_map.139), channel_id=1, source_target_pairs={{0,1},{1,2},{2,3},{3,0},{4,5},{5,6},{6,7},{7,4},{8,9},{9,10},{10,1... | collective-permute-start | bytes 995336 | tf_op jit(solution)/shard_map/ppermute | solution.py:540
  82.8 13.7 %collective-permute-start.16 = (bf16[1280,128]{1,0:T(8,128)(2,1)S(1)}, bf16[1280,128]{1,0:T(8,128)(2,1)S(1)}, u32[]{:S(2)}, u32[]{:S(2)}) collective-permute-start(bf16[1280,128]{1,0:T(8,128)(2,1)S(1)} %get-tuple-element.55), channel_id=1, source_target_pairs={{0,3},{1,0},{2,1},{3,2},{4,7},{5,4},{6,5},{7,6},{8,11},{9,8},{10,9... | collective-permute-start | bytes 983048 | tf_op jit(solution)/shard_map/ppermute | solution.py:540
  86.0 14.0 %collective-permute-start.17 = (bf16[1280,128]{1,0:T(8,128)(2,1)S(1)}, bf16[1280,128]{1,0:T(8,128)(2,1)S(1)}, u32[]{:S(2)}, u32[]{:S(2)}) collective-permute-start(bf16[1280,128]{1,0:T(8,128)(2,1)S(1)} %get-tuple-element.56), channel_id=1, source_target_pairs={{0,1},{1,2},{2,3},{3,0},{4,5},{5,6},{6,7},{7,4},{8,9},{9,10},{10,1... | collective-permute-start | bytes 983048 | tf_op jit(solution)/shard_map/ppermute | solution.py:540

commit v5 on v4

--- a/solution.py
+++ b/solution.py
@@ -24,7 +24,7 @@
 RAW_LIMIT = 24 * MIB
 FRONT_LIMIT = 24 * MIB
 INSIDE_LIMIT = 12 * MIB
-TAIL_LIMIT = 24 * MIB
+TAIL_LIMIT = 16 * MIB
 SMALL_LIMIT = 8 * MIB
 
 
@@ -294,7 +294,7 @@
     )(*in_hbm(raw_in), raw_bc, edge, cum, dt, lead, taps, offset, taps_bc, offset_bc)
 
 
-def inside_kernel(x_ref, bc_ref, cum_ref, dt_ref, prior_ref, skip_ref, out_ref):
+def inside_kernel(first, x_ref, bc_ref, cum_ref, dt_ref, prior_ref, skip_ref, out_ref):
     tiles = x_ref.shape[1] // LANES
     row = lax.broadcasted_iota(jnp.int32, (SPAN, SPAN), 0)
     col = lax.broadcasted_iota(jnp.int32, (SPAN, SPAN), 1)
@@ -306,7 +306,7 @@
     cum = cum_ref[...]
     cum_t = jnp.transpose(cum)
     dt_t = jnp.transpose(dt_ref[...])
-    grown = jnp.where(pl.program_id(0) > 0, jnp.exp(cum), 0.0)
+    grown = jnp.where(pl.program_id(0) + first > 0, jnp.exp(cum), 0.0)
     for t in range(tiles):
         at = slice(t * LANES, (t + 1) * LANES)
         x = x_ref[:, at]
@@ -326,23 +326,23 @@
         out_ref[:, at] = total + scale * dot(read, prior_ref[0, t])
 
 
-def inside(x, bc, cum, dt, prior, skip):
-    rows, channels = x.shape
+def inside(first, count, x, bc, cum, dt, prior, skip):
+    channels = x.shape[1]
     tiles = channels // LANES
-    at = lambda s: (s, 0)
+    at = lambda s: (s + first, 0)
     return pl.pallas_call(
-        inside_kernel,
-        grid=(rows // SPAN,),
+        functools.partial(inside_kernel, first),
+        grid=(count,),
         in_specs=[
             pl.BlockSpec((SPAN, channels), at),
             pl.BlockSpec((SPAN, 2 * STATE), at),
             pl.BlockSpec((SPAN, LANES), at),
             pl.BlockSpec((SPAN, LANES), at),
-            pl.BlockSpec((1, tiles, STATE, LANES), lambda s: (jnp.maximum(s - 1, 0), 0, 0, 0)),
+            pl.BlockSpec((1, tiles, STATE, LANES), lambda s: (jnp.maximum(s + first - 1, 0), 0, 0, 0)),
             pl.BlockSpec((1, channels), lambda s: (0, 0)),
         ],
-        out_specs=pl.BlockSpec((SPAN, channels), at),
-        out_shape=pltpu.HBM(x.shape, F32),
+        out_specs=pl.BlockSpec((SPAN, channels), lambda s: (s, 0)),
+        out_shape=pltpu.HBM((count * SPAN, channels), F32),
         compiler_params=pltpu.CompilerParams(vmem_limit_bytes=INSIDE_LIMIT),
         cost_estimate=pl.CostEstimate(
             flops=1_000_000, bytes_accessed=1_000_000, transcendentals=0
@@ -373,43 +373,109 @@
     return out.astype(BF16)
 
 
-def tail_kernel(
-    inner_total, which, read_hbm, lead_hbm, local_hbm, gate_hbm, state_ref, norm_ref, w_hbm, *refs,
+def ready_kernel(
+    which, read_hbm, lead_hbm, low_hbm, high_hbm, gate_hbm, w_hbm,
+    read_ref, lead_ref, local_ref, gate_ref, w_ref, sems,
 ):
-    *outs, read_ref, lead_ref, local_ref, gate_ref, gated, w_ref, sems, w_sems = refs
-    count = which.shape[0]
+    copies = rows_copies(
+        which[0], (read_hbm, lead_hbm, gate_hbm), (read_ref, lead_ref, gate_ref), 0, sems
+    )
+    local = local_copies(which[0], low_hbm, high_hbm, local_ref, 0, sems.at[3])
+    weights = pltpu.make_async_copy(w_hbm, w_ref, sems.at[4])
+    weights.start()
+    for copy in copies:
+        copy.start()
+    start_local(which[0], local)
+    for copy in copies:
+        copy.wait()
+    local[0].wait()
+    weights.wait()
+
+
+def rows_copies(span, sources, targets, place, sems):
+    at = pl.ds(pl.multiple_of(span * SPAN, SPAN), SPAN)
+    return [
+        pltpu.make_async_copy(
+            source.at[at, :], target.at[pl.ds(place * SPAN, SPAN), :], sems.at[k]
+        )
+        for k, (source, target) in enumerate(zip(sources, targets))
+    ]
+
+
+def local_copies(span, low, high, target, place, sem):
+    half = low.shape[0] // SPAN
+    to = target.at[pl.ds(place * SPAN, SPAN), :]
+    out = []
+    for source, start in ((low, 0), (high, half)):
+        row = pl.multiple_of(jnp.clip(span - start, 0, half - 1) * SPAN, SPAN)
+        out.append(pltpu.make_async_copy(source.at[pl.ds(row, SPAN), :], to, sem))
+    return out + [half]
+
+
+def start_local(span, local):
+    low, high, half = local
+    pl.when(span < half)(low.start)
+    pl.when(span >= half)(high.start)
+
+
+def ready(which, read, lead, low, high, gate, weight):
+    channels = gate.shape[1]
+    vmem = pl.BlockSpec(memory_space=pltpu.VMEM)
+    hbm = pl.BlockSpec(memory_space=pltpu.HBM)
+    return pl.pallas_call(
+        ready_kernel,
+        in_specs=[pl.BlockSpec(memory_space=pltpu.SMEM)] + [hbm] * 6,
+        out_specs=[vmem] * 5,
+        out_shape=[
+            jax.ShapeDtypeStruct((SPAN, STATE), BF16),
+            jax.ShapeDtypeStruct((SPAN, LANES), F32),
+            jax.ShapeDtypeStruct((SPAN, channels), F32),
+            jax.ShapeDtypeStruct((SPAN, channels), BF16),
+            jax.ShapeDtypeStruct(weight.shape, BF16),
+        ],
+        scratch_shapes=[pltpu.SemaphoreType.DMA((5,))],
+        compiler_params=pltpu.CompilerParams(vmem_limit_bytes=SMALL_LIMIT),
+        cost_estimate=pl.CostEstimate(flops=1000000, bytes_accessed=10**6, transcendentals=0),
+        name="ready",
+    )(which, *in_hbm(read, lead, low, high, gate, weight))
+
+
+def tail_kernel(inner_total, has_rows, count, *refs):
+    if has_rows:
+        read_ref, lead_ref, local_ref, gate_ref, state_ref, norm_ref, w_ref, *outs, gated = refs
+    else:
+        (which, read_hbm, lead_hbm, low_hbm, high_hbm, gate_hbm, state_ref, norm_ref, w_hbm,
+         *outs, read_ref, lead_ref, local_ref, gate_ref, gated, w_ref, sems, w_sems) = refs
+        waits = []
+        for i in range(count):
+            copies = rows_copies(
+                which[i], (read_hbm, lead_hbm, gate_hbm), (read_ref, lead_ref, gate_ref), i,
+                sems.at[i],
+            )
+            local = local_copies(which[i], low_hbm, high_hbm, local_ref, i, sems.at[i, 3])
+            for copy in copies:
+                copy.start()
+            start_local(which[i], local)
+            waits.append(copies + local[:1])
+        weights = []
+        for side in range(2):
+            at = slice(side * w_hbm.shape[1] // 2, (side + 1) * w_hbm.shape[1] // 2)
+            weights.append(
+                pltpu.make_async_copy(w_hbm.at[:, at], w_ref.at[:, at], w_sems.at[side])
+            )
+        weights[0].start()
     channels = local_ref.shape[1]
     tiles = channels // LANES
-    side_width = w_ref.shape[2]
-    side_rows = side_width // LANES * SPAN
-
-    def rows_of(i):
-        span = pl.ds(pl.multiple_of(which[i] * SPAN, SPAN), SPAN)
-        pairs = (
-            (read_hbm, read_ref), (lead_hbm, lead_ref), (local_hbm, local_ref), (gate_hbm, gate_ref)
-        )
-        return [
-            pltpu.make_async_copy(
-                source.at[span, :], target.at[pl.ds(i * SPAN, SPAN), :], sems.at[4 * i + k]
-            )
-            for k, (source, target) in enumerate(pairs)
-        ]
-
-    def weights(side):
-        at = slice(side * side_width, (side + 1) * side_width)
-        return pltpu.make_async_copy(w_hbm.at[:, at], w_ref.at[side], w_sems.at[side])
-
-    copies = [rows_of(i) for i in range(count)]
-    for group in copies:
-        for copy in group:
-            copy.start()
-    weights(0).start()
+    width = w_ref.shape[1]
+    side_tiles = width // 2 // LANES
+    side_rows = side_tiles * SPAN
     sums = []
     for i in range(count):
-        for copy in copies[i]:
-            copy.wait()
-        if i == count - 1:
-            weights(1).start()
+        if not has_rows:
+            for copy in waits[i]:
+                copy.wait()
+            if i == count - 1:
+                weights[1].start()
         rows = slice(i * SPAN, (i + 1) * SPAN)
         read = read_ref[rows, :]
         lead = lead_ref[rows, :]
@@ -423,17 +489,16 @@
             gated[rows, at] = (pre * norm_ref[:, at]).astype(BF16)
         total = jnp.sum(squares, axis=1, keepdims=True) * (1.0 / inner_total)
         sums.append(jnp.transpose(jnp.broadcast_to(total, (SPAN, LANES)))[:1])
-    for side in range(2):
-        weights(side).wait()
-        for j in range(side_width // BLOCK):
-            part = dot(gated[...], w_ref[side, :, j * BLOCK : (j + 1) * BLOCK])
-            part = part.astype(outs[0].dtype)
-            for u in range(BLOCK // LANES):
-                tile = j * (BLOCK // LANES) + u
-                for i in range(count):
-                    outs[2 * i + side][tile * SPAN : (tile + 1) * SPAN, :] = part[
-                        i * SPAN : (i + 1) * SPAN, u * LANES : (u + 1) * LANES
-                    ]
+    for j in range(width // BLOCK):
+        if not has_rows and j * BLOCK % (width // 2) == 0:
+            weights[j * BLOCK // (width // 2)].wait()
+        part = dot(gated[...], w_ref[:, j * BLOCK : (j + 1) * BLOCK]).astype(outs[0].dtype)
+        for u in range(BLOCK // LANES):
+            side, tile = divmod(j * (BLOCK // LANES) + u, side_tiles)
+            for i in range(count):
+                outs[2 * i + side][tile * SPAN : (tile + 1) * SPAN, :] = part[
+                    i * SPAN : (i + 1) * SPAN, u * LANES : (u + 1) * LANES
+                ]
     for i in range(count):
         for side in range(2):
             out = outs[2 * i + side]
@@ -443,10 +508,9 @@
         outs[2 * count][...] = jnp.broadcast_to(sums[0], (8, LANES))
 
 
-def tail(which, read, lead, inner, gate, state, norm, weight, squares_in):
-    count = which.shape[0]
-    channels = inner.shape[1]
-    width = weight.shape[1]
+def tail(which, rows_in, state, norm, weight, squares_in):
+    count = 1 if which is None else which.shape[0]
+    channels, width = weight.shape
     side_rows = width // 2 // LANES * SPAN
     vmem = pl.BlockSpec(memory_space=pltpu.VMEM)
     hbm = pl.BlockSpec(memory_space=pltpu.HBM)
@@ -458,28 +522,31 @@
     if not squares_in:
         shapes.append(jax.ShapeDtypeStruct((8, LANES), F32))
     rows = count * SPAN
-    return pl.pallas_call(
-        functools.partial(tail_kernel, HEADS * HEADDIM),
-        in_specs=[pl.BlockSpec(memory_space=pltpu.SMEM)] + [hbm] * 4 + [vmem] * 2 + [hbm],
-        out_specs=[vmem] * len(shapes),
-        out_shape=shapes,
-        scratch_shapes=[
+    gated = pltpu.VMEM((rows, channels), BF16)
+    if which is None:
+        in_specs, args, scratch = [vmem] * 4, list(rows_in), [gated]
+    else:
+        in_specs = [pl.BlockSpec(memory_space=pltpu.SMEM)] + [hbm] * 5
+        args = [which, *in_hbm(*rows_in)]
+        scratch = [
             pltpu.VMEM((rows, STATE), BF16),
             pltpu.VMEM((rows, LANES), F32),
             pltpu.VMEM((rows, channels), F32),
             pltpu.VMEM((rows, channels), BF16),
-            pltpu.VMEM((rows, channels), BF16),
-            pltpu.VMEM((2, channels, width // 2), BF16),
-            pltpu.SemaphoreType.DMA((4 * count,)),
+            gated,
+            pltpu.VMEM(weight.shape, BF16),
+            pltpu.SemaphoreType.DMA((count, 4)),
             pltpu.SemaphoreType.DMA((2,)),
-        ],
+        ]
+    return pl.pallas_call(
+        functools.partial(tail_kernel, HEADS * HEADDIM, which is None, count),
+        in_specs=in_specs + [vmem] * 2 + [vmem if which is None else hbm],
+        out_specs=[vmem] * len(shapes),
+        out_shape=shapes,
+        scratch_shapes=scratch,
         compiler_params=pltpu.CompilerParams(vmem_limit_bytes=TAIL_LIMIT),
-        cost_estimate=pl.CostEstimate(
-            flops=2 * count * SPAN * channels * width,
-            bytes_accessed=2 * channels * width,
-            transcendentals=0,
-        ),
-    )(which, *in_hbm(read, lead, inner, gate), state, norm, *in_hbm(weight))
+        cost_estimate=pl.CostEstimate(flops=1000000, bytes_accessed=10**6, transcendentals=0),
+    )(*args, state, norm, *([weight] if which is None else in_hbm(weight)))
 
 
 def merge_kernel(a_ref, b_ref, b_squares, out_ref):
@@ -632,6 +699,8 @@
     norm_weight,
     out_weight,
 ):
+    rows = tokens.shape[0]
+    spans = rows // SPAN
     devices = lax.axis_size(SEQ)
     raw_in, raw_bc, raw_step, edge, gate = raw_projections(
         tokens, proj_bc, proj_step.T, proj_inner, proj_gate
@@ -644,28 +713,33 @@
     )
     state = incoming_state(local, decay[:, 0])
     skip = jnp.repeat(skip_gain, HEADDIM)[None]
-    inner = inside(x, bc, *later[:2], prior, skip)
+    inner = []
+    for part in range(2):
+        half = spans // 2
+        inner.append(inside(part * half, half, x, bc, *later[:2], prior, skip))
 
     head = lax.axis_index("head")
     size = lax.axis_size("head")
 
-    def run(which, squares_in):
-        order = jnp.stack([(head + k) & (size - 1) for k in which]).astype(jnp.int32)
-        return tail(
-            order, read, later[2], inner, gate, state, norm_weight[None], out_weight,
-            squares_in,
-        )
+    def order(*which):
+        return jnp.stack([(head + k) & (size - 1) for k in which]).astype(jnp.int32)
+
+    norm = norm_weight[None]
+    sources = (read, later[2], *inner, gate)
+    *far_rows, far_weight = ready(order(2), *sources, out_weight)
 
     def moved(value, distance):
         return ring(value, "head", distance)
 
-    far_left, far_right = run((2,), {(0, 0), (0, 1)})
+    far_left, far_right = tail(None, far_rows, state, norm, far_weight, {(0, 0), (0, 1)})
     relay_up = moved(far_left, 1)
     relay_down = moved(far_right, -1)
-    next_left, next_right, last_left, last_right = run((1, 3), {(0, 0), (1, 1)})
+    next_left, next_right, last_left, last_right = tail(
+        order(1, 3), sources, state, norm, out_weight, {(0, 0), (1, 1)}
+    )
     direct_up = moved(next_right, 1)
     direct_down = moved(last_left, -1)
-    own_left, own_right, own_squares = run((0,), set())
+    own_left, own_right, own_squares = tail(order(0), sources, state, norm, out_weight, set())
     up = merge(next_left, relay_up, True)
     up = moved(up, 1)
     down = merge(last_right, relay_down, False)

time: 102 us -> 104 us (1.020)
  Pallas kernels: 45.4 us -> 48.1 us
    pallas_call x4 -> x6, Pallas kernels: 20.6 us -> 23.3 us  [the longest x3 12.1 us: tail(): pl.pallas_call(functools.partial(tail_kernel, HEADS * HEADDIM, which is N...]
  transfers between devices with their start and end apart: 18 -> 18, of which waited for: 13 -> 13; matrix products, arithmetic and copies ran while one was open for 0% -> 0% of each run, Pallas kernels for 18% -> 23%
where the time goes in v5:
time: 104 us; the launch traced here: 103 us
  Pallas kernels  48.1 us (46%)
  starting transfers between devices  27.5 us (26%)
  waiting for transfers between devices  26 us (25%)
    ppermute x17, starting transfers between devices, ring(): lax.ppermute(value, axis, [(i, (i + distance) % size) for i in range(size)])  26.2 us
    ppermute x17, waiting for transfers between devices, ring(): lax.ppermute(value, axis, [(i, (i + distance) % size) for i in range(size)])  26 us
    pallas_call x1, Pallas kernels, raw_projections(): pl.pallas_call(raw_kernel, in_specs=[hbm] * 5, out_specs=[hbm] + [vmem] *...  14.4 us
    pallas_call x3, Pallas kernels, tail(): pl.pallas_call(functools.partial(tail_kernel, HEADS * HEADDIM, which is N...  12.1 us
    pallas_call x2, Pallas kernels, inside(): pl.pallas_call(functools.partial(inside_kernel, first), grid=(count,), in...  8.04 us
    pallas_call x1, Pallas kernels, front(): pl.pallas_call(front_kernel, grid=(groups + 1,), in_specs=[late((rows, BL...  7.73 us
    pallas_call x1, Pallas kernels, ready(): pl.pallas_call(ready_kernel, in_specs=[pl.BlockSpec(memory_space=pltpu.SM...  3.14 us
  transfers between devices with their start and end apart: 18, of which 13 were waited for; matrix products, arithmetic and copies ran while one was open for 0% of the time, Pallas kernels for 23%

profile of v5, /device:TPU:0, one launch (start us, length us, event | category | flops | bytes accessed | tf_op | source)
XLA Modules:
  0.0 103.2 jit_solution(624482917186014779)
XLA Ops:
  0.0 14.4 %raw.1 = (bf16[512,1280]{1,0:T(8,128)(2,1)}, bf16[512,256]{1,0:T(8,128)(2,1)S(1)}, f32[512,128]{1,0:T(8,128)S(1)}, bf16[8,1536]{1,0:T(8,128)(2,1)S(1)}, bf16[512,1280]{1,0:T(8,128)(2,1)}) custom-call(bf16[512,2560]{1,0:T(8,128)(2,1)} %tok_hbm.1, bf16[2560,256]{1,0:T(8,128)(2,1)} %bc_hbm.1, bf16[20,2560]{1,0:T(8,128)(2,1)} %bitcast.53, ...), custom_call_target="tpu_custom_call" | custom-call | flops 7717519360 | bytes 17039360 | tf_op jit(solution)/shard_map/raw/pallas_call | solution.py:100
  14.4 1.3 %collective-permute-start = (bf16[8,1536]{1,0:T(8,128)(2,1)S(1)}, bf16[8,1536]{1,0:T(8,128)(2,1)S(1)}, u32[]{:S(2)}, u32[]{:S(2)}) collective-permute-start(bf16[8,1536]{1,0:T(8,128)(2,1)S(1)} %get-tuple-element.38), channel_id=1, source_target_pairs={{0,4},{4,8},{8,12},{12,16},{16,20},{20,24},{24,28},{28,32},{32,36}... | collective-permute-start | bytes 73736 | tf_op jit(solution)/shard_map/ppermute | solution.py:708
  15.7 1.4 %steps.1 = (f32[512,128]{1,0:T(8,128)S(1)}, f32[512,128]{1,0:T(8,128)S(1)}, f32[512,128]{1,0:T(8,128)S(1)}, f32[512,128]{1,0:T(8,128)}, f32[512,128]{1,0:T(8,128)}, /*index=5*/f32[512,128]{1,0:T(8,128)}) custom-call(f32[512,128]{1,0:T(8,128)S(1)} %get-tuple-element.39.raw_step, f32[1,20]{1,0:T(1,128)S(1)} %bitcast.37, f32[1,20]{1,0:T(1,128)S(1)} %bitcast.38), custom_call_target="tpu_custom_call" | custom-call | flops 1000000000 | bytes 1000000 | tf_op jit(solution)/shard_map/steps/pallas_call | solution.py:159
  17.2 7.7 %front.1 = (bf16[512,1280]{1,0:T(8,128)(2,1)}, bf16[512,256]{1,0:T(8,128)(2,1)}, bf16[512,128]{1,0:T(8,128)(2,1)}, bf16[10,128,128]{2,1,0:T(8,128)(2,1)S(1)}, bf...) custom-call(bf16[512,1280]{1,0:T(8,128)(2,1)} %get-tuple-element.36.raw_in, ...), custom_call_target="tpu_custom_call" | custom-call | flops 3355443200 | bytes 2621440 | tf_op jit(solution)/shard_map/front/pallas_call | solution.py:255
  25.0 2.5 %collective-permute-start.1 = (bf16[656,128]{1,0:T(8,128)(2,1)S(1)}, bf16[656,128]{1,0:T(8,128)(2,1)S(1)}, u32[]{:S(2)}, u32[]{:S(2)}) collective-permute-start(bf16[656,128]{1,0:T(8,128)(2,1)S(1)} %pad_maximum_fusion.1), channel_id=1, source_target_pairs={{0,4},{4,0},{1,5},{5,1},{2,6},{6,2},{3,7},{7,3},{8,12},{12,8},{9,1... | collective-permute-start | bytes 503816 | tf_op jit(solution)/shard_map/ppermute | solution.py:607
  27.5 1.0 %collective-permute-done.1 = bf16[656,128]{1,0:T(8,128)(2,1)S(1)} collective-permute-done((bf16[656,128]{1,0:T(8,128)(2,1)S(1)}, bf16[656,128]{1,0:T(8,128)(2,1)S(1)}, u32[]{:S(2)}, u32[]{:S(2)}) %collective-permute-start.1) | collective-permute-done | bytes 167968 | tf_op jit(solution)/shard_map/ppermute | solution.py:607
  28.6 0.1 fusion
  28.8 3.5 %collective-permute-start.2 = (bf16[176,128]{1,0:T(8,128)(2,1)S(1)}, bf16[176,128]{1,0:T(8,128)(2,1)S(1)}, u32[]{:S(2)}, u32[]{:S(2)}) collective-permute-start(bf16[176,128]{1,0:T(8,128)(2,1)S(1)} %get-tuple-element.105), channel_id=1, source_target_pairs={{0,24},{8,0},{16,8},{24,16},{1,25},{9,1},{17,9},{25,17},{2,26},{10... | collective-permute-start | bytes 135176 | tf_op jit(solution)/shard_map/ppermute | solution.py:607
  32.3 0.6 collective-permute-start.3
  32.9 1.0 collective-permute-start.4
  33.9 0.4 collective-permute-done.2
  34.3 3.5 %collective-permute-done.3 = bf16[176,128]{1,0:T(8,128)(2,1)S(1)} collective-permute-done((bf16[176,128]{1,0:T(8,128)(2,1)S(1)}, bf16[176,128]{1,0:T(8,128)(2,1)S(1)}, u32[]{:S(2)}, u32[]{:S(2)}) %collective-permute-start.3) | collective-permute-done | bytes 45088 | tf_op jit(solution)/shard_map/ppermute | solution.py:607
  37.8 0.5 collective-permute-done.4
  38.4 0.1 fusion.2
  38.5 4.1 %collective-permute-start.5 = (bf16[176,128]{1,0:T(8,128)(2,1)S(1)}, bf16[176,128]{1,0:T(8,128)(2,1)S(1)}, u32[]{:S(2)}, u32[]{:S(2)}) collective-permute-start(bf16[176,128]{1,0:T(8,128)(2,1)S(1)} %pad_maximum_fusion.3), channel_id=1, source_target_pairs={{0,96},{32,0},{64,32},{96,64},{1,97},{33,1},{65,33},{97,65},{2,98}... | collective-permute-start | bytes 135176 | tf_op jit(solution)/shard_map/ppermute | solution.py:607
  42.6 1.3 %collective-permute-start.7 = (bf16[176,128]{1,0:T(8,128)(2,1)S(1)}, bf16[176,128]{1,0:T(8,128)(2,1)S(1)}, u32[]{:S(2)}, u32[]{:S(2)}) collective-permute-start(bf16[176,128]{1,0:T(8,128)(2,1)S(1)} %pad_maximum_fusion.3), channel_id=1, source_target_pairs={{0,32},{32,64},{64,96},{96,0},{1,33},{33,65},{65,97},{97,1},{2,34}... | collective-permute-start | bytes 135176 | tf_op jit(solution)/shard_map/ppermute | solution.py:607
  43.9 0.5 collective-permute-done.5
  44.3 3.9 %collective-permute-done.6 = bf16[176,128]{1,0:T(8,128)(2,1)S(1)} collective-permute-done((bf16[176,128]{1,0:T(8,128)(2,1)S(1)}, bf16[176,128]{1,0:T(8,128)(2,1)S(1)}, u32[]{:S(2)}, u32[]{:S(2)}) %collective-permute-start.6) | collective-permute-done | bytes 45088 | tf_op jit(solution)/shard_map/ppermute | solution.py:607
  48.2 0.1 collective-permute-done.7
  48.4 0.1 select_convert_fusion.1
  48.6 2.1 %collective-permute-start.8 = (bf16[5,32,128]{2,1,0:T(8,128)(2,1)S(1)}, bf16[5,32,128]{2,1,0:T(8,128)(2,1)S(1)}, u32[]{:S(2)}, u32[]{:S(2)}) collective-permute-start(bf16[5,32,128]{2,1,0:T(8,128)(2,1)S(1)} %get-tuple-element.90), channel_id=1, source_target_pairs={{0,24},{8,0},{16,8},{24,16},{1,25},{9,1},{17,9},{25,17},{2,26},{10... | collective-permute-start | bytes 122888 | tf_op jit(solution)/shard_map/ppermute | solution.py:607
  50.6 0.9 collective-permute-start.9
  51.5 0.3 collective-permute-start.10
  51.8 1.0 %collective-permute-done.8 = bf16[5,32,128]{2,1,0:T(8,128)(2,1)S(1)} collective-permute-done((bf16[5,32,128]{2,1,0:T(8,128)(2,1)S(1)}, bf16[5,32,128]{2,1,0:T(8,128)(2,1)S(1)}, u32[]{:S(2)}, u32[]{:S(2)}) %collective-permute-start.8) | collective-permute-done | bytes 40992 | tf_op jit(solution)/shard_map/ppermute | solution.py:607
  52.8 3.3 %collective-permute-done.9 = bf16[5,32,128]{2,1,0:T(8,128)(2,1)S(1)} collective-permute-done((bf16[5,32,128]{2,1,0:T(8,128)(2,1)S(1)}, bf16[5,32,128]{2,1,0:T(8,128)(2,1)S(1)}, u32[]{:S(2)}, u32[]{:S(2)}) %collective-permute-start.9) | collective-permute-done | bytes 40992 | tf_op jit(solution)/shard_map/ppermute | solution.py:607
  56.1 0.6 collective-permute-done.10
  56.8 0.1 broadcast_select_fusion.2
  57.0 0.1 collective-permute-start.11
  57.1 0.1 broadcast_in_dim.35
  57.1 0.1 broadcast_in_dim_reshape.3.skip_ref
  57.2 4.0 %inside.3.refs_4_.high_hbm = f32[256,1280]{1,0:T(8,128)} custom-call(bf16[512,1280]{1,0:T(8,128)(2,1)} %get-tuple-element.45.x_ref, bf16[512,256]{1,0:T(8,128)(2,1)} %get-tuple-element.46.bc_ref, f32[512,128]{1,0:T(8,128)} %get-tuple-element.47.cum_ref, f32[512,128]{1,0:T(8,128)} %get-tuple-element.48.dt_ref, ...), custom_call_target="tpu_custom_call" | custom-call | flops 1000000 | bytes 1000000 | tf_op jit(solution)/shard_map/inside/pallas_call | solution.py:333
  61.3 4.0 %inside.2.refs_3_.low_hbm = f32[256,1280]{1,0:T(8,128)} custom-call(bf16[512,1280]{1,0:T(8,128)(2,1)} %get-tuple-element.45.x_ref, bf16[512,256]{1,0:T(8,128)(2,1)} %get-tuple-element.46.bc_ref, f32[512,128]{1,0:T(8,128)} %get-tuple-element.47.cum_ref, f32[512,128]{1,0:T(8,128)} %get-tuple-element.48.dt_ref, ...), custom_call_target="tpu_custom_call" | custom-call | flops 1000000 | bytes 1000000 | tf_op jit(solution)/shard_map/inside/pallas_call | solution.py:333
  65.3 3.1 %ready.1 = (bf16[128,128]{1,0:T(8,128)(2,1)S(1)}, f32[128,128]{1,0:T(8,128)S(1)}, f32[128,1280]{1,0:T(8,128)S(1)}, bf16[128,1280]{1,0:T(8,128)(2,1)S(1)}, bf16[1280,2560]{1,0:T(8,128)(2,1)S(1)}) custom-call(s32[1]{0:T(128)} %bitcast.24.which, bf16[512,128]{1,0:T(8,128)(2,1)} %get-tuple-element.43.refs_1_.read_hbm, ...), custom_call_target="tpu_custom_call" | custom-call | flops 1000000 | bytes 1000000 | tf_op jit(solution)/shard_map/ready/pallas_call | solution.py:425
  68.4 0.2 broadcast_select_fusion.1
  68.6 1.6 %shard_map.138 = (bf16[1296,128]{1,0:T(8,128)(2,1)S(1)}, bf16[1296,128]{1,0:T(8,128)(2,1)S(1)}) custom-call(bf16[128,128]{1,0:T(8,128)(2,1)S(1)} %get-tuple-element.57.refs_0_, f32[128,128]{1,0:T(8,128)S(1)} %get-tuple-element.58.refs_1_, f32[128,1280]{1,0:T(8,128)S(1)} %get-tuple-element.59.refs_2_, bf16[128,1280]{1,0:T(8,128)(2,1)S(1)} %get-tuple-element.60.refs_3_, ...), custom_call_target="tpu_custom_call" | custom-call | flops 1000000 | bytes 1000000 | tf_op jit(solution)/shard_map/pallas_call | solution.py:541
  70.2 2.8 %collective-permute-start.14 = (bf16[1296,128]{1,0:T(8,128)(2,1)S(1)}, bf16[1296,128]{1,0:T(8,128)(2,1)S(1)}, u32[]{:S(2)}, u32[]{:S(2)}) collective-permute-start(bf16[1296,128]{1,0:T(8,128)(2,1)S(1)} %get-tuple-element.64), channel_id=1, source_target_pairs={{0,3},{1,0},{2,1},{3,2},{4,7},{5,4},{6,5},{7,6},{8,11},{9,8},{10,9... | collective-permute-start | bytes 995336 | tf_op jit(solution)/shard_map/ppermute | solution.py:607
  73.1 0.1 pad_add_fusion.refs_0_
  73.2 6.3 %shard_map.137 = (bf16[1296,128]{1,0:T(8,128)(2,1)S(1)}, bf16[1280,128]{1,0:T(8,128)(2,1)S(1)}, bf16[1280,128]{1,0:T(8,128)(2,1)S(1)}, bf16[1296,128]{1,0:T(8,128)(2,1)S(1)}) custom-call(s32[2]{0:T(128)S(1)} %pad_add_fusion.refs_0_, bf16[512,128]{1,0:T(8,128)(2,1)} %get-tuple-element.43.refs_1_.read_hbm, f32[512,128]{1,0:T(8,128)} %get-tuple-element.44.refs_2_.lead_hbm, ...), custom_call_target="tpu_custom_call" | custom-call | flops 1000000 | bytes 1000000 | tf_op jit(solution)/shard_map/pallas_call | solution.py:541
  79.5 1.3 %collective-permute-done.14.b_ref = bf16[1296,128]{1,0:T(8,128)(2,1)S(1)} collective-permute-done((bf16[1296,128]{1,0:T(8,128)(2,1)S(1)}, bf16[1296,128]{1,0:T(8,128)(2,1)S(1)}, u32[]{:S(2)}, u32[]{:S(2)}) %collective-permute-start.14) | collective-permute-done | bytes 331808 | tf_op jit(solution)/shard_map/ppermute | solution.py:607
  80.8 0.1 shard_map.140
  80.9 3.8 %collective-permute-start.15 = (bf16[1296,128]{1,0:T(8,128)(2,1)S(1)}, bf16[1296,128]{1,0:T(8,128)(2,1)S(1)}, u32[]{:S(2)}, u32[]{:S(2)}) collective-permute-start(bf16[1296,128]{1,0:T(8,128)(2,1)S(1)} %shard_map.140), channel_id=1, source_target_pairs={{0,3},{1,0},{2,1},{3,2},{4,7},{5,4},{6,5},{7,6},{8,11},{9,8},{10,9... | collective-permute-start | bytes 995336 | tf_op jit(solution)/shard_map/ppermute | solution.py:607
  84.6 0.1 shard_map.139
  84.7 0.1 collective-permute-start.13
  84.8 3.2 %collective-permute-start.16 = (bf16[1280,128]{1,0:T(8,128)(2,1)S(1)}, bf16[1280,128]{1,0:T(8,128)(2,1)S(1)}, u32[]{:S(2)}, u32[]{:S(2)}) collective-permute-start(bf16[1280,128]{1,0:T(8,128)(2,1)S(1)} %get-tuple-element.65), channel_id=1, source_target_pairs={{0,3},{1,0},{2,1},{3,2},{4,7},{5,4},{6,5},{7,6},{8,11},{9,8},{10,9... | collective-permute-start | bytes 983048 | tf_op jit(solution)/shard_map/ppermute | solution.py:607
  88.0 4.2 %shard_map.136 = (bf16[1280,128]{1,0:T(8,128)(2,1)S(1)}, bf16[1280,128]{1,0:T(8,128)(2,1)S(1)}, f32[8,128]{1,0:T(8,128)S(1)}) custom-call(s32[1]{0:T(128)} %bitcast.refs_0_, bf16[512,128]{1,0:T(8,128)(2,1)} %get-tuple-element.43.refs_1_.read_hbm, f32[512,128]{1,0:T(8,128)} %get-tuple-element.44.refs_2_.lead_hbm, f32[256,1280]{1,0:T(8,128)} %inside.2.refs_3_.low_hbm, ...), custom_call_target="tpu_custom_call" | custom-call | flops 1000000 | bytes 1000000 | tf_op jit(solution)/shard_map/pallas_call | solution.py:541
  92.3 6.2 %collective-permute-done.16.direct_l = bf16[1280,128]{1,0:T(8,128)(2,1)S(1)} collective-permute-done((bf16[1280,128]{1,0:T(8,128)(2,1)S(1)}, bf16[1280,128]{1,0:T(8,128)(2,1)S(1)}, u32[]{:S(2)}, u32[]{:S(2)}) %collective-permute-start.16) | collective-permute-done | bytes 327712 | tf_op jit(solution)/shard_map/ppermute | solution.py:607
  98.5 3.6 %collective-permute-done.17.direct_r = bf16[1280,128]{1,0:T(8,128)(2,1)S(1)} collective-permute-done((bf16[1280,128]{1,0:T(8,128)(2,1)S(1)}, bf16[1280,128]{1,0:T(8,128)(2,1)S(1)}, u32[]{:S(2)}, u32[]{:S(2)}) %collective-permute-start.17) | collective-permute-done | bytes 327712 | tf_op jit(solution)/shard_map/ppermute | solution.py:607
  102.1 1.2 %final.1 = bf16[128,2560]{1,0:T(8,128)(2,1)} custom-call(bf16[1280,128]{1,0:T(8,128)(2,1)S(1)} %get-tuple-element.53.own_l, bf16[1280,128]{1,0:T(8,128)(2,1)S(1)} %get-tuple-element.54.own_r, f32[8,128]{1,0:T(8,128)S(1)} %get-tuple-element.55.own_sq, bf16[1296,128]{1,0:T(8,128)(2,1)S(1)} %collective-permute-done.13.up, ...), custom_call_target="tpu_custom_call" | custom-call | flops 1000000 | bytes 1000000 | tf_op jit(solution)/shard_map/final/pallas_call | solution.py:594
  (53 shorter events, 0.5 us)
Async XLA Ops:
  0.0 15.7 %copy-start.3 = (f32[20]{0:T(128)S(1)}, f32[20]{0:T(128)}, u32[]{:S(2)}) copy-start(f32[20]{0:T(128)} %param.23) | copy-start | bytes 244
  0.0 15.7 %copy-start.4 = (f32[20]{0:T(128)S(1)}, f32[20]{0:T(128)}, u32[]{:S(2)}) copy-start(f32[20]{0:T(128)} %param.24) | copy-start | bytes 244
  14.4 2.8 %collective-permute-start = (bf16[8,1536]{1,0:T(8,128)(2,1)S(1)}, bf16[8,1536]{1,0:T(8,128)(2,1)S(1)}, u32[]{:S(2)}, u32[]{:S(2)}) collective-permute-start(bf16[8,1536]{1,0:T(8,128)(2,1)S(1)} %get-tuple-element.38), channel_id=1, source_target_pairs={{0,4},{4,8},{8,12},{12,16},{16,20},{20,24},{24,28},{28,32},{32,36}... | collective-permute-start | bytes 73736 | tf_op jit(solution)/shard_map/ppermute | solution.py:708
  15.7 1.4 %copy-start.5 = (f32[1280]{0:T(1024)S(1)}, f32[1280]{0:T(1024)}, u32[]{:S(2)}) copy-start(f32[1280]{0:T(1024)} %param.21) | copy-start | bytes 15364
  15.7 1.4 %copy-start = (f32[4,1280]{1,0:T(4,128)S(1)}, f32[4,1280]{1,0:T(4,128)}, u32[]{:S(2)}) copy-start(f32[4,1280]{1,0:T(4,128)} %taps.1) | copy-start | bytes 61444
  15.7 1.4 %copy-start.1 = (f32[4,256]{1,0:T(4,128)S(1)}, f32[4,256]{1,0:T(4,128)}, u32[]{:S(2)}) copy-start(f32[4,256]{1,0:T(4,128)} %taps_bc.1) | copy-start | bytes 12292
  15.7 1.4 %copy-start.2 = (f32[256]{0:T(256)S(1)}, f32[256]{0:T(256)}, u32[]{:S(2)}) copy-start(f32[256]{0:T(256)} %param.22) | copy-start | bytes 3076
  25.0 3.5 %collective-permute-start.1 = (bf16[656,128]{1,0:T(8,128)(2,1)S(1)}, bf16[656,128]{1,0:T(8,128)(2,1)S(1)}, u32[]{:S(2)}, u32[]{:S(2)}) collective-permute-start(bf16[656,128]{1,0:T(8,128)(2,1)S(1)} %pad_maximum_fusion.1), channel_id=1, source_target_pairs={{0,4},{4,0},{1,5},{5,1},{2,6},{6,2},{3,7},{7,3},{8,12},{12,8},{9,1... | collective-permute-start | bytes 503816 | tf_op jit(solution)/shard_map/ppermute | solution.py:607
  28.8 5.5 %collective-permute-start.2 = (bf16[176,128]{1,0:T(8,128)(2,1)S(1)}, bf16[176,128]{1,0:T(8,128)(2,1)S(1)}, u32[]{:S(2)}, u32[]{:S(2)}) collective-permute-start(bf16[176,128]{1,0:T(8,128)(2,1)S(1)} %get-tuple-element.105), channel_id=1, source_target_pairs={{0,24},{8,0},{16,8},{24,16},{1,25},{9,1},{17,9},{25,17},{2,26},{10... | collective-permute-start | bytes 135176 | tf_op jit(solution)/shard_map/ppermute | solution.py:607
  32.3 5.6 %collective-permute-start.3 = (bf16[176,128]{1,0:T(8,128)(2,1)S(1)}, bf16[176,128]{1,0:T(8,128)(2,1)S(1)}, u32[]{:S(2)}, u32[]{:S(2)}) collective-permute-start(bf16[176,128]{1,0:T(8,128)(2,1)S(1)} %get-tuple-element.104), channel_id=1, source_target_pairs={{0,16},{8,24},{16,0},{24,8},{1,17},{9,25},{17,1},{25,9},{2,18},{10... | collective-permute-start | bytes 135176 | tf_op jit(solution)/shard_map/ppermute | solution.py:607
  32.9 5.4 %collective-permute-start.4 = (bf16[176,128]{1,0:T(8,128)(2,1)S(1)}, bf16[176,128]{1,0:T(8,128)(2,1)S(1)}, u32[]{:S(2)}, u32[]{:S(2)}) collective-permute-start(bf16[176,128]{1,0:T(8,128)(2,1)S(1)} %get-tuple-element.103), channel_id=1, source_target_pairs={{0,8},{8,16},{16,24},{24,0},{1,9},{9,17},{17,25},{25,1},{2,10},{10... | collective-permute-start | bytes 135176 | tf_op jit(solution)/shard_map/ppermute | solution.py:607
  38.5 5.8 %collective-permute-start.5 = (bf16[176,128]{1,0:T(8,128)(2,1)S(1)}, bf16[176,128]{1,0:T(8,128)(2,1)S(1)}, u32[]{:S(2)}, u32[]{:S(2)}) collective-permute-start(bf16[176,128]{1,0:T(8,128)(2,1)S(1)} %pad_maximum_fusion.3), channel_id=1, source_target_pairs={{0,96},{32,0},{64,32},{96,64},{1,97},{33,1},{65,33},{97,65},{2,98}... | collective-permute-start | bytes 135176 | tf_op jit(solution)/shard_map/ppermute | solution.py:607
  42.6 5.6 %collective-permute-start.6 = (bf16[176,128]{1,0:T(8,128)(2,1)S(1)}, bf16[176,128]{1,0:T(8,128)(2,1)S(1)}, u32[]{:S(2)}, u32[]{:S(2)}) collective-permute-start(bf16[176,128]{1,0:T(8,128)(2,1)S(1)} %pad_maximum_fusion.3), channel_id=1, source_target_pairs={{0,64},{32,96},{64,0},{96,32},{1,65},{33,97},{65,1},{97,33},{2,66}... | collective-permute-start | bytes 135176 | tf_op jit(solution)/shard_map/ppermute | solution.py:607
  42.6 5.7 %collective-permute-start.7 = (bf16[176,128]{1,0:T(8,128)(2,1)S(1)}, bf16[176,128]{1,0:T(8,128)(2,1)S(1)}, u32[]{:S(2)}, u32[]{:S(2)}) collective-permute-start(bf16[176,128]{1,0:T(8,128)(2,1)S(1)} %pad_maximum_fusion.3), channel_id=1, source_target_pairs={{0,32},{32,64},{64,96},{96,0},{1,33},{33,65},{65,97},{97,1},{2,34}... | collective-permute-start | bytes 135176 | tf_op jit(solution)/shard_map/ppermute | solution.py:607
  48.4 8.6 %copy-start.7 = (f32[20]{0:T(128)S(1)}, f32[20]{0:T(128)}, u32[]{:S(2)}) copy-start(f32[20]{0:T(128)} %param.25) | copy-start | bytes 244
  48.4 8.8 %copy-start.6 = (f32[1280]{0:T(1024)S(1)}, f32[1280]{0:T(1024)}, u32[]{:S(2)}) copy-start(f32[1280]{0:T(1024)} %param.26) | copy-start | bytes 15364
  48.6 4.3 %collective-permute-start.8 = (bf16[5,32,128]{2,1,0:T(8,128)(2,1)S(1)}, bf16[5,32,128]{2,1,0:T(8,128)(2,1)S(1)}, u32[]{:S(2)}, u32[]{:S(2)}) collective-permute-start(bf16[5,32,128]{2,1,0:T(8,128)(2,1)S(1)} %get-tuple-element.90), channel_id=1, source_target_pairs={{0,24},{8,0},{16,8},{24,16},{1,25},{9,1},{17,9},{25,17},{2,26},{10... | collective-permute-start | bytes 122888 | tf_op jit(solution)/shard_map/ppermute | solution.py:607
  50.6 5.5 %collective-permute-start.9 = (bf16[5,32,128]{2,1,0:T(8,128)(2,1)S(1)}, bf16[5,32,128]{2,1,0:T(8,128)(2,1)S(1)}, u32[]{:S(2)}, u32[]{:S(2)}) collective-permute-start(bf16[5,32,128]{2,1,0:T(8,128)(2,1)S(1)} %get-tuple-element.89), channel_id=1, source_target_pairs={{0,16},{8,24},{16,0},{24,8},{1,17},{9,25},{17,1},{25,9},{2,18},{10... | collective-permute-start | bytes 122888 | tf_op jit(solution)/shard_map/ppermute | solution.py:607
  51.5 5.2 %collective-permute-start.10 = (bf16[5,32,128]{2,1,0:T(8,128)(2,1)S(1)}, bf16[5,32,128]{2,1,0:T(8,128)(2,1)S(1)}, u32[]{:S(2)}, u32[]{:S(2)}) collective-permute-start(bf16[5,32,128]{2,1,0:T(8,128)(2,1)S(1)} %get-tuple-element.71), channel_id=1, source_target_pairs={{0,8},{8,16},{16,24},{24,0},{1,9},{9,17},{17,25},{25,1},{2,10},{10... | collective-permute-start | bytes 122888 | tf_op jit(solution)/shard_map/ppermute | solution.py:607
  57.0 11.5 %collective-permute-start.11 = (bf16[5,128,128]{2,1,0:T(8,128)(2,1)S(1)}, bf16[5,128,128]{2,1,0:T(8,128)(2,1)S(1)}, u32[]{:S(2)}, u32[]{:S(2)}) collective-permute-start(bf16[5,128,128]{2,1,0:T(8,128)(2,1)S(1)} %broadcast_select_fusion.2), channel_id=1, source_target_pairs={{0,4},{4,0},{1,5},{5,1},{2,6},{6,2},{3,7},{7,3},{8,12},{12,8},{9,1... | collective-permute-start | bytes 491528 | tf_op jit(solution)/shard_map/ppermute | solution.py:607
  70.2 10.5 %collective-permute-start.14 = (bf16[1296,128]{1,0:T(8,128)(2,1)S(1)}, bf16[1296,128]{1,0:T(8,128)(2,1)S(1)}, u32[]{:S(2)}, u32[]{:S(2)}) collective-permute-start(bf16[1296,128]{1,0:T(8,128)(2,1)S(1)} %get-tuple-element.64), channel_id=1, source_target_pairs={{0,3},{1,0},{2,1},{3,2},{4,7},{5,4},{6,5},{7,6},{8,11},{9,8},{10,9... | collective-permute-start | bytes 995336 | tf_op jit(solution)/shard_map/ppermute | solution.py:607
  73.1 11.6 %collective-permute-start.12 = (bf16[1296,128]{1,0:T(8,128)(2,1)S(1)}, bf16[1296,128]{1,0:T(8,128)(2,1)S(1)}, u32[]{:S(2)}, u32[]{:S(2)}) collective-permute-start(bf16[1296,128]{1,0:T(8,128)(2,1)S(1)} %get-tuple-element.62), channel_id=1, source_target_pairs={{0,1},{1,2},{2,3},{3,0},{4,5},{5,6},{6,7},{7,4},{8,9},{9,10},{10,1... | collective-permute-start | bytes 995336 | tf_op jit(solution)/shard_map/ppermute | solution.py:607
  80.9 21.2 %collective-permute-start.15 = (bf16[1296,128]{1,0:T(8,128)(2,1)S(1)}, bf16[1296,128]{1,0:T(8,128)(2,1)S(1)}, u32[]{:S(2)}, u32[]{:S(2)}) collective-permute-start(bf16[1296,128]{1,0:T(8,128)(2,1)S(1)} %shard_map.140), channel_id=1, source_target_pairs={{0,3},{1,0},{2,1},{3,2},{4,7},{5,4},{6,5},{7,6},{8,11},{9,8},{10,9... | collective-permute-start | bytes 995336 | tf_op jit(solution)/shard_map/ppermute | solution.py:607
  84.7 17.4 %collective-permute-start.13 = (bf16[1296,128]{1,0:T(8,128)(2,1)S(1)}, bf16[1296,128]{1,0:T(8,128)(2,1)S(1)}, u32[]{:S(2)}, u32[]{:S(2)}) collective-permute-start(bf16[1296,128]{1,0:T(8,128)(2,1)S(1)} %shard_map.139), channel_id=1, source_target_pairs={{0,1},{1,2},{2,3},{3,0},{4,5},{5,6},{6,7},{7,4},{8,9},{9,10},{10,1... | collective-permute-start | bytes 995336 | tf_op jit(solution)/shard_map/ppermute | solution.py:607
  84.8 13.7 %collective-permute-start.16 = (bf16[1280,128]{1,0:T(8,128)(2,1)S(1)}, bf16[1280,128]{1,0:T(8,128)(2,1)S(1)}, u32[]{:S(2)}, u32[]{:S(2)}) collective-permute-start(bf16[1280,128]{1,0:T(8,128)(2,1)S(1)} %get-tuple-element.65), channel_id=1, source_target_pairs={{0,3},{1,0},{2,1},{3,2},{4,7},{5,4},{6,5},{7,6},{8,11},{9,8},{10,9... | collective-permute-start | bytes 983048 | tf_op jit(solution)/shard_map/ppermute | solution.py:607
  88.0 14.0 %collective-permute-start.17 = (bf16[1280,128]{1,0:T(8,128)(2,1)S(1)}, bf16[1280,128]{1,0:T(8,128)(2,1)S(1)}, u32[]{:S(2)}, u32[]{:S(2)}) collective-permute-start(bf16[1280,128]{1,0:T(8,128)(2,1)S(1)} %get-tuple-element.66), channel_id=1, source_target_pairs={{0,1},{1,2},{2,3},{3,0},{4,5},{5,6},{6,7},{7,4},{8,9},{9,10},{10,1... | collective-permute-start | bytes 983048 | tf_op jit(solution)/shard_map/ppermute | solution.py:607

commit v6 on v5

--- a/solution.py
+++ b/solution.py
@@ -15,14 +15,13 @@
 KERNEL = 4
 SPAN = 128
 LANES = 128
-EDGE = 8
+EDGE = 16
 BLOCK = 256
 SEQ = ("seq_0", "seq_1", "seq_2")
 SEQ_HEAD = ("seq_0", "seq_1", "seq_2", "head")
 
 MIB = 2**20
-RAW_LIMIT = 24 * MIB
-FRONT_LIMIT = 24 * MIB
+FIRST_LIMIT = 48 * MIB
 INSIDE_LIMIT = 12 * MIB
 TAIL_LIMIT = 16 * MIB
 SMALL_LIMIT = 8 * MIB
@@ -49,249 +48,191 @@
     return jnp.where(lane < HEADDIM, first, second)
 
 
-def raw_kernel(
-    tok_hbm, bc_hbm, step_hbm, in_hbm, gate_hbm,
-    in_out, bc_out, step_out, edge_out, gate_out,
-    tok, w_bc, w_step, w_in, w_gate, inner, gate, sems,
+def first_kernel(
+    edge, tok_hbm, bc_hbm, step_hbm, in_hbm, gate_hbm, s0, s1, s2, s3, s4, s5,
+    x_hbm, maps_hbm, read_hbm, cum_hbm, dt_hbm, lead_hbm, prior_hbm, gate_out, local_out, decay_out,
+    tok, w_bc, w_step, w_in, w_gate, padded, padded_bc,
+    x_ref, maps_ref, read_ref, cum_ref, dt_ref, lead_ref, prior_ref, gate_ref,
+    taps, offset, taps_bc, offset_bc, step_bias, decay_log, sems,
 ):
-    rows = tok.shape[0]
-    heads = w_step.shape[0]
+    rows = x_ref.shape[0]
+    above = edge.shape[0]
+    channels = x_ref.shape[1]
+    heads = step_bias.shape[1]
+    spans = rows // SPAN
+    per = BLOCK // HEADDIM
+    tiles = BLOCK // LANES
+
     first = [
-        pltpu.make_async_copy(tok_hbm, tok, sems.at[0]),
+        pltpu.make_async_copy(tok_hbm, tok.at[pl.ds(above, rows), :], sems.at[0]),
         pltpu.make_async_copy(bc_hbm, w_bc, sems.at[1]),
         pltpu.make_async_copy(step_hbm, w_step, sems.at[2]),
     ]
     inner_copy = pltpu.make_async_copy(in_hbm, w_in, sems.at[3])
     gate_copy = pltpu.make_async_copy(gate_hbm, w_gate, sems.at[4])
+    small = (taps, offset, taps_bc, offset_bc, step_bias, decay_log)
+    for k, (source, target) in enumerate(zip((s0, s1, s2, s3, s4, s5), small)):
+        first.append(pltpu.make_async_copy(source, target, sems.at[14 + k]))
     for copy in first:
         copy.start()
+    tok[:above, :] = edge[...]
     for copy in first:
         copy.wait()
     inner_copy.start()
-    bc = dot(tok[...], w_bc[...]).astype(BF16)
-    bc_out[...] = bc
-    edge_out[:, :BLOCK] = bc[rows - EDGE :]
-    step_out[:, :heads] = lax.dot_general(
-        tok[...], w_step[...], (((1,), (1,)), ((), ())), preferred_element_type=F32
+
+    def conv(source, at, tap, off):
+        total = off
+        for k in range(KERNEL):
+            begin = above - (KERNEL - 1) + k
+            total = total + tap[k : k + 1, at] * source[begin : begin + rows, at]
+        return silu(total).astype(BF16)
+
+    padded_bc[...] = dot(tok[...], w_bc[...]).astype(BF16).astype(F32)
+    steps = lax.dot_general(
+        tok[above:, :], w_step[...], (((1,), (1,)), ((), ())), preferred_element_type=F32
     )
     inner_copy.wait()
     gate_copy.start()
-    raw = dot(tok[...], w_in[...]).astype(BF16)
-    inner[...] = raw
-    edge_out[:, BLOCK:] = raw[rows - EDGE :]
-    stored = [pltpu.make_async_copy(inner, in_out, sems.at[7])]
-    stored[0].start()
+    padded[...] = dot(tok[...], w_in[...]).astype(BF16).astype(F32)
+
+    maps = conv(padded_bc, slice(0, 2 * STATE), taps_bc, offset_bc[...])
+    maps_ref[...] = maps
+    read_ref[...] = maps[:, STATE:]
+    v = steps + step_bias[...]
+    dt = jnp.maximum(v, 0.0) + jnp.log1p(jnp.exp(-jnp.abs(v)))
+    log_decay = -jnp.exp(decay_log[...]) * dt
+    cum_ref[...] = jnp.zeros_like(cum_ref)
+    dt_ref[...] = jnp.zeros_like(dt_ref)
+    lead_ref[...] = jnp.zeros_like(lead_ref)
+    dt_ref[:, :heads] = dt
+    row = lax.broadcasted_iota(jnp.int32, (SPAN, SPAN), 0)
+    col = lax.broadcasted_iota(jnp.int32, (SPAN, SPAN), 1)
+    lower = (row >= col).astype(F32)
+    lead = jnp.zeros((1, heads), F32)
+    ends, gone, write_t = [], [], []
+    for s in range(spans):
+        at = slice(s * SPAN, (s + 1) * SPAN)
+        write_t.append(jnp.transpose(maps[at, :STATE].astype(F32)).astype(BF16))
+        cum = jnp.dot(
+            lower, log_decay[at], preferred_element_type=F32, precision=lax.Precision.HIGHEST
+        )
+        cum_ref[at, :heads] = cum
+        lead_ref[at, :heads] = jnp.exp(cum + lead)
+        last = cum[SPAN - 1 :, :]
+        lead = lead + last
+        ends.append(jnp.exp(last - cum) * dt[at])
+        gone.append(jnp.exp(last))
+    gone.append(jnp.exp(lead))
+
     gate_copy.wait()
+    early = [
+        pltpu.make_async_copy(source, target, sems.at[5 + k])
+        for k, (source, target) in enumerate(
+            (
+                (maps_ref, maps_hbm), (read_ref, read_hbm), (cum_ref, cum_hbm), (dt_ref, dt_hbm),
+                (lead_ref, lead_hbm),
+            )
+        )
+    ]
+    for copy in early:
+        copy.start()
     half = rows // 2
+    gate_ref[:half, :] = dot(tok[above : above + half, :], w_gate[...]).astype(BF16)
+    for g in range(channels // BLOCK):
+        at = slice(g * BLOCK, (g + 1) * BLOCK)
+        x = conv(padded, at, taps, offset[:, at])
+        x_ref[:, at] = x
+        running = jnp.zeros((STATE, BLOCK), F32)
+        for s in range(spans):
+            if s > 0:
+                for t in range(tiles):
+                    prior_ref[s - 1, g * tiles + t] = running[
+                        :, t * LANES : (t + 1) * LANES
+                    ].astype(BF16)
+
+            def wide(value):
+                return jnp.concatenate(
+                    [
+                        lane_pair(value[:, h : h + 1], value[:, h + 1 : h + 2])
+                        for h in range(g * per, (g + 1) * per, 2)
+                    ],
+                    axis=1,
+                )
+
+            here = x[s * SPAN : (s + 1) * SPAN].astype(F32)
+            local = dot(write_t[s], (here * wide(ends[s])).astype(BF16))
+            running = wide(gone[s]) * running + local
+        for t in range(tiles):
+            to = g * tiles + t
+            local_out[to] = running[:, t * LANES : (t + 1) * LANES].astype(BF16)
+            h = g * per + 2 * t
+            decay_out[to] = jnp.broadcast_to(
+                lane_pair(gone[spans][:, h : h + 1], gone[spans][:, h + 1 : h + 2]), (8, LANES)
+            )
+    late = [
+        pltpu.make_async_copy(x_ref, x_hbm, sems.at[10]),
+        pltpu.make_async_copy(prior_ref, prior_hbm, sems.at[11]),
+    ]
     for k in range(2):
         at = slice(k * half, (k + 1) * half)
-        gate[at, :] = dot(tok[at, :], w_gate[...]).astype(BF16)
-        stored.append(pltpu.make_async_copy(gate.at[at, :], gate_out.at[at, :], sems.at[5 + k]))
-        stored[-1].start()
-    for copy in stored:
+        late.append(
+            pltpu.make_async_copy(gate_ref.at[at, :], gate_out.at[at, :], sems.at[12 + k])
+        )
+    for copy in late[:3]:
+        copy.start()
+    gate_ref[half:, :] = dot(tok[above + half :, :], w_gate[...]).astype(BF16)
+    late[3].start()
+    for copy in early + late:
         copy.wait()
 
 
-def raw_projections(tokens, w_bc, w_step, w_in, w_gate):
+def first_part(edge, tokens, w_bc, w_step, w_in, w_gate, *small):
     rows, width = tokens.shape
+    above = edge.shape[0]
     channels = w_in.shape[1]
+    spans = rows // SPAN
+    tiles = channels // LANES
     vmem = pl.BlockSpec(memory_space=pltpu.VMEM)
     hbm = pl.BlockSpec(memory_space=pltpu.HBM)
+    kept = [
+        ((rows, channels), BF16),
+        ((rows, 2 * STATE), BF16),
+        ((rows, STATE), BF16),
+        ((rows, LANES), F32),
+        ((rows, LANES), F32),
+        ((rows, LANES), F32),
+        ((spans - 1, tiles, STATE, LANES), BF16),
+        ((rows, channels), BF16),
+    ]
     return pl.pallas_call(
-        raw_kernel,
-        in_specs=[hbm] * 5,
-        out_specs=[hbm] + [vmem] * 3 + [hbm],
-        out_shape=[
-            pltpu.HBM((rows, channels), BF16),
-            jax.ShapeDtypeStruct((rows, BLOCK), BF16),
-            jax.ShapeDtypeStruct((rows, LANES), F32),
-            jax.ShapeDtypeStruct((EDGE, channels + BLOCK), BF16),
-            pltpu.HBM((rows, channels), BF16),
+        first_kernel,
+        in_specs=[vmem] + [hbm] * (5 + len(small)),
+        out_specs=[hbm] * len(kept) + [vmem] * 2,
+        out_shape=[pltpu.HBM(*a) for a in kept]
+        + [
+            jax.ShapeDtypeStruct((tiles, STATE, LANES), BF16),
+            jax.ShapeDtypeStruct((tiles, 8, LANES), F32),
         ],
         scratch_shapes=[
-            pltpu.VMEM(tokens.shape, BF16),
+            pltpu.VMEM((above + rows, width), BF16),
             pltpu.VMEM(w_bc.shape, BF16),
             pltpu.VMEM(w_step.shape, BF16),
-            pltpu.VMEM((width, channels), BF16),
-            pltpu.VMEM((width, channels), BF16),
-            pltpu.VMEM((rows, channels), BF16),
-            pltpu.VMEM((rows, channels), BF16),
-            pltpu.SemaphoreType.DMA((8,)),
+            pltpu.VMEM(w_in.shape, BF16),
+            pltpu.VMEM(w_gate.shape, BF16),
+            pltpu.VMEM((above + rows, channels), F32),
+            pltpu.VMEM((above + rows, 2 * STATE), F32),
+            *[pltpu.VMEM(*a) for a in kept],
+            *[pltpu.VMEM(a.shape, F32) for a in small],
+            pltpu.SemaphoreType.DMA((20,)),
         ],
-        compiler_params=pltpu.CompilerParams(vmem_limit_bytes=RAW_LIMIT),
+        compiler_params=pltpu.CompilerParams(vmem_limit_bytes=FIRST_LIMIT),
         cost_estimate=pl.CostEstimate(
             flops=2 * rows * width * (2 * channels + BLOCK + LANES),
             bytes_accessed=2 * width * (rows + 2 * channels + BLOCK),
             transcendentals=0,
         ),
-        name="raw",
-    )(*in_hbm(tokens, w_bc, w_step, w_in, w_gate))
-
-
-def steps_kernel(raw_step, step_bias, decay_log, cum_out, dt_out, lead_out, *later):
-    rows = raw_step.shape[0]
-    heads = step_bias.shape[1]
-    v = raw_step[:, :heads] + step_bias[...]
-    dt = jnp.maximum(v, 0.0) + jnp.log1p(jnp.exp(-jnp.abs(v)))
-    log_decay = -jnp.exp(decay_log[...]) * dt
-    cum_out[...] = jnp.zeros_like(cum_out)
-    dt_out[...] = jnp.zeros_like(dt_out)
-    lead_out[...] = jnp.zeros_like(lead_out)
-    dt_out[:, :heads] = dt
-    row = lax.broadcasted_iota(jnp.int32, (SPAN, SPAN), 0)
-    col = lax.broadcasted_iota(jnp.int32, (SPAN, SPAN), 1)
-    lower = (row >= col).astype(F32)
-    lead = jnp.zeros((1, heads), F32)
-    for s in range(rows // SPAN):
-        at = slice(s * SPAN, (s + 1) * SPAN)
-        cum = jnp.dot(
-            lower, log_decay[at], preferred_element_type=F32, precision=lax.Precision.HIGHEST
-        )
-        cum_out[at, :heads] = cum
-        lead_out[at, :heads] = jnp.exp(cum + lead)
-        lead = lead + cum[SPAN - 1 :, :]
-    for out, value in zip(later, (cum_out, dt_out, lead_out)):
-        out[...] = value[...]
-
-
-def steps(raw_step, step_bias, decay_log):
-    vmem = pl.BlockSpec(memory_space=pltpu.VMEM)
-    return pl.pallas_call(
-        steps_kernel,
-        in_specs=[vmem] * 3,
-        out_specs=[vmem] * 6,
-        out_shape=[jax.ShapeDtypeStruct(raw_step.shape, F32)] * 3
-        + [pltpu.HBM(raw_step.shape, F32)] * 3,
-        compiler_params=pltpu.CompilerParams(vmem_limit_bytes=SMALL_LIMIT),
-        cost_estimate=pl.CostEstimate(flops=10**9, bytes_accessed=10**6, transcendentals=0),
-        name="steps",
-    )(raw_step, step_bias, decay_log)
-
-
-def front_kernel(
-    raw_in, raw_bc, edge, cum_ref, dt_ref, lead_ref, taps, offset, taps_bc, offset_bc,
-    x_out, bc_out, read_out, local_out, prior_out, decay_out,
-    padded, end_w, span_d, write_t,
-):
-    step = pl.program_id(0)
-    rows = raw_in.shape[0]
-    spans = rows // SPAN
-    per = BLOCK // HEADDIM
-    groups = end_w.shape[0]
-
-    def conv(raw, tap, off):
-        padded[EDGE:, :] = raw[...].astype(F32)
-        padded[:EDGE, :] = edge[...].astype(F32)
-        total = off + tap[0:1, :] * padded[EDGE - 3 : EDGE - 3 + rows, :]
-        for k in range(1, KERNEL):
-            total = total + tap[k : k + 1, :] * padded[EDGE - 3 + k : EDGE - 3 + k + rows, :]
-        return silu(total).astype(BF16)
-
-    @pl.when(step == 0)
-    def _():
-        bc = conv(raw_bc, taps_bc, offset_bc[...])
-        bc_out[...] = bc
-        read_out[...] = bc[:, STATE:]
-        for s in range(spans):
-            block = bc[s * SPAN : (s + 1) * SPAN, :STATE].astype(F32)
-            write_t[s] = jnp.transpose(block).astype(BF16)
-        for s in range(spans):
-            at = slice(s * SPAN, (s + 1) * SPAN)
-            cum = cum_ref[at, :]
-            last = cum[SPAN - 1 :, :]
-            ends = jnp.exp(last - cum) * dt_ref[at, :]
-            gone = jnp.exp(last)
-            for g in range(groups):
-                end_w[g, at, :per] = ends[:, g * per : (g + 1) * per]
-                span_d[g, s : s + 1, :per] = gone[:, g * per : (g + 1) * per]
-        for g in range(groups):
-            span_d[g, spans : spans + 1, :per] = lead_ref[rows - 1 :, g * per : (g + 1) * per]
-
-    @pl.when(step > 0)
-    def _():
-        g = step - 1
-        x = conv(raw_in, taps, offset[...])
-        x_out[...] = x
-        ends = end_w[g]
-        gone = span_d[g]
-        wide = jnp.concatenate(
-            [lane_pair(ends[:, t : t + 1], ends[:, t + 1 : t + 2]) for t in range(0, per, 2)], axis=1
-        )
-        gone_wide = jnp.concatenate(
-            [lane_pair(gone[:, t : t + 1], gone[:, t + 1 : t + 2]) for t in range(0, per, 2)], axis=1
-        )
-        weighted = (x.astype(F32) * wide).astype(BF16)
-        running = jnp.zeros((STATE, BLOCK), F32)
-        tiles = BLOCK // LANES
-        for s in range(spans):
-            if s > 0:
-                for t in range(tiles):
-                    prior_out[s - 1, t] = running[:, t * LANES : (t + 1) * LANES].astype(BF16)
-            local = dot(write_t[s], weighted[s * SPAN : (s + 1) * SPAN])
-            running = gone_wide[s : s + 1] * running + local
-        for t in range(tiles):
-            local_out[t] = running[:, t * LANES : (t + 1) * LANES].astype(BF16)
-            decay_out[t] = jnp.broadcast_to(
-                gone_wide[spans : spans + 1, t * LANES : (t + 1) * LANES], (8, LANES)
-            )
-
-
-def front(raw_in, raw_bc, edge, cum, dt, lead, taps, offset, taps_bc, offset_bc):
-    rows, channels = raw_in.shape
-    groups = channels // BLOCK
-    spans = rows // SPAN
-    tiles = channels // LANES
-    per_block = BLOCK // LANES
-
-    def whole(a):
-        return pl.BlockSpec(a.shape, lambda i: (0,) * a.ndim)
-
-    def late(shape, dim):
-        return pl.BlockSpec(
-            shape,
-            lambda i: tuple(jnp.maximum(i - 1, 0) if d == dim else 0 for d in range(len(shape))),
-        )
-
-    return pl.pallas_call(
-        front_kernel,
-        grid=(groups + 1,),
-        in_specs=[
-            late((rows, BLOCK), 1), whole(raw_bc),
-            pl.BlockSpec((EDGE, BLOCK), lambda i: (0, i)),
-            whole(cum), whole(dt), whole(lead),
-            late((KERNEL, BLOCK), 1), late((1, BLOCK), 1),
-            whole(taps_bc), whole(offset_bc),
-        ],
-        out_specs=[
-            late((rows, BLOCK), 1),
-            pl.BlockSpec((rows, 2 * STATE), lambda i: (0, 0)),
-            pl.BlockSpec((rows, STATE), lambda i: (0, 0)),
-            late((per_block, STATE, LANES), 0),
-            late((spans - 1, per_block, STATE, LANES), 1),
-            late((per_block, 8, LANES), 0),
-        ],
-        out_shape=[
-            pltpu.HBM((rows, channels), BF16),
-            pltpu.HBM((rows, 2 * STATE), BF16),
-            pltpu.HBM((rows, STATE), BF16),
-            jax.ShapeDtypeStruct((tiles, STATE, LANES), BF16),
-            pltpu.HBM((spans - 1, tiles, STATE, LANES), BF16),
-            jax.ShapeDtypeStruct((tiles, 8, LANES), F32),
-        ],
-        scratch_shapes=[
-            pltpu.VMEM((rows + EDGE, BLOCK), F32),
-            pltpu.VMEM((groups, rows, LANES), F32),
-            pltpu.VMEM((groups, 8, LANES), F32),
-            pltpu.VMEM((spans, STATE, SPAN), BF16),
-        ],
-        compiler_params=pltpu.CompilerParams(vmem_limit_bytes=FRONT_LIMIT),
-        cost_estimate=pl.CostEstimate(
-            flops=2 * rows * 2560 * channels,
-            bytes_accessed=4 * rows * channels,
-            transcendentals=rows * channels,
-        ),
-        name="front",
-    )(*in_hbm(raw_in), raw_bc, edge, cum, dt, lead, taps, offset, taps_bc, offset_bc)
+        name="first",
+    )(edge, *in_hbm(tokens, w_bc, w_step, w_in, w_gate, *small))
 
 
 def inside_kernel(first, x_ref, bc_ref, cum_ref, dt_ref, prior_ref, skip_ref, out_ref):
@@ -702,21 +643,17 @@
     rows = tokens.shape[0]
     spans = rows // SPAN
     devices = lax.axis_size(SEQ)
-    raw_in, raw_bc, raw_step, edge, gate = raw_projections(
-        tokens, proj_bc, proj_step.T, proj_inner, proj_gate
-    )
-    edge = lax.ppermute(edge, SEQ, [(i, i + 1) for i in range(devices - 1)])
-    cum, dt, lead, *later = steps(raw_step, step_bias[None], decay_log[None])
-    x, bc, read, local, prior, decay = front(
-        raw_in, raw_bc, edge, cum, dt, lead, conv_inner, offset_inner[None],
-        conv_bc, offset_bc[None],
+    edge = lax.ppermute(tokens[rows - EDGE :], SEQ, [(i, i + 1) for i in range(devices - 1)])
+    x, bc, read, cum, dt, lead, prior, gate, local, decay = first_part(
+        edge, tokens, proj_bc, proj_step.T, proj_inner, proj_gate, conv_inner, offset_inner[None],
+        conv_bc, offset_bc[None], step_bias[None], decay_log[None],
     )
     state = incoming_state(local, decay[:, 0])
     skip = jnp.repeat(skip_gain, HEADDIM)[None]
     inner = []
     for part in range(2):
         half = spans // 2
-        inner.append(inside(part * half, half, x, bc, *later[:2], prior, skip))
+        inner.append(inside(part * half, half, x, bc, cum, dt, prior, skip))
 
     head = lax.axis_index("head")
     size = lax.axis_size("head")
@@ -725,7 +662,7 @@
         return jnp.stack([(head + k) & (size - 1) for k in which]).astype(jnp.int32)
 
     norm = norm_weight[None]
-    sources = (read, later[2], *inner, gate)
+    sources = (read, lead, *inner, gate)
     *far_rows, far_weight = ready(order(2), *sources, out_weight)
 
     def moved(value, distance):

time: 104 us -> 99.9 us (0.961)
  Pallas kernels: 48.1 us -> 41.8 us
  local copies, waits for them, and re-layouts: 0.25 us -> 2.4 us
    pallas_call x3 -> x1, Pallas kernels: 23.5 us -> 17.1 us  [first_part(): pl.pallas_call(first_kernel, in_specs=[vmem] + [hbm] * (5 + len(small)),...]
    broadcast_in_dim x1, local copies, waits for them, and re-layouts: 0.01 us -> 1.3 us  [per_device(): offset_inner[None]]
  transfers between devices with their start and end apart: 18 -> 18, of which waited for: 13 -> 13; matrix products, arithmetic and copies ran while one was open for 0% -> 2% of each run, Pallas kernels for 23% -> 22%
where the time goes in v6:
time: 99.9 us; the launch traced here: 99.6 us
  Pallas kernels  41.8 us (42%)
  starting transfers between devices  28 us (28%)
  waiting for transfers between devices  26 us (26%)
  local copies, waits for them, and re-layouts  2.4 us (2%)
  other arithmetic  1.01 us (1%)
    ppermute x17, starting transfers between devices, ring(): lax.ppermute(value, axis, [(i, (i + distance) % size) for i in range(size)])  26.8 us
    ppermute x17, waiting for transfers between devices, ring(): lax.ppermute(value, axis, [(i, (i + distance) % size) for i in range(size)])  26 us
    pallas_call x1, Pallas kernels, first_part(): pl.pallas_call(first_kernel, in_specs=[vmem] + [hbm] * (5 + len(small)),...  17.1 us
    pallas_call x3, Pallas kernels, tail(): pl.pallas_call(functools.partial(tail_kernel, HEADS * HEADDIM, which is N...  12.1 us
    pallas_call x2, Pallas kernels, inside(): pl.pallas_call(functools.partial(inside_kernel, first), grid=(count,), in...  8.05 us
    pallas_call x1, Pallas kernels, ready(): pl.pallas_call(ready_kernel, in_specs=[pl.BlockSpec(memory_space=pltpu.SM...  3.14 us
  transfers between devices with their start and end apart: 18, of which 13 were waited for; matrix products, arithmetic and copies ran while one was open for 2% of the time, Pallas kernels for 22%

profile of v6, /device:TPU:0, one launch (start us, length us, event | category | flops | bytes accessed | tf_op | source)
XLA Modules:
  0.0 99.6 jit_solution(12311587917829407858)
XLA Ops:
  0.0 0.9 slice.99
  0.9 1.3 %collective-permute-start = (bf16[16,2560]{1,0:T(8,128)(2,1)S(1)}, bf16[16,2560]{1,0:T(8,128)(2,1)S(1)}, u32[]{:S(2)}, u32[]{:S(2)}) collective-permute-start(bf16[16,2560]{1,0:T(8,128)(2,1)S(1)} %slice.99), channel_id=1, source_target_pairs={{0,4},{4,8},{8,12},{12,16},{16,20},{20,24},{24,28},{28,32},{32,36}... | collective-permute-start | bytes 245768 | tf_op jit(solution)/shard_map/ppermute | solution.py:646
  2.2 1.3 %broadcast_in_dim.31.s1 = f32[1,1280]{1,0:T(1,128)} reshape(f32[1280]{0:T(1024)} %param.21) | data formatting | bytes 10240 | tf_op jit(solution)/shard_map/broadcast_in_dim | solution.py:648
  3.5 17.1 %first.1 = (bf16[512,1280]{1,0:T(8,128)(2,1)}, bf16[512,256]{1,0:T(8,128)(2,1)}, bf16[512,128]{1,0:T(8,128)(2,1)}, f32[512,128]{1,0:T(8,128)}, f32[512,128]{1,0:...) custom-call(bf16[16,2560]{1,0:T(8,128)(2,1)S(1)} %collective-permute, ...), custom_call_target="tpu_custom_call" | custom-call | flops 7717519360 | bytes 17039360 | tf_op jit(solution)/shard_map/first/pallas_call | solution.py:207
  20.7 2.7 %collective-permute-start.1 = (bf16[656,128]{1,0:T(8,128)(2,1)S(1)}, bf16[656,128]{1,0:T(8,128)(2,1)S(1)}, u32[]{:S(2)}, u32[]{:S(2)}) collective-permute-start(bf16[656,128]{1,0:T(8,128)(2,1)S(1)} %pad_maximum_fusion.1), channel_id=1, source_target_pairs={{0,4},{4,0},{1,5},{5,1},{2,6},{6,2},{3,7},{7,3},{8,12},{12,8},{9,1... | collective-permute-start | bytes 503816 | tf_op jit(solution)/shard_map/ppermute | solution.py:548
  23.4 1.0 %collective-permute-done.1 = bf16[656,128]{1,0:T(8,128)(2,1)S(1)} collective-permute-done((bf16[656,128]{1,0:T(8,128)(2,1)S(1)}, bf16[656,128]{1,0:T(8,128)(2,1)S(1)}, u32[]{:S(2)}, u32[]{:S(2)}) %collective-permute-start.1) | collective-permute-done | bytes 167968 | tf_op jit(solution)/shard_map/ppermute | solution.py:548
  24.5 0.1 fusion
  24.7 4.2 %collective-permute-start.2 = (bf16[176,128]{1,0:T(8,128)(2,1)S(1)}, bf16[176,128]{1,0:T(8,128)(2,1)S(1)}, u32[]{:S(2)}, u32[]{:S(2)}) collective-permute-start(bf16[176,128]{1,0:T(8,128)(2,1)S(1)} %get-tuple-element.91), channel_id=1, source_target_pairs={{0,24},{8,0},{16,8},{24,16},{1,25},{9,1},{17,9},{25,17},{2,26},{10... | collective-permute-start | bytes 135176 | tf_op jit(solution)/shard_map/ppermute | solution.py:548
  28.8 0.6 collective-permute-start.3
  29.4 1.0 collective-permute-start.4
  30.4 0.4 collective-permute-done.2
  30.8 3.5 %collective-permute-done.3 = bf16[176,128]{1,0:T(8,128)(2,1)S(1)} collective-permute-done((bf16[176,128]{1,0:T(8,128)(2,1)S(1)}, bf16[176,128]{1,0:T(8,128)(2,1)S(1)}, u32[]{:S(2)}, u32[]{:S(2)}) %collective-permute-start.3) | collective-permute-done | bytes 45088 | tf_op jit(solution)/shard_map/ppermute | solution.py:548
  34.4 0.5 collective-permute-done.4
  34.9 0.1 fusion.2
  35.0 4.1 %collective-permute-start.5 = (bf16[176,128]{1,0:T(8,128)(2,1)S(1)}, bf16[176,128]{1,0:T(8,128)(2,1)S(1)}, u32[]{:S(2)}, u32[]{:S(2)}) collective-permute-start(bf16[176,128]{1,0:T(8,128)(2,1)S(1)} %pad_maximum_fusion.3), channel_id=1, source_target_pairs={{0,96},{32,0},{64,32},{96,64},{1,97},{33,1},{65,33},{97,65},{2,98}... | collective-permute-start | bytes 135176 | tf_op jit(solution)/shard_map/ppermute | solution.py:548
  39.1 1.2 %collective-permute-start.7 = (bf16[176,128]{1,0:T(8,128)(2,1)S(1)}, bf16[176,128]{1,0:T(8,128)(2,1)S(1)}, u32[]{:S(2)}, u32[]{:S(2)}) collective-permute-start(bf16[176,128]{1,0:T(8,128)(2,1)S(1)} %pad_maximum_fusion.3), channel_id=1, source_target_pairs={{0,32},{32,64},{64,96},{96,0},{1,33},{33,65},{65,97},{97,1},{2,34}... | collective-permute-start | bytes 135176 | tf_op jit(solution)/shard_map/ppermute | solution.py:548
  40.4 0.5 collective-permute-done.5
  40.8 3.9 %collective-permute-done.6 = bf16[176,128]{1,0:T(8,128)(2,1)S(1)} collective-permute-done((bf16[176,128]{1,0:T(8,128)(2,1)S(1)}, bf16[176,128]{1,0:T(8,128)(2,1)S(1)}, u32[]{:S(2)}, u32[]{:S(2)}) %collective-permute-start.6) | collective-permute-done | bytes 45088 | tf_op jit(solution)/shard_map/ppermute | solution.py:548
  44.8 0.1 collective-permute-done.7
  44.9 0.1 select_convert_fusion.1
  45.1 1.9 %collective-permute-start.8 = (bf16[5,32,128]{2,1,0:T(8,128)(2,1)S(1)}, bf16[5,32,128]{2,1,0:T(8,128)(2,1)S(1)}, u32[]{:S(2)}, u32[]{:S(2)}) collective-permute-start(bf16[5,32,128]{2,1,0:T(8,128)(2,1)S(1)} %get-tuple-element.76), channel_id=1, source_target_pairs={{0,24},{8,0},{16,8},{24,16},{1,25},{9,1},{17,9},{25,17},{2,26},{10... | collective-permute-start | bytes 122888 | tf_op jit(solution)/shard_map/ppermute | solution.py:548
  47.0 0.9 collective-permute-start.9
  47.9 0.3 collective-permute-start.10
  48.1 1.0 %collective-permute-done.8 = bf16[5,32,128]{2,1,0:T(8,128)(2,1)S(1)} collective-permute-done((bf16[5,32,128]{2,1,0:T(8,128)(2,1)S(1)}, bf16[5,32,128]{2,1,0:T(8,128)(2,1)S(1)}, u32[]{:S(2)}, u32[]{:S(2)}) %collective-permute-start.8) | collective-permute-done | bytes 40992 | tf_op jit(solution)/shard_map/ppermute | solution.py:548
  49.2 3.3 %collective-permute-done.9 = bf16[5,32,128]{2,1,0:T(8,128)(2,1)S(1)} collective-permute-done((bf16[5,32,128]{2,1,0:T(8,128)(2,1)S(1)}, bf16[5,32,128]{2,1,0:T(8,128)(2,1)S(1)}, u32[]{:S(2)}, u32[]{:S(2)}) %collective-permute-start.9) | collective-permute-done | bytes 40992 | tf_op jit(solution)/shard_map/ppermute | solution.py:548
  52.5 0.6 collective-permute-done.10
  53.2 0.1 broadcast_select_fusion.2
  53.3 0.1 collective-permute-start.11
  53.4 0.1 broadcast_in_dim.35
  53.5 0.1 broadcast_in_dim_reshape.3.skip_ref
  53.6 4.0 %inside.3.refs_4_.high_hbm = f32[256,1280]{1,0:T(8,128)} custom-call(bf16[512,1280]{1,0:T(8,128)(2,1)} %get-tuple-element.31.x_ref, bf16[512,256]{1,0:T(8,128)(2,1)} %get-tuple-element.32.bc_ref, f32[512,128]{1,0:T(8,128)} %get-tuple-element.33.cum_ref, f32[512,128]{1,0:T(8,128)} %get-tuple-element.34.dt_ref, ...), custom_call_target="tpu_custom_call" | custom-call | flops 1000000 | bytes 1000000 | tf_op jit(solution)/shard_map/inside/pallas_call | solution.py:274
  57.6 4.0 %inside.2.refs_3_.low_hbm = f32[256,1280]{1,0:T(8,128)} custom-call(bf16[512,1280]{1,0:T(8,128)(2,1)} %get-tuple-element.31.x_ref, bf16[512,256]{1,0:T(8,128)(2,1)} %get-tuple-element.32.bc_ref, f32[512,128]{1,0:T(8,128)} %get-tuple-element.33.cum_ref, f32[512,128]{1,0:T(8,128)} %get-tuple-element.34.dt_ref, ...), custom_call_target="tpu_custom_call" | custom-call | flops 1000000 | bytes 1000000 | tf_op jit(solution)/shard_map/inside/pallas_call | solution.py:274
  61.6 3.1 %ready.1 = (bf16[128,128]{1,0:T(8,128)(2,1)S(1)}, f32[128,128]{1,0:T(8,128)S(1)}, f32[128,1280]{1,0:T(8,128)S(1)}, bf16[128,1280]{1,0:T(8,128)(2,1)S(1)}, bf16[1280,2560]{1,0:T(8,128)(2,1)S(1)}) custom-call(s32[1]{0:T(128)} %bitcast.24.which, bf16[512,128]{1,0:T(8,128)(2,1)} %get-tuple-element.29.refs_1_.read_hbm, ...), custom_call_target="tpu_custom_call" | custom-call | flops 1000000 | bytes 1000000 | tf_op jit(solution)/shard_map/ready/pallas_call | solution.py:366
  64.8 0.2 broadcast_select_fusion.1
  65.0 1.6 %shard_map.138 = (bf16[1296,128]{1,0:T(8,128)(2,1)S(1)}, bf16[1296,128]{1,0:T(8,128)(2,1)S(1)}) custom-call(bf16[128,128]{1,0:T(8,128)(2,1)S(1)} %get-tuple-element.43.refs_0_, f32[128,128]{1,0:T(8,128)S(1)} %get-tuple-element.44.refs_1_, f32[128,1280]{1,0:T(8,128)S(1)} %get-tuple-element.45.refs_2_, bf16[128,1280]{1,0:T(8,128)(2,1)S(1)} %get-tuple-element.46.refs_3_, ...), custom_call_target="tpu_custom_call" | custom-call | flops 1000000 | bytes 1000000 | tf_op jit(solution)/shard_map/pallas_call | solution.py:482
  66.6 2.8 %collective-permute-start.14 = (bf16[1296,128]{1,0:T(8,128)(2,1)S(1)}, bf16[1296,128]{1,0:T(8,128)(2,1)S(1)}, u32[]{:S(2)}, u32[]{:S(2)}) collective-permute-start(bf16[1296,128]{1,0:T(8,128)(2,1)S(1)} %get-tuple-element.50), channel_id=1, source_target_pairs={{0,3},{1,0},{2,1},{3,2},{4,7},{5,4},{6,5},{7,6},{8,11},{9,8},{10,9... | collective-permute-start | bytes 995336 | tf_op jit(solution)/shard_map/ppermute | solution.py:548
  69.4 0.1 pad_add_fusion.refs_0_
  69.5 6.3 %shard_map.137 = (bf16[1296,128]{1,0:T(8,128)(2,1)S(1)}, bf16[1280,128]{1,0:T(8,128)(2,1)S(1)}, bf16[1280,128]{1,0:T(8,128)(2,1)S(1)}, bf16[1296,128]{1,0:T(8,128)(2,1)S(1)}) custom-call(s32[2]{0:T(128)S(1)} %pad_add_fusion.refs_0_, bf16[512,128]{1,0:T(8,128)(2,1)} %get-tuple-element.29.refs_1_.read_hbm, f32[512,128]{1,0:T(8,128)} %get-tuple-element.30.refs_2_.lead_hbm, ...), custom_call_target="tpu_custom_call" | custom-call | flops 1000000 | bytes 1000000 | tf_op jit(solution)/shard_map/pallas_call | solution.py:482
  75.8 1.3 %collective-permute-done.14.b_ref = bf16[1296,128]{1,0:T(8,128)(2,1)S(1)} collective-permute-done((bf16[1296,128]{1,0:T(8,128)(2,1)S(1)}, bf16[1296,128]{1,0:T(8,128)(2,1)S(1)}, u32[]{:S(2)}, u32[]{:S(2)}) %collective-permute-start.14) | collective-permute-done | bytes 331808 | tf_op jit(solution)/shard_map/ppermute | solution.py:548
  77.1 0.1 shard_map.140
  77.2 3.8 %collective-permute-start.15 = (bf16[1296,128]{1,0:T(8,128)(2,1)S(1)}, bf16[1296,128]{1,0:T(8,128)(2,1)S(1)}, u32[]{:S(2)}, u32[]{:S(2)}) collective-permute-start(bf16[1296,128]{1,0:T(8,128)(2,1)S(1)} %shard_map.140), channel_id=1, source_target_pairs={{0,3},{1,0},{2,1},{3,2},{4,7},{5,4},{6,5},{7,6},{8,11},{9,8},{10,9... | collective-permute-start | bytes 995336 | tf_op jit(solution)/shard_map/ppermute | solution.py:548
  81.0 0.1 shard_map.139
  81.1 0.1 collective-permute-start.13
  81.1 3.2 %collective-permute-start.16 = (bf16[1280,128]{1,0:T(8,128)(2,1)S(1)}, bf16[1280,128]{1,0:T(8,128)(2,1)S(1)}, u32[]{:S(2)}, u32[]{:S(2)}) collective-permute-start(bf16[1280,128]{1,0:T(8,128)(2,1)S(1)} %get-tuple-element.51), channel_id=1, source_target_pairs={{0,3},{1,0},{2,1},{3,2},{4,7},{5,4},{6,5},{7,6},{8,11},{9,8},{10,9... | collective-permute-start | bytes 983048 | tf_op jit(solution)/shard_map/ppermute | solution.py:548
  84.4 4.2 %shard_map.136 = (bf16[1280,128]{1,0:T(8,128)(2,1)S(1)}, bf16[1280,128]{1,0:T(8,128)(2,1)S(1)}, f32[8,128]{1,0:T(8,128)S(1)}) custom-call(s32[1]{0:T(128)} %bitcast.refs_0_, bf16[512,128]{1,0:T(8,128)(2,1)} %get-tuple-element.29.refs_1_.read_hbm, f32[512,128]{1,0:T(8,128)} %get-tuple-element.30.refs_2_.lead_hbm, f32[256,1280]{1,0:T(8,128)} %inside.2.refs_3_.low_hbm, ...), custom_call_target="tpu_custom_call" | custom-call | flops 1000000 | bytes 1000000 | tf_op jit(solution)/shard_map/pallas_call | solution.py:482
  88.6 6.2 %collective-permute-done.16.direct_l = bf16[1280,128]{1,0:T(8,128)(2,1)S(1)} collective-permute-done((bf16[1280,128]{1,0:T(8,128)(2,1)S(1)}, bf16[1280,128]{1,0:T(8,128)(2,1)S(1)}, u32[]{:S(2)}, u32[]{:S(2)}) %collective-permute-start.16) | collective-permute-done | bytes 327712 | tf_op jit(solution)/shard_map/ppermute | solution.py:548
  94.8 3.6 %collective-permute-done.17.direct_r = bf16[1280,128]{1,0:T(8,128)(2,1)S(1)} collective-permute-done((bf16[1280,128]{1,0:T(8,128)(2,1)S(1)}, bf16[1280,128]{1,0:T(8,128)(2,1)S(1)}, u32[]{:S(2)}, u32[]{:S(2)}) %collective-permute-start.17) | collective-permute-done | bytes 327712 | tf_op jit(solution)/shard_map/ppermute | solution.py:548
  98.4 1.2 %final.1 = bf16[128,2560]{1,0:T(8,128)(2,1)} custom-call(bf16[1280,128]{1,0:T(8,128)(2,1)S(1)} %get-tuple-element.39.own_l, bf16[1280,128]{1,0:T(8,128)(2,1)S(1)} %get-tuple-element.40.own_r, f32[8,128]{1,0:T(8,128)S(1)} %get-tuple-element.41.own_sq, bf16[1296,128]{1,0:T(8,128)(2,1)S(1)} %collective-permute-done.13.up, ...), custom_call_target="tpu_custom_call" | custom-call | flops 1000000 | bytes 1000000 | tf_op jit(solution)/shard_map/final/pallas_call | solution.py:535
  (40 shorter events, 0.5 us)
Async XLA Ops:
  0.9 2.6 %collective-permute-start = (bf16[16,2560]{1,0:T(8,128)(2,1)S(1)}, bf16[16,2560]{1,0:T(8,128)(2,1)S(1)}, u32[]{:S(2)}, u32[]{:S(2)}) collective-permute-start(bf16[16,2560]{1,0:T(8,128)(2,1)S(1)} %slice.99), channel_id=1, source_target_pairs={{0,4},{4,8},{8,12},{12,16},{16,20},{20,24},{24,28},{28,32},{32,36}... | collective-permute-start | bytes 245768 | tf_op jit(solution)/shard_map/ppermute | solution.py:646
  20.7 3.7 %collective-permute-start.1 = (bf16[656,128]{1,0:T(8,128)(2,1)S(1)}, bf16[656,128]{1,0:T(8,128)(2,1)S(1)}, u32[]{:S(2)}, u32[]{:S(2)}) collective-permute-start(bf16[656,128]{1,0:T(8,128)(2,1)S(1)} %pad_maximum_fusion.1), channel_id=1, source_target_pairs={{0,4},{4,0},{1,5},{5,1},{2,6},{6,2},{3,7},{7,3},{8,12},{12,8},{9,1... | collective-permute-start | bytes 503816 | tf_op jit(solution)/shard_map/ppermute | solution.py:548
  24.6 28.8 %copy-start.1 = (f32[20]{0:T(128)S(1)}, f32[20]{0:T(128)}, u32[]{:S(2)}) copy-start(f32[20]{0:T(128)} %param.25) | copy-start | bytes 244
  24.6 29.0 %copy-start = (f32[1280]{0:T(1024)S(1)}, f32[1280]{0:T(1024)}, u32[]{:S(2)}) copy-start(f32[1280]{0:T(1024)} %param.26) | copy-start | bytes 15364
  24.7 6.2 %collective-permute-start.2 = (bf16[176,128]{1,0:T(8,128)(2,1)S(1)}, bf16[176,128]{1,0:T(8,128)(2,1)S(1)}, u32[]{:S(2)}, u32[]{:S(2)}) collective-permute-start(bf16[176,128]{1,0:T(8,128)(2,1)S(1)} %get-tuple-element.91), channel_id=1, source_target_pairs={{0,24},{8,0},{16,8},{24,16},{1,25},{9,1},{17,9},{25,17},{2,26},{10... | collective-permute-start | bytes 135176 | tf_op jit(solution)/shard_map/ppermute | solution.py:548
  28.8 5.6 %collective-permute-start.3 = (bf16[176,128]{1,0:T(8,128)(2,1)S(1)}, bf16[176,128]{1,0:T(8,128)(2,1)S(1)}, u32[]{:S(2)}, u32[]{:S(2)}) collective-permute-start(bf16[176,128]{1,0:T(8,128)(2,1)S(1)} %get-tuple-element.90), channel_id=1, source_target_pairs={{0,16},{8,24},{16,0},{24,8},{1,17},{9,25},{17,1},{25,9},{2,18},{10... | collective-permute-start | bytes 135176 | tf_op jit(solution)/shard_map/ppermute | solution.py:548
  29.4 5.4 %collective-permute-start.4 = (bf16[176,128]{1,0:T(8,128)(2,1)S(1)}, bf16[176,128]{1,0:T(8,128)(2,1)S(1)}, u32[]{:S(2)}, u32[]{:S(2)}) collective-permute-start(bf16[176,128]{1,0:T(8,128)(2,1)S(1)} %get-tuple-element.89), channel_id=1, source_target_pairs={{0,8},{8,16},{16,24},{24,0},{1,9},{9,17},{17,25},{25,1},{2,10},{10... | collective-permute-start | bytes 135176 | tf_op jit(solution)/shard_map/ppermute | solution.py:548
  35.0 5.8 %collective-permute-start.5 = (bf16[176,128]{1,0:T(8,128)(2,1)S(1)}, bf16[176,128]{1,0:T(8,128)(2,1)S(1)}, u32[]{:S(2)}, u32[]{:S(2)}) collective-permute-start(bf16[176,128]{1,0:T(8,128)(2,1)S(1)} %pad_maximum_fusion.3), channel_id=1, source_target_pairs={{0,96},{32,0},{64,32},{96,64},{1,97},{33,1},{65,33},{97,65},{2,98}... | collective-permute-start | bytes 135176 | tf_op jit(solution)/shard_map/ppermute | solution.py:548
  39.1 5.6 %collective-permute-start.6 = (bf16[176,128]{1,0:T(8,128)(2,1)S(1)}, bf16[176,128]{1,0:T(8,128)(2,1)S(1)}, u32[]{:S(2)}, u32[]{:S(2)}) collective-permute-start(bf16[176,128]{1,0:T(8,128)(2,1)S(1)} %pad_maximum_fusion.3), channel_id=1, source_target_pairs={{0,64},{32,96},{64,0},{96,32},{1,65},{33,97},{65,1},{97,33},{2,66}... | collective-permute-start | bytes 135176 | tf_op jit(solution)/shard_map/ppermute | solution.py:548
  39.1 5.7 %collective-permute-start.7 = (bf16[176,128]{1,0:T(8,128)(2,1)S(1)}, bf16[176,128]{1,0:T(8,128)(2,1)S(1)}, u32[]{:S(2)}, u32[]{:S(2)}) collective-permute-start(bf16[176,128]{1,0:T(8,128)(2,1)S(1)} %pad_maximum_fusion.3), channel_id=1, source_target_pairs={{0,32},{32,64},{64,96},{96,0},{1,33},{33,65},{65,97},{97,1},{2,34}... | collective-permute-start | bytes 135176 | tf_op jit(solution)/shard_map/ppermute | solution.py:548
  45.1 4.1 %collective-permute-start.8 = (bf16[5,32,128]{2,1,0:T(8,128)(2,1)S(1)}, bf16[5,32,128]{2,1,0:T(8,128)(2,1)S(1)}, u32[]{:S(2)}, u32[]{:S(2)}) collective-permute-start(bf16[5,32,128]{2,1,0:T(8,128)(2,1)S(1)} %get-tuple-element.76), channel_id=1, source_target_pairs={{0,24},{8,0},{16,8},{24,16},{1,25},{9,1},{17,9},{25,17},{2,26},{10... | collective-permute-start | bytes 122888 | tf_op jit(solution)/shard_map/ppermute | solution.py:548
  47.0 5.5 %collective-permute-start.9 = (bf16[5,32,128]{2,1,0:T(8,128)(2,1)S(1)}, bf16[5,32,128]{2,1,0:T(8,128)(2,1)S(1)}, u32[]{:S(2)}, u32[]{:S(2)}) collective-permute-start(bf16[5,32,128]{2,1,0:T(8,128)(2,1)S(1)} %get-tuple-element.75), channel_id=1, source_target_pairs={{0,16},{8,24},{16,0},{24,8},{1,17},{9,25},{17,1},{25,9},{2,18},{10... | collective-permute-start | bytes 122888 | tf_op jit(solution)/shard_map/ppermute | solution.py:548
  47.9 5.2 %collective-permute-start.10 = (bf16[5,32,128]{2,1,0:T(8,128)(2,1)S(1)}, bf16[5,32,128]{2,1,0:T(8,128)(2,1)S(1)}, u32[]{:S(2)}, u32[]{:S(2)}) collective-permute-start(bf16[5,32,128]{2,1,0:T(8,128)(2,1)S(1)} %get-tuple-element.57), channel_id=1, source_target_pairs={{0,8},{8,16},{16,24},{24,0},{1,9},{9,17},{17,25},{25,1},{2,10},{10... | collective-permute-start | bytes 122888 | tf_op jit(solution)/shard_map/ppermute | solution.py:548
  53.3 11.5 %collective-permute-start.11 = (bf16[5,128,128]{2,1,0:T(8,128)(2,1)S(1)}, bf16[5,128,128]{2,1,0:T(8,128)(2,1)S(1)}, u32[]{:S(2)}, u32[]{:S(2)}) collective-permute-start(bf16[5,128,128]{2,1,0:T(8,128)(2,1)S(1)} %broadcast_select_fusion.2), channel_id=1, source_target_pairs={{0,4},{4,0},{1,5},{5,1},{2,6},{6,2},{3,7},{7,3},{8,12},{12,8},{9,1... | collective-permute-start | bytes 491528 | tf_op jit(solution)/shard_map/ppermute | solution.py:548
  66.6 10.5 %collective-permute-start.14 = (bf16[1296,128]{1,0:T(8,128)(2,1)S(1)}, bf16[1296,128]{1,0:T(8,128)(2,1)S(1)}, u32[]{:S(2)}, u32[]{:S(2)}) collective-permute-start(bf16[1296,128]{1,0:T(8,128)(2,1)S(1)} %get-tuple-element.50), channel_id=1, source_target_pairs={{0,3},{1,0},{2,1},{3,2},{4,7},{5,4},{6,5},{7,6},{8,11},{9,8},{10,9... | collective-permute-start | bytes 995336 | tf_op jit(solution)/shard_map/ppermute | solution.py:548
  69.4 11.6 %collective-permute-start.12 = (bf16[1296,128]{1,0:T(8,128)(2,1)S(1)}, bf16[1296,128]{1,0:T(8,128)(2,1)S(1)}, u32[]{:S(2)}, u32[]{:S(2)}) collective-permute-start(bf16[1296,128]{1,0:T(8,128)(2,1)S(1)} %get-tuple-element.48), channel_id=1, source_target_pairs={{0,1},{1,2},{2,3},{3,0},{4,5},{5,6},{6,7},{7,4},{8,9},{9,10},{10,1... | collective-permute-start | bytes 995336 | tf_op jit(solution)/shard_map/ppermute | solution.py:548
  77.2 21.2 %collective-permute-start.15 = (bf16[1296,128]{1,0:T(8,128)(2,1)S(1)}, bf16[1296,128]{1,0:T(8,128)(2,1)S(1)}, u32[]{:S(2)}, u32[]{:S(2)}) collective-permute-start(bf16[1296,128]{1,0:T(8,128)(2,1)S(1)} %shard_map.140), channel_id=1, source_target_pairs={{0,3},{1,0},{2,1},{3,2},{4,7},{5,4},{6,5},{7,6},{8,11},{9,8},{10,9... | collective-permute-start | bytes 995336 | tf_op jit(solution)/shard_map/ppermute | solution.py:548
  81.1 17.4 %collective-permute-start.13 = (bf16[1296,128]{1,0:T(8,128)(2,1)S(1)}, bf16[1296,128]{1,0:T(8,128)(2,1)S(1)}, u32[]{:S(2)}, u32[]{:S(2)}) collective-permute-start(bf16[1296,128]{1,0:T(8,128)(2,1)S(1)} %shard_map.139), channel_id=1, source_target_pairs={{0,1},{1,2},{2,3},{3,0},{4,5},{5,6},{6,7},{7,4},{8,9},{9,10},{10,1... | collective-permute-start | bytes 995336 | tf_op jit(solution)/shard_map/ppermute | solution.py:548
  81.1 13.7 %collective-permute-start.16 = (bf16[1280,128]{1,0:T(8,128)(2,1)S(1)}, bf16[1280,128]{1,0:T(8,128)(2,1)S(1)}, u32[]{:S(2)}, u32[]{:S(2)}) collective-permute-start(bf16[1280,128]{1,0:T(8,128)(2,1)S(1)} %get-tuple-element.51), channel_id=1, source_target_pairs={{0,3},{1,0},{2,1},{3,2},{4,7},{5,4},{6,5},{7,6},{8,11},{9,8},{10,9... | collective-permute-start | bytes 983048 | tf_op jit(solution)/shard_map/ppermute | solution.py:548
  84.4 14.0 %collective-permute-start.17 = (bf16[1280,128]{1,0:T(8,128)(2,1)S(1)}, bf16[1280,128]{1,0:T(8,128)(2,1)S(1)}, u32[]{:S(2)}, u32[]{:S(2)}) collective-permute-start(bf16[1280,128]{1,0:T(8,128)(2,1)S(1)} %get-tuple-element.52), channel_id=1, source_target_pairs={{0,1},{1,2},{2,3},{3,0},{4,5},{5,6},{6,7},{7,4},{8,9},{9,10},{10,1... | collective-permute-start | bytes 983048 | tf_op jit(solution)/shard_map/ppermute | solution.py:548

commit v7 on v6

--- a/solution.py
+++ b/solution.py
@@ -16,6 +16,8 @@
 SPAN = 128
 LANES = 128
 EDGE = 16
+CHUNKS = 4
+PIECES = 4
 BLOCK = 256
 SEQ = ("seq_0", "seq_1", "seq_2")
 SEQ_HEAD = ("seq_0", "seq_1", "seq_2", "head")
@@ -53,7 +55,7 @@
     x_hbm, maps_hbm, read_hbm, cum_hbm, dt_hbm, lead_hbm, prior_hbm, gate_out, local_out, decay_out,
     tok, w_bc, w_step, w_in, w_gate, padded, padded_bc,
     x_ref, maps_ref, read_ref, cum_ref, dt_ref, lead_ref, prior_ref, gate_ref,
-    taps, offset, taps_bc, offset_bc, step_bias, decay_log, sems,
+    taps, taps_bc, offset_bc, step_bias, decay_log, sems,
 ):
     rows = x_ref.shape[0]
     above = edge.shape[0]
@@ -63,22 +65,45 @@
     per = BLOCK // HEADDIM
     tiles = BLOCK // LANES
 
+    width = tok.shape[1]
+    chunk = width // CHUNKS
+    pairs = []
+    for k in range(CHUNKS):
+        at = slice(k * chunk, (k + 1) * chunk)
+        pairs.append(
+            [
+                pltpu.make_async_copy(
+                    tok_hbm.at[:, at], tok.at[pl.ds(above, rows), at], sems.at[20 + 2 * k]
+                ),
+                pltpu.make_async_copy(in_hbm.at[at, :], w_in.at[at, :], sems.at[21 + 2 * k]),
+            ]
+        )
+    offset = s1
+    small = (taps, offset, taps_bc, offset_bc, step_bias, decay_log)
     first = [
-        pltpu.make_async_copy(tok_hbm, tok.at[pl.ds(above, rows), :], sems.at[0]),
         pltpu.make_async_copy(bc_hbm, w_bc, sems.at[1]),
         pltpu.make_async_copy(step_hbm, w_step, sems.at[2]),
     ]
-    inner_copy = pltpu.make_async_copy(in_hbm, w_in, sems.at[3])
+    for k, (source, target) in enumerate(zip((s0, s1, s2, s3, s4, s5), small)):
+        if k != 1:
+            first.append(pltpu.make_async_copy(source, target, sems.at[14 + k]))
     gate_copy = pltpu.make_async_copy(gate_hbm, w_gate, sems.at[4])
-    small = (taps, offset, taps_bc, offset_bc, step_bias, decay_log)
-    for k, (source, target) in enumerate(zip((s0, s1, s2, s3, s4, s5), small)):
-        first.append(pltpu.make_async_copy(source, target, sems.at[14 + k]))
-    for copy in first:
-        copy.start()
+    for k in range(2):
+        for copy in pairs[k]:
+            copy.start()
     tok[:above, :] = edge[...]
+    for k in range(CHUNKS):
+        for copy in pairs[k]:
+            copy.wait()
+        for copy in pairs[k + 2] if k + 2 < CHUNKS else first if k + 2 == CHUNKS else [gate_copy]:
+            copy.start()
+        at = slice(k * chunk, (k + 1) * chunk)
+        part = dot(tok[:, at], w_in[at, :])
+        if k > 0:
+            part = padded[...] + part
+        padded[...] = part if k + 1 < CHUNKS else part.astype(BF16).astype(F32)
     for copy in first:
         copy.wait()
-    inner_copy.start()
 
     def conv(source, at, tap, off):
         total = off
@@ -91,9 +116,6 @@
     steps = lax.dot_general(
         tok[above:, :], w_step[...], (((1,), (1,)), ((), ())), preferred_element_type=F32
     )
-    inner_copy.wait()
-    gate_copy.start()
-    padded[...] = dot(tok[...], w_in[...]).astype(BF16).astype(F32)
 
     maps = conv(padded_bc, slice(0, 2 * STATE), taps_bc, offset_bc[...])
     maps_ref[...] = maps
@@ -206,7 +228,7 @@
     ]
     return pl.pallas_call(
         first_kernel,
-        in_specs=[vmem] + [hbm] * (5 + len(small)),
+        in_specs=[vmem] + [hbm] * 6 + [vmem] + [hbm] * 4,
         out_specs=[hbm] * len(kept) + [vmem] * 2,
         out_shape=[pltpu.HBM(*a) for a in kept]
         + [
@@ -222,8 +244,8 @@
             pltpu.VMEM((above + rows, channels), F32),
             pltpu.VMEM((above + rows, 2 * STATE), F32),
             *[pltpu.VMEM(*a) for a in kept],
-            *[pltpu.VMEM(a.shape, F32) for a in small],
-            pltpu.SemaphoreType.DMA((20,)),
+            *[pltpu.VMEM(a.shape, F32) for k, a in enumerate(small) if k != 1],
+            pltpu.SemaphoreType.DMA((20 + 2 * CHUNKS,)),
         ],
         compiler_params=pltpu.CompilerParams(vmem_limit_bytes=FIRST_LIMIT),
         cost_estimate=pl.CostEstimate(
@@ -232,7 +254,7 @@
             transcendentals=0,
         ),
         name="first",
-    )(edge, *in_hbm(tokens, w_bc, w_step, w_in, w_gate, *small))
+    )(edge, *in_hbm(tokens, w_bc, w_step, w_in, w_gate, small[0]), small[1], *in_hbm(*small[2:]))
 
 
 def inside_kernel(first, x_ref, bc_ref, cum_ref, dt_ref, prior_ref, skip_ref, out_ref):
@@ -399,10 +421,11 @@
             start_local(which[i], local)
             waits.append(copies + local[:1])
         weights = []
-        for side in range(2):
-            at = slice(side * w_hbm.shape[1] // 2, (side + 1) * w_hbm.shape[1] // 2)
+        piece = w_hbm.shape[1] // PIECES
+        for k in range(PIECES):
+            at = slice(k * piece, (k + 1) * piece)
             weights.append(
-                pltpu.make_async_copy(w_hbm.at[:, at], w_ref.at[:, at], w_sems.at[side])
+                pltpu.make_async_copy(w_hbm.at[:, at], w_ref.at[:, at], w_sems.at[k])
             )
         weights[0].start()
     channels = local_ref.shape[1]
@@ -415,8 +438,10 @@
         if not has_rows:
             for copy in waits[i]:
                 copy.wait()
+            if i == 0:
+                weights[1].start()
             if i == count - 1:
-                weights[1].start()
+                weights[2].start()
         rows = slice(i * SPAN, (i + 1) * SPAN)
         read = read_ref[rows, :]
         lead = lead_ref[rows, :]
@@ -430,9 +455,15 @@
             gated[rows, at] = (pre * norm_ref[:, at]).astype(BF16)
         total = jnp.sum(squares, axis=1, keepdims=True) * (1.0 / inner_total)
         sums.append(jnp.transpose(jnp.broadcast_to(total, (SPAN, LANES)))[:1])
+    arrived = 0
     for j in range(width // BLOCK):
-        if not has_rows and j * BLOCK % (width // 2) == 0:
-            weights[j * BLOCK // (width // 2)].wait()
+        if not has_rows:
+            needed = ((j + 1) * BLOCK - 1) // (width // PIECES)
+            if needed == arrived:
+                weights[arrived].wait()
+                arrived += 1
+                if arrived + 1 < PIECES and arrived > 1:
+                    weights[arrived + 1].start()
         part = dot(gated[...], w_ref[:, j * BLOCK : (j + 1) * BLOCK]).astype(outs[0].dtype)
         for u in range(BLOCK // LANES):
             side, tile = divmod(j * (BLOCK // LANES) + u, side_tiles)
@@ -477,7 +508,7 @@
             gated,
             pltpu.VMEM(weight.shape, BF16),
             pltpu.SemaphoreType.DMA((count, 4)),
-            pltpu.SemaphoreType.DMA((2,)),
+            pltpu.SemaphoreType.DMA((PIECES,)),
         ]
     return pl.pallas_call(
         functools.partial(tail_kernel, HEADS * HEADDIM, which is None, count),

time: 99.9 us -> 101 us (1.011)
  Pallas kernels: 41.8 us -> 43.2 us
  transfers between devices with their start and end apart: 18 -> 18, of which waited for: 13 -> 14; matrix products, arithmetic and copies ran while one was open for 2% -> 1% of each run, Pallas kernels for 22% -> 22%
where the time goes in v7:
time: 101 us; the launch traced here: 100 us
  Pallas kernels  43.2 us (43%)
  starting transfers between devices  28.5 us (28%)
  waiting for transfers between devices  25.6 us (25%)
  local copies, waits for them, and re-layouts  1.81 us (2%)
  other arithmetic  1.01 us (1%)
    ppermute x17, starting transfers between devices, ring(): lax.ppermute(value, axis, [(i, (i + distance) % size) for i in range(size)])  27.2 us
    ppermute x17, waiting for transfers between devices, ring(): lax.ppermute(value, axis, [(i, (i + distance) % size) for i in range(size)])  25.4 us
    pallas_call x1, Pallas kernels, first_part(): pl.pallas_call(first_kernel, in_specs=[vmem] + [hbm] * 6 + [vmem] + [hbm]...  17.9 us
    pallas_call x3, Pallas kernels, tail(): pl.pallas_call(functools.partial(tail_kernel, HEADS * HEADDIM, which is N...  12.7 us
    pallas_call x2, Pallas kernels, inside(): pl.pallas_call(functools.partial(inside_kernel, first), grid=(count,), in...  8.04 us
    pallas_call x1, Pallas kernels, ready(): pl.pallas_call(ready_kernel, in_specs=[pl.BlockSpec(memory_space=pltpu.SM...  3.14 us
  transfers between devices with their start and end apart: 18, of which 14 were waited for; matrix products, arithmetic and copies ran while one was open for 1% of the time, Pallas kernels for 22%

profile of v7, /device:TPU:0, one launch (start us, length us, event | category | flops | bytes accessed | tf_op | source)
XLA Modules:
  0.0 100.4 jit_solution(5556037711634877840)
XLA Ops:
  0.0 0.9 slice.99
  0.9 1.3 %collective-permute-start = (bf16[16,2560]{1,0:T(8,128)(2,1)S(1)}, bf16[16,2560]{1,0:T(8,128)(2,1)S(1)}, u32[]{:S(2)}, u32[]{:S(2)}) collective-permute-start(bf16[16,2560]{1,0:T(8,128)(2,1)S(1)} %slice.99), channel_id=1, source_target_pairs={{0,4},{4,8},{8,12},{12,16},{16,20},{20,24},{24,28},{28,32},{32,36}... | collective-permute-start | bytes 245768 | tf_op jit(solution)/shard_map/ppermute | solution.py:677
  2.2 0.7 broadcast_in_dim.31.s1
  2.9 0.2 collective-permute-done.edge
  3.1 17.9 %first.1 = (bf16[512,1280]{1,0:T(8,128)(2,1)}, bf16[512,256]{1,0:T(8,128)(2,1)}, bf16[512,128]{1,0:T(8,128)(2,1)}, f32[512,128]{1,0:T(8,128)}, f32[512,128]{1,0:...) custom-call(bf16[16,2560]{1,0:T(8,128)(2,1)S(1)} %collective-permute, ...), custom_call_target="tpu_custom_call" | custom-call | flops 7717519360 | bytes 17039360 | tf_op jit(solution)/shard_map/first/pallas_call | solution.py:229
  21.1 3.1 %collective-permute-start.1 = (bf16[656,128]{1,0:T(8,128)(2,1)S(1)}, bf16[656,128]{1,0:T(8,128)(2,1)S(1)}, u32[]{:S(2)}, u32[]{:S(2)}) collective-permute-start(bf16[656,128]{1,0:T(8,128)(2,1)S(1)} %pad_maximum_fusion.1), channel_id=1, source_target_pairs={{0,4},{4,0},{1,5},{5,1},{2,6},{6,2},{3,7},{7,3},{8,12},{12,8},{9,1... | collective-permute-start | bytes 503816 | tf_op jit(solution)/shard_map/ppermute | solution.py:579
  24.2 1.0 %collective-permute-done.1 = bf16[656,128]{1,0:T(8,128)(2,1)S(1)} collective-permute-done((bf16[656,128]{1,0:T(8,128)(2,1)S(1)}, bf16[656,128]{1,0:T(8,128)(2,1)S(1)}, u32[]{:S(2)}, u32[]{:S(2)}) %collective-permute-start.1) | collective-permute-done | bytes 167968 | tf_op jit(solution)/shard_map/ppermute | solution.py:579
  25.3 0.1 fusion
  25.5 4.1 %collective-permute-start.2 = (bf16[176,128]{1,0:T(8,128)(2,1)S(1)}, bf16[176,128]{1,0:T(8,128)(2,1)S(1)}, u32[]{:S(2)}, u32[]{:S(2)}) collective-permute-start(bf16[176,128]{1,0:T(8,128)(2,1)S(1)} %get-tuple-element.91), channel_id=1, source_target_pairs={{0,24},{8,0},{16,8},{24,16},{1,25},{9,1},{17,9},{25,17},{2,26},{10... | collective-permute-start | bytes 135176 | tf_op jit(solution)/shard_map/ppermute | solution.py:579
  29.6 0.6 collective-permute-start.3
  30.2 1.0 collective-permute-start.4
  31.2 0.4 collective-permute-done.2
  31.6 3.5 %collective-permute-done.3 = bf16[176,128]{1,0:T(8,128)(2,1)S(1)} collective-permute-done((bf16[176,128]{1,0:T(8,128)(2,1)S(1)}, bf16[176,128]{1,0:T(8,128)(2,1)S(1)}, u32[]{:S(2)}, u32[]{:S(2)}) %collective-permute-start.3) | collective-permute-done | bytes 45088 | tf_op jit(solution)/shard_map/ppermute | solution.py:579
  35.2 0.5 collective-permute-done.4
  35.7 0.1 fusion.2
  35.8 4.1 %collective-permute-start.5 = (bf16[176,128]{1,0:T(8,128)(2,1)S(1)}, bf16[176,128]{1,0:T(8,128)(2,1)S(1)}, u32[]{:S(2)}, u32[]{:S(2)}) collective-permute-start(bf16[176,128]{1,0:T(8,128)(2,1)S(1)} %pad_maximum_fusion.3), channel_id=1, source_target_pairs={{0,96},{32,0},{64,32},{96,64},{1,97},{33,1},{65,33},{97,65},{2,98}... | collective-permute-start | bytes 135176 | tf_op jit(solution)/shard_map/ppermute | solution.py:579
  39.9 1.3 %collective-permute-start.7 = (bf16[176,128]{1,0:T(8,128)(2,1)S(1)}, bf16[176,128]{1,0:T(8,128)(2,1)S(1)}, u32[]{:S(2)}, u32[]{:S(2)}) collective-permute-start(bf16[176,128]{1,0:T(8,128)(2,1)S(1)} %pad_maximum_fusion.3), channel_id=1, source_target_pairs={{0,32},{32,64},{64,96},{96,0},{1,33},{33,65},{65,97},{97,1},{2,34}... | collective-permute-start | bytes 135176 | tf_op jit(solution)/shard_map/ppermute | solution.py:579
  41.2 0.4 collective-permute-done.5
  41.6 3.9 %collective-permute-done.6 = bf16[176,128]{1,0:T(8,128)(2,1)S(1)} collective-permute-done((bf16[176,128]{1,0:T(8,128)(2,1)S(1)}, bf16[176,128]{1,0:T(8,128)(2,1)S(1)}, u32[]{:S(2)}, u32[]{:S(2)}) %collective-permute-start.6) | collective-permute-done | bytes 45088 | tf_op jit(solution)/shard_map/ppermute | solution.py:579
  45.6 0.1 collective-permute-done.7
  45.9 1.9 %collective-permute-start.8 = (bf16[5,32,128]{2,1,0:T(8,128)(2,1)S(1)}, bf16[5,32,128]{2,1,0:T(8,128)(2,1)S(1)}, u32[]{:S(2)}, u32[]{:S(2)}) collective-permute-start(bf16[5,32,128]{2,1,0:T(8,128)(2,1)S(1)} %get-tuple-element.76), channel_id=1, source_target_pairs={{0,24},{8,0},{16,8},{24,16},{1,25},{9,1},{17,9},{25,17},{2,26},{10... | collective-permute-start | bytes 122888 | tf_op jit(solution)/shard_map/ppermute | solution.py:579
  47.8 0.9 collective-permute-start.9
  48.7 0.3 collective-permute-start.10
  48.9 1.0 %collective-permute-done.8 = bf16[5,32,128]{2,1,0:T(8,128)(2,1)S(1)} collective-permute-done((bf16[5,32,128]{2,1,0:T(8,128)(2,1)S(1)}, bf16[5,32,128]{2,1,0:T(8,128)(2,1)S(1)}, u32[]{:S(2)}, u32[]{:S(2)}) %collective-permute-start.8) | collective-permute-done | bytes 40992 | tf_op jit(solution)/shard_map/ppermute | solution.py:579
  50.0 3.3 %collective-permute-done.9 = bf16[5,32,128]{2,1,0:T(8,128)(2,1)S(1)} collective-permute-done((bf16[5,32,128]{2,1,0:T(8,128)(2,1)S(1)}, bf16[5,32,128]{2,1,0:T(8,128)(2,1)S(1)}, u32[]{:S(2)}, u32[]{:S(2)}) %collective-permute-start.9) | collective-permute-done | bytes 40992 | tf_op jit(solution)/shard_map/ppermute | solution.py:579
  53.3 0.6 collective-permute-done.10
  54.0 0.1 broadcast_select_fusion.2
  54.1 0.1 collective-permute-start.11
  54.2 0.1 broadcast_in_dim.35
  54.3 0.1 broadcast_in_dim_reshape.3.skip_ref
  54.4 4.0 %inside.3.refs_4_.high_hbm = f32[256,1280]{1,0:T(8,128)} custom-call(bf16[512,1280]{1,0:T(8,128)(2,1)} %get-tuple-element.31.x_ref, bf16[512,256]{1,0:T(8,128)(2,1)} %get-tuple-element.32.bc_ref, f32[512,128]{1,0:T(8,128)} %get-tuple-element.33.cum_ref, f32[512,128]{1,0:T(8,128)} %get-tuple-element.34.dt_ref, ...), custom_call_target="tpu_custom_call" | custom-call | flops 1000000 | bytes 1000000 | tf_op jit(solution)/shard_map/inside/pallas_call | solution.py:296
  58.4 4.0 %inside.2.refs_3_.low_hbm = f32[256,1280]{1,0:T(8,128)} custom-call(bf16[512,1280]{1,0:T(8,128)(2,1)} %get-tuple-element.31.x_ref, bf16[512,256]{1,0:T(8,128)(2,1)} %get-tuple-element.32.bc_ref, f32[512,128]{1,0:T(8,128)} %get-tuple-element.33.cum_ref, f32[512,128]{1,0:T(8,128)} %get-tuple-element.34.dt_ref, ...), custom_call_target="tpu_custom_call" | custom-call | flops 1000000 | bytes 1000000 | tf_op jit(solution)/shard_map/inside/pallas_call | solution.py:296
  62.4 3.1 %ready.1 = (bf16[128,128]{1,0:T(8,128)(2,1)S(1)}, f32[128,128]{1,0:T(8,128)S(1)}, f32[128,1280]{1,0:T(8,128)S(1)}, bf16[128,1280]{1,0:T(8,128)(2,1)S(1)}, bf16[1280,2560]{1,0:T(8,128)(2,1)S(1)}) custom-call(s32[1]{0:T(128)} %bitcast.24.which, bf16[512,128]{1,0:T(8,128)(2,1)} %get-tuple-element.29.refs_1_.read_hbm, ...), custom_call_target="tpu_custom_call" | custom-call | flops 1000000 | bytes 1000000 | tf_op jit(solution)/shard_map/ready/pallas_call | solution.py:388
  65.6 0.2 broadcast_select_fusion.1
  65.8 1.6 %shard_map.138 = (bf16[1296,128]{1,0:T(8,128)(2,1)S(1)}, bf16[1296,128]{1,0:T(8,128)(2,1)S(1)}) custom-call(bf16[128,128]{1,0:T(8,128)(2,1)S(1)} %get-tuple-element.43.refs_0_, f32[128,128]{1,0:T(8,128)S(1)} %get-tuple-element.44.refs_1_, f32[128,1280]{1,0:T(8,128)S(1)} %get-tuple-element.45.refs_2_, bf16[128,1280]{1,0:T(8,128)(2,1)S(1)} %get-tuple-element.46.refs_3_, ...), custom_call_target="tpu_custom_call" | custom-call | flops 1000000 | bytes 1000000 | tf_op jit(solution)/shard_map/pallas_call | solution.py:513
  67.4 2.8 %collective-permute-start.14 = (bf16[1296,128]{1,0:T(8,128)(2,1)S(1)}, bf16[1296,128]{1,0:T(8,128)(2,1)S(1)}, u32[]{:S(2)}, u32[]{:S(2)}) collective-permute-start(bf16[1296,128]{1,0:T(8,128)(2,1)S(1)} %get-tuple-element.50), channel_id=1, source_target_pairs={{0,3},{1,0},{2,1},{3,2},{4,7},{5,4},{6,5},{7,6},{8,11},{9,8},{10,9... | collective-permute-start | bytes 995336 | tf_op jit(solution)/shard_map/ppermute | solution.py:579
  70.2 0.1 pad_add_fusion.refs_0_
  70.3 6.2 %shard_map.137 = (bf16[1296,128]{1,0:T(8,128)(2,1)S(1)}, bf16[1280,128]{1,0:T(8,128)(2,1)S(1)}, bf16[1280,128]{1,0:T(8,128)(2,1)S(1)}, bf16[1296,128]{1,0:T(8,128)(2,1)S(1)}) custom-call(s32[2]{0:T(128)S(1)} %pad_add_fusion.refs_0_, bf16[512,128]{1,0:T(8,128)(2,1)} %get-tuple-element.29.refs_1_.read_hbm, f32[512,128]{1,0:T(8,128)} %get-tuple-element.30.refs_2_.lead_hbm, ...), custom_call_target="tpu_custom_call" | custom-call | flops 1000000 | bytes 1000000 | tf_op jit(solution)/shard_map/pallas_call | solution.py:513
  76.5 1.4 %collective-permute-done.14.b_ref = bf16[1296,128]{1,0:T(8,128)(2,1)S(1)} collective-permute-done((bf16[1296,128]{1,0:T(8,128)(2,1)S(1)}, bf16[1296,128]{1,0:T(8,128)(2,1)S(1)}, u32[]{:S(2)}, u32[]{:S(2)}) %collective-permute-start.14) | collective-permute-done | bytes 331808 | tf_op jit(solution)/shard_map/ppermute | solution.py:579
  77.9 0.1 shard_map.140
  78.0 3.8 %collective-permute-start.15 = (bf16[1296,128]{1,0:T(8,128)(2,1)S(1)}, bf16[1296,128]{1,0:T(8,128)(2,1)S(1)}, u32[]{:S(2)}, u32[]{:S(2)}) collective-permute-start(bf16[1296,128]{1,0:T(8,128)(2,1)S(1)} %shard_map.140), channel_id=1, source_target_pairs={{0,3},{1,0},{2,1},{3,2},{4,7},{5,4},{6,5},{7,6},{8,11},{9,8},{10,9... | collective-permute-start | bytes 995336 | tf_op jit(solution)/shard_map/ppermute | solution.py:579
  81.8 0.1 shard_map.139
  81.9 0.1 collective-permute-start.13
  81.9 3.2 %collective-permute-start.16 = (bf16[1280,128]{1,0:T(8,128)(2,1)S(1)}, bf16[1280,128]{1,0:T(8,128)(2,1)S(1)}, u32[]{:S(2)}, u32[]{:S(2)}) collective-permute-start(bf16[1280,128]{1,0:T(8,128)(2,1)S(1)} %get-tuple-element.51), channel_id=1, source_target_pairs={{0,3},{1,0},{2,1},{3,2},{4,7},{5,4},{6,5},{7,6},{8,11},{9,8},{10,9... | collective-permute-start | bytes 983048 | tf_op jit(solution)/shard_map/ppermute | solution.py:579
  85.2 4.9 %shard_map.136 = (bf16[1280,128]{1,0:T(8,128)(2,1)S(1)}, bf16[1280,128]{1,0:T(8,128)(2,1)S(1)}, f32[8,128]{1,0:T(8,128)S(1)}) custom-call(s32[1]{0:T(128)} %bitcast.refs_0_, bf16[512,128]{1,0:T(8,128)(2,1)} %get-tuple-element.29.refs_1_.read_hbm, f32[512,128]{1,0:T(8,128)} %get-tuple-element.30.refs_2_.lead_hbm, f32[256,1280]{1,0:T(8,128)} %inside.2.refs_3_.low_hbm, ...), custom_call_target="tpu_custom_call" | custom-call | flops 1000000 | bytes 1000000 | tf_op jit(solution)/shard_map/pallas_call | solution.py:513
  90.1 5.5 %collective-permute-done.16.direct_l = bf16[1280,128]{1,0:T(8,128)(2,1)S(1)} collective-permute-done((bf16[1280,128]{1,0:T(8,128)(2,1)S(1)}, bf16[1280,128]{1,0:T(8,128)(2,1)S(1)}, u32[]{:S(2)}, u32[]{:S(2)}) %collective-permute-start.16) | collective-permute-done | bytes 327712 | tf_op jit(solution)/shard_map/ppermute | solution.py:579
  95.6 3.6 %collective-permute-done.17.direct_r = bf16[1280,128]{1,0:T(8,128)(2,1)S(1)} collective-permute-done((bf16[1280,128]{1,0:T(8,128)(2,1)S(1)}, bf16[1280,128]{1,0:T(8,128)(2,1)S(1)}, u32[]{:S(2)}, u32[]{:S(2)}) %collective-permute-start.17) | collective-permute-done | bytes 327712 | tf_op jit(solution)/shard_map/ppermute | solution.py:579
  99.2 1.2 %final.1 = bf16[128,2560]{1,0:T(8,128)(2,1)} custom-call(bf16[1280,128]{1,0:T(8,128)(2,1)S(1)} %get-tuple-element.39.own_l, bf16[1280,128]{1,0:T(8,128)(2,1)S(1)} %get-tuple-element.40.own_r, f32[8,128]{1,0:T(8,128)S(1)} %get-tuple-element.41.own_sq, bf16[1296,128]{1,0:T(8,128)(2,1)S(1)} %collective-permute-done.13.up, ...), custom_call_target="tpu_custom_call" | custom-call | flops 1000000 | bytes 1000000 | tf_op jit(solution)/shard_map/final/pallas_call | solution.py:566
  (40 shorter events, 0.6 us)
Async XLA Ops:
  0.9 2.2 %collective-permute-start = (bf16[16,2560]{1,0:T(8,128)(2,1)S(1)}, bf16[16,2560]{1,0:T(8,128)(2,1)S(1)}, u32[]{:S(2)}, u32[]{:S(2)}) collective-permute-start(bf16[16,2560]{1,0:T(8,128)(2,1)S(1)} %slice.99), channel_id=1, source_target_pairs={{0,4},{4,8},{8,12},{12,16},{16,20},{20,24},{24,28},{28,32},{32,36}... | collective-permute-start | bytes 245768 | tf_op jit(solution)/shard_map/ppermute | solution.py:677
  21.1 4.1 %collective-permute-start.1 = (bf16[656,128]{1,0:T(8,128)(2,1)S(1)}, bf16[656,128]{1,0:T(8,128)(2,1)S(1)}, u32[]{:S(2)}, u32[]{:S(2)}) collective-permute-start(bf16[656,128]{1,0:T(8,128)(2,1)S(1)} %pad_maximum_fusion.1), channel_id=1, source_target_pairs={{0,4},{4,0},{1,5},{5,1},{2,6},{6,2},{3,7},{7,3},{8,12},{12,8},{9,1... | collective-permute-start | bytes 503816 | tf_op jit(solution)/shard_map/ppermute | solution.py:579
  25.4 28.8 %copy-start.1 = (f32[20]{0:T(128)S(1)}, f32[20]{0:T(128)}, u32[]{:S(2)}) copy-start(f32[20]{0:T(128)} %param.25) | copy-start | bytes 244
  25.4 29.0 %copy-start = (f32[1280]{0:T(1024)S(1)}, f32[1280]{0:T(1024)}, u32[]{:S(2)}) copy-start(f32[1280]{0:T(1024)} %param.26) | copy-start | bytes 15364
  25.5 6.1 %collective-permute-start.2 = (bf16[176,128]{1,0:T(8,128)(2,1)S(1)}, bf16[176,128]{1,0:T(8,128)(2,1)S(1)}, u32[]{:S(2)}, u32[]{:S(2)}) collective-permute-start(bf16[176,128]{1,0:T(8,128)(2,1)S(1)} %get-tuple-element.91), channel_id=1, source_target_pairs={{0,24},{8,0},{16,8},{24,16},{1,25},{9,1},{17,9},{25,17},{2,26},{10... | collective-permute-start | bytes 135176 | tf_op jit(solution)/shard_map/ppermute | solution.py:579
  29.6 5.6 %collective-permute-start.3 = (bf16[176,128]{1,0:T(8,128)(2,1)S(1)}, bf16[176,128]{1,0:T(8,128)(2,1)S(1)}, u32[]{:S(2)}, u32[]{:S(2)}) collective-permute-start(bf16[176,128]{1,0:T(8,128)(2,1)S(1)} %get-tuple-element.90), channel_id=1, source_target_pairs={{0,16},{8,24},{16,0},{24,8},{1,17},{9,25},{17,1},{25,9},{2,18},{10... | collective-permute-start | bytes 135176 | tf_op jit(solution)/shard_map/ppermute | solution.py:579
  30.2 5.4 %collective-permute-start.4 = (bf16[176,128]{1,0:T(8,128)(2,1)S(1)}, bf16[176,128]{1,0:T(8,128)(2,1)S(1)}, u32[]{:S(2)}, u32[]{:S(2)}) collective-permute-start(bf16[176,128]{1,0:T(8,128)(2,1)S(1)} %get-tuple-element.89), channel_id=1, source_target_pairs={{0,8},{8,16},{16,24},{24,0},{1,9},{9,17},{17,25},{25,1},{2,10},{10... | collective-permute-start | bytes 135176 | tf_op jit(solution)/shard_map/ppermute | solution.py:579
  35.8 5.8 %collective-permute-start.5 = (bf16[176,128]{1,0:T(8,128)(2,1)S(1)}, bf16[176,128]{1,0:T(8,128)(2,1)S(1)}, u32[]{:S(2)}, u32[]{:S(2)}) collective-permute-start(bf16[176,128]{1,0:T(8,128)(2,1)S(1)} %pad_maximum_fusion.3), channel_id=1, source_target_pairs={{0,96},{32,0},{64,32},{96,64},{1,97},{33,1},{65,33},{97,65},{2,98}... | collective-permute-start | bytes 135176 | tf_op jit(solution)/shard_map/ppermute | solution.py:579
  39.9 5.6 %collective-permute-start.6 = (bf16[176,128]{1,0:T(8,128)(2,1)S(1)}, bf16[176,128]{1,0:T(8,128)(2,1)S(1)}, u32[]{:S(2)}, u32[]{:S(2)}) collective-permute-start(bf16[176,128]{1,0:T(8,128)(2,1)S(1)} %pad_maximum_fusion.3), channel_id=1, source_target_pairs={{0,64},{32,96},{64,0},{96,32},{1,65},{33,97},{65,1},{97,33},{2,66}... | collective-permute-start | bytes 135176 | tf_op jit(solution)/shard_map/ppermute | solution.py:579
  39.9 5.7 %collective-permute-start.7 = (bf16[176,128]{1,0:T(8,128)(2,1)S(1)}, bf16[176,128]{1,0:T(8,128)(2,1)S(1)}, u32[]{:S(2)}, u32[]{:S(2)}) collective-permute-start(bf16[176,128]{1,0:T(8,128)(2,1)S(1)} %pad_maximum_fusion.3), channel_id=1, source_target_pairs={{0,32},{32,64},{64,96},{96,0},{1,33},{33,65},{65,97},{97,1},{2,34}... | collective-permute-start | bytes 135176 | tf_op jit(solution)/shard_map/ppermute | solution.py:579
  45.9 4.1 %collective-permute-start.8 = (bf16[5,32,128]{2,1,0:T(8,128)(2,1)S(1)}, bf16[5,32,128]{2,1,0:T(8,128)(2,1)S(1)}, u32[]{:S(2)}, u32[]{:S(2)}) collective-permute-start(bf16[5,32,128]{2,1,0:T(8,128)(2,1)S(1)} %get-tuple-element.76), channel_id=1, source_target_pairs={{0,24},{8,0},{16,8},{24,16},{1,25},{9,1},{17,9},{25,17},{2,26},{10... | collective-permute-start | bytes 122888 | tf_op jit(solution)/shard_map/ppermute | solution.py:579
  47.8 5.5 %collective-permute-start.9 = (bf16[5,32,128]{2,1,0:T(8,128)(2,1)S(1)}, bf16[5,32,128]{2,1,0:T(8,128)(2,1)S(1)}, u32[]{:S(2)}, u32[]{:S(2)}) collective-permute-start(bf16[5,32,128]{2,1,0:T(8,128)(2,1)S(1)} %get-tuple-element.75), channel_id=1, source_target_pairs={{0,16},{8,24},{16,0},{24,8},{1,17},{9,25},{17,1},{25,9},{2,18},{10... | collective-permute-start | bytes 122888 | tf_op jit(solution)/shard_map/ppermute | solution.py:579
  48.7 5.2 %collective-permute-start.10 = (bf16[5,32,128]{2,1,0:T(8,128)(2,1)S(1)}, bf16[5,32,128]{2,1,0:T(8,128)(2,1)S(1)}, u32[]{:S(2)}, u32[]{:S(2)}) collective-permute-start(bf16[5,32,128]{2,1,0:T(8,128)(2,1)S(1)} %get-tuple-element.57), channel_id=1, source_target_pairs={{0,8},{8,16},{16,24},{24,0},{1,9},{9,17},{17,25},{25,1},{2,10},{10... | collective-permute-start | bytes 122888 | tf_op jit(solution)/shard_map/ppermute | solution.py:579
  54.1 11.5 %collective-permute-start.11 = (bf16[5,128,128]{2,1,0:T(8,128)(2,1)S(1)}, bf16[5,128,128]{2,1,0:T(8,128)(2,1)S(1)}, u32[]{:S(2)}, u32[]{:S(2)}) collective-permute-start(bf16[5,128,128]{2,1,0:T(8,128)(2,1)S(1)} %broadcast_select_fusion.2), channel_id=1, source_target_pairs={{0,4},{4,0},{1,5},{5,1},{2,6},{6,2},{3,7},{7,3},{8,12},{12,8},{9,1... | collective-permute-start | bytes 491528 | tf_op jit(solution)/shard_map/ppermute | solution.py:579
  67.4 10.5 %collective-permute-start.14 = (bf16[1296,128]{1,0:T(8,128)(2,1)S(1)}, bf16[1296,128]{1,0:T(8,128)(2,1)S(1)}, u32[]{:S(2)}, u32[]{:S(2)}) collective-permute-start(bf16[1296,128]{1,0:T(8,128)(2,1)S(1)} %get-tuple-element.50), channel_id=1, source_target_pairs={{0,3},{1,0},{2,1},{3,2},{4,7},{5,4},{6,5},{7,6},{8,11},{9,8},{10,9... | collective-permute-start | bytes 995336 | tf_op jit(solution)/shard_map/ppermute | solution.py:579
  70.2 11.6 %collective-permute-start.12 = (bf16[1296,128]{1,0:T(8,128)(2,1)S(1)}, bf16[1296,128]{1,0:T(8,128)(2,1)S(1)}, u32[]{:S(2)}, u32[]{:S(2)}) collective-permute-start(bf16[1296,128]{1,0:T(8,128)(2,1)S(1)} %get-tuple-element.48), channel_id=1, source_target_pairs={{0,1},{1,2},{2,3},{3,0},{4,5},{5,6},{6,7},{7,4},{8,9},{9,10},{10,1... | collective-permute-start | bytes 995336 | tf_op jit(solution)/shard_map/ppermute | solution.py:579
  78.0 21.2 %collective-permute-start.15 = (bf16[1296,128]{1,0:T(8,128)(2,1)S(1)}, bf16[1296,128]{1,0:T(8,128)(2,1)S(1)}, u32[]{:S(2)}, u32[]{:S(2)}) collective-permute-start(bf16[1296,128]{1,0:T(8,128)(2,1)S(1)} %shard_map.140), channel_id=1, source_target_pairs={{0,3},{1,0},{2,1},{3,2},{4,7},{5,4},{6,5},{7,6},{8,11},{9,8},{10,9... | collective-permute-start | bytes 995336 | tf_op jit(solution)/shard_map/ppermute | solution.py:579
  81.9 17.4 %collective-permute-start.13 = (bf16[1296,128]{1,0:T(8,128)(2,1)S(1)}, bf16[1296,128]{1,0:T(8,128)(2,1)S(1)}, u32[]{:S(2)}, u32[]{:S(2)}) collective-permute-start(bf16[1296,128]{1,0:T(8,128)(2,1)S(1)} %shard_map.139), channel_id=1, source_target_pairs={{0,1},{1,2},{2,3},{3,0},{4,5},{5,6},{6,7},{7,4},{8,9},{9,10},{10,1... | collective-permute-start | bytes 995336 | tf_op jit(solution)/shard_map/ppermute | solution.py:579
  81.9 13.7 %collective-permute-start.16 = (bf16[1280,128]{1,0:T(8,128)(2,1)S(1)}, bf16[1280,128]{1,0:T(8,128)(2,1)S(1)}, u32[]{:S(2)}, u32[]{:S(2)}) collective-permute-start(bf16[1280,128]{1,0:T(8,128)(2,1)S(1)} %get-tuple-element.51), channel_id=1, source_target_pairs={{0,3},{1,0},{2,1},{3,2},{4,7},{5,4},{6,5},{7,6},{8,11},{9,8},{10,9... | collective-permute-start | bytes 983048 | tf_op jit(solution)/shard_map/ppermute | solution.py:579
  85.2 14.0 %collective-permute-start.17 = (bf16[1280,128]{1,0:T(8,128)(2,1)S(1)}, bf16[1280,128]{1,0:T(8,128)(2,1)S(1)}, u32[]{:S(2)}, u32[]{:S(2)}) collective-permute-start(bf16[1280,128]{1,0:T(8,128)(2,1)S(1)} %get-tuple-element.52), channel_id=1, source_target_pairs={{0,1},{1,2},{2,3},{3,0},{4,5},{5,6},{6,7},{7,4},{8,9},{9,10},{10,1... | collective-permute-start | bytes 983048 | tf_op jit(solution)/shard_map/ppermute | solution.py:579

commit v8 on v6

--- a/solution.py
+++ b/solution.py
@@ -51,7 +51,7 @@
 def first_kernel(
     edge, tok_hbm, bc_hbm, step_hbm, in_hbm, gate_hbm, s0, s1, s2, s3, s4, s5,
     x_hbm, maps_hbm, read_hbm, cum_hbm, dt_hbm, lead_hbm, prior_hbm, gate_out, local_out, decay_out,
-    tok, w_bc, w_step, w_in, w_gate, padded, padded_bc,
+    tok, w_bc, w_step, w_wide, padded, padded_bc, ends, gone, write_t,
     x_ref, maps_ref, read_ref, cum_ref, dt_ref, lead_ref, prior_ref, gate_ref,
     taps, offset, taps_bc, offset_bc, step_bias, decay_log, sems,
 ):
@@ -60,25 +60,26 @@
     channels = x_ref.shape[1]
     heads = step_bias.shape[1]
     spans = rows // SPAN
-    per = BLOCK // HEADDIM
-    tiles = BLOCK // LANES
-
+    side = channels // 2
     first = [
         pltpu.make_async_copy(tok_hbm, tok.at[pl.ds(above, rows), :], sems.at[0]),
         pltpu.make_async_copy(bc_hbm, w_bc, sems.at[1]),
         pltpu.make_async_copy(step_hbm, w_step, sems.at[2]),
     ]
-    inner_copy = pltpu.make_async_copy(in_hbm, w_in, sems.at[3])
-    gate_copy = pltpu.make_async_copy(gate_hbm, w_gate, sems.at[4])
     small = (taps, offset, taps_bc, offset_bc, step_bias, decay_log)
     for k, (source, target) in enumerate(zip((s0, s1, s2, s3, s4, s5), small)):
         first.append(pltpu.make_async_copy(source, target, sems.at[14 + k]))
+    weights = []
+    for k in range(4):
+        source = in_hbm if k < 2 else gate_hbm
+        at = slice(k % 2 * side, (k % 2 + 1) * side)
+        weights.append(pltpu.make_async_copy(source.at[:, at], w_wide.at[k], sems.at[20 + k]))
     for copy in first:
         copy.start()
     tok[:above, :] = edge[...]
     for copy in first:
         copy.wait()
-    inner_copy.start()
+    weights[0].start()
 
     def conv(source, at, tap, off):
         total = off
@@ -91,10 +92,9 @@
     steps = lax.dot_general(
         tok[above:, :], w_step[...], (((1,), (1,)), ((), ())), preferred_element_type=F32
     )
-    inner_copy.wait()
-    gate_copy.start()
-    padded[...] = dot(tok[...], w_in[...]).astype(BF16).astype(F32)
-
+
+    weights[0].wait()
+    weights[1].start()
     maps = conv(padded_bc, slice(0, 2 * STATE), taps_bc, offset_bc[...])
     maps_ref[...] = maps
     read_ref[...] = maps[:, STATE:]
@@ -109,10 +109,9 @@
     col = lax.broadcasted_iota(jnp.int32, (SPAN, SPAN), 1)
     lower = (row >= col).astype(F32)
     lead = jnp.zeros((1, heads), F32)
-    ends, gone, write_t = [], [], []
     for s in range(spans):
         at = slice(s * SPAN, (s + 1) * SPAN)
-        write_t.append(jnp.transpose(maps[at, :STATE].astype(F32)).astype(BF16))
+        write_t[s] = jnp.transpose(maps[at, :STATE].astype(F32)).astype(BF16)
         cum = jnp.dot(
             lower, log_decay[at], preferred_element_type=F32, precision=lax.Precision.HIGHEST
         )
@@ -120,12 +119,60 @@
         lead_ref[at, :heads] = jnp.exp(cum + lead)
         last = cum[SPAN - 1 :, :]
         lead = lead + last
-        ends.append(jnp.exp(last - cum) * dt[at])
-        gone.append(jnp.exp(last))
-    gone.append(jnp.exp(lead))
-
-    gate_copy.wait()
-    early = [
+        ends[at, :heads] = jnp.exp(last - cum) * dt[at]
+        gone[s : s + 1, :heads] = jnp.exp(last)
+    gone[spans : spans + 1, :heads] = jnp.exp(lead)
+    padded[:, :side] = dot(tok[...], w_wide[0]).astype(BF16).astype(F32)
+
+    def states(begin, end):
+        at = slice(begin, end)
+        count = (end - begin) // LANES
+        to = begin // LANES
+        x = conv(padded, at, taps, offset[:, at])
+        x_ref[:, at] = x
+
+        def wide(value):
+            return jnp.concatenate(
+                [
+                    lane_pair(value[:, h : h + 1], value[:, h + 1 : h + 2])
+                    for h in range(begin // HEADDIM, end // HEADDIM, 2)
+                ],
+                axis=1,
+            )
+
+        running = jnp.zeros((STATE, end - begin), F32)
+        for s in range(spans):
+            if s > 0:
+                for t in range(count):
+                    prior_ref[s - 1, to + t] = running[:, t * LANES : (t + 1) * LANES].astype(BF16)
+            span = slice(s * SPAN, (s + 1) * SPAN)
+            here = x[span].astype(F32) * wide(ends[span, :])
+            running = wide(gone[s : s + 1, :]) * running + dot(write_t[s], here.astype(BF16))
+        total = wide(gone[spans : spans + 1, :])
+        for t in range(count):
+            part = slice(t * LANES, (t + 1) * LANES)
+            local_out[to + t] = running[:, part].astype(BF16)
+            decay_out[to + t] = jnp.broadcast_to(total[:, part], (8, LANES))
+
+    def side_states(k):
+        for begin in range(k * side, (k + 1) * side, BLOCK):
+            states(begin, min(begin + BLOCK, (k + 1) * side))
+
+    def side_copies(k):
+        at = slice(k * side, (k + 1) * side)
+        tiles = slice(k * side // LANES, (k + 1) * side // LANES)
+        return [
+            pltpu.make_async_copy(x_ref.at[:, at], x_hbm.at[:, at], sems.at[24 + k]),
+            pltpu.make_async_copy(prior_ref.at[:, tiles], prior_hbm.at[:, tiles], sems.at[26 + k]),
+        ]
+
+    def gate_copy(k):
+        at = slice(k * side, (k + 1) * side)
+        return pltpu.make_async_copy(gate_ref.at[:, at], gate_out.at[:, at], sems.at[12 + k])
+
+    weights[1].wait()
+    weights[2].start()
+    stored = [
         pltpu.make_async_copy(source, target, sems.at[5 + k])
         for k, (source, target) in enumerate(
             (
@@ -134,55 +181,25 @@
             )
         )
     ]
-    for copy in early:
+    for copy in stored:
         copy.start()
-    half = rows // 2
-    gate_ref[:half, :] = dot(tok[above : above + half, :], w_gate[...]).astype(BF16)
-    for g in range(channels // BLOCK):
-        at = slice(g * BLOCK, (g + 1) * BLOCK)
-        x = conv(padded, at, taps, offset[:, at])
-        x_ref[:, at] = x
-        running = jnp.zeros((STATE, BLOCK), F32)
-        for s in range(spans):
-            if s > 0:
-                for t in range(tiles):
-                    prior_ref[s - 1, g * tiles + t] = running[
-                        :, t * LANES : (t + 1) * LANES
-                    ].astype(BF16)
-
-            def wide(value):
-                return jnp.concatenate(
-                    [
-                        lane_pair(value[:, h : h + 1], value[:, h + 1 : h + 2])
-                        for h in range(g * per, (g + 1) * per, 2)
-                    ],
-                    axis=1,
-                )
-
-            here = x[s * SPAN : (s + 1) * SPAN].astype(F32)
-            local = dot(write_t[s], (here * wide(ends[s])).astype(BF16))
-            running = wide(gone[s]) * running + local
-        for t in range(tiles):
-            to = g * tiles + t
-            local_out[to] = running[:, t * LANES : (t + 1) * LANES].astype(BF16)
-            h = g * per + 2 * t
-            decay_out[to] = jnp.broadcast_to(
-                lane_pair(gone[spans][:, h : h + 1], gone[spans][:, h + 1 : h + 2]), (8, LANES)
-            )
-    late = [
-        pltpu.make_async_copy(x_ref, x_hbm, sems.at[10]),
-        pltpu.make_async_copy(prior_ref, prior_hbm, sems.at[11]),
-    ]
-    for k in range(2):
-        at = slice(k * half, (k + 1) * half)
-        late.append(
-            pltpu.make_async_copy(gate_ref.at[at, :], gate_out.at[at, :], sems.at[12 + k])
-        )
-    for copy in late[:3]:
+    side_states(0)
+    padded[:, side:] = dot(tok[...], w_wide[1]).astype(BF16).astype(F32)
+
+    weights[2].wait()
+    weights[3].start()
+    for copy in side_copies(0):
         copy.start()
-    gate_ref[half:, :] = dot(tok[above + half :, :], w_gate[...]).astype(BF16)
-    late[3].start()
-    for copy in early + late:
+    side_states(1)
+    gate_ref[:, :side] = dot(tok[above:, :], w_wide[2]).astype(BF16)
+
+    weights[3].wait()
+    late = side_copies(1) + [gate_copy(0)]
+    for copy in late:
+        copy.start()
+    gate_ref[:, side:] = dot(tok[above:, :], w_wide[3]).astype(BF16)
+    gate_copy(1).start()
+    for copy in stored + side_copies(0) + late + [gate_copy(1)]:
         copy.wait()
 
 
@@ -217,13 +234,15 @@
             pltpu.VMEM((above + rows, width), BF16),
             pltpu.VMEM(w_bc.shape, BF16),
             pltpu.VMEM(w_step.shape, BF16),
-            pltpu.VMEM(w_in.shape, BF16),
-            pltpu.VMEM(w_gate.shape, BF16),
+            pltpu.VMEM((4, width, channels // 2), BF16),
             pltpu.VMEM((above + rows, channels), F32),
             pltpu.VMEM((above + rows, 2 * STATE), F32),
+            pltpu.VMEM((rows, LANES), F32),
+            pltpu.VMEM((8, LANES), F32),
+            pltpu.VMEM((spans, STATE, SPAN), BF16),
             *[pltpu.VMEM(*a) for a in kept],
             *[pltpu.VMEM(a.shape, F32) for a in small],
-            pltpu.SemaphoreType.DMA((20,)),
+            pltpu.SemaphoreType.DMA((28,)),
         ],
         compiler_params=pltpu.CompilerParams(vmem_limit_bytes=FIRST_LIMIT),
         cost_estimate=pl.CostEstimate(

time: 99.9 us -> 106 us (1.061)
  Pallas kernels: 41.8 us -> 47.2 us
    pallas_call x1, Pallas kernels: 17.1 us -> 22.5 us  [first_part(): pl.pallas_call(first_kernel, in_specs=[vmem] + [hbm] * (5 + len(small)),...]
  transfers between devices with their start and end apart: 18 -> 18, of which waited for: 13 -> 13; matrix products, arithmetic and copies ran while one was open for 2% -> 1% of each run, Pallas kernels for 22% -> 21%
where the time goes in v8:
time: 106 us; the launch traced here: 105 us
  Pallas kernels  47.2 us (45%)
  starting transfers between devices  28.3 us (27%)
  waiting for transfers between devices  26 us (25%)
  local copies, waits for them, and re-layouts  2.4 us (2%)
    ppermute x17, starting transfers between devices, ring(): lax.ppermute(value, axis, [(i, (i + distance) % size) for i in range(size)])  27 us
    ppermute x17, waiting for transfers between devices, ring(): lax.ppermute(value, axis, [(i, (i + distance) % size) for i in range(size)])  26 us
    pallas_call x1, Pallas kernels, first_part(): pl.pallas_call(first_kernel, in_specs=[vmem] + [hbm] * (5 + len(small)),...  22.5 us
    pallas_call x3, Pallas kernels, tail(): pl.pallas_call(functools.partial(tail_kernel, HEADS * HEADDIM, which is N...  12.1 us
    pallas_call x2, Pallas kernels, inside(): pl.pallas_call(functools.partial(inside_kernel, first), grid=(count,), in...  8.05 us
    pallas_call x1, Pallas kernels, ready(): pl.pallas_call(ready_kernel, in_specs=[pl.BlockSpec(memory_space=pltpu.SM...  3.14 us
  transfers between devices with their start and end apart: 18, of which 13 were waited for; matrix products, arithmetic and copies ran while one was open for 1% of the time, Pallas kernels for 21%

profile of v8, /device:TPU:0, one launch (start us, length us, event | category | flops | bytes accessed | tf_op | source)
XLA Modules:
  0.0 105.2 jit_solution(1616160925217431064)
XLA Ops:
  0.0 0.9 slice.99
  0.9 1.3 %collective-permute-start = (bf16[16,2560]{1,0:T(8,128)(2,1)S(1)}, bf16[16,2560]{1,0:T(8,128)(2,1)S(1)}, u32[]{:S(2)}, u32[]{:S(2)}) collective-permute-start(bf16[16,2560]{1,0:T(8,128)(2,1)S(1)} %slice.99), channel_id=1, source_target_pairs={{0,4},{4,8},{8,12},{12,16},{16,20},{20,24},{24,28},{28,32},{32,36}... | collective-permute-start | bytes 245768 | tf_op jit(solution)/shard_map/ppermute | solution.py:665
  2.2 1.3 %broadcast_in_dim.31.s1 = f32[1,1280]{1,0:T(1,128)} reshape(f32[1280]{0:T(1024)} %param.21) | data formatting | bytes 10240 | tf_op jit(solution)/shard_map/broadcast_in_dim | solution.py:667
  3.5 22.5 %first.1 = (bf16[512,1280]{1,0:T(8,128)(2,1)}, bf16[512,256]{1,0:T(8,128)(2,1)}, bf16[512,128]{1,0:T(8,128)(2,1)}, f32[512,128]{1,0:T(8,128)}, f32[512,128]{1,0:...) custom-call(bf16[16,2560]{1,0:T(8,128)(2,1)S(1)} %collective-permute, ...), custom_call_target="tpu_custom_call" | custom-call | flops 7717519360 | bytes 17039360 | tf_op jit(solution)/shard_map/first/pallas_call | solution.py:224
  26.2 2.7 %collective-permute-start.1 = (bf16[656,128]{1,0:T(8,128)(2,1)S(1)}, bf16[656,128]{1,0:T(8,128)(2,1)S(1)}, u32[]{:S(2)}, u32[]{:S(2)}) collective-permute-start(bf16[656,128]{1,0:T(8,128)(2,1)S(1)} %pad_maximum_fusion.1), channel_id=1, source_target_pairs={{0,4},{4,0},{1,5},{5,1},{2,6},{6,2},{3,7},{7,3},{8,12},{12,8},{9,1... | collective-permute-start | bytes 503816 | tf_op jit(solution)/shard_map/ppermute | solution.py:567
  28.8 1.0 collective-permute-done.1
  29.9 0.1 fusion
  30.1 4.1 %collective-permute-start.2 = (bf16[176,128]{1,0:T(8,128)(2,1)S(1)}, bf16[176,128]{1,0:T(8,128)(2,1)S(1)}, u32[]{:S(2)}, u32[]{:S(2)}) collective-permute-start(bf16[176,128]{1,0:T(8,128)(2,1)S(1)} %get-tuple-element.91), channel_id=1, source_target_pairs={{0,24},{8,0},{16,8},{24,16},{1,25},{9,1},{17,9},{25,17},{2,26},{10... | collective-permute-start | bytes 135176 | tf_op jit(solution)/shard_map/ppermute | solution.py:567
  34.2 0.6 collective-permute-start.3
  34.9 1.0 collective-permute-start.4
  35.8 0.4 collective-permute-done.2
  36.2 3.5 %collective-permute-done.3 = bf16[176,128]{1,0:T(8,128)(2,1)S(1)} collective-permute-done((bf16[176,128]{1,0:T(8,128)(2,1)S(1)}, bf16[176,128]{1,0:T(8,128)(2,1)S(1)}, u32[]{:S(2)}, u32[]{:S(2)}) %collective-permute-start.3) | collective-permute-done | bytes 45088 | tf_op jit(solution)/shard_map/ppermute | solution.py:567
  39.8 0.5 collective-permute-done.4
  40.3 0.1 fusion.2
  40.4 4.1 %collective-permute-start.5 = (bf16[176,128]{1,0:T(8,128)(2,1)S(1)}, bf16[176,128]{1,0:T(8,128)(2,1)S(1)}, u32[]{:S(2)}, u32[]{:S(2)}) collective-permute-start(bf16[176,128]{1,0:T(8,128)(2,1)S(1)} %pad_maximum_fusion.3), channel_id=1, source_target_pairs={{0,96},{32,0},{64,32},{96,64},{1,97},{33,1},{65,33},{97,65},{2,98}... | collective-permute-start | bytes 135176 | tf_op jit(solution)/shard_map/ppermute | solution.py:567
  44.5 1.3 %collective-permute-start.7 = (bf16[176,128]{1,0:T(8,128)(2,1)S(1)}, bf16[176,128]{1,0:T(8,128)(2,1)S(1)}, u32[]{:S(2)}, u32[]{:S(2)}) collective-permute-start(bf16[176,128]{1,0:T(8,128)(2,1)S(1)} %pad_maximum_fusion.3), channel_id=1, source_target_pairs={{0,32},{32,64},{64,96},{96,0},{1,33},{33,65},{65,97},{97,1},{2,34}... | collective-permute-start | bytes 135176 | tf_op jit(solution)/shard_map/ppermute | solution.py:567
  45.8 0.4 collective-permute-done.5
  46.3 3.9 %collective-permute-done.6 = bf16[176,128]{1,0:T(8,128)(2,1)S(1)} collective-permute-done((bf16[176,128]{1,0:T(8,128)(2,1)S(1)}, bf16[176,128]{1,0:T(8,128)(2,1)S(1)}, u32[]{:S(2)}, u32[]{:S(2)}) %collective-permute-start.6) | collective-permute-done | bytes 45088 | tf_op jit(solution)/shard_map/ppermute | solution.py:567
  50.2 0.1 collective-permute-done.7
  50.4 0.1 select_convert_fusion.1
  50.5 1.9 %collective-permute-start.8 = (bf16[5,32,128]{2,1,0:T(8,128)(2,1)S(1)}, bf16[5,32,128]{2,1,0:T(8,128)(2,1)S(1)}, u32[]{:S(2)}, u32[]{:S(2)}) collective-permute-start(bf16[5,32,128]{2,1,0:T(8,128)(2,1)S(1)} %get-tuple-element.76), channel_id=1, source_target_pairs={{0,24},{8,0},{16,8},{24,16},{1,25},{9,1},{17,9},{25,17},{2,26},{10... | collective-permute-start | bytes 122888 | tf_op jit(solution)/shard_map/ppermute | solution.py:567
  52.4 0.9 collective-permute-start.9
  53.3 0.3 collective-permute-start.10
  53.5 1.0 collective-permute-done.8
  54.6 3.3 %collective-permute-done.9 = bf16[5,32,128]{2,1,0:T(8,128)(2,1)S(1)} collective-permute-done((bf16[5,32,128]{2,1,0:T(8,128)(2,1)S(1)}, bf16[5,32,128]{2,1,0:T(8,128)(2,1)S(1)}, u32[]{:S(2)}, u32[]{:S(2)}) %collective-permute-start.9) | collective-permute-done | bytes 40992 | tf_op jit(solution)/shard_map/ppermute | solution.py:567
  57.9 0.6 collective-permute-done.10
  58.6 0.1 broadcast_select_fusion.2
  58.7 0.1 collective-permute-start.11
  58.8 0.1 broadcast_in_dim.35
  58.9 0.1 broadcast_in_dim_reshape.3.skip_ref
  59.0 4.0 %inside.3.refs_4_.high_hbm = f32[256,1280]{1,0:T(8,128)} custom-call(bf16[512,1280]{1,0:T(8,128)(2,1)} %get-tuple-element.31.x_ref, bf16[512,256]{1,0:T(8,128)(2,1)} %get-tuple-element.32.bc_ref, f32[512,128]{1,0:T(8,128)} %get-tuple-element.33.cum_ref, f32[512,128]{1,0:T(8,128)} %get-tuple-element.34.dt_ref, ...), custom_call_target="tpu_custom_call" | custom-call | flops 1000000 | bytes 1000000 | tf_op jit(solution)/shard_map/inside/pallas_call | solution.py:293
  63.0 4.0 %inside.2.refs_3_.low_hbm = f32[256,1280]{1,0:T(8,128)} custom-call(bf16[512,1280]{1,0:T(8,128)(2,1)} %get-tuple-element.31.x_ref, bf16[512,256]{1,0:T(8,128)(2,1)} %get-tuple-element.32.bc_ref, f32[512,128]{1,0:T(8,128)} %get-tuple-element.33.cum_ref, f32[512,128]{1,0:T(8,128)} %get-tuple-element.34.dt_ref, ...), custom_call_target="tpu_custom_call" | custom-call | flops 1000000 | bytes 1000000 | tf_op jit(solution)/shard_map/inside/pallas_call | solution.py:293
  67.0 3.1 %ready.1 = (bf16[128,128]{1,0:T(8,128)(2,1)S(1)}, f32[128,128]{1,0:T(8,128)S(1)}, f32[128,1280]{1,0:T(8,128)S(1)}, bf16[128,1280]{1,0:T(8,128)(2,1)S(1)}, bf16[1280,2560]{1,0:T(8,128)(2,1)S(1)}) custom-call(s32[1]{0:T(128)} %bitcast.24.which, bf16[512,128]{1,0:T(8,128)(2,1)} %get-tuple-element.29.refs_1_.read_hbm, ...), custom_call_target="tpu_custom_call" | custom-call | flops 1000000 | bytes 1000000 | tf_op jit(solution)/shard_map/ready/pallas_call | solution.py:385
  70.2 0.2 broadcast_select_fusion.1
  70.4 1.6 %shard_map.138 = (bf16[1296,128]{1,0:T(8,128)(2,1)S(1)}, bf16[1296,128]{1,0:T(8,128)(2,1)S(1)}) custom-call(bf16[128,128]{1,0:T(8,128)(2,1)S(1)} %get-tuple-element.43.refs_0_, f32[128,128]{1,0:T(8,128)S(1)} %get-tuple-element.44.refs_1_, f32[128,1280]{1,0:T(8,128)S(1)} %get-tuple-element.45.refs_2_, bf16[128,1280]{1,0:T(8,128)(2,1)S(1)} %get-tuple-element.46.refs_3_, ...), custom_call_target="tpu_custom_call" | custom-call | flops 1000000 | bytes 1000000 | tf_op jit(solution)/shard_map/pallas_call | solution.py:501
  72.0 2.8 %collective-permute-start.14 = (bf16[1296,128]{1,0:T(8,128)(2,1)S(1)}, bf16[1296,128]{1,0:T(8,128)(2,1)S(1)}, u32[]{:S(2)}, u32[]{:S(2)}) collective-permute-start(bf16[1296,128]{1,0:T(8,128)(2,1)S(1)} %get-tuple-element.50), channel_id=1, source_target_pairs={{0,3},{1,0},{2,1},{3,2},{4,7},{5,4},{6,5},{7,6},{8,11},{9,8},{10,9... | collective-permute-start | bytes 995336 | tf_op jit(solution)/shard_map/ppermute | solution.py:567
  74.8 0.1 pad_add_fusion.refs_0_
  74.9 6.3 %shard_map.137 = (bf16[1296,128]{1,0:T(8,128)(2,1)S(1)}, bf16[1280,128]{1,0:T(8,128)(2,1)S(1)}, bf16[1280,128]{1,0:T(8,128)(2,1)S(1)}, bf16[1296,128]{1,0:T(8,128)(2,1)S(1)}) custom-call(s32[2]{0:T(128)S(1)} %pad_add_fusion.refs_0_, bf16[512,128]{1,0:T(8,128)(2,1)} %get-tuple-element.29.refs_1_.read_hbm, f32[512,128]{1,0:T(8,128)} %get-tuple-element.30.refs_2_.lead_hbm, ...), custom_call_target="tpu_custom_call" | custom-call | flops 1000000 | bytes 1000000 | tf_op jit(solution)/shard_map/pallas_call | solution.py:501
  81.2 1.3 %collective-permute-done.14.b_ref = bf16[1296,128]{1,0:T(8,128)(2,1)S(1)} collective-permute-done((bf16[1296,128]{1,0:T(8,128)(2,1)S(1)}, bf16[1296,128]{1,0:T(8,128)(2,1)S(1)}, u32[]{:S(2)}, u32[]{:S(2)}) %collective-permute-start.14) | collective-permute-done | bytes 331808 | tf_op jit(solution)/shard_map/ppermute | solution.py:567
  82.5 0.1 shard_map.140
  82.6 4.0 %collective-permute-start.15 = (bf16[1296,128]{1,0:T(8,128)(2,1)S(1)}, bf16[1296,128]{1,0:T(8,128)(2,1)S(1)}, u32[]{:S(2)}, u32[]{:S(2)}) collective-permute-start(bf16[1296,128]{1,0:T(8,128)(2,1)S(1)} %shard_map.140), channel_id=1, source_target_pairs={{0,3},{1,0},{2,1},{3,2},{4,7},{5,4},{6,5},{7,6},{8,11},{9,8},{10,9... | collective-permute-start | bytes 995336 | tf_op jit(solution)/shard_map/ppermute | solution.py:567
  86.6 0.1 shard_map.139
  86.7 0.1 collective-permute-start.13
  86.8 3.2 %collective-permute-start.16 = (bf16[1280,128]{1,0:T(8,128)(2,1)S(1)}, bf16[1280,128]{1,0:T(8,128)(2,1)S(1)}, u32[]{:S(2)}, u32[]{:S(2)}) collective-permute-start(bf16[1280,128]{1,0:T(8,128)(2,1)S(1)} %get-tuple-element.51), channel_id=1, source_target_pairs={{0,3},{1,0},{2,1},{3,2},{4,7},{5,4},{6,5},{7,6},{8,11},{9,8},{10,9... | collective-permute-start | bytes 983048 | tf_op jit(solution)/shard_map/ppermute | solution.py:567
  90.0 4.2 %shard_map.136 = (bf16[1280,128]{1,0:T(8,128)(2,1)S(1)}, bf16[1280,128]{1,0:T(8,128)(2,1)S(1)}, f32[8,128]{1,0:T(8,128)S(1)}) custom-call(s32[1]{0:T(128)} %bitcast.refs_0_, bf16[512,128]{1,0:T(8,128)(2,1)} %get-tuple-element.29.refs_1_.read_hbm, f32[512,128]{1,0:T(8,128)} %get-tuple-element.30.refs_2_.lead_hbm, f32[256,1280]{1,0:T(8,128)} %inside.2.refs_3_.low_hbm, ...), custom_call_target="tpu_custom_call" | custom-call | flops 1000000 | bytes 1000000 | tf_op jit(solution)/shard_map/pallas_call | solution.py:501
  94.2 6.2 %collective-permute-done.16.direct_l = bf16[1280,128]{1,0:T(8,128)(2,1)S(1)} collective-permute-done((bf16[1280,128]{1,0:T(8,128)(2,1)S(1)}, bf16[1280,128]{1,0:T(8,128)(2,1)S(1)}, u32[]{:S(2)}, u32[]{:S(2)}) %collective-permute-start.16) | collective-permute-done | bytes 327712 | tf_op jit(solution)/shard_map/ppermute | solution.py:567
  100.5 3.6 %collective-permute-done.17.direct_r = bf16[1280,128]{1,0:T(8,128)(2,1)S(1)} collective-permute-done((bf16[1280,128]{1,0:T(8,128)(2,1)S(1)}, bf16[1280,128]{1,0:T(8,128)(2,1)S(1)}, u32[]{:S(2)}, u32[]{:S(2)}) %collective-permute-start.17) | collective-permute-done | bytes 327712 | tf_op jit(solution)/shard_map/ppermute | solution.py:567
  104.1 1.2 %final.1 = bf16[128,2560]{1,0:T(8,128)(2,1)} custom-call(bf16[1280,128]{1,0:T(8,128)(2,1)S(1)} %get-tuple-element.39.own_l, bf16[1280,128]{1,0:T(8,128)(2,1)S(1)} %get-tuple-element.40.own_r, f32[8,128]{1,0:T(8,128)S(1)} %get-tuple-element.41.own_sq, bf16[1296,128]{1,0:T(8,128)(2,1)S(1)} %collective-permute-done.13.up, ...), custom_call_target="tpu_custom_call" | custom-call | flops 1000000 | bytes 1000000 | tf_op jit(solution)/shard_map/final/pallas_call | solution.py:554
  (40 shorter events, 0.5 us)
Async XLA Ops:
  0.9 2.6 %collective-permute-start = (bf16[16,2560]{1,0:T(8,128)(2,1)S(1)}, bf16[16,2560]{1,0:T(8,128)(2,1)S(1)}, u32[]{:S(2)}, u32[]{:S(2)}) collective-permute-start(bf16[16,2560]{1,0:T(8,128)(2,1)S(1)} %slice.99), channel_id=1, source_target_pairs={{0,4},{4,8},{8,12},{12,16},{16,20},{20,24},{24,28},{28,32},{32,36}... | collective-permute-start | bytes 245768 | tf_op jit(solution)/shard_map/ppermute | solution.py:665
  26.2 3.7 %collective-permute-start.1 = (bf16[656,128]{1,0:T(8,128)(2,1)S(1)}, bf16[656,128]{1,0:T(8,128)(2,1)S(1)}, u32[]{:S(2)}, u32[]{:S(2)}) collective-permute-start(bf16[656,128]{1,0:T(8,128)(2,1)S(1)} %pad_maximum_fusion.1), channel_id=1, source_target_pairs={{0,4},{4,0},{1,5},{5,1},{2,6},{6,2},{3,7},{7,3},{8,12},{12,8},{9,1... | collective-permute-start | bytes 503816 | tf_op jit(solution)/shard_map/ppermute | solution.py:567
  30.0 28.8 %copy-start.1 = (f32[20]{0:T(128)S(1)}, f32[20]{0:T(128)}, u32[]{:S(2)}) copy-start(f32[20]{0:T(128)} %param.25) | copy-start | bytes 244
  30.0 29.0 %copy-start = (f32[1280]{0:T(1024)S(1)}, f32[1280]{0:T(1024)}, u32[]{:S(2)}) copy-start(f32[1280]{0:T(1024)} %param.26) | copy-start | bytes 15364
  30.1 6.1 %collective-permute-start.2 = (bf16[176,128]{1,0:T(8,128)(2,1)S(1)}, bf16[176,128]{1,0:T(8,128)(2,1)S(1)}, u32[]{:S(2)}, u32[]{:S(2)}) collective-permute-start(bf16[176,128]{1,0:T(8,128)(2,1)S(1)} %get-tuple-element.91), channel_id=1, source_target_pairs={{0,24},{8,0},{16,8},{24,16},{1,25},{9,1},{17,9},{25,17},{2,26},{10... | collective-permute-start | bytes 135176 | tf_op jit(solution)/shard_map/ppermute | solution.py:567
  34.2 5.6 %collective-permute-start.3 = (bf16[176,128]{1,0:T(8,128)(2,1)S(1)}, bf16[176,128]{1,0:T(8,128)(2,1)S(1)}, u32[]{:S(2)}, u32[]{:S(2)}) collective-permute-start(bf16[176,128]{1,0:T(8,128)(2,1)S(1)} %get-tuple-element.90), channel_id=1, source_target_pairs={{0,16},{8,24},{16,0},{24,8},{1,17},{9,25},{17,1},{25,9},{2,18},{10... | collective-permute-start | bytes 135176 | tf_op jit(solution)/shard_map/ppermute | solution.py:567
  34.9 5.4 %collective-permute-start.4 = (bf16[176,128]{1,0:T(8,128)(2,1)S(1)}, bf16[176,128]{1,0:T(8,128)(2,1)S(1)}, u32[]{:S(2)}, u32[]{:S(2)}) collective-permute-start(bf16[176,128]{1,0:T(8,128)(2,1)S(1)} %get-tuple-element.89), channel_id=1, source_target_pairs={{0,8},{8,16},{16,24},{24,0},{1,9},{9,17},{17,25},{25,1},{2,10},{10... | collective-permute-start | bytes 135176 | tf_op jit(solution)/shard_map/ppermute | solution.py:567
  40.4 5.8 %collective-permute-start.5 = (bf16[176,128]{1,0:T(8,128)(2,1)S(1)}, bf16[176,128]{1,0:T(8,128)(2,1)S(1)}, u32[]{:S(2)}, u32[]{:S(2)}) collective-permute-start(bf16[176,128]{1,0:T(8,128)(2,1)S(1)} %pad_maximum_fusion.3), channel_id=1, source_target_pairs={{0,96},{32,0},{64,32},{96,64},{1,97},{33,1},{65,33},{97,65},{2,98}... | collective-permute-start | bytes 135176 | tf_op jit(solution)/shard_map/ppermute | solution.py:567
  44.5 5.6 %collective-permute-start.6 = (bf16[176,128]{1,0:T(8,128)(2,1)S(1)}, bf16[176,128]{1,0:T(8,128)(2,1)S(1)}, u32[]{:S(2)}, u32[]{:S(2)}) collective-permute-start(bf16[176,128]{1,0:T(8,128)(2,1)S(1)} %pad_maximum_fusion.3), channel_id=1, source_target_pairs={{0,64},{32,96},{64,0},{96,32},{1,65},{33,97},{65,1},{97,33},{2,66}... | collective-permute-start | bytes 135176 | tf_op jit(solution)/shard_map/ppermute | solution.py:567
  44.5 5.7 %collective-permute-start.7 = (bf16[176,128]{1,0:T(8,128)(2,1)S(1)}, bf16[176,128]{1,0:T(8,128)(2,1)S(1)}, u32[]{:S(2)}, u32[]{:S(2)}) collective-permute-start(bf16[176,128]{1,0:T(8,128)(2,1)S(1)} %pad_maximum_fusion.3), channel_id=1, source_target_pairs={{0,32},{32,64},{64,96},{96,0},{1,33},{33,65},{65,97},{97,1},{2,34}... | collective-permute-start | bytes 135176 | tf_op jit(solution)/shard_map/ppermute | solution.py:567
  50.5 4.1 %collective-permute-start.8 = (bf16[5,32,128]{2,1,0:T(8,128)(2,1)S(1)}, bf16[5,32,128]{2,1,0:T(8,128)(2,1)S(1)}, u32[]{:S(2)}, u32[]{:S(2)}) collective-permute-start(bf16[5,32,128]{2,1,0:T(8,128)(2,1)S(1)} %get-tuple-element.76), channel_id=1, source_target_pairs={{0,24},{8,0},{16,8},{24,16},{1,25},{9,1},{17,9},{25,17},{2,26},{10... | collective-permute-start | bytes 122888 | tf_op jit(solution)/shard_map/ppermute | solution.py:567
  52.4 5.5 %collective-permute-start.9 = (bf16[5,32,128]{2,1,0:T(8,128)(2,1)S(1)}, bf16[5,32,128]{2,1,0:T(8,128)(2,1)S(1)}, u32[]{:S(2)}, u32[]{:S(2)}) collective-permute-start(bf16[5,32,128]{2,1,0:T(8,128)(2,1)S(1)} %get-tuple-element.75), channel_id=1, source_target_pairs={{0,16},{8,24},{16,0},{24,8},{1,17},{9,25},{17,1},{25,9},{2,18},{10... | collective-permute-start | bytes 122888 | tf_op jit(solution)/shard_map/ppermute | solution.py:567
  53.3 5.2 %collective-permute-start.10 = (bf16[5,32,128]{2,1,0:T(8,128)(2,1)S(1)}, bf16[5,32,128]{2,1,0:T(8,128)(2,1)S(1)}, u32[]{:S(2)}, u32[]{:S(2)}) collective-permute-start(bf16[5,32,128]{2,1,0:T(8,128)(2,1)S(1)} %get-tuple-element.57), channel_id=1, source_target_pairs={{0,8},{8,16},{16,24},{24,0},{1,9},{9,17},{17,25},{25,1},{2,10},{10... | collective-permute-start | bytes 122888 | tf_op jit(solution)/shard_map/ppermute | solution.py:567
  58.7 11.5 %collective-permute-start.11 = (bf16[5,128,128]{2,1,0:T(8,128)(2,1)S(1)}, bf16[5,128,128]{2,1,0:T(8,128)(2,1)S(1)}, u32[]{:S(2)}, u32[]{:S(2)}) collective-permute-start(bf16[5,128,128]{2,1,0:T(8,128)(2,1)S(1)} %broadcast_select_fusion.2), channel_id=1, source_target_pairs={{0,4},{4,0},{1,5},{5,1},{2,6},{6,2},{3,7},{7,3},{8,12},{12,8},{9,1... | collective-permute-start | bytes 491528 | tf_op jit(solution)/shard_map/ppermute | solution.py:567
  72.0 10.5 %collective-permute-start.14 = (bf16[1296,128]{1,0:T(8,128)(2,1)S(1)}, bf16[1296,128]{1,0:T(8,128)(2,1)S(1)}, u32[]{:S(2)}, u32[]{:S(2)}) collective-permute-start(bf16[1296,128]{1,0:T(8,128)(2,1)S(1)} %get-tuple-element.50), channel_id=1, source_target_pairs={{0,3},{1,0},{2,1},{3,2},{4,7},{5,4},{6,5},{7,6},{8,11},{9,8},{10,9... | collective-permute-start | bytes 995336 | tf_op jit(solution)/shard_map/ppermute | solution.py:567
  74.8 11.8 %collective-permute-start.12 = (bf16[1296,128]{1,0:T(8,128)(2,1)S(1)}, bf16[1296,128]{1,0:T(8,128)(2,1)S(1)}, u32[]{:S(2)}, u32[]{:S(2)}) collective-permute-start(bf16[1296,128]{1,0:T(8,128)(2,1)S(1)} %get-tuple-element.48), channel_id=1, source_target_pairs={{0,1},{1,2},{2,3},{3,0},{4,5},{5,6},{6,7},{7,4},{8,9},{9,10},{10,1... | collective-permute-start | bytes 995336 | tf_op jit(solution)/shard_map/ppermute | solution.py:567
  82.6 21.4 %collective-permute-start.15 = (bf16[1296,128]{1,0:T(8,128)(2,1)S(1)}, bf16[1296,128]{1,0:T(8,128)(2,1)S(1)}, u32[]{:S(2)}, u32[]{:S(2)}) collective-permute-start(bf16[1296,128]{1,0:T(8,128)(2,1)S(1)} %shard_map.140), channel_id=1, source_target_pairs={{0,3},{1,0},{2,1},{3,2},{4,7},{5,4},{6,5},{7,6},{8,11},{9,8},{10,9... | collective-permute-start | bytes 995336 | tf_op jit(solution)/shard_map/ppermute | solution.py:567
  86.7 17.4 %collective-permute-start.13 = (bf16[1296,128]{1,0:T(8,128)(2,1)S(1)}, bf16[1296,128]{1,0:T(8,128)(2,1)S(1)}, u32[]{:S(2)}, u32[]{:S(2)}) collective-permute-start(bf16[1296,128]{1,0:T(8,128)(2,1)S(1)} %shard_map.139), channel_id=1, source_target_pairs={{0,1},{1,2},{2,3},{3,0},{4,5},{5,6},{6,7},{7,4},{8,9},{9,10},{10,1... | collective-permute-start | bytes 995336 | tf_op jit(solution)/shard_map/ppermute | solution.py:567
  86.8 13.7 %collective-permute-start.16 = (bf16[1280,128]{1,0:T(8,128)(2,1)S(1)}, bf16[1280,128]{1,0:T(8,128)(2,1)S(1)}, u32[]{:S(2)}, u32[]{:S(2)}) collective-permute-start(bf16[1280,128]{1,0:T(8,128)(2,1)S(1)} %get-tuple-element.51), channel_id=1, source_target_pairs={{0,3},{1,0},{2,1},{3,2},{4,7},{5,4},{6,5},{7,6},{8,11},{9,8},{10,9... | collective-permute-start | bytes 983048 | tf_op jit(solution)/shard_map/ppermute | solution.py:567
  90.0 14.0 %collective-permute-start.17 = (bf16[1280,128]{1,0:T(8,128)(2,1)S(1)}, bf16[1280,128]{1,0:T(8,128)(2,1)S(1)}, u32[]{:S(2)}, u32[]{:S(2)}) collective-permute-start(bf16[1280,128]{1,0:T(8,128)(2,1)S(1)} %get-tuple-element.52), channel_id=1, source_target_pairs={{0,1},{1,2},{2,3},{3,0},{4,5},{5,6},{6,7},{7,4},{8,9},{9,10},{10,1... | collective-permute-start | bytes 983048 | tf_op jit(solution)/shard_map/ppermute | solution.py:567

commit v9 on v6

--- a/solution.py
+++ b/solution.py
@@ -12,7 +12,6 @@
 HEADS = 80
 HEADDIM = 64
 STATE = 128
-KERNEL = 4
 SPAN = 128
 LANES = 128
 EDGE = 16
@@ -40,7 +39,8 @@
 
 
 def silu(v):
-    return v * (0.5 + 0.5 * jnp.tanh(0.5 * v))
+    half = 0.5 * v
+    return half + half * jnp.tanh(half)
 
 
 def lane_pair(first, second):
@@ -81,11 +81,13 @@
     inner_copy.start()
 
     def conv(source, at, tap, off):
-        total = off
-        for k in range(KERNEL):
-            begin = above - (KERNEL - 1) + k
-            total = total + tap[k : k + 1, at] * source[begin : begin + rows, at]
-        return silu(total).astype(BF16)
+        x = source[:, at]
+        half = 0.5 * tap[:, at]
+        one = pltpu.roll(x, 1, 0)
+        older = half[0:1] * one + half[1:2] * x
+        newer = half[2:3] * one + half[3:4] * x + 0.5 * off
+        v = pltpu.roll(older, 2, 0)[above:] + newer[above:]
+        return (v + v * jnp.tanh(v)).astype(BF16)
 
     padded_bc[...] = dot(tok[...], w_bc[...]).astype(BF16).astype(F32)
     steps = lax.dot_general(

time: 99.9 us -> 98.4 us (0.985)
  Pallas kernels: 41.8 us -> 40.1 us
    pallas_call x1, Pallas kernels: 17.1 us -> 15.4 us  [first_part(): pl.pallas_call(first_kernel, in_specs=[vmem] + [hbm] * (5 + len(small)),...]
where the time goes in v9:
time: 98.4 us; the launch traced here: 98.1 us
  Pallas kernels  40.1 us (41%)
  starting transfers between devices  28.2 us (29%)
  waiting for transfers between devices  26 us (26%)
  local copies, waits for them, and re-layouts  2.4 us (2%)
  other arithmetic  1.01 us (1%)
    ppermute x17, starting transfers between devices, ring(): lax.ppermute(value, axis, [(i, (i + distance) % size) for i in range(size)])  26.9 us
    ppermute x17, waiting for transfers between devices, ring(): lax.ppermute(value, axis, [(i, (i + distance) % size) for i in range(size)])  26 us
    pallas_call x1, Pallas kernels, first_part(): pl.pallas_call(first_kernel, in_specs=[vmem] + [hbm] * (5 + len(small)),...  15.4 us
    pallas_call x3, Pallas kernels, tail(): pl.pallas_call(functools.partial(tail_kernel, HEADS * HEADDIM, which is N...  12.1 us
    pallas_call x2, Pallas kernels, inside(): pl.pallas_call(functools.partial(inside_kernel, first), grid=(count,), in...  8.05 us
    pallas_call x1, Pallas kernels, ready(): pl.pallas_call(ready_kernel, in_specs=[pl.BlockSpec(memory_space=pltpu.SM...  3.14 us
  transfers between devices with their start and end apart: 18, of which 13 were waited for; matrix products, arithmetic and copies ran while one was open for 2% of the time, Pallas kernels for 22%

profile of v9, /device:TPU:0, one launch (start us, length us, event | category | flops | bytes accessed | tf_op | source)
XLA Modules:
  0.0 98.1 jit_solution(4159507932589507172)
XLA Ops:
  0.0 0.9 slice.99
  0.9 1.3 %collective-permute-start = (bf16[16,2560]{1,0:T(8,128)(2,1)S(1)}, bf16[16,2560]{1,0:T(8,128)(2,1)S(1)}, u32[]{:S(2)}, u32[]{:S(2)}) collective-permute-start(bf16[16,2560]{1,0:T(8,128)(2,1)S(1)} %slice.99), channel_id=1, source_target_pairs={{0,4},{4,8},{8,12},{12,16},{16,20},{20,24},{24,28},{28,32},{32,36}... | collective-permute-start | bytes 245768 | tf_op jit(solution)/shard_map/ppermute | solution.py:648
  2.2 1.3 %broadcast_in_dim.31.s1 = f32[1,1280]{1,0:T(1,128)} reshape(f32[1280]{0:T(1024)} %param.21) | data formatting | bytes 10240 | tf_op jit(solution)/shard_map/broadcast_in_dim | solution.py:650
  3.5 15.4 %first.1 = (bf16[512,1280]{1,0:T(8,128)(2,1)}, bf16[512,256]{1,0:T(8,128)(2,1)}, bf16[512,128]{1,0:T(8,128)(2,1)}, f32[512,128]{1,0:T(8,128)}, f32[512,128]{1,0:...) custom-call(bf16[16,2560]{1,0:T(8,128)(2,1)S(1)} %collective-permute, ...), custom_call_target="tpu_custom_call" | custom-call | flops 7717519360 | bytes 17039360 | tf_op jit(solution)/shard_map/first/pallas_call | solution.py:209
  19.1 2.7 %collective-permute-start.1 = (bf16[656,128]{1,0:T(8,128)(2,1)S(1)}, bf16[656,128]{1,0:T(8,128)(2,1)S(1)}, u32[]{:S(2)}, u32[]{:S(2)}) collective-permute-start(bf16[656,128]{1,0:T(8,128)(2,1)S(1)} %pad_maximum_fusion.1), channel_id=1, source_target_pairs={{0,4},{4,0},{1,5},{5,1},{2,6},{6,2},{3,7},{7,3},{8,12},{12,8},{9,1... | collective-permute-start | bytes 503816 | tf_op jit(solution)/shard_map/ppermute | solution.py:550
  21.7 1.0 %collective-permute-done.1 = bf16[656,128]{1,0:T(8,128)(2,1)S(1)} collective-permute-done((bf16[656,128]{1,0:T(8,128)(2,1)S(1)}, bf16[656,128]{1,0:T(8,128)(2,1)S(1)}, u32[]{:S(2)}, u32[]{:S(2)}) %collective-permute-start.1) | collective-permute-done | bytes 167968 | tf_op jit(solution)/shard_map/ppermute | solution.py:550
  22.8 0.1 fusion
  23.0 4.1 %collective-permute-start.2 = (bf16[176,128]{1,0:T(8,128)(2,1)S(1)}, bf16[176,128]{1,0:T(8,128)(2,1)S(1)}, u32[]{:S(2)}, u32[]{:S(2)}) collective-permute-start(bf16[176,128]{1,0:T(8,128)(2,1)S(1)} %get-tuple-element.91), channel_id=1, source_target_pairs={{0,24},{8,0},{16,8},{24,16},{1,25},{9,1},{17,9},{25,17},{2,26},{10... | collective-permute-start | bytes 135176 | tf_op jit(solution)/shard_map/ppermute | solution.py:550
  27.1 0.6 collective-permute-start.3
  27.8 1.0 collective-permute-start.4
  28.7 0.4 collective-permute-done.2
  29.1 3.5 %collective-permute-done.3 = bf16[176,128]{1,0:T(8,128)(2,1)S(1)} collective-permute-done((bf16[176,128]{1,0:T(8,128)(2,1)S(1)}, bf16[176,128]{1,0:T(8,128)(2,1)S(1)}, u32[]{:S(2)}, u32[]{:S(2)}) %collective-permute-start.3) | collective-permute-done | bytes 45088 | tf_op jit(solution)/shard_map/ppermute | solution.py:550
  32.7 0.5 collective-permute-done.4
  33.2 0.1 fusion.2
  33.3 4.1 %collective-permute-start.5 = (bf16[176,128]{1,0:T(8,128)(2,1)S(1)}, bf16[176,128]{1,0:T(8,128)(2,1)S(1)}, u32[]{:S(2)}, u32[]{:S(2)}) collective-permute-start(bf16[176,128]{1,0:T(8,128)(2,1)S(1)} %pad_maximum_fusion.3), channel_id=1, source_target_pairs={{0,96},{32,0},{64,32},{96,64},{1,97},{33,1},{65,33},{97,65},{2,98}... | collective-permute-start | bytes 135176 | tf_op jit(solution)/shard_map/ppermute | solution.py:550
  37.5 1.3 %collective-permute-start.7 = (bf16[176,128]{1,0:T(8,128)(2,1)S(1)}, bf16[176,128]{1,0:T(8,128)(2,1)S(1)}, u32[]{:S(2)}, u32[]{:S(2)}) collective-permute-start(bf16[176,128]{1,0:T(8,128)(2,1)S(1)} %pad_maximum_fusion.3), channel_id=1, source_target_pairs={{0,32},{32,64},{64,96},{96,0},{1,33},{33,65},{65,97},{97,1},{2,34}... | collective-permute-start | bytes 135176 | tf_op jit(solution)/shard_map/ppermute | solution.py:550
  38.7 0.4 collective-permute-done.5
  39.2 3.9 %collective-permute-done.6 = bf16[176,128]{1,0:T(8,128)(2,1)S(1)} collective-permute-done((bf16[176,128]{1,0:T(8,128)(2,1)S(1)}, bf16[176,128]{1,0:T(8,128)(2,1)S(1)}, u32[]{:S(2)}, u32[]{:S(2)}) %collective-permute-start.6) | collective-permute-done | bytes 45088 | tf_op jit(solution)/shard_map/ppermute | solution.py:550
  43.1 0.1 collective-permute-done.7
  43.3 0.1 select_convert_fusion.1
  43.4 2.1 %collective-permute-start.8 = (bf16[5,32,128]{2,1,0:T(8,128)(2,1)S(1)}, bf16[5,32,128]{2,1,0:T(8,128)(2,1)S(1)}, u32[]{:S(2)}, u32[]{:S(2)}) collective-permute-start(bf16[5,32,128]{2,1,0:T(8,128)(2,1)S(1)} %get-tuple-element.76), channel_id=1, source_target_pairs={{0,24},{8,0},{16,8},{24,16},{1,25},{9,1},{17,9},{25,17},{2,26},{10... | collective-permute-start | bytes 122888 | tf_op jit(solution)/shard_map/ppermute | solution.py:550
  45.5 0.9 collective-permute-start.9
  46.4 0.3 collective-permute-start.10
  46.6 1.0 %collective-permute-done.8 = bf16[5,32,128]{2,1,0:T(8,128)(2,1)S(1)} collective-permute-done((bf16[5,32,128]{2,1,0:T(8,128)(2,1)S(1)}, bf16[5,32,128]{2,1,0:T(8,128)(2,1)S(1)}, u32[]{:S(2)}, u32[]{:S(2)}) %collective-permute-start.8) | collective-permute-done | bytes 40992 | tf_op jit(solution)/shard_map/ppermute | solution.py:550
  47.6 3.3 %collective-permute-done.9 = bf16[5,32,128]{2,1,0:T(8,128)(2,1)S(1)} collective-permute-done((bf16[5,32,128]{2,1,0:T(8,128)(2,1)S(1)}, bf16[5,32,128]{2,1,0:T(8,128)(2,1)S(1)}, u32[]{:S(2)}, u32[]{:S(2)}) %collective-permute-start.9) | collective-permute-done | bytes 40992 | tf_op jit(solution)/shard_map/ppermute | solution.py:550
  51.0 0.6 collective-permute-done.10
  51.7 0.1 broadcast_select_fusion.2
  51.8 0.1 collective-permute-start.11
  51.9 0.1 broadcast_in_dim.35
  52.0 0.1 broadcast_in_dim_reshape.3.skip_ref
  52.1 4.0 %inside.3.refs_4_.high_hbm = f32[256,1280]{1,0:T(8,128)} custom-call(bf16[512,1280]{1,0:T(8,128)(2,1)} %get-tuple-element.31.x_ref, bf16[512,256]{1,0:T(8,128)(2,1)} %get-tuple-element.32.bc_ref, f32[512,128]{1,0:T(8,128)} %get-tuple-element.33.cum_ref, f32[512,128]{1,0:T(8,128)} %get-tuple-element.34.dt_ref, ...), custom_call_target="tpu_custom_call" | custom-call | flops 1000000 | bytes 1000000 | tf_op jit(solution)/shard_map/inside/pallas_call | solution.py:276
  56.1 4.0 %inside.2.refs_3_.low_hbm = f32[256,1280]{1,0:T(8,128)} custom-call(bf16[512,1280]{1,0:T(8,128)(2,1)} %get-tuple-element.31.x_ref, bf16[512,256]{1,0:T(8,128)(2,1)} %get-tuple-element.32.bc_ref, f32[512,128]{1,0:T(8,128)} %get-tuple-element.33.cum_ref, f32[512,128]{1,0:T(8,128)} %get-tuple-element.34.dt_ref, ...), custom_call_target="tpu_custom_call" | custom-call | flops 1000000 | bytes 1000000 | tf_op jit(solution)/shard_map/inside/pallas_call | solution.py:276
  60.1 3.1 %ready.1 = (bf16[128,128]{1,0:T(8,128)(2,1)S(1)}, f32[128,128]{1,0:T(8,128)S(1)}, f32[128,1280]{1,0:T(8,128)S(1)}, bf16[128,1280]{1,0:T(8,128)(2,1)S(1)}, bf16[1280,2560]{1,0:T(8,128)(2,1)S(1)}) custom-call(s32[1]{0:T(128)} %bitcast.24.which, bf16[512,128]{1,0:T(8,128)(2,1)} %get-tuple-element.29.refs_1_.read_hbm, ...), custom_call_target="tpu_custom_call" | custom-call | flops 1000000 | bytes 1000000 | tf_op jit(solution)/shard_map/ready/pallas_call | solution.py:368
  63.3 0.2 broadcast_select_fusion.1
  63.5 1.6 %shard_map.138 = (bf16[1296,128]{1,0:T(8,128)(2,1)S(1)}, bf16[1296,128]{1,0:T(8,128)(2,1)S(1)}) custom-call(bf16[128,128]{1,0:T(8,128)(2,1)S(1)} %get-tuple-element.43.refs_0_, f32[128,128]{1,0:T(8,128)S(1)} %get-tuple-element.44.refs_1_, f32[128,1280]{1,0:T(8,128)S(1)} %get-tuple-element.45.refs_2_, bf16[128,1280]{1,0:T(8,128)(2,1)S(1)} %get-tuple-element.46.refs_3_, ...), custom_call_target="tpu_custom_call" | custom-call | flops 1000000 | bytes 1000000 | tf_op jit(solution)/shard_map/pallas_call | solution.py:484
  65.1 2.8 %collective-permute-start.14 = (bf16[1296,128]{1,0:T(8,128)(2,1)S(1)}, bf16[1296,128]{1,0:T(8,128)(2,1)S(1)}, u32[]{:S(2)}, u32[]{:S(2)}) collective-permute-start(bf16[1296,128]{1,0:T(8,128)(2,1)S(1)} %get-tuple-element.50), channel_id=1, source_target_pairs={{0,3},{1,0},{2,1},{3,2},{4,7},{5,4},{6,5},{7,6},{8,11},{9,8},{10,9... | collective-permute-start | bytes 995336 | tf_op jit(solution)/shard_map/ppermute | solution.py:550
  67.9 0.1 pad_add_fusion.refs_0_
  68.0 6.3 %shard_map.137 = (bf16[1296,128]{1,0:T(8,128)(2,1)S(1)}, bf16[1280,128]{1,0:T(8,128)(2,1)S(1)}, bf16[1280,128]{1,0:T(8,128)(2,1)S(1)}, bf16[1296,128]{1,0:T(8,128)(2,1)S(1)}) custom-call(s32[2]{0:T(128)S(1)} %pad_add_fusion.refs_0_, bf16[512,128]{1,0:T(8,128)(2,1)} %get-tuple-element.29.refs_1_.read_hbm, f32[512,128]{1,0:T(8,128)} %get-tuple-element.30.refs_2_.lead_hbm, ...), custom_call_target="tpu_custom_call" | custom-call | flops 1000000 | bytes 1000000 | tf_op jit(solution)/shard_map/pallas_call | solution.py:484
  74.3 1.3 %collective-permute-done.14.b_ref = bf16[1296,128]{1,0:T(8,128)(2,1)S(1)} collective-permute-done((bf16[1296,128]{1,0:T(8,128)(2,1)S(1)}, bf16[1296,128]{1,0:T(8,128)(2,1)S(1)}, u32[]{:S(2)}, u32[]{:S(2)}) %collective-permute-start.14) | collective-permute-done | bytes 331808 | tf_op jit(solution)/shard_map/ppermute | solution.py:550
  75.6 0.1 shard_map.140
  75.7 3.8 %collective-permute-start.15 = (bf16[1296,128]{1,0:T(8,128)(2,1)S(1)}, bf16[1296,128]{1,0:T(8,128)(2,1)S(1)}, u32[]{:S(2)}, u32[]{:S(2)}) collective-permute-start(bf16[1296,128]{1,0:T(8,128)(2,1)S(1)} %shard_map.140), channel_id=1, source_target_pairs={{0,3},{1,0},{2,1},{3,2},{4,7},{5,4},{6,5},{7,6},{8,11},{9,8},{10,9... | collective-permute-start | bytes 995336 | tf_op jit(solution)/shard_map/ppermute | solution.py:550
  79.5 0.1 shard_map.139
  79.6 0.1 collective-permute-start.13
  79.6 3.2 %collective-permute-start.16 = (bf16[1280,128]{1,0:T(8,128)(2,1)S(1)}, bf16[1280,128]{1,0:T(8,128)(2,1)S(1)}, u32[]{:S(2)}, u32[]{:S(2)}) collective-permute-start(bf16[1280,128]{1,0:T(8,128)(2,1)S(1)} %get-tuple-element.51), channel_id=1, source_target_pairs={{0,3},{1,0},{2,1},{3,2},{4,7},{5,4},{6,5},{7,6},{8,11},{9,8},{10,9... | collective-permute-start | bytes 983048 | tf_op jit(solution)/shard_map/ppermute | solution.py:550
  82.9 4.2 %shard_map.136 = (bf16[1280,128]{1,0:T(8,128)(2,1)S(1)}, bf16[1280,128]{1,0:T(8,128)(2,1)S(1)}, f32[8,128]{1,0:T(8,128)S(1)}) custom-call(s32[1]{0:T(128)} %bitcast.refs_0_, bf16[512,128]{1,0:T(8,128)(2,1)} %get-tuple-element.29.refs_1_.read_hbm, f32[512,128]{1,0:T(8,128)} %get-tuple-element.30.refs_2_.lead_hbm, f32[256,1280]{1,0:T(8,128)} %inside.2.refs_3_.low_hbm, ...), custom_call_target="tpu_custom_call" | custom-call | flops 1000000 | bytes 1000000 | tf_op jit(solution)/shard_map/pallas_call | solution.py:484
  87.1 6.2 %collective-permute-done.16.direct_l = bf16[1280,128]{1,0:T(8,128)(2,1)S(1)} collective-permute-done((bf16[1280,128]{1,0:T(8,128)(2,1)S(1)}, bf16[1280,128]{1,0:T(8,128)(2,1)S(1)}, u32[]{:S(2)}, u32[]{:S(2)}) %collective-permute-start.16) | collective-permute-done | bytes 327712 | tf_op jit(solution)/shard_map/ppermute | solution.py:550
  93.3 3.6 %collective-permute-done.17.direct_r = bf16[1280,128]{1,0:T(8,128)(2,1)S(1)} collective-permute-done((bf16[1280,128]{1,0:T(8,128)(2,1)S(1)}, bf16[1280,128]{1,0:T(8,128)(2,1)S(1)}, u32[]{:S(2)}, u32[]{:S(2)}) %collective-permute-start.17) | collective-permute-done | bytes 327712 | tf_op jit(solution)/shard_map/ppermute | solution.py:550
  96.9 1.2 %final.1 = bf16[128,2560]{1,0:T(8,128)(2,1)} custom-call(bf16[1280,128]{1,0:T(8,128)(2,1)S(1)} %get-tuple-element.39.own_l, bf16[1280,128]{1,0:T(8,128)(2,1)S(1)} %get-tuple-element.40.own_r, f32[8,128]{1,0:T(8,128)S(1)} %get-tuple-element.41.own_sq, bf16[1296,128]{1,0:T(8,128)(2,1)S(1)} %collective-permute-done.13.up, ...), custom_call_target="tpu_custom_call" | custom-call | flops 1000000 | bytes 1000000 | tf_op jit(solution)/shard_map/final/pallas_call | solution.py:537
  (40 shorter events, 0.5 us)
Async XLA Ops:
  0.9 2.6 %collective-permute-start = (bf16[16,2560]{1,0:T(8,128)(2,1)S(1)}, bf16[16,2560]{1,0:T(8,128)(2,1)S(1)}, u32[]{:S(2)}, u32[]{:S(2)}) collective-permute-start(bf16[16,2560]{1,0:T(8,128)(2,1)S(1)} %slice.99), channel_id=1, source_target_pairs={{0,4},{4,8},{8,12},{12,16},{16,20},{20,24},{24,28},{28,32},{32,36}... | collective-permute-start | bytes 245768 | tf_op jit(solution)/shard_map/ppermute | solution.py:648
  19.1 3.7 %collective-permute-start.1 = (bf16[656,128]{1,0:T(8,128)(2,1)S(1)}, bf16[656,128]{1,0:T(8,128)(2,1)S(1)}, u32[]{:S(2)}, u32[]{:S(2)}) collective-permute-start(bf16[656,128]{1,0:T(8,128)(2,1)S(1)} %pad_maximum_fusion.1), channel_id=1, source_target_pairs={{0,4},{4,0},{1,5},{5,1},{2,6},{6,2},{3,7},{7,3},{8,12},{12,8},{9,1... | collective-permute-start | bytes 503816 | tf_op jit(solution)/shard_map/ppermute | solution.py:550
  22.9 29.0 %copy-start.1 = (f32[20]{0:T(128)S(1)}, f32[20]{0:T(128)}, u32[]{:S(2)}) copy-start(f32[20]{0:T(128)} %param.25) | copy-start | bytes 244
  22.9 29.2 %copy-start = (f32[1280]{0:T(1024)S(1)}, f32[1280]{0:T(1024)}, u32[]{:S(2)}) copy-start(f32[1280]{0:T(1024)} %param.26) | copy-start | bytes 15364
  23.0 6.1 %collective-permute-start.2 = (bf16[176,128]{1,0:T(8,128)(2,1)S(1)}, bf16[176,128]{1,0:T(8,128)(2,1)S(1)}, u32[]{:S(2)}, u32[]{:S(2)}) collective-permute-start(bf16[176,128]{1,0:T(8,128)(2,1)S(1)} %get-tuple-element.91), channel_id=1, source_target_pairs={{0,24},{8,0},{16,8},{24,16},{1,25},{9,1},{17,9},{25,17},{2,26},{10... | collective-permute-start | bytes 135176 | tf_op jit(solution)/shard_map/ppermute | solution.py:550
  27.1 5.6 %collective-permute-start.3 = (bf16[176,128]{1,0:T(8,128)(2,1)S(1)}, bf16[176,128]{1,0:T(8,128)(2,1)S(1)}, u32[]{:S(2)}, u32[]{:S(2)}) collective-permute-start(bf16[176,128]{1,0:T(8,128)(2,1)S(1)} %get-tuple-element.90), channel_id=1, source_target_pairs={{0,16},{8,24},{16,0},{24,8},{1,17},{9,25},{17,1},{25,9},{2,18},{10... | collective-permute-start | bytes 135176 | tf_op jit(solution)/shard_map/ppermute | solution.py:550
  27.8 5.4 %collective-permute-start.4 = (bf16[176,128]{1,0:T(8,128)(2,1)S(1)}, bf16[176,128]{1,0:T(8,128)(2,1)S(1)}, u32[]{:S(2)}, u32[]{:S(2)}) collective-permute-start(bf16[176,128]{1,0:T(8,128)(2,1)S(1)} %get-tuple-element.89), channel_id=1, source_target_pairs={{0,8},{8,16},{16,24},{24,0},{1,9},{9,17},{17,25},{25,1},{2,10},{10... | collective-permute-start | bytes 135176 | tf_op jit(solution)/shard_map/ppermute | solution.py:550
  33.3 5.8 %collective-permute-start.5 = (bf16[176,128]{1,0:T(8,128)(2,1)S(1)}, bf16[176,128]{1,0:T(8,128)(2,1)S(1)}, u32[]{:S(2)}, u32[]{:S(2)}) collective-permute-start(bf16[176,128]{1,0:T(8,128)(2,1)S(1)} %pad_maximum_fusion.3), channel_id=1, source_target_pairs={{0,96},{32,0},{64,32},{96,64},{1,97},{33,1},{65,33},{97,65},{2,98}... | collective-permute-start | bytes 135176 | tf_op jit(solution)/shard_map/ppermute | solution.py:550
  37.4 5.6 %collective-permute-start.6 = (bf16[176,128]{1,0:T(8,128)(2,1)S(1)}, bf16[176,128]{1,0:T(8,128)(2,1)S(1)}, u32[]{:S(2)}, u32[]{:S(2)}) collective-permute-start(bf16[176,128]{1,0:T(8,128)(2,1)S(1)} %pad_maximum_fusion.3), channel_id=1, source_target_pairs={{0,64},{32,96},{64,0},{96,32},{1,65},{33,97},{65,1},{97,33},{2,66}... | collective-permute-start | bytes 135176 | tf_op jit(solution)/shard_map/ppermute | solution.py:550
  37.5 5.7 %collective-permute-start.7 = (bf16[176,128]{1,0:T(8,128)(2,1)S(1)}, bf16[176,128]{1,0:T(8,128)(2,1)S(1)}, u32[]{:S(2)}, u32[]{:S(2)}) collective-permute-start(bf16[176,128]{1,0:T(8,128)(2,1)S(1)} %pad_maximum_fusion.3), channel_id=1, source_target_pairs={{0,32},{32,64},{64,96},{96,0},{1,33},{33,65},{65,97},{97,1},{2,34}... | collective-permute-start | bytes 135176 | tf_op jit(solution)/shard_map/ppermute | solution.py:550
  43.4 4.3 %collective-permute-start.8 = (bf16[5,32,128]{2,1,0:T(8,128)(2,1)S(1)}, bf16[5,32,128]{2,1,0:T(8,128)(2,1)S(1)}, u32[]{:S(2)}, u32[]{:S(2)}) collective-permute-start(bf16[5,32,128]{2,1,0:T(8,128)(2,1)S(1)} %get-tuple-element.76), channel_id=1, source_target_pairs={{0,24},{8,0},{16,8},{24,16},{1,25},{9,1},{17,9},{25,17},{2,26},{10... | collective-permute-start | bytes 122888 | tf_op jit(solution)/shard_map/ppermute | solution.py:550
  45.5 5.5 %collective-permute-start.9 = (bf16[5,32,128]{2,1,0:T(8,128)(2,1)S(1)}, bf16[5,32,128]{2,1,0:T(8,128)(2,1)S(1)}, u32[]{:S(2)}, u32[]{:S(2)}) collective-permute-start(bf16[5,32,128]{2,1,0:T(8,128)(2,1)S(1)} %get-tuple-element.75), channel_id=1, source_target_pairs={{0,16},{8,24},{16,0},{24,8},{1,17},{9,25},{17,1},{25,9},{2,18},{10... | collective-permute-start | bytes 122888 | tf_op jit(solution)/shard_map/ppermute | solution.py:550
  46.4 5.2 %collective-permute-start.10 = (bf16[5,32,128]{2,1,0:T(8,128)(2,1)S(1)}, bf16[5,32,128]{2,1,0:T(8,128)(2,1)S(1)}, u32[]{:S(2)}, u32[]{:S(2)}) collective-permute-start(bf16[5,32,128]{2,1,0:T(8,128)(2,1)S(1)} %get-tuple-element.57), channel_id=1, source_target_pairs={{0,8},{8,16},{16,24},{24,0},{1,9},{9,17},{17,25},{25,1},{2,10},{10... | collective-permute-start | bytes 122888 | tf_op jit(solution)/shard_map/ppermute | solution.py:550
  51.8 11.5 %collective-permute-start.11 = (bf16[5,128,128]{2,1,0:T(8,128)(2,1)S(1)}, bf16[5,128,128]{2,1,0:T(8,128)(2,1)S(1)}, u32[]{:S(2)}, u32[]{:S(2)}) collective-permute-start(bf16[5,128,128]{2,1,0:T(8,128)(2,1)S(1)} %broadcast_select_fusion.2), channel_id=1, source_target_pairs={{0,4},{4,0},{1,5},{5,1},{2,6},{6,2},{3,7},{7,3},{8,12},{12,8},{9,1... | collective-permute-start | bytes 491528 | tf_op jit(solution)/shard_map/ppermute | solution.py:550
  65.1 10.5 %collective-permute-start.14 = (bf16[1296,128]{1,0:T(8,128)(2,1)S(1)}, bf16[1296,128]{1,0:T(8,128)(2,1)S(1)}, u32[]{:S(2)}, u32[]{:S(2)}) collective-permute-start(bf16[1296,128]{1,0:T(8,128)(2,1)S(1)} %get-tuple-element.50), channel_id=1, source_target_pairs={{0,3},{1,0},{2,1},{3,2},{4,7},{5,4},{6,5},{7,6},{8,11},{9,8},{10,9... | collective-permute-start | bytes 995336 | tf_op jit(solution)/shard_map/ppermute | solution.py:550
  67.9 11.6 %collective-permute-start.12 = (bf16[1296,128]{1,0:T(8,128)(2,1)S(1)}, bf16[1296,128]{1,0:T(8,128)(2,1)S(1)}, u32[]{:S(2)}, u32[]{:S(2)}) collective-permute-start(bf16[1296,128]{1,0:T(8,128)(2,1)S(1)} %get-tuple-element.48), channel_id=1, source_target_pairs={{0,1},{1,2},{2,3},{3,0},{4,5},{5,6},{6,7},{7,4},{8,9},{9,10},{10,1... | collective-permute-start | bytes 995336 | tf_op jit(solution)/shard_map/ppermute | solution.py:550
  75.7 21.2 %collective-permute-start.15 = (bf16[1296,128]{1,0:T(8,128)(2,1)S(1)}, bf16[1296,128]{1,0:T(8,128)(2,1)S(1)}, u32[]{:S(2)}, u32[]{:S(2)}) collective-permute-start(bf16[1296,128]{1,0:T(8,128)(2,1)S(1)} %shard_map.140), channel_id=1, source_target_pairs={{0,3},{1,0},{2,1},{3,2},{4,7},{5,4},{6,5},{7,6},{8,11},{9,8},{10,9... | collective-permute-start | bytes 995336 | tf_op jit(solution)/shard_map/ppermute | solution.py:550
  79.6 17.4 %collective-permute-start.13 = (bf16[1296,128]{1,0:T(8,128)(2,1)S(1)}, bf16[1296,128]{1,0:T(8,128)(2,1)S(1)}, u32[]{:S(2)}, u32[]{:S(2)}) collective-permute-start(bf16[1296,128]{1,0:T(8,128)(2,1)S(1)} %shard_map.139), channel_id=1, source_target_pairs={{0,1},{1,2},{2,3},{3,0},{4,5},{5,6},{6,7},{7,4},{8,9},{9,10},{10,1... | collective-permute-start | bytes 995336 | tf_op jit(solution)/shard_map/ppermute | solution.py:550
  79.6 13.7 %collective-permute-start.16 = (bf16[1280,128]{1,0:T(8,128)(2,1)S(1)}, bf16[1280,128]{1,0:T(8,128)(2,1)S(1)}, u32[]{:S(2)}, u32[]{:S(2)}) collective-permute-start(bf16[1280,128]{1,0:T(8,128)(2,1)S(1)} %get-tuple-element.51), channel_id=1, source_target_pairs={{0,3},{1,0},{2,1},{3,2},{4,7},{5,4},{6,5},{7,6},{8,11},{9,8},{10,9... | collective-permute-start | bytes 983048 | tf_op jit(solution)/shard_map/ppermute | solution.py:550
  82.9 14.0 %collective-permute-start.17 = (bf16[1280,128]{1,0:T(8,128)(2,1)S(1)}, bf16[1280,128]{1,0:T(8,128)(2,1)S(1)}, u32[]{:S(2)}, u32[]{:S(2)}) collective-permute-start(bf16[1280,128]{1,0:T(8,128)(2,1)S(1)} %get-tuple-element.52), channel_id=1, source_target_pairs={{0,1},{1,2},{2,3},{3,0},{4,5},{5,6},{6,7},{7,4},{8,9},{9,10},{10,1... | collective-permute-start | bytes 983048 | tf_op jit(solution)/shard_map/ppermute | solution.py:550

commit v10 on v9

--- a/solution.py
+++ b/solution.py
@@ -142,7 +142,8 @@
     gate_ref[:half, :] = dot(tok[above : above + half, :], w_gate[...]).astype(BF16)
     for g in range(channels // BLOCK):
         at = slice(g * BLOCK, (g + 1) * BLOCK)
-        x = conv(padded, at, taps, offset[:, at])
+        here = [offset[t : t + 1, :] for t in range(at.start // LANES, at.stop // LANES)]
+        x = conv(padded, at, taps, jnp.concatenate(here, axis=1))
         x_ref[:, at] = x
         running = jnp.zeros((STATE, BLOCK), F32)
         for s in range(spans):
@@ -647,7 +648,7 @@
     devices = lax.axis_size(SEQ)
     edge = lax.ppermute(tokens[rows - EDGE :], SEQ, [(i, i + 1) for i in range(devices - 1)])
     x, bc, read, cum, dt, lead, prior, gate, local, decay = first_part(
-        edge, tokens, proj_bc, proj_step.T, proj_inner, proj_gate, conv_inner, offset_inner[None],
+        edge, tokens, proj_bc, proj_step.T, proj_inner, proj_gate, conv_inner, offset_inner.reshape(-1, LANES),
         conv_bc, offset_bc[None], step_bias[None], decay_log[None],
     )
     state = incoming_state(local, decay[:, 0])

time: 98.4 us -> 98.3 us (level)
  local copies, waits for them, and re-layouts: 2.4 us -> 1.1 us
    broadcast_in_dim x1 -> x0, local copies, waits for them, and re-layouts: 1.3 us -> none  [per_device(): offset_inner[None]]
  transfers between devices with their start and end apart: 18 -> 18, of which waited for: 13 -> 14; matrix products, arithmetic and copies ran while one was open for 2% -> 0% of each run, Pallas kernels for 22% -> 22%
where the time goes in v10:
time: 98.3 us; the launch traced here: 98 us
  Pallas kernels  40.1 us (41%)
  starting transfers between devices  28.6 us (29%)
  waiting for transfers between devices  26.9 us (27%)
  local copies, waits for them, and re-layouts  1.1 us (1%)
  other arithmetic  1.01 us (1%)
    ppermute x17, starting transfers between devices, ring(): lax.ppermute(value, axis, [(i, (i + distance) % size) for i in range(size)])  27.4 us
    ppermute x17, waiting for transfers between devices, ring(): lax.ppermute(value, axis, [(i, (i + distance) % size) for i in range(size)])  26 us
    pallas_call x1, Pallas kernels, first_part(): pl.pallas_call(first_kernel, in_specs=[vmem] + [hbm] * (5 + len(small)),...  15.4 us
    pallas_call x3, Pallas kernels, tail(): pl.pallas_call(functools.partial(tail_kernel, HEADS * HEADDIM, which is N...  12.1 us
    pallas_call x2, Pallas kernels, inside(): pl.pallas_call(functools.partial(inside_kernel, first), grid=(count,), in...  8.05 us
    pallas_call x1, Pallas kernels, ready(): pl.pallas_call(ready_kernel, in_specs=[pl.BlockSpec(memory_space=pltpu.SM...  3.14 us
  transfers between devices with their start and end apart: 18, of which 14 were waited for; matrix products, arithmetic and copies ran while one was open for 0% of the time, Pallas kernels for 22%

profile of v10, /device:TPU:0, one launch (start us, length us, event | category | flops | bytes accessed | tf_op | source)
XLA Modules:
  0.0 98.0 jit_solution(14116689457022272821)
XLA Ops:
  0.0 0.9 slice.99
  0.9 1.3 %collective-permute-start = (bf16[16,2560]{1,0:T(8,128)(2,1)S(1)}, bf16[16,2560]{1,0:T(8,128)(2,1)S(1)}, u32[]{:S(2)}, u32[]{:S(2)}) collective-permute-start(bf16[16,2560]{1,0:T(8,128)(2,1)S(1)} %slice.99), channel_id=1, source_target_pairs={{0,4},{4,8},{8,12},{12,16},{16,20},{20,24},{24,28},{28,32},{32,36}... | collective-permute-start | bytes 245768 | tf_op jit(solution)/shard_map/ppermute | solution.py:649
  2.2 0.9 collective-permute-done.edge
  3.1 15.4 %first.1 = (bf16[512,1280]{1,0:T(8,128)(2,1)}, bf16[512,256]{1,0:T(8,128)(2,1)}, bf16[512,128]{1,0:T(8,128)(2,1)}, f32[512,128]{1,0:T(8,128)}, f32[512,128]{1,0:...) custom-call(bf16[16,2560]{1,0:T(8,128)(2,1)S(1)} %collective-permute, ...), custom_call_target="tpu_custom_call" | custom-call | flops 7717519360 | bytes 17039360 | tf_op jit(solution)/shard_map/first/pallas_call | solution.py:210
  18.6 3.1 %collective-permute-start.1 = (bf16[656,128]{1,0:T(8,128)(2,1)S(1)}, bf16[656,128]{1,0:T(8,128)(2,1)S(1)}, u32[]{:S(2)}, u32[]{:S(2)}) collective-permute-start(bf16[656,128]{1,0:T(8,128)(2,1)S(1)} %pad_maximum_fusion.1), channel_id=1, source_target_pairs={{0,4},{4,0},{1,5},{5,1},{2,6},{6,2},{3,7},{7,3},{8,12},{12,8},{9,1... | collective-permute-start | bytes 503816 | tf_op jit(solution)/shard_map/ppermute | solution.py:551
  21.7 1.0 %collective-permute-done.1 = bf16[656,128]{1,0:T(8,128)(2,1)S(1)} collective-permute-done((bf16[656,128]{1,0:T(8,128)(2,1)S(1)}, bf16[656,128]{1,0:T(8,128)(2,1)S(1)}, u32[]{:S(2)}, u32[]{:S(2)}) %collective-permute-start.1) | collective-permute-done | bytes 167968 | tf_op jit(solution)/shard_map/ppermute | solution.py:551
  22.8 0.1 fusion
  23.0 4.1 %collective-permute-start.2 = (bf16[176,128]{1,0:T(8,128)(2,1)S(1)}, bf16[176,128]{1,0:T(8,128)(2,1)S(1)}, u32[]{:S(2)}, u32[]{:S(2)}) collective-permute-start(bf16[176,128]{1,0:T(8,128)(2,1)S(1)} %get-tuple-element.91), channel_id=1, source_target_pairs={{0,24},{8,0},{16,8},{24,16},{1,25},{9,1},{17,9},{25,17},{2,26},{10... | collective-permute-start | bytes 135176 | tf_op jit(solution)/shard_map/ppermute | solution.py:551
  27.1 0.6 collective-permute-start.3
  27.7 1.0 collective-permute-start.4
  28.7 0.4 collective-permute-done.2
  29.1 3.5 %collective-permute-done.3 = bf16[176,128]{1,0:T(8,128)(2,1)S(1)} collective-permute-done((bf16[176,128]{1,0:T(8,128)(2,1)S(1)}, bf16[176,128]{1,0:T(8,128)(2,1)S(1)}, u32[]{:S(2)}, u32[]{:S(2)}) %collective-permute-start.3) | collective-permute-done | bytes 45088 | tf_op jit(solution)/shard_map/ppermute | solution.py:551
  32.7 0.5 collective-permute-done.4
  33.2 0.1 fusion.2
  33.3 4.1 %collective-permute-start.5 = (bf16[176,128]{1,0:T(8,128)(2,1)S(1)}, bf16[176,128]{1,0:T(8,128)(2,1)S(1)}, u32[]{:S(2)}, u32[]{:S(2)}) collective-permute-start(bf16[176,128]{1,0:T(8,128)(2,1)S(1)} %pad_maximum_fusion.3), channel_id=1, source_target_pairs={{0,96},{32,0},{64,32},{96,64},{1,97},{33,1},{65,33},{97,65},{2,98}... | collective-permute-start | bytes 135176 | tf_op jit(solution)/shard_map/ppermute | solution.py:551
  37.4 1.3 %collective-permute-start.7 = (bf16[176,128]{1,0:T(8,128)(2,1)S(1)}, bf16[176,128]{1,0:T(8,128)(2,1)S(1)}, u32[]{:S(2)}, u32[]{:S(2)}) collective-permute-start(bf16[176,128]{1,0:T(8,128)(2,1)S(1)} %pad_maximum_fusion.3), channel_id=1, source_target_pairs={{0,32},{32,64},{64,96},{96,0},{1,33},{33,65},{65,97},{97,1},{2,34}... | collective-permute-start | bytes 135176 | tf_op jit(solution)/shard_map/ppermute | solution.py:551
  38.7 0.4 collective-permute-done.5
  39.1 3.9 %collective-permute-done.6 = bf16[176,128]{1,0:T(8,128)(2,1)S(1)} collective-permute-done((bf16[176,128]{1,0:T(8,128)(2,1)S(1)}, bf16[176,128]{1,0:T(8,128)(2,1)S(1)}, u32[]{:S(2)}, u32[]{:S(2)}) %collective-permute-start.6) | collective-permute-done | bytes 45088 | tf_op jit(solution)/shard_map/ppermute | solution.py:551
  43.1 0.1 collective-permute-done.7
  43.2 0.1 select_convert_fusion.1
  43.4 2.1 %collective-permute-start.8 = (bf16[5,32,128]{2,1,0:T(8,128)(2,1)S(1)}, bf16[5,32,128]{2,1,0:T(8,128)(2,1)S(1)}, u32[]{:S(2)}, u32[]{:S(2)}) collective-permute-start(bf16[5,32,128]{2,1,0:T(8,128)(2,1)S(1)} %get-tuple-element.76), channel_id=1, source_target_pairs={{0,24},{8,0},{16,8},{24,16},{1,25},{9,1},{17,9},{25,17},{2,26},{10... | collective-permute-start | bytes 122888 | tf_op jit(solution)/shard_map/ppermute | solution.py:551
  45.4 0.9 collective-permute-start.9
  46.3 0.3 collective-permute-start.10
  46.6 1.0 %collective-permute-done.8 = bf16[5,32,128]{2,1,0:T(8,128)(2,1)S(1)} collective-permute-done((bf16[5,32,128]{2,1,0:T(8,128)(2,1)S(1)}, bf16[5,32,128]{2,1,0:T(8,128)(2,1)S(1)}, u32[]{:S(2)}, u32[]{:S(2)}) %collective-permute-start.8) | collective-permute-done | bytes 40992 | tf_op jit(solution)/shard_map/ppermute | solution.py:551
  47.6 3.3 %collective-permute-done.9 = bf16[5,32,128]{2,1,0:T(8,128)(2,1)S(1)} collective-permute-done((bf16[5,32,128]{2,1,0:T(8,128)(2,1)S(1)}, bf16[5,32,128]{2,1,0:T(8,128)(2,1)S(1)}, u32[]{:S(2)}, u32[]{:S(2)}) %collective-permute-start.9) | collective-permute-done | bytes 40992 | tf_op jit(solution)/shard_map/ppermute | solution.py:551
  50.9 0.6 collective-permute-done.10
  51.7 0.1 broadcast_select_fusion.2
  51.8 0.1 collective-permute-start.11
  51.9 0.1 broadcast_in_dim.31
  52.0 0.1 broadcast_in_dim_reshape.3.skip_ref
  52.0 4.0 %inside.3.refs_4_.high_hbm = f32[256,1280]{1,0:T(8,128)} custom-call(bf16[512,1280]{1,0:T(8,128)(2,1)} %get-tuple-element.31.x_ref, bf16[512,256]{1,0:T(8,128)(2,1)} %get-tuple-element.32.bc_ref, f32[512,128]{1,0:T(8,128)} %get-tuple-element.33.cum_ref, f32[512,128]{1,0:T(8,128)} %get-tuple-element.34.dt_ref, ...), custom_call_target="tpu_custom_call" | custom-call | flops 1000000 | bytes 1000000 | tf_op jit(solution)/shard_map/inside/pallas_call | solution.py:277
  56.1 4.0 %inside.2.refs_3_.low_hbm = f32[256,1280]{1,0:T(8,128)} custom-call(bf16[512,1280]{1,0:T(8,128)(2,1)} %get-tuple-element.31.x_ref, bf16[512,256]{1,0:T(8,128)(2,1)} %get-tuple-element.32.bc_ref, f32[512,128]{1,0:T(8,128)} %get-tuple-element.33.cum_ref, f32[512,128]{1,0:T(8,128)} %get-tuple-element.34.dt_ref, ...), custom_call_target="tpu_custom_call" | custom-call | flops 1000000 | bytes 1000000 | tf_op jit(solution)/shard_map/inside/pallas_call | solution.py:277
  60.1 3.1 %ready.1 = (bf16[128,128]{1,0:T(8,128)(2,1)S(1)}, f32[128,128]{1,0:T(8,128)S(1)}, f32[128,1280]{1,0:T(8,128)S(1)}, bf16[128,1280]{1,0:T(8,128)(2,1)S(1)}, bf16[1280,2560]{1,0:T(8,128)(2,1)S(1)}) custom-call(s32[1]{0:T(128)} %bitcast.25.which, bf16[512,128]{1,0:T(8,128)(2,1)} %get-tuple-element.29.refs_1_.read_hbm, ...), custom_call_target="tpu_custom_call" | custom-call | flops 1000000 | bytes 1000000 | tf_op jit(solution)/shard_map/ready/pallas_call | solution.py:369
  63.2 0.2 broadcast_select_fusion.1
  63.5 1.6 %shard_map.138 = (bf16[1296,128]{1,0:T(8,128)(2,1)S(1)}, bf16[1296,128]{1,0:T(8,128)(2,1)S(1)}) custom-call(bf16[128,128]{1,0:T(8,128)(2,1)S(1)} %get-tuple-element.43.refs_0_, f32[128,128]{1,0:T(8,128)S(1)} %get-tuple-element.44.refs_1_, f32[128,1280]{1,0:T(8,128)S(1)} %get-tuple-element.45.refs_2_, bf16[128,1280]{1,0:T(8,128)(2,1)S(1)} %get-tuple-element.46.refs_3_, ...), custom_call_target="tpu_custom_call" | custom-call | flops 1000000 | bytes 1000000 | tf_op jit(solution)/shard_map/pallas_call | solution.py:485
  65.1 2.8 %collective-permute-start.14 = (bf16[1296,128]{1,0:T(8,128)(2,1)S(1)}, bf16[1296,128]{1,0:T(8,128)(2,1)S(1)}, u32[]{:S(2)}, u32[]{:S(2)}) collective-permute-start(bf16[1296,128]{1,0:T(8,128)(2,1)S(1)} %get-tuple-element.50), channel_id=1, source_target_pairs={{0,3},{1,0},{2,1},{3,2},{4,7},{5,4},{6,5},{7,6},{8,11},{9,8},{10,9... | collective-permute-start | bytes 995336 | tf_op jit(solution)/shard_map/ppermute | solution.py:551
  67.9 0.1 pad_add_fusion.refs_0_
  68.0 6.3 %shard_map.137 = (bf16[1296,128]{1,0:T(8,128)(2,1)S(1)}, bf16[1280,128]{1,0:T(8,128)(2,1)S(1)}, bf16[1280,128]{1,0:T(8,128)(2,1)S(1)}, bf16[1296,128]{1,0:T(8,128)(2,1)S(1)}) custom-call(s32[2]{0:T(128)S(1)} %pad_add_fusion.refs_0_, bf16[512,128]{1,0:T(8,128)(2,1)} %get-tuple-element.29.refs_1_.read_hbm, f32[512,128]{1,0:T(8,128)} %get-tuple-element.30.refs_2_.lead_hbm, ...), custom_call_target="tpu_custom_call" | custom-call | flops 1000000 | bytes 1000000 | tf_op jit(solution)/shard_map/pallas_call | solution.py:485
  74.3 1.3 %collective-permute-done.14.b_ref = bf16[1296,128]{1,0:T(8,128)(2,1)S(1)} collective-permute-done((bf16[1296,128]{1,0:T(8,128)(2,1)S(1)}, bf16[1296,128]{1,0:T(8,128)(2,1)S(1)}, u32[]{:S(2)}, u32[]{:S(2)}) %collective-permute-start.14) | collective-permute-done | bytes 331808 | tf_op jit(solution)/shard_map/ppermute | solution.py:551
  75.6 0.1 shard_map.140
  75.7 3.8 %collective-permute-start.15 = (bf16[1296,128]{1,0:T(8,128)(2,1)S(1)}, bf16[1296,128]{1,0:T(8,128)(2,1)S(1)}, u32[]{:S(2)}, u32[]{:S(2)}) collective-permute-start(bf16[1296,128]{1,0:T(8,128)(2,1)S(1)} %shard_map.140), channel_id=1, source_target_pairs={{0,3},{1,0},{2,1},{3,2},{4,7},{5,4},{6,5},{7,6},{8,11},{9,8},{10,9... | collective-permute-start | bytes 995336 | tf_op jit(solution)/shard_map/ppermute | solution.py:551
  79.4 0.1 shard_map.139
  79.5 0.1 collective-permute-start.13
  79.6 3.2 %collective-permute-start.16 = (bf16[1280,128]{1,0:T(8,128)(2,1)S(1)}, bf16[1280,128]{1,0:T(8,128)(2,1)S(1)}, u32[]{:S(2)}, u32[]{:S(2)}) collective-permute-start(bf16[1280,128]{1,0:T(8,128)(2,1)S(1)} %get-tuple-element.51), channel_id=1, source_target_pairs={{0,3},{1,0},{2,1},{3,2},{4,7},{5,4},{6,5},{7,6},{8,11},{9,8},{10,9... | collective-permute-start | bytes 983048 | tf_op jit(solution)/shard_map/ppermute | solution.py:551
  82.8 4.2 %shard_map.136 = (bf16[1280,128]{1,0:T(8,128)(2,1)S(1)}, bf16[1280,128]{1,0:T(8,128)(2,1)S(1)}, f32[8,128]{1,0:T(8,128)S(1)}) custom-call(s32[1]{0:T(128)} %bitcast.refs_0_, bf16[512,128]{1,0:T(8,128)(2,1)} %get-tuple-element.29.refs_1_.read_hbm, f32[512,128]{1,0:T(8,128)} %get-tuple-element.30.refs_2_.lead_hbm, f32[256,1280]{1,0:T(8,128)} %inside.2.refs_3_.low_hbm, ...), custom_call_target="tpu_custom_call" | custom-call | flops 1000000 | bytes 1000000 | tf_op jit(solution)/shard_map/pallas_call | solution.py:485
  87.1 6.2 %collective-permute-done.16.direct_l = bf16[1280,128]{1,0:T(8,128)(2,1)S(1)} collective-permute-done((bf16[1280,128]{1,0:T(8,128)(2,1)S(1)}, bf16[1280,128]{1,0:T(8,128)(2,1)S(1)}, u32[]{:S(2)}, u32[]{:S(2)}) %collective-permute-start.16) | collective-permute-done | bytes 327712 | tf_op jit(solution)/shard_map/ppermute | solution.py:551
  93.3 3.6 %collective-permute-done.17.direct_r = bf16[1280,128]{1,0:T(8,128)(2,1)S(1)} collective-permute-done((bf16[1280,128]{1,0:T(8,128)(2,1)S(1)}, bf16[1280,128]{1,0:T(8,128)(2,1)S(1)}, u32[]{:S(2)}, u32[]{:S(2)}) %collective-permute-start.17) | collective-permute-done | bytes 327712 | tf_op jit(solution)/shard_map/ppermute | solution.py:551
  96.9 1.2 %final.1 = bf16[128,2560]{1,0:T(8,128)(2,1)} custom-call(bf16[1280,128]{1,0:T(8,128)(2,1)S(1)} %get-tuple-element.39.own_l, bf16[1280,128]{1,0:T(8,128)(2,1)S(1)} %get-tuple-element.40.own_r, f32[8,128]{1,0:T(8,128)S(1)} %get-tuple-element.41.own_sq, bf16[1296,128]{1,0:T(8,128)(2,1)S(1)} %collective-permute-done.13.up, ...), custom_call_target="tpu_custom_call" | custom-call | flops 1000000 | bytes 1000000 | tf_op jit(solution)/shard_map/final/pallas_call | solution.py:538
  (39 shorter events, 0.5 us)
Async XLA Ops:
  0.9 2.2 %collective-permute-start = (bf16[16,2560]{1,0:T(8,128)(2,1)S(1)}, bf16[16,2560]{1,0:T(8,128)(2,1)S(1)}, u32[]{:S(2)}, u32[]{:S(2)}) collective-permute-start(bf16[16,2560]{1,0:T(8,128)(2,1)S(1)} %slice.99), channel_id=1, source_target_pairs={{0,4},{4,8},{8,12},{12,16},{16,20},{20,24},{24,28},{28,32},{32,36}... | collective-permute-start | bytes 245768 | tf_op jit(solution)/shard_map/ppermute | solution.py:649
  18.6 4.1 %collective-permute-start.1 = (bf16[656,128]{1,0:T(8,128)(2,1)S(1)}, bf16[656,128]{1,0:T(8,128)(2,1)S(1)}, u32[]{:S(2)}, u32[]{:S(2)}) collective-permute-start(bf16[656,128]{1,0:T(8,128)(2,1)S(1)} %pad_maximum_fusion.1), channel_id=1, source_target_pairs={{0,4},{4,0},{1,5},{5,1},{2,6},{6,2},{3,7},{7,3},{8,12},{12,8},{9,1... | collective-permute-start | bytes 503816 | tf_op jit(solution)/shard_map/ppermute | solution.py:551
  22.9 29.0 %copy-start.1 = (f32[20]{0:T(128)S(1)}, f32[20]{0:T(128)}, u32[]{:S(2)}) copy-start(f32[20]{0:T(128)} %param.25) | copy-start | bytes 244
  22.9 29.2 %copy-start = (f32[1280]{0:T(1024)S(1)}, f32[1280]{0:T(1024)}, u32[]{:S(2)}) copy-start(f32[1280]{0:T(1024)} %param.26) | copy-start | bytes 15364
  23.0 6.1 %collective-permute-start.2 = (bf16[176,128]{1,0:T(8,128)(2,1)S(1)}, bf16[176,128]{1,0:T(8,128)(2,1)S(1)}, u32[]{:S(2)}, u32[]{:S(2)}) collective-permute-start(bf16[176,128]{1,0:T(8,128)(2,1)S(1)} %get-tuple-element.91), channel_id=1, source_target_pairs={{0,24},{8,0},{16,8},{24,16},{1,25},{9,1},{17,9},{25,17},{2,26},{10... | collective-permute-start | bytes 135176 | tf_op jit(solution)/shard_map/ppermute | solution.py:551
  27.1 5.6 %collective-permute-start.3 = (bf16[176,128]{1,0:T(8,128)(2,1)S(1)}, bf16[176,128]{1,0:T(8,128)(2,1)S(1)}, u32[]{:S(2)}, u32[]{:S(2)}) collective-permute-start(bf16[176,128]{1,0:T(8,128)(2,1)S(1)} %get-tuple-element.90), channel_id=1, source_target_pairs={{0,16},{8,24},{16,0},{24,8},{1,17},{9,25},{17,1},{25,9},{2,18},{10... | collective-permute-start | bytes 135176 | tf_op jit(solution)/shard_map/ppermute | solution.py:551
  27.7 5.4 %collective-permute-start.4 = (bf16[176,128]{1,0:T(8,128)(2,1)S(1)}, bf16[176,128]{1,0:T(8,128)(2,1)S(1)}, u32[]{:S(2)}, u32[]{:S(2)}) collective-permute-start(bf16[176,128]{1,0:T(8,128)(2,1)S(1)} %get-tuple-element.89), channel_id=1, source_target_pairs={{0,8},{8,16},{16,24},{24,0},{1,9},{9,17},{17,25},{25,1},{2,10},{10... | collective-permute-start | bytes 135176 | tf_op jit(solution)/shard_map/ppermute | solution.py:551
  33.3 5.8 %collective-permute-start.5 = (bf16[176,128]{1,0:T(8,128)(2,1)S(1)}, bf16[176,128]{1,0:T(8,128)(2,1)S(1)}, u32[]{:S(2)}, u32[]{:S(2)}) collective-permute-start(bf16[176,128]{1,0:T(8,128)(2,1)S(1)} %pad_maximum_fusion.3), channel_id=1, source_target_pairs={{0,96},{32,0},{64,32},{96,64},{1,97},{33,1},{65,33},{97,65},{2,98}... | collective-permute-start | bytes 135176 | tf_op jit(solution)/shard_map/ppermute | solution.py:551
  37.4 5.6 %collective-permute-start.6 = (bf16[176,128]{1,0:T(8,128)(2,1)S(1)}, bf16[176,128]{1,0:T(8,128)(2,1)S(1)}, u32[]{:S(2)}, u32[]{:S(2)}) collective-permute-start(bf16[176,128]{1,0:T(8,128)(2,1)S(1)} %pad_maximum_fusion.3), channel_id=1, source_target_pairs={{0,64},{32,96},{64,0},{96,32},{1,65},{33,97},{65,1},{97,33},{2,66}... | collective-permute-start | bytes 135176 | tf_op jit(solution)/shard_map/ppermute | solution.py:551
  37.4 5.7 %collective-permute-start.7 = (bf16[176,128]{1,0:T(8,128)(2,1)S(1)}, bf16[176,128]{1,0:T(8,128)(2,1)S(1)}, u32[]{:S(2)}, u32[]{:S(2)}) collective-permute-start(bf16[176,128]{1,0:T(8,128)(2,1)S(1)} %pad_maximum_fusion.3), channel_id=1, source_target_pairs={{0,32},{32,64},{64,96},{96,0},{1,33},{33,65},{65,97},{97,1},{2,34}... | collective-permute-start | bytes 135176 | tf_op jit(solution)/shard_map/ppermute | solution.py:551
  43.4 4.3 %collective-permute-start.8 = (bf16[5,32,128]{2,1,0:T(8,128)(2,1)S(1)}, bf16[5,32,128]{2,1,0:T(8,128)(2,1)S(1)}, u32[]{:S(2)}, u32[]{:S(2)}) collective-permute-start(bf16[5,32,128]{2,1,0:T(8,128)(2,1)S(1)} %get-tuple-element.76), channel_id=1, source_target_pairs={{0,24},{8,0},{16,8},{24,16},{1,25},{9,1},{17,9},{25,17},{2,26},{10... | collective-permute-start | bytes 122888 | tf_op jit(solution)/shard_map/ppermute | solution.py:551
  45.4 5.5 %collective-permute-start.9 = (bf16[5,32,128]{2,1,0:T(8,128)(2,1)S(1)}, bf16[5,32,128]{2,1,0:T(8,128)(2,1)S(1)}, u32[]{:S(2)}, u32[]{:S(2)}) collective-permute-start(bf16[5,32,128]{2,1,0:T(8,128)(2,1)S(1)} %get-tuple-element.75), channel_id=1, source_target_pairs={{0,16},{8,24},{16,0},{24,8},{1,17},{9,25},{17,1},{25,9},{2,18},{10... | collective-permute-start | bytes 122888 | tf_op jit(solution)/shard_map/ppermute | solution.py:551
  46.3 5.2 %collective-permute-start.10 = (bf16[5,32,128]{2,1,0:T(8,128)(2,1)S(1)}, bf16[5,32,128]{2,1,0:T(8,128)(2,1)S(1)}, u32[]{:S(2)}, u32[]{:S(2)}) collective-permute-start(bf16[5,32,128]{2,1,0:T(8,128)(2,1)S(1)} %get-tuple-element.57), channel_id=1, source_target_pairs={{0,8},{8,16},{16,24},{24,0},{1,9},{9,17},{17,25},{25,1},{2,10},{10... | collective-permute-start | bytes 122888 | tf_op jit(solution)/shard_map/ppermute | solution.py:551
  51.8 11.5 %collective-permute-start.11 = (bf16[5,128,128]{2,1,0:T(8,128)(2,1)S(1)}, bf16[5,128,128]{2,1,0:T(8,128)(2,1)S(1)}, u32[]{:S(2)}, u32[]{:S(2)}) collective-permute-start(bf16[5,128,128]{2,1,0:T(8,128)(2,1)S(1)} %broadcast_select_fusion.2), channel_id=1, source_target_pairs={{0,4},{4,0},{1,5},{5,1},{2,6},{6,2},{3,7},{7,3},{8,12},{12,8},{9,1... | collective-permute-start | bytes 491528 | tf_op jit(solution)/shard_map/ppermute | solution.py:551
  65.1 10.5 %collective-permute-start.14 = (bf16[1296,128]{1,0:T(8,128)(2,1)S(1)}, bf16[1296,128]{1,0:T(8,128)(2,1)S(1)}, u32[]{:S(2)}, u32[]{:S(2)}) collective-permute-start(bf16[1296,128]{1,0:T(8,128)(2,1)S(1)} %get-tuple-element.50), channel_id=1, source_target_pairs={{0,3},{1,0},{2,1},{3,2},{4,7},{5,4},{6,5},{7,6},{8,11},{9,8},{10,9... | collective-permute-start | bytes 995336 | tf_op jit(solution)/shard_map/ppermute | solution.py:551
  67.9 11.6 %collective-permute-start.12 = (bf16[1296,128]{1,0:T(8,128)(2,1)S(1)}, bf16[1296,128]{1,0:T(8,128)(2,1)S(1)}, u32[]{:S(2)}, u32[]{:S(2)}) collective-permute-start(bf16[1296,128]{1,0:T(8,128)(2,1)S(1)} %get-tuple-element.48), channel_id=1, source_target_pairs={{0,1},{1,2},{2,3},{3,0},{4,5},{5,6},{6,7},{7,4},{8,9},{9,10},{10,1... | collective-permute-start | bytes 995336 | tf_op jit(solution)/shard_map/ppermute | solution.py:551
  75.7 21.2 %collective-permute-start.15 = (bf16[1296,128]{1,0:T(8,128)(2,1)S(1)}, bf16[1296,128]{1,0:T(8,128)(2,1)S(1)}, u32[]{:S(2)}, u32[]{:S(2)}) collective-permute-start(bf16[1296,128]{1,0:T(8,128)(2,1)S(1)} %shard_map.140), channel_id=1, source_target_pairs={{0,3},{1,0},{2,1},{3,2},{4,7},{5,4},{6,5},{7,6},{8,11},{9,8},{10,9... | collective-permute-start | bytes 995336 | tf_op jit(solution)/shard_map/ppermute | solution.py:551
  79.5 17.4 %collective-permute-start.13 = (bf16[1296,128]{1,0:T(8,128)(2,1)S(1)}, bf16[1296,128]{1,0:T(8,128)(2,1)S(1)}, u32[]{:S(2)}, u32[]{:S(2)}) collective-permute-start(bf16[1296,128]{1,0:T(8,128)(2,1)S(1)} %shard_map.139), channel_id=1, source_target_pairs={{0,1},{1,2},{2,3},{3,0},{4,5},{5,6},{6,7},{7,4},{8,9},{9,10},{10,1... | collective-permute-start | bytes 995336 | tf_op jit(solution)/shard_map/ppermute | solution.py:551
  79.6 13.7 %collective-permute-start.16 = (bf16[1280,128]{1,0:T(8,128)(2,1)S(1)}, bf16[1280,128]{1,0:T(8,128)(2,1)S(1)}, u32[]{:S(2)}, u32[]{:S(2)}) collective-permute-start(bf16[1280,128]{1,0:T(8,128)(2,1)S(1)} %get-tuple-element.51), channel_id=1, source_target_pairs={{0,3},{1,0},{2,1},{3,2},{4,7},{5,4},{6,5},{7,6},{8,11},{9,8},{10,9... | collective-permute-start | bytes 983048 | tf_op jit(solution)/shard_map/ppermute | solution.py:551
  82.8 14.0 %collective-permute-start.17 = (bf16[1280,128]{1,0:T(8,128)(2,1)S(1)}, bf16[1280,128]{1,0:T(8,128)(2,1)S(1)}, u32[]{:S(2)}, u32[]{:S(2)}) collective-permute-start(bf16[1280,128]{1,0:T(8,128)(2,1)S(1)} %get-tuple-element.52), channel_id=1, source_target_pairs={{0,1},{1,2},{2,3},{3,0},{4,5},{5,6},{6,7},{7,4},{8,9},{9,10},{10,1... | collective-permute-start | bytes 983048 | tf_op jit(solution)/shard_map/ppermute | solution.py:551
